TPU v7x, 32 devices: a whole 2x2x4 slice. The times are simulated.
32 devices in a mesh: tx: 8 (over y, x, core), ty: 4 (over z).
Axes of the slice: x: 2, y: 2, z: 4, core: 2. Of those that a mesh axis runs over, the one named last changes fastest.
Arguments:
- potential: float32 [512, 1024], P('tx', 'ty'), may hold values from -6 to 6
- elevation: float32 [512, 1024], P('tx', 'ty'), may hold values from -5 to 5
- normal_flux: float32 [512, 1024], P('tx', 'ty'), may hold values from -4 to 4
- box_owner: int32 [512, 1024], P('tx', 'ty'), may hold values from 0 to 31, as said below
- box_place: int32 [512, 1024], P('tx', 'ty'), may hold values from 0 to 16383, as said below
- near_boxes: int32 [4096, 8], P(('tx', 'ty')), may hold values from 0 to 4095, as said below
Outputs:
- elevation_rate: float32 [512, 1024], P('tx', 'ty')
- potential_rate: float32 [512, 1024], P('tx', 'ty')
Inputs may be any that keep to these rules, and one draw needn't show every extreme that they name: Devices are numbered p times the number of ty devices plus q, for position p along tx and q along ty. box_owner 64 * 256 + box_place is a permutation of the 524288 positions. A node in the tile of device (p, q) has its owner at position (p or p - 1, q or q - 1) along tx and ty, taken modulo the axis sizes. The nodes of one tile with one owner other than the tile's own device number at most 6400, and exactly 6400 for some pair of devices. `box_place`: see box_owner. near_boxes[b, 0] = b; the other entries are distinct boxes other than b, each within 128 of b in box number, a distance of exactly 128 occurring in both directions.
All inputs are finite; a program needn't handle non-finite values.
Results may differ from a plain program's by a relative error of at most 0.0049.
Values sent between devices are 32-bit elements; how exact they have to be, the bound alone decides.
No kernel may reach another device: no remote copies, remote signals or barrier semaphores. Data moves between devices by JAX's collectives and lax.ppermute only.
A program may use at most 128 MiB of HBM per device.

v0:
```python
import math

import jax
import jax.numpy as jnp
from jax import lax
from jax.sharding import PartitionSpec as P

NEAR = 8


def padded_2(block, sides, width, periodic):
    for axis, dim in sides:
        count = lax.axis_size(axis)
        forward = [(i, i + 1) for i in range(count - 1)]
        if periodic:
            forward.append((count - 1, 0))
        backward = [(target, source) for source, target in forward]
        low = lax.ppermute(
            lax.slice_in_dim(block, block.shape[dim] - width, None, axis=dim), axis, forward
        )
        high = lax.ppermute(lax.slice_in_dim(block, 0, width, axis=dim), axis, backward)
        block = jnp.concatenate([low, block, high], axis=dim)
    return block


def from_behind(value, axis, steps):
    count = lax.axis_size(axis)
    pairs = [(source, (source + steps) % count) for source in range(count)]
    return lax.ppermute(value, axis, pairs)


def surface_slopes(fields):
    padded = padded_2(fields, (("tx", 1), ("ty", 2)), 2, True)
    middle_cols = padded[:, :, 2:-2]
    along_rows = (
        middle_cols[:, 0:-4]
        - 8.0 * middle_cols[:, 1:-3]
        + 8.0 * middle_cols[:, 3:-1]
        - middle_cols[:, 4:]
    ) / 12.0
    central_rows = padded[:, 2:-2, :]
    along_cols = (
        central_rows[:, :, 0:-4]
        - 8.0 * central_rows[:, :, 1:-3]
        + 8.0 * central_rows[:, :, 3:-1]
        - central_rows[:, :, 4:]
    ) / 12.0
    return (along_rows, along_cols)


def kernel_apply(targets, sources):
    delta_x = targets[0][:, None, :, None] - sources[0][:, :, None, :]
    delta_y = targets[1][:, None, :, None] - sources[1][:, :, None, :]
    delta_z = targets[2][:, None, :, None] - sources[2][:, :, None, :]
    squared = delta_x * delta_x + delta_y * delta_y + delta_z * delta_z + 0.04
    inverse = lax.rsqrt(squared)
    single = inverse.astype(jnp.bfloat16)
    double = (delta_z * inverse * inverse * inverse).astype(jnp.bfloat16)
    flux_low = sources[4].astype(jnp.bfloat16)
    pot_low = sources[3].astype(jnp.bfloat16)
    first = jnp.einsum("bkts,bks->bt", single, flux_low, preferred_element_type=jnp.float32)
    second = jnp.einsum("bkts,bks->bt", double, pot_low, preferred_element_type=jnp.float32)
    return (first - second) * (1.0 / math.sqrt(NEAR * 128))


def into_boxes(values, marks, box_count):
    box_of = jnp.where(marks >= 0, marks // 128, -1)
    within = marks % 128
    box_hit = (box_of[None, :] == jnp.arange(box_count, dtype=jnp.int32)[:, None]).astype(
        jnp.float32
    )
    spread_factor = values[:, None, :] * box_hit[None, :, :]
    inside_match = (within[:, None] == jnp.arange(128, dtype=jnp.int32)[None, :]).astype(
        jnp.float32
    )
    return jnp.einsum("eto,of->etf", spread_factor, inside_match, precision=lax.Precision.HIGHEST)


def read_boxes(field_three, marks, box_count):
    box_of = jnp.where(marks >= 0, marks // 128, -1)
    within = marks % 128
    inside_match = (within[:, None] == jnp.arange(128, dtype=jnp.int32)[None, :]).astype(
        jnp.float32
    )
    per_box = jnp.dot(inside_match, field_three.T, precision=lax.Precision.HIGHEST)
    box_hit = (box_of[:, None] == jnp.arange(box_count, dtype=jnp.int32)[None, :]).astype(
        jnp.float32
    )
    return jnp.sum(per_box * box_hit, axis=1)[None, :]


def shards(potential, elevation, normal_flux, box_owner, box_place, near_boxes):
    tile_rows, tile_cols = potential.shape
    tile_count_across = lax.axis_size("tx")
    count_ty = lax.axis_size("ty")
    node_count = tile_rows * tile_cols
    box_count = node_count // 128
    index_tx = lax.axis_index("tx")
    index_ty = lax.axis_index("ty")
    my_rank = index_tx * count_ty + index_ty
    grid_rows = (
        (index_tx * tile_rows + jnp.arange(tile_rows, dtype=jnp.int32)).astype(jnp.float32) + 0.5
    ) / (tile_rows * tile_count_across)
    grid_cols = (
        (index_ty * tile_cols + jnp.arange(tile_cols, dtype=jnp.int32)).astype(jnp.float32) + 0.5
    ) / (tile_cols * count_ty)
    pos_x = jnp.broadcast_to(grid_rows[:, None], (tile_rows, tile_cols))
    pos_y = jnp.broadcast_to(grid_cols[None, :], (tile_rows, tile_cols))
    fields = jnp.stack([potential, elevation])
    node_features = jnp.stack([pos_x, pos_y, 0.25 * elevation, potential, normal_flux]).reshape(
        5, node_count
    )
    owner_flat = box_owner.reshape(node_count)
    flat_placement = box_place.reshape(node_count)
    step_down = (index_tx - owner_flat // count_ty) % tile_count_across
    step_left = (index_ty - owner_flat % count_ty) % count_ty
    bucket = step_down * 2 + step_left

    def select(which):
        chosen = bucket == which
        return (
            jnp.where(chosen[None, :], node_features, 0.0),
            jnp.where(chosen, flat_placement, -1),
        )

    own_vals, own_marks = select(0)
    left_vals, left_marks = select(1)
    below_vals, below_marks = select(2)
    corner_vals, corner_marks = select(3)
    got_left_vals, got_left_marks, relayed_values, relay_marks = from_behind(
        (left_vals, left_marks, corner_vals, corner_marks), "ty", -1
    )
    got_below_vals, got_below_marks, got_corner_vals, got_corner_marks = from_behind(
        (below_vals, below_marks, relayed_values, relay_marks), "tx", -1
    )
    boxed_three = into_boxes(own_vals, own_marks, box_count)
    boxed_three = boxed_three + into_boxes(got_left_vals, got_left_marks, box_count)
    boxed_three = boxed_three + into_boxes(got_below_vals, got_below_marks, box_count)
    boxed_three = boxed_three + into_boxes(got_corner_vals, got_corner_marks, box_count)
    boxed = boxed_three.reshape(5, node_count)
    extended = padded_2(boxed, ((("tx", "ty"), 1),), node_count, False)
    extended_three = extended.reshape(5, 3 * box_count, 128)
    local_lists = near_boxes - (my_rank - 1) * box_count
    block_boxes = math.gcd(box_count, 32)

    def near_block(block_id):
        start = block_id * block_boxes
        targets = lax.dynamic_slice_in_dim(boxed_three, start, block_boxes, 1)
        listed = lax.dynamic_slice_in_dim(local_lists, start, block_boxes, 0)
        list_hit = (
            listed[:, :, None] == jnp.arange(3 * box_count, dtype=jnp.int32)[None, None, :]
        ).astype(jnp.float32)
        sources = jnp.einsum(
            "bkm,cms->cbks", list_hit, extended_three, precision=lax.Precision.HIGHEST
        )
        return kernel_apply(targets, sources)

    near_three = lax.map(near_block, jnp.arange(box_count // block_boxes, dtype=jnp.int32)).reshape(
        box_count, 128
    )
    answer_own = read_boxes(near_three, own_marks, box_count)
    answer_left = read_boxes(near_three, got_left_marks, box_count)
    answer_below = read_boxes(near_three, got_below_marks, box_count)
    answer_corner = read_boxes(near_three, got_corner_marks, box_count)
    came_below, relay_back = from_behind((answer_below, answer_corner), "tx", 1)
    came_left, came_corner = from_behind((answer_left, relay_back), "ty", 1)
    merged = jnp.where(
        bucket == 0,
        answer_own[0],
        jnp.where(bucket == 1, came_left[0], jnp.where(bucket == 2, came_below[0], came_corner[0])),
    )
    vertical = merged.reshape(tile_rows, tile_cols)
    gradients = surface_slopes(fields)
    along_rows, along_cols = gradients
    pot_x, elev_x = (along_rows[0], along_rows[1])
    pot_y, elev_y = (along_cols[0], along_cols[1])
    lift = 1.0 + elev_x * elev_x + elev_y * elev_y
    elevation_rate = vertical * lift - (pot_x * elev_x + pot_y * elev_y)
    potential_rate = (
        -elevation - 0.5 * (pot_x * pot_x + pot_y * pot_y) + 0.5 * vertical * vertical * lift
    )
    return (elevation_rate, potential_rate)


def solution(mesh):
    in_specs = (
        P("tx", "ty"),
        P("tx", "ty"),
        P("tx", "ty"),
        P("tx", "ty"),
        P("tx", "ty"),
        P(("tx", "ty"), None),
    )
    out_specs = (P("tx", "ty"), P("tx", "ty"))
    return jax.shard_map(shards, mesh=mesh, in_specs=in_specs, out_specs=out_specs, check_vma=False)
```

profile of v0, /device:TPU:0, one launch (start us, length us, event | category | flops | bytes accessed | tf_op | source)
XLA Modules:
  0.0 305.8 jit_solution(7082366297568535475)
XLA Ops:
  23.4 6.5 %fusion.132 = f32[5,128,16384]{2,1,0:T(8,128)S(1)} fusion(f32[128,16384]{1,0:T(8,128)} %fusion.41, f32[5,16384]{1,0:T(8,128)S(1)} %get-tuple-element.71), kind=kLoop, calls=%fused_computation.35.clone | loop fusion | flops 10485760 | bytes 50659328 | tf_op jit(solution)/shard_map/eto,of->etf/dot_general | solution.py:76
  30.0 22.7 %fusion.23 = f32[5,128,128]{2,1,0:T(8,128)S(1)} fusion(s32[16384]{0:T(1024)S(1)} %get-tuple-element.78, f32[5,128,16384]{2,1,0:T(8,128)S(1)} %fusion.132), kind=kOutput, calls=%fused_computation.34 | convolution fusion | flops 16108224512 | bytes 42336256 | tf_op jit(solution)/shard_map/eto,of->etf/dot_general | solution.py:76
  60.3 8.6 %collective-permute-done.6 = s32[16384]{0:T(1024)S(1)} collective-permute-done((s32[16384]{0:T(1024)S(1)}, s32[16384]{0:T(1024)S(1)}, u32[]{:S(2)}, u32[]{:S(2)}) %collective-permute-start.6) | collective-permute-done | bytes 65568 | tf_op jit(solution)/shard_map/ppermute | solution.py:29
  80.0 6.5 %fusion.130 = f32[5,128,16384]{2,1,0:T(8,128)S(1)} fusion(f32[128,16384]{1,0:T(8,128)} %fusion.44, f32[5,16384]{1,0:T(8,128)S(1)} %collective-permute-done.2), kind=kLoop, calls=%fused_computation.31.clone.2 | loop fusion | flops 10485760 | bytes 50659328 | tf_op jit(solution)/shard_map/eto,of->etf/dot_general | solution.py:76
  86.5 22.7 %fusion.19 = f32[5,128,128]{2,1,0:T(8,128)S(1)} fusion(s32[16384]{0:T(1024)S(1)} %get-tuple-element.88, f32[5,128,16384]{2,1,0:T(8,128)S(1)} %fusion.130), kind=kOutput, calls=%fused_computation.30 | convolution fusion | flops 16108224512 | bytes 42336256 | tf_op jit(solution)/shard_map/eto,of->etf/dot_general | solution.py:76
  110.0 6.5 %fusion.134 = f32[5,128,16384]{2,1,0:T(8,128)S(1)} fusion(f32[128,16384]{1,0:T(8,128)} %fusion.42, f32[5,16384]{1,0:T(8,128)S(1)} %collective-permute-done), kind=kLoop, calls=%fused_computation.33.clone.clone.clone.clone.clone.2 | loop fusion | flops 10485760 | bytes 50659328 | tf_op jit(solution)/shard_map/eto,of->etf/dot_general | solution.py:76
  116.5 23.0 %fusion.62 = f32[5,128,128]{2,1,0:T(8,128)S(1)} fusion(f32[5,128,128]{2,1,0:T(8,128)S(1)} %fusion.19, f32[5,128,128]{2,1,0:T(8,128)S(1)} %fusion.23, s32[16384]{0:T(1024)S(1)} %get-tuple-element.87, f32[5,128,16384]{2,1,0:T(8,128)S(1)} %fusion.134), kind=kOutput, calls=%fused_computation.81 | convolution fusion | flops 16108388352 | bytes 42991616 | tf_op jit(solution)/shard_map/eto,of->etf/dot_general | solution.py:76
  139.5 6.5 %fusion.136 = f32[5,128,16384]{2,1,0:T(8,128)S(1)} fusion(f32[128,16384]{1,0:T(8,128)} %fusion.46, f32[5,16384]{1,0:T(8,128)S(1)} %collective-permute-done.5), kind=kLoop, calls=%fused_computation.29.clone.clone.clone.2 | loop fusion | flops 10485760 | bytes 50659328 | tf_op jit(solution)/shard_map/eto,of->etf/dot_general | solution.py:76
  146.0 22.8 %fusion.67 = f32[5,128,128]{2,1,0:T(8,128)S(1)} fusion(f32[5,128,128]{2,1,0:T(8,128)S(1)} %fusion.62, s32[16384]{0:T(1024)S(1)} %get-tuple-element.85, f32[5,128,16384]{2,1,0:T(8,128)S(1)} %fusion.136), kind=kOutput, calls=%fused_computation.82 | convolution fusion | flops 16108306432 | bytes 42663936 | tf_op jit(solution)/shard_map/eto,of->etf/dot_general | solution.py:76
  176.9 8.7 %collective-permute-done.9 = f32[5,16384]{1,0:T(8,128)S(1)} collective-permute-done((f32[5,16384]{1,0:T(8,128)S(1)}, f32[5,16384]{1,0:T(8,128)S(1)}, u32[]{:S(2)}, u32[]{:S(2)}) %collective-permute-start.9) | collective-permute-done | bytes 327712 | tf_op jit(solution)/shard_map/ppermute | solution.py:21
  187.4 75.0 %while.10 = (s32[]{:T(128)}, f32[4,32,128]{2,1,0:T(8,128)S(1)}, s32[4]{0:T(128)S(1)}, f32[5,128,128]{2,1,0:T(8,128)S(1)}, s32[128,8]{1,0:T(8,128)S(1)}, /*index=...) while((s32[]{:T(128)}, f32[4,32,128]{2,1,0:T(8,128)S(1)}, ...), condition=%wide.region_1.2_spmd, body=%wide.region_0.1_spmd.sunk | while | flops 868491264 | bytes 4213979 | solution.py:158
  189.6 9.1 %fusion.151 = f32[32,1,128,1]{2,1,3,0:T(1,128)S(1)} fusion(f32[32,8,128]{2,1,0:T(8,128)S(1)} %get-tuple-element.140, f32[32,128]{1,0:T(8,128)S(1)} %get-tuple-element.141, f32[32,8,128]{2,1,0:T(8,128)S(1)} %get-tuple-element.142, f32[32,128]{1,0:T(8,128)S(1)} %get-tuple-element.143, f32[32,8,128]{2,1,0:T(8,128)S(1)} %get-tuple-element.144, ...), kind=kOutput, calls=%fused_computation.8.clone.1 | convolution fusion | flops 62914560 | bytes 524288 | tf_op jit(solution)/shard_map/while/body/eval_jaxpr/bkts,bks->bt/dot_general | solution.py:62
  198.6 7.5 %fusion.150 = f32[32,1,128,1]{2,1,3,0:T(1,128)S(1)} fusion(f32[32,8,128]{2,1,0:T(8,128)S(1)} %get-tuple-element.140, f32[32,128]{1,0:T(8,128)S(1)} %get-tuple-element.141, f32[32,8,128]{2,1,0:T(8,128)S(1)} %get-tuple-element.142, f32[32,128]{1,0:T(8,128)S(1)} %get-tuple-element.143, f32[32,8,128]{2,1,0:T(8,128)S(1)} %get-tuple-element.144, ...), kind=kOutput, calls=%fused_computation.7.clone.1 | convolution fusion | flops 50331648 | bytes 524288 | tf_op jit(solution)/shard_map/while/body/eval_jaxpr/bkts,bks->bt/dot_general | solution.py:61
  208.3 9.1 %fusion.151 = f32[32,1,128,1]{2,1,3,0:T(1,128)S(1)} fusion(f32[32,8,128]{2,1,0:T(8,128)S(1)} %get-tuple-element.140, f32[32,128]{1,0:T(8,128)S(1)} %get-tuple-element.141, f32[32,8,128]{2,1,0:T(8,128)S(1)} %get-tuple-element.142, f32[32,128]{1,0:T(8,128)S(1)} %get-tuple-element.143, f32[32,8,128]{2,1,0:T(8,128)S(1)} %get-tuple-element.144, ...), kind=kOutput, calls=%fused_computation.8.clone.1 | convolution fusion | flops 62914560 | bytes 524288 | tf_op jit(solution)/shard_map/while/body/eval_jaxpr/bkts,bks->bt/dot_general | solution.py:62
  217.4 7.5 %fusion.150 = f32[32,1,128,1]{2,1,3,0:T(1,128)S(1)} fusion(f32[32,8,128]{2,1,0:T(8,128)S(1)} %get-tuple-element.140, f32[32,128]{1,0:T(8,128)S(1)} %get-tuple-element.141, f32[32,8,128]{2,1,0:T(8,128)S(1)} %get-tuple-element.142, f32[32,128]{1,0:T(8,128)S(1)} %get-tuple-element.143, f32[32,8,128]{2,1,0:T(8,128)S(1)} %get-tuple-element.144, ...), kind=kOutput, calls=%fused_computation.7.clone.1 | convolution fusion | flops 50331648 | bytes 524288 | tf_op jit(solution)/shard_map/while/body/eval_jaxpr/bkts,bks->bt/dot_general | solution.py:61
  227.1 9.1 %fusion.151 = f32[32,1,128,1]{2,1,3,0:T(1,128)S(1)} fusion(f32[32,8,128]{2,1,0:T(8,128)S(1)} %get-tuple-element.140, f32[32,128]{1,0:T(8,128)S(1)} %get-tuple-element.141, f32[32,8,128]{2,1,0:T(8,128)S(1)} %get-tuple-element.142, f32[32,128]{1,0:T(8,128)S(1)} %get-tuple-element.143, f32[32,8,128]{2,1,0:T(8,128)S(1)} %get-tuple-element.144, ...), kind=kOutput, calls=%fused_computation.8.clone.1 | convolution fusion | flops 62914560 | bytes 524288 | tf_op jit(solution)/shard_map/while/body/eval_jaxpr/bkts,bks->bt/dot_general | solution.py:62
  236.1 7.5 %fusion.150 = f32[32,1,128,1]{2,1,3,0:T(1,128)S(1)} fusion(f32[32,8,128]{2,1,0:T(8,128)S(1)} %get-tuple-element.140, f32[32,128]{1,0:T(8,128)S(1)} %get-tuple-element.141, f32[32,8,128]{2,1,0:T(8,128)S(1)} %get-tuple-element.142, f32[32,128]{1,0:T(8,128)S(1)} %get-tuple-element.143, f32[32,8,128]{2,1,0:T(8,128)S(1)} %get-tuple-element.144, ...), kind=kOutput, calls=%fused_computation.7.clone.1 | convolution fusion | flops 50331648 | bytes 524288 | tf_op jit(solution)/shard_map/while/body/eval_jaxpr/bkts,bks->bt/dot_general | solution.py:61
  245.8 9.1 %fusion.151 = f32[32,1,128,1]{2,1,3,0:T(1,128)S(1)} fusion(f32[32,8,128]{2,1,0:T(8,128)S(1)} %get-tuple-element.140, f32[32,128]{1,0:T(8,128)S(1)} %get-tuple-element.141, f32[32,8,128]{2,1,0:T(8,128)S(1)} %get-tuple-element.142, f32[32,128]{1,0:T(8,128)S(1)} %get-tuple-element.143, f32[32,8,128]{2,1,0:T(8,128)S(1)} %get-tuple-element.144, ...), kind=kOutput, calls=%fused_computation.8.clone.1 | convolution fusion | flops 62914560 | bytes 524288 | tf_op jit(solution)/shard_map/while/body/eval_jaxpr/bkts,bks->bt/dot_general | solution.py:62
  254.9 7.5 %fusion.150 = f32[32,1,128,1]{2,1,3,0:T(1,128)S(1)} fusion(f32[32,8,128]{2,1,0:T(8,128)S(1)} %get-tuple-element.140, f32[32,128]{1,0:T(8,128)S(1)} %get-tuple-element.141, f32[32,8,128]{2,1,0:T(8,128)S(1)} %get-tuple-element.142, f32[32,128]{1,0:T(8,128)S(1)} %get-tuple-element.143, f32[32,8,128]{2,1,0:T(8,128)S(1)} %get-tuple-element.144, ...), kind=kOutput, calls=%fused_computation.7.clone.1 | convolution fusion | flops 50331648 | bytes 524288 | tf_op jit(solution)/shard_map/while/body/eval_jaxpr/bkts,bks->bt/dot_general | solution.py:61
  262.4 6.8 %select_reduce_fusion = f32[16384]{0:T(1024)S(1)} fusion(s32[16384]{0:T(1024)S(1)} %copy-done.14, f32[128,128]{1,0:T(8,128)S(1)} %bitcast.175, s32[16384]{0:T(1024)S(1)} %copy-done.16), kind=kOutput, calls=%fused_computation.45 | convolution fusion | flops 3229597696 | bytes 262144 | tf_op jit(solution)/shard_map/dot_general | solution.py:85
  269.3 6.8 %select_reduce_fusion.1 = f32[16384]{0:T(1024)S(1)} fusion(s32[16384]{0:T(1024)S(1)} %copy-done.8, f32[128,128]{1,0:T(8,128)S(1)} %bitcast.176, s32[16384]{0:T(1024)S(1)} %copy-done.6), kind=kOutput, calls=%fused_computation.47 | convolution fusion | flops 3229597696 | bytes 262144 | tf_op jit(solution)/shard_map/dot_general | solution.py:85
  276.2 9.0 %collective-permute-start.12 = (f32[1,16384]{1,0:T(1,128)S(1)}, f32[1,16384]{1,0:T(1,128)S(1)}, u32[]{:S(2)}, u32[]{:S(2)}) collective-permute-start(f32[1,16384]{1,0:T(1,128)S(1)} %bitcast.181), channel_id=1, source_target_pairs={{0,4},{4,8},{8,12},{12,16},{16,20},{20,24},{24,28},{28,0},{1,5},{5... | collective-permute-start | bytes 196616 | tf_op jit(solution)/shard_map/ppermute | solution.py:29
  285.2 6.8 %select_reduce_fusion.2 = f32[16384]{0:T(1024)S(1)} fusion(s32[16384]{0:T(1024)S(1)} %copy-done.10, f32[128,128]{1,0:T(8,128)S(1)} %bitcast.177, s32[16384]{0:T(1024)S(1)} %copy-done.12), kind=kOutput, calls=%fused_computation.49 | convolution fusion | flops 3229597696 | bytes 262144 | tf_op jit(solution)/shard_map/dot_general | solution.py:85
  294.4 6.8 %fusion.56 = f32[16384]{0:T(1024)S(1)} fusion(f32[128,128]{1,0:T(8,128)S(1)} %bitcast.178, s32[16384]{0:T(1024)S(1)} %copy-done.20, s32[16384]{0:T(1024)S(1)} %copy-done.18), kind=kOutput, calls=%fused_computation.79 | convolution fusion | flops 3229597696 | bytes 262144 | tf_op jit(solution)/shard_map/dot_general | solution.py:85
  (165 shorter events, 64.7 us)
Async XLA Ops:
  8.1 71.9 %collective-permute-start.2 = (f32[5,16384]{1,0:T(8,128)}, f32[5,16384]{1,0:T(8,128)S(1)}, u32[]{:S(2)}, u32[]{:S(2)}) collective-permute-start(f32[5,16384]{1,0:T(8,128)} %get-tuple-element.69), channel_id=1, source_target_pairs={{0,28},{4,0},{8,4},{12,8},{16,12},{20,16},{24,20},{28,24},{1,29},{... | collective-permute-start | bytes 983048 | tf_op jit(solution)/shard_map/ppermute | solution.py:29
  11.4 42.4 %collective-permute-start.3 = (s32[16384]{0:T(1024)}, s32[16384]{0:T(1024)S(1)}, u32[]{:S(2)}, u32[]{:S(2)}) collective-permute-start(s32[16384]{0:T(1024)} %get-tuple-element.76), channel_id=1, source_target_pairs={{0,28},{4,0},{8,4},{12,8},{16,12},{20,16},{24,20},{28,24},{1,29},{... | collective-permute-start | bytes 196616 | tf_op jit(solution)/shard_map/ppermute | solution.py:29
  12.1 97.9 %collective-permute-start = (f32[5,16384]{1,0:T(8,128)}, f32[5,16384]{1,0:T(8,128)S(1)}, u32[]{:S(2)}, u32[]{:S(2)}) collective-permute-start(f32[5,16384]{1,0:T(8,128)} %get-tuple-element.70), channel_id=1, source_target_pairs={{0,3},{1,0},{2,1},{3,2},{4,7},{5,4},{6,5},{7,6},{8,11},{9,8},{10,9... | collective-permute-start | bytes 983048 | tf_op jit(solution)/shard_map/ppermute | solution.py:29
  16.5 36.2 %collective-permute-start.14 = (f32[2,2,256]{2,1,0:T(2,128)S(1)}, f32[2,2,256]{2,1,0:T(2,128)S(1)}, u32[]{:S(2)}, u32[]{:S(2)}) collective-permute-start(f32[2,2,256]{2,1,0:T(2,128)S(1)} %get-tuple-element.82), channel_id=1, source_target_pairs={{0,4},{4,8},{8,12},{12,16},{16,20},{20,24},{24,28},{28,0},{1,5},{5... | collective-permute-start | bytes 12296 | tf_op jit(solution)/shard_map/ppermute | solution.py:18
  16.5 36.8 %collective-permute-start.15 = (f32[2,2,256]{2,1,0:T(2,128)S(1)}, f32[2,2,256]{2,1,0:T(2,128)S(1)}, u32[]{:S(2)}, u32[]{:S(2)}) collective-permute-start(f32[2,2,256]{2,1,0:T(2,128)S(1)} %get-tuple-element.83), channel_id=1, source_target_pairs={{4,0},{8,4},{12,8},{16,12},{20,16},{24,20},{28,24},{0,28},{5,1},{9... | collective-permute-start | bytes 12296 | tf_op jit(solution)/shard_map/ppermute | solution.py:21
  52.7 5.9 %collective-permute-start.1 = (s32[16384]{0:T(1024)S(1)}, s32[16384]{0:T(1024)S(1)}, u32[]{:S(2)}, u32[]{:S(2)}) collective-permute-start(s32[16384]{0:T(1024)S(1)} %get-tuple-element.52), channel_id=1, source_target_pairs={{0,3},{1,0},{2,1},{3,2},{4,7},{5,4},{6,5},{7,6},{8,11},{9,8},{10,9... | collective-permute-start | bytes 196616 | tf_op jit(solution)/shard_map/ppermute | solution.py:29
  53.2 56.0 %collective-permute-start.4 = (f32[5,16384]{1,0:T(8,128)S(1)}, f32[5,16384]{1,0:T(8,128)}, u32[]{:S(2)}, u32[]{:S(2)}) collective-permute-start(f32[5,16384]{1,0:T(8,128)S(1)} %get-tuple-element.68), channel_id=1, source_target_pairs={{0,3},{1,0},{2,1},{3,2},{4,7},{5,4},{6,5},{7,6},{8,11},{9,8},{10,9... | collective-permute-start | bytes 983048 | tf_op jit(solution)/shard_map/ppermute | solution.py:29
  53.8 15.1 %collective-permute-start.6 = (s32[16384]{0:T(1024)S(1)}, s32[16384]{0:T(1024)S(1)}, u32[]{:S(2)}, u32[]{:S(2)}) collective-permute-start(s32[16384]{0:T(1024)S(1)} %get-tuple-element.49), channel_id=1, source_target_pairs={{0,3},{1,0},{2,1},{3,2},{4,7},{5,4},{6,5},{7,6},{8,11},{9,8},{10,9... | collective-permute-start | bytes 196616 | tf_op jit(solution)/shard_map/ppermute | solution.py:29
  54.4 32.1 %copy-start.5 = (s32[16384]{0:T(1024)}, s32[16384]{0:T(1024)S(1)}, u32[]{:S(2)}) copy-start(s32[16384]{0:T(1024)S(1)} %get-tuple-element.88) | copy-start | bytes 196612
  58.6 116.3 %collective-permute-start.16 = (f32[2,68,2]{2,1,0:T(8,128)S(1)}, f32[2,68,2]{2,1,0:T(8,128)S(1)}, u32[]{:S(2)}, u32[]{:S(2)}) collective-permute-start(f32[2,68,2]{2,1,0:T(8,128)S(1)} %get-tuple-element.72), channel_id=1, source_target_pairs={{0,1},{1,2},{2,3},{3,0},{4,5},{5,6},{6,7},{7,4},{8,9},{9,10},{10,1... | collective-permute-start | bytes 3272 | tf_op jit(solution)/shard_map/ppermute | solution.py:18
  60.3 56.2 %copy-start.11 = (s32[16384]{0:T(1024)}, s32[16384]{0:T(1024)S(1)}, u32[]{:S(2)}) copy-start(s32[16384]{0:T(1024)S(1)} %get-tuple-element.87) | copy-start | bytes 196612
  68.9 6.1 %collective-permute-start.7 = (s32[16384]{0:T(1024)S(1)}, s32[16384]{0:T(1024)S(1)}, u32[]{:S(2)}, u32[]{:S(2)}) collective-permute-start(s32[16384]{0:T(1024)S(1)} %collective-permute-done.6), channel_id=1, source_target_pairs={{0,28},{4,0},{8,4},{12,8},{16,12},{20,16},{24,20},{28,24},{1,29},{... | collective-permute-start | bytes 196616 | tf_op jit(solution)/shard_map/ppermute | solution.py:29
  75.0 99.9 %collective-permute-start.17 = (f32[2,68,2]{2,1,0:T(8,128)S(1)}, f32[2,68,2]{2,1,0:T(8,128)}, u32[]{:S(2)}, u32[]{:S(2)}) collective-permute-start(f32[2,68,2]{2,1,0:T(8,128)S(1)} %get-tuple-element.73), channel_id=1, source_target_pairs={{1,0},{2,1},{3,2},{0,3},{5,4},{6,5},{7,6},{4,7},{9,8},{10,9},{11,1... | collective-permute-start | bytes 3272 | tf_op jit(solution)/shard_map/ppermute | solution.py:21
  75.8 70.2 %copy-start.15 = (s32[16384]{0:T(1024)}, s32[16384]{0:T(1024)S(1)}, u32[]{:S(2)}) copy-start(s32[16384]{0:T(1024)S(1)} %get-tuple-element.85) | copy-start | bytes 196612
  109.2 30.3 %collective-permute-start.5 = (f32[5,16384]{1,0:T(8,128)}, f32[5,16384]{1,0:T(8,128)S(1)}, u32[]{:S(2)}, u32[]{:S(2)}) collective-permute-start(f32[5,16384]{1,0:T(8,128)} %collective-permute-done.4), channel_id=1, source_target_pairs={{0,28},{4,0},{8,4},{12,8},{16,12},{20,16},{24,20},{28,24},{1,29},{... | collective-permute-start | bytes 983048 | tf_op jit(solution)/shard_map/ppermute | solution.py:29
  146.0 41.3 %copy-start.27 = (f32[4,32,128]{2,1,0:T(8,128)S(1)}, f32[4,32,128]{2,1,0:T(8,128)}, u32[]{:S(2)}) copy-start(f32[4,32,128]{2,1,0:T(8,128)} %custom-call) | copy-start | bytes 196612
  169.0 16.5 %collective-permute-start.9 = (f32[5,16384]{1,0:T(8,128)S(1)}, f32[5,16384]{1,0:T(8,128)S(1)}, u32[]{:S(2)}, u32[]{:S(2)}) collective-permute-start(f32[5,16384]{1,0:T(8,128)S(1)} %bitcast.160), channel_id=1, source_target_pairs={{1,0},{2,1},{3,2},{4,3},{5,4},{6,5},{7,6},{8,7},{9,8},{10,9},{11,1... | collective-permute-start | bytes 983048 | tf_op jit(solution)/shard_map/ppermute | solution.py:21
  170.3 16.8 %collective-permute-start.8 = (f32[5,16384]{1,0:T(8,128)S(1)}, f32[5,16384]{1,0:T(8,128)S(1)}, u32[]{:S(2)}, u32[]{:S(2)}) collective-permute-start(f32[5,16384]{1,0:T(8,128)S(1)} %bitcast.161), channel_id=1, source_target_pairs={{0,1},{1,2},{2,3},{3,4},{4,5},{5,6},{6,7},{7,8},{8,9},{9,10},{10,1... | collective-permute-start | bytes 983048 | tf_op jit(solution)/shard_map/ppermute | solution.py:18
  187.4 75.0 %copy-start.14 = (s32[16384]{0:T(1024)S(1)}, s32[16384]{0:T(1024)}, u32[]{:S(2)}) copy-start(s32[16384]{0:T(1024)} %copy-done.13) | copy-start | bytes 196612
  187.4 75.0 %copy-start.16 = (s32[16384]{0:T(1024)S(1)}, s32[16384]{0:T(1024)}, u32[]{:S(2)}) copy-start(s32[16384]{0:T(1024)} %copy-done.15) | copy-start | bytes 196612
  276.2 17.3 %collective-permute-start.12 = (f32[1,16384]{1,0:T(1,128)S(1)}, f32[1,16384]{1,0:T(1,128)S(1)}, u32[]{:S(2)}, u32[]{:S(2)}) collective-permute-start(f32[1,16384]{1,0:T(1,128)S(1)} %bitcast.181), channel_id=1, source_target_pairs={{0,4},{4,8},{8,12},{12,16},{16,20},{20,24},{24,28},{28,0},{1,5},{5... | collective-permute-start | bytes 196616 | tf_op jit(solution)/shard_map/ppermute | solution.py:29
  292.1 9.2 %collective-permute-start.11 = (f32[1,16384]{1,0:T(1,128)S(1)}, f32[1,16384]{1,0:T(1,128)S(1)}, u32[]{:S(2)}, u32[]{:S(2)}) collective-permute-start(f32[1,16384]{1,0:T(1,128)S(1)} %bitcast.180), channel_id=1, source_target_pairs={{0,4},{4,8},{8,12},{12,16},{16,20},{20,24},{24,28},{28,0},{1,5},{5... | collective-permute-start | bytes 196616 | tf_op jit(solution)/shard_map/ppermute | solution.py:29
  292.8 9.8 %collective-permute-start.10 = (f32[1,16384]{1,0:T(1,128)S(1)}, f32[1,16384]{1,0:T(1,128)S(1)}, u32[]{:S(2)}, u32[]{:S(2)}) collective-permute-start(f32[1,16384]{1,0:T(1,128)S(1)} %bitcast.179), channel_id=1, source_target_pairs={{0,1},{1,2},{2,3},{3,0},{4,5},{5,6},{6,7},{7,4},{8,9},{9,10},{10,1... | collective-permute-start | bytes 196616 | tf_op jit(solution)/shard_map/ppermute | solution.py:29
  293.5 10.0 %collective-permute-start.13 = (f32[1,16384]{1,0:T(1,128)S(1)}, f32[1,16384]{1,0:T(1,128)S(1)}, u32[]{:S(2)}, u32[]{:S(2)}) collective-permute-start(f32[1,16384]{1,0:T(1,128)S(1)} %collective-permute-done.12), channel_id=1, source_target_pairs={{0,1},{1,2},{2,3},{3,0},{4,5},{5,6},{6,7},{7,4},{8,9},{9,10},{10,1... | collective-permute-start | bytes 196616 | tf_op jit(solution)/shard_map/ppermute | solution.py:29
  (22 other events, 352.5 us)
where the time goes:
time: 306 us
  matrix products  188 us (61%)
  other arithmetic  52.4 us (17%)
  starting transfers between devices  34 us (11%)
  waiting for transfers between devices  18.9 us (6%)
  local copies, waits for them, and re-layouts  8.26 us (3%)
    dot_general x4, matrix products, into_boxes(): jnp.einsum('eto,of->etf', spread_factor, inside_match, precision=lax.Prec...  91.1 us
    dot_general x4, matrix products, kernel_apply(): jnp.einsum('bkts,bks->bt', double, pot_low, preferred_element_type=jnp.fl...  36.2 us
    dot_general x4, matrix products, kernel_apply(): jnp.einsum('bkts,bks->bt', single, flux_low, preferred_element_type=jnp.f...  29.9 us
    dot_general x4, matrix products, read_boxes(): jnp.dot(inside_match, field_three.T, precision=lax.Precision.HIGHEST)  27.4 us
    dot_general x4, other arithmetic, into_boxes(): jnp.einsum('eto,of->etf', spread_factor, inside_match, precision=lax.Prec...  25.9 us
    ppermute x12, starting transfers between devices, from_behind(): return lax.ppermute(value, axis, pairs)  23.2 us
    convert_element_type x4, other arithmetic, into_boxes(): (box_of[None, :] == jnp.arange(box_count, dtype=jnp.int32)[:, None]).asty...  16.6 us
    ppermute x3, waiting for transfers between devices, padded_2(): lax.ppermute(lax.slice_in_dim(block, 0, width, axis=dim), axis, backward)  8.66 us
  transfers between devices with their start and end apart: 18, of which 3 were waited for; matrix products, arithmetic and copies ran while one was open for 50% of the time, Pallas kernels for 0%

commit v1 on v0

v1 whole, which is shorter than its diff:
```python
import math

import jax
import jax.numpy as jnp
from jax import lax
from jax.experimental import pallas as pl
from jax.experimental.pallas import tpu as pltpu
from jax.sharding import PartitionSpec as P

LANES = 128
WIDE = 256
PIECES = 6
FEATURES = 32
BF16 = jnp.bfloat16
F32 = jnp.float32


def shifted(value, axis, steps):
    count = lax.axis_size(axis)
    pairs = [(source, (source + steps) % count) for source in range(count)]
    return lax.ppermute(value, axis, pairs)


def rounded(value):
    return value.astype(BF16).astype(F32)


def scatter_kernel(first, last, sizes, info, tile, *refs):
    if first:
        acc = refs[0]
    else:
        acc_in, acc = refs[:2]
    rows, cols, high_count, node_rows, node_cols = sizes
    base = info[0].astype(F32)
    off_i = info[1].astype(F32)
    off_j = info[2].astype(F32)
    acc[...] = jnp.zeros(acc.shape, F32) if first else acc_in[...]
    units = [(r, c) for r in range(rows // 8) for c in range(cols // LANES)]

    def split(r, c):
        rel = tile[0, 8 * r : 8 * r + 8, LANES * c : LANES * c + LANES] - base
        high = jnp.floor(rel * (1.0 / WIDE))
        return high, rel - high * WIDE

    flags = []
    for r, c in units:
        high, _ = split(r, c)
        mine = (high >= 0.0) & (high < high_count)
        flags.append(jnp.max(jnp.where(mine, 1.0, 0.0)) > 0.0)

    for (r, c), flag in zip(units, flags):

        @pl.when(flag)
        def _():
            high, low = split(r, c)
            window = (slice(8 * r, 8 * r + 8), slice(LANES * c, LANES * c + LANES))
            z = 0.25 * tile[(1,) + window]
            z_high = rounded(z)
            z_low = z - z_high
            pot = tile[(2,) + window]
            flux = tile[(3,) + window]
            col_index = (lax.broadcasted_iota(jnp.int32, (high_count, LANES), 1) + LANES * c).astype(F32) + off_j
            high_iota = lax.broadcasted_iota(jnp.int32, (high_count, LANES), 0).astype(F32)
            low_iota = lax.broadcasted_iota(jnp.int32, (WIDE, LANES), 0).astype(F32)
            lefts = []
            rights = []
            for s in range(8):

                def row(v):
                    return v[s : s + 1, :]

                hit = high_iota == row(high)
                row_index = jnp.full((1, LANES), 8 * r + s, F32) + off_i
                values = [row_index, col_index, row(z_high), row(z_low), row(pot), row(flux)]
                lefts.append(
                    jnp.concatenate([jnp.where(hit, v, 0.0).astype(BF16) for v in values], axis=0)
                )
                rights.append(jnp.where(low_iota == row(low), 1.0, 0.0).astype(BF16))
            acc[...] += lax.dot_general(
                jnp.concatenate(lefts, axis=1),
                jnp.concatenate(rights, axis=1),
                (((1,), (1,)), ((), ())),
                preferred_element_type=F32,
            )

    if last:
        boxed = refs[-1]
        h = high_count
        row0 = info[3].astype(F32)
        col0 = info[4].astype(F32)
        i = acc[0:h] + row0
        i = jnp.where(i >= node_rows, i - node_rows, i)
        j = acc[h : 2 * h] + col0
        j = jnp.where(j >= node_cols, j - node_cols, j)
        fields = [
            (i + 0.5) / node_rows,
            (j + 0.5) / node_cols,
            acc[2 * h : 3 * h] + acc[3 * h : 4 * h],
            acc[4 * h : 5 * h],
            acc[5 * h : 6 * h],
        ]
        for k, f in enumerate(fields):
            boxed[k, 0:h, :] = f[:, :LANES]
            boxed[k, h : 2 * h, :] = f[:, LANES:]


def scatter(info, tile, acc, last, node_rows, node_cols):
    _, rows, cols = tile.shape
    high_count = rows * cols // WIDE
    first = acc is None
    vmem = pl.BlockSpec(memory_space=pltpu.VMEM)
    smem = pl.BlockSpec(memory_space=pltpu.SMEM)
    out_shape = [jax.ShapeDtypeStruct((PIECES * high_count, WIDE), F32)]
    if last:
        out_shape.append(jax.ShapeDtypeStruct((5, 2 * high_count, LANES), F32))
    args = (info, tile) if first else (info, tile, acc)
    out = pl.pallas_call(
        lambda *refs: scatter_kernel(
            first, last, (rows, cols, high_count, node_rows, node_cols), *refs
        ),
        out_shape=out_shape,
        in_specs=[smem] + [vmem] * (len(args) - 1),
        out_specs=[vmem] * len(out_shape),
        name="scatter_last" if last else "scatter_first" if first else "scatter",
        cost_estimate=pl.CostEstimate(
            flops=2 * PIECES * high_count * WIDE * rows * cols // 2,
            transcendentals=0,
            bytes_accessed=4 * (2 * PIECES * high_count * WIDE + 4 * rows * cols),
        ),
    )(*args)
    return out[1] if last else out[0]


def thirds(value):
    high = rounded(value)
    middle = rounded(value - high)
    return high, middle, value - high - middle


def near_kernel(near, listed, own, lower, upper, out, tfeat, sfeat, smeta, even, odd):
    boxes = out.shape[0]
    scale = 1.0 / math.sqrt(near * LANES)

    def features(ref, group):
        window = (slice(8 * group, 8 * group + 8), slice(None))
        x = ref[(0,) + window]
        y = ref[(1,) + window]
        z = ref[(2,) + window]
        pieces = []
        total = None
        for v in (x, y, z):
            high = rounded(v)
            low = rounded(v - high)
            kept = high + low
            pieces.append((high, low))
            total = kept * kept if total is None else total + kept * kept
        return pieces, total, ref[(3,) + window], ref[(4,) + window]

    zeros = jnp.zeros((8, LANES), F32)
    ones = jnp.ones((8, LANES), F32)

    for which, ref in enumerate((lower, own, upper)):
        for group in range(boxes // 8):
            pieces, total, pot, flux = features(ref, group)
            start = which * boxes + 8 * group
            source = []
            for high, low in pieces:
                source += [-2.0 * high, -2.0 * low, -2.0 * high, -2.0 * low]
            source += list(thirds(total)) + [ones, ones, ones]
            source += [zeros] * (FEATURES - len(source))
            for k, v in enumerate(source):
                sfeat[pl.ds(start * FEATURES + k, 8, stride=FEATURES), :] = v
            z = pieces[2][0] + pieces[2][1]
            smeta[0, start : start + 8, :] = pot
            smeta[1, start : start + 8, :] = pot * z
            smeta[2, start : start + 8, :] = flux
            if which == 1:
                target = []
                for high, low in pieces:
                    target += [high, high, low, low]
                target += [ones, ones, ones] + list(thirds(total + 0.04)) + [z]
                target += [zeros] * (FEATURES - len(target))
                for k, v in enumerate(target):
                    tfeat[pl.ds(8 * group * FEATURES + k, 8, stride=FEATURES), :] = v

    def distances(box, squared, z_ref):
        left = tfeat[pl.ds(pl.multiple_of(box * FEATURES, FEATURES), FEATURES), :].T
        z_ref[...] = jnp.broadcast_to(left[:, 18:19], (LANES, LANES))
        rights = []
        for k in range(near):
            n = listed[box * near + k]
            rights.append(
                sfeat[pl.ds(pl.multiple_of(n * FEATURES, FEATURES), FEATURES), :].astype(BF16)
            )
        squared[...] = jnp.dot(
            left.astype(BF16), jnp.concatenate(rights, axis=1), preferred_element_type=F32
        )

    def apply(box, squared, z_ref):
        metas = []
        for k in range(near):
            n = listed[box * near + k]
            metas.append(
                [jnp.broadcast_to(smeta[m, pl.ds(n, 1), :], (8, LANES)) for m in range(3)]
            )
        parts = []
        for t in range(LANES // 8):
            rows = slice(8 * t, 8 * t + 8)
            z = z_ref[rows, :]
            total = None
            for k in range(near):
                pot, pot_z, flux = metas[k]
                inverse = lax.rsqrt(squared[rows, LANES * k : LANES * k + LANES])
                value = inverse * (flux - (inverse * inverse) * (z * pot - pot_z))
                total = value if total is None else total + value
            parts.append(total)
        summed = jnp.concatenate(parts, axis=0).T
        out[pl.ds(box, 1), :] = jnp.sum(summed, axis=0, keepdims=True) * scale

    (even_sq, even_z), (odd_sq, odd_z) = even, odd
    distances(0, even_sq, even_z)

    def step(i, carry):
        distances(2 * i + 1, odd_sq, odd_z)
        apply(2 * i, even_sq, even_z)
        distances(jnp.minimum(2 * i + 2, boxes - 1), even_sq, even_z)
        apply(2 * i + 1, odd_sq, odd_z)
        return carry

    lax.fori_loop(0, boxes // 2, step, 0)


def near_apply(listed, own, lower, upper, near):
    boxes = own.shape[1]
    vmem = pl.BlockSpec(memory_space=pltpu.VMEM)
    smem = pl.BlockSpec(memory_space=pltpu.SMEM)
    buffers = [pltpu.VMEM((LANES, near * LANES), F32), pltpu.VMEM((LANES, LANES), F32)]

    def kernel(listed, own, lower, upper, out, tfeat, sfeat, smeta, e0, e1, o0, o1):
        near_kernel(near, listed, own, lower, upper, out, tfeat, sfeat, smeta, (e0, e1), (o0, o1))

    pairs = boxes * near * LANES * LANES
    return pl.pallas_call(
        kernel,
        out_shape=jax.ShapeDtypeStruct((boxes, LANES), F32),
        in_specs=[smem] + [vmem] * 3,
        out_specs=vmem,
        scratch_shapes=[
            pltpu.VMEM((boxes * FEATURES, LANES), F32),
            pltpu.VMEM((3 * boxes * FEATURES, LANES), F32),
            pltpu.VMEM((3, 3 * boxes, LANES), F32),
        ]
        + buffers
        + buffers,
        name="near_field",
        cost_estimate=pl.CostEstimate(
            flops=pairs * 2 * FEATURES * 4, transcendentals=pairs, bytes_accessed=4 * 16 * boxes * LANES
        ),
    )(listed, own, lower, upper)


def gather_kernel(bases, slot, own, behind_x, behind_y, behind_xy, out):
    rows, cols = slot.shape
    boxes = own.shape[0]
    half = boxes // 2
    count = boxes * LANES
    tiles = [(r, c) for r in range(rows // 8) for c in range(cols // LANES)]
    lanes = []
    wanted = []
    for r, c in tiles:
        value = slot[8 * r : 8 * r + 8, LANES * c : LANES * c + LANES]
        row = jnp.full((8, LANES), -1, jnp.int32)
        lane = jnp.zeros((8, LANES), jnp.int32)
        for which in range(4):
            rel = value - bases[which].astype(F32)
            inside = (rel >= 0.0) & (rel < count)
            rel = jnp.where(inside, rel, 0.0).astype(jnp.int32)
            box = rel // LANES
            place = (box % 2) * half + box // 2
            row = jnp.where(inside, place + which * boxes, row)
            lane = jnp.where(inside, rel % LANES, lane)
        lanes.append(lane)
        wanted.append(row)
    found = [jnp.zeros((8, LANES), F32) for _ in tiles]
    for which, table in enumerate((own, behind_x, behind_y, behind_xy)):

        def step(g, found):
            for s in range(8):
                index = g * 8 + s
                line = jnp.broadcast_to(table[pl.ds(index, 1), :], (8, LANES))
                found = [
                    jnp.where(w == index + which * boxes, jnp.take_along_axis(line, l, axis=1), f)
                    for w, l, f in zip(wanted, lanes, found)
                ]
            return found

        found = lax.fori_loop(0, boxes // 8, step, found)
    for (r, c), f in zip(tiles, found):
        out[8 * r : 8 * r + 8, LANES * c : LANES * c + LANES] = f


def gather(bases, slot, tables):
    vmem = pl.BlockSpec(memory_space=pltpu.VMEM)
    smem = pl.BlockSpec(memory_space=pltpu.SMEM)
    return pl.pallas_call(
        gather_kernel,
        out_shape=jax.ShapeDtypeStruct(slot.shape, F32),
        in_specs=[smem] + [vmem] * 5,
        out_specs=vmem,
        name="gather",
    )(bases, slot, *tables)


def padded_2(block, sides, width):
    for axis, dim in sides:
        low = shifted(lax.slice_in_dim(block, block.shape[dim] - width, None, axis=dim), axis, 1)
        high = shifted(lax.slice_in_dim(block, 0, width, axis=dim), axis, -1)
        block = jnp.concatenate([low, block, high], axis=dim)
    return block


def surface_slopes(fields):
    padded = padded_2(fields, (("tx", 1), ("ty", 2)), 2)
    middle_cols = padded[:, :, 2:-2]
    along_rows = (
        middle_cols[:, 0:-4] - 8.0 * middle_cols[:, 1:-3] + 8.0 * middle_cols[:, 3:-1] - middle_cols[:, 4:]
    ) / 12.0
    central_rows = padded[:, 2:-2, :]
    along_cols = (
        central_rows[:, :, 0:-4]
        - 8.0 * central_rows[:, :, 1:-3]
        + 8.0 * central_rows[:, :, 3:-1]
        - central_rows[:, :, 4:]
    ) / 12.0
    return (along_rows, along_cols)


def shards(potential, elevation, normal_flux, box_owner, box_place, near_boxes):
    rows, cols = potential.shape
    count_tx = lax.axis_size("tx")
    count_ty = lax.axis_size("ty")
    node_count = rows * cols
    boxes = node_count // LANES
    near = near_boxes.shape[1]
    half = boxes // 2
    assert node_count % WIDE == 0 and cols <= 256 and 2 * rows <= 256
    assert node_count * count_tx * count_ty < 2**24
    p = lax.axis_index("tx")
    q = lax.axis_index("ty")
    rank = p * count_ty + q
    base = rank * node_count

    slot = (box_owner * node_count + box_place).astype(F32)
    tile = jnp.stack([slot, elevation, potential, normal_flux])
    ahead_x = shifted(tile, "tx", -1)
    ahead_y = shifted(tile, "ty", -1)
    ahead_xy = shifted(ahead_y, "tx", -1)

    def info(di, dj):
        return jnp.stack(
            [base, jnp.int32(di * rows), jnp.int32((dj - 1) * cols), p * rows, (q + 1) * cols]
        ).astype(jnp.int32)

    sizes = (rows * count_tx, cols * count_ty)
    acc = scatter(info(0, 0), tile, None, False, *sizes)
    acc = scatter(info(1, 0), ahead_x, acc, False, *sizes)
    acc = scatter(info(0, 1), ahead_y, acc, False, *sizes)
    boxed = scatter(info(1, 1), ahead_xy, acc, True, *sizes)

    total = count_tx * count_ty
    both = ("tx", "ty")
    lower = lax.ppermute(boxed, both, [(i, i + 1) for i in range(total - 1)])
    upper = lax.ppermute(boxed, both, [(i + 1, i) for i in range(total - 1)])

    local = near_boxes - (rank - 1) * boxes
    inner = local % boxes
    listed = (local // boxes) * boxes + (inner % 2) * half + inner // 2
    listed = listed.reshape(half, 2, near).transpose(1, 0, 2).reshape(boxes * near)
    near_value = near_apply(listed, boxed, lower, upper, near)

    behind_x = shifted(near_value, "tx", 1)
    behind_y = shifted(near_value, "ty", 1)
    behind_xy = shifted(behind_x, "ty", 1)
    before_p = (p - 1) % count_tx
    before_q = (q - 1) % count_ty
    bases = (
        jnp.stack([rank, before_p * count_ty + q, p * count_ty + before_q, before_p * count_ty + before_q])
        * node_count
    ).astype(jnp.int32)
    vertical = gather(bases, slot, (near_value, behind_x, behind_y, behind_xy))

    along_rows, along_cols = surface_slopes(tile[1:3])
    elev_x, pot_x = (along_rows[0], along_rows[1])
    elev_y, pot_y = (along_cols[0], along_cols[1])
    lift = 1.0 + elev_x * elev_x + elev_y * elev_y
    elevation_rate = vertical * lift - (pot_x * elev_x + pot_y * elev_y)
    potential_rate = (
        -elevation - 0.5 * (pot_x * pot_x + pot_y * pot_y) + 0.5 * vertical * vertical * lift
    )
    return (elevation_rate, potential_rate)


def solution(mesh):
    in_specs = (
        P("tx", "ty"),
        P("tx", "ty"),
        P("tx", "ty"),
        P("tx", "ty"),
        P("tx", "ty"),
        P(("tx", "ty"), None),
    )
    out_specs = (P("tx", "ty"), P("tx", "ty"))
    return jax.shard_map(shards, mesh=mesh, in_specs=in_specs, out_specs=out_specs, check_vma=False)
```

time: 306 us -> 138 us (0.45)
  matrix products: 188 us -> 0 us
  Pallas kernels: 0 us -> 85.8 us
  other arithmetic: 52.4 us -> 4.18 us
  starting transfers between devices: 34 us -> 19 us
    dot_general x20 -> x0, matrix products: 188 us -> none  [the longest x4 91.1 us: into_boxes(): jnp.einsum('eto,of->etf', spread_factor, inside_match, precision=lax.Prec...]
    pallas_call x0 -> x6, Pallas kernels: none -> 85.8 us  [the longest x1 37.6 us: near_apply(): pl.pallas_call(kernel, out_shape=jax.ShapeDtypeStruct((boxes, LANES), F32...]
    dot_general x4 -> x0, other arithmetic: 25.9 us -> none  [into_boxes(): jnp.einsum('eto,of->etf', spread_factor, inside_match, precision=lax.Prec...]
    convert_element_type x4 -> x1, other arithmetic: 16.6 us -> 0.92 us  [shards(): slot = (box_owner * node_count + box_place).astype(F32)]
    ppermute x18 -> x12, starting transfers between devices: 34 us -> 19 us  [the longest x10 16.4 us: shifted(): return lax.ppermute(value, axis, pairs)]
    ppermute x18 -> x12, waiting for transfers between devices: 18.9 us -> 21.2 us  [the longest x1 11.4 us: shards(): upper = lax.ppermute(boxed, both, [(i + 1, i) for i in range(total - 1)])]
  transfers between devices with their start and end apart: 18 -> 12, of which waited for: 3 -> 5; matrix products, arithmetic and copies ran while one was open for 50% -> 3% of each run, Pallas kernels for 0% -> 37%
where the time goes in v1:
time: 138 us
  Pallas kernels  85.8 us (62%)
  waiting for transfers between devices  21.2 us (15%)
  starting transfers between devices  19 us (14%)
  local copies, waits for them, and re-layouts  6.59 us (5%)
  other arithmetic  4.18 us (3%)
    pallas_call x1, Pallas kernels, near_apply(): pl.pallas_call(kernel, out_shape=jax.ShapeDtypeStruct((boxes, LANES), F32...  37.6 us
    pallas_call x1, Pallas kernels, gather(): pl.pallas_call(gather_kernel, out_shape=jax.ShapeDtypeStruct(slot.shape,...  29.3 us
    pallas_call x4, Pallas kernels, scatter(): pl.pallas_call(lambda *refs: scatter_kernel(first, last, (rows, cols, hig...  18.9 us
    ppermute x10, starting transfers between devices, shifted(): return lax.ppermute(value, axis, pairs)  16.4 us
    ppermute x1, waiting for transfers between devices, shards(): upper = lax.ppermute(boxed, both, [(i + 1, i) for i in range(total - 1)])  11.4 us
    ppermute x10, waiting for transfers between devices, shifted(): return lax.ppermute(value, axis, pairs)  8.72 us
    unnamed x30, local copies, waits for them, and re-layouts  3.9 us
  transfers between devices with their start and end apart: 12, of which 5 were waited for; matrix products, arithmetic and copies ran while one was open for 3% of the time, Pallas kernels for 37%

profile of v1, /device:TPU:0, one launch (start us, length us, event | category | flops | bytes accessed | tf_op | source)
XLA Modules:
  0.0 137.6 jit_solution(9639458961227508472)
XLA Ops:
  0.7 0.9 add_convert_fusion.slot
  2.2 3.4 %collective-permute-start.2 = (f32[4,64,256]{2,1,0:T(8,128)S(1)}, f32[4,64,256]{2,1,0:T(8,128)S(1)}, u32[]{:S(2)}, u32[]{:S(2)}) collective-permute-start(f32[4,64,256]{2,1,0:T(8,128)S(1)} %pad_maximum_fusion.refs_1_), channel_id=1, source_target_pairs={{0,28},{4,0},{8,4},{12,8},{16,12},{20,16},{24,20},{28,24},{1,29},{... | collective-permute-start | bytes 786440 | tf_op jit(solution)/shard_map/ppermute | solution.py:21
  5.6 3.6 %collective-permute-start = (f32[4,64,256]{2,1,0:T(8,128)S(1)}, f32[4,64,256]{2,1,0:T(8,128)S(1)}, u32[]{:S(2)}, u32[]{:S(2)}) collective-permute-start(f32[4,64,256]{2,1,0:T(8,128)S(1)} %pad_maximum_fusion.refs_1_), channel_id=1, source_target_pairs={{0,3},{1,0},{2,1},{3,2},{4,7},{5,4},{6,5},{7,6},{8,11},{9,8},{10,9... | collective-permute-start | bytes 786440 | tf_op jit(solution)/shard_map/ppermute | solution.py:21
  9.2 2.6 %collective-permute-start.9 = (f32[2,2,256]{2,1,0:T(2,128)S(1)}, f32[2,2,256]{2,1,0:T(2,128)S(1)}, u32[]{:S(2)}, u32[]{:S(2)}) collective-permute-start(f32[2,2,256]{2,1,0:T(2,128)S(1)} %get-tuple-element.13), channel_id=1, source_target_pairs={{0,28},{4,0},{8,4},{12,8},{16,12},{20,16},{24,20},{28,24},{1,29},{... | collective-permute-start | bytes 12296 | tf_op jit(solution)/shard_map/ppermute | solution.py:21
  12.4 3.1 %scatter_first.1.refs_2_ = f32[384,256]{1,0:T(8,128)} custom-call(s32[5]{0:T(128)} %stack.78.refs_0_, f32[4,64,256]{2,1,0:T(8,128)} %copy-done.3), custom_call_target="tpu_custom_call" | custom-call | flops 1610612736 | bytes 1048576 | tf_op jit(solution)/shard_map/scatter_first/pallas_call | solution.py:117
  18.3 0.7 reshape.24.listed
  19.1 0.7 copy-done.13
  19.8 4.1 %scatter.2.refs_2_ = f32[384,256]{1,0:T(8,128)} custom-call(s32[5]{0:T(128)} %stack.77.refs_0_, f32[4,64,256]{2,1,0:T(8,128)} %copy-done.13, f32[384,256]{1,0:T(8,128)} %scatter_first.1.refs_2_), custom_call_target="tpu_custom_call" | custom-call | flops 1610612736 | bytes 1048576 | tf_op jit(solution)/shard_map/scatter/pallas_call | solution.py:117
  23.9 5.5 %scatter.3.refs_2_ = f32[384,256]{1,0:T(8,128)} custom-call(s32[5]{0:T(128)} %pad_add_fusion.refs_0_, f32[4,64,256]{2,1,0:T(8,128)} %copy-done.12, f32[384,256]{1,0:T(8,128)} %scatter.2.refs_2_), custom_call_target="tpu_custom_call" | custom-call | flops 1610612736 | bytes 1048576 | tf_op jit(solution)/shard_map/scatter/pallas_call | solution.py:117
  29.3 0.7 copy-done.14
  30.0 6.2 %scatter_last.1 = (f32[384,256]{1,0:T(8,128)}, f32[5,128,128]{2,1,0:T(8,128)}) custom-call(s32[5]{0:T(128)} %stack.70.refs_0_, f32[4,64,256]{2,1,0:T(8,128)} %copy-done.14, f32[384,256]{1,0:T(8,128)} %scatter.3.refs_2_), custom_call_target="tpu_custom_call" | custom-call | flops 1610612736 | bytes 1048576 | tf_op jit(solution)/shard_map/scatter_last/pallas_call | solution.py:117
  36.3 1.3 collective-permute-start.3
  37.6 1.3 collective-permute-start.4
  39.0 2.7 %collective-permute-start.10 = (f32[2,68,2]{2,1,0:T(8,128)S(1)}, f32[2,68,2]{2,1,0:T(8,128)S(1)}, u32[]{:S(2)}, u32[]{:S(2)}) collective-permute-start(f32[2,68,2]{2,1,0:T(8,128)S(1)} %get-tuple-element.6), channel_id=1, source_target_pairs={{0,1},{1,2},{2,3},{3,0},{4,5},{5,6},{6,7},{7,4},{8,9},{9,10},{10,1... | collective-permute-start | bytes 3272 | tf_op jit(solution)/shard_map/ppermute | solution.py:21
  41.7 2.8 %collective-permute-start.11 = (f32[2,68,2]{2,1,0:T(8,128)S(1)}, f32[2,68,2]{2,1,0:T(8,128)S(1)}, u32[]{:S(2)}, u32[]{:S(2)}) collective-permute-start(f32[2,68,2]{2,1,0:T(8,128)S(1)} %get-tuple-element.7), channel_id=1, source_target_pairs={{0,3},{1,0},{2,1},{3,2},{4,7},{5,4},{6,5},{7,6},{8,11},{9,8},{10,9... | collective-permute-start | bytes 3272 | tf_op jit(solution)/shard_map/ppermute | solution.py:21
  44.4 1.1 collective-permute-done.3.lower
  45.6 11.4 %collective-permute-done.4.upper = f32[5,128,128]{2,1,0:T(8,128)S(1)} collective-permute-done((f32[5,128,128]{2,1,0:T(8,128)}, f32[5,128,128]{2,1,0:T(8,128)S(1)}, u32[]{:S(2)}, u32[]{:S(2)}) %collective-permute-start.4) | collective-permute-done | bytes 327712 | tf_op jit(solution)/shard_map/ppermute | solution.py:373
  57.0 0.7 copy-done.11
  57.7 37.6 %near_field.1.own = f32[128,128]{1,0:T(8,128)} custom-call(s32[1024]{0:T(1024)} %reshape.24.listed, f32[5,128,128]{2,1,0:T(8,128)} %get-tuple-element.3.own, f32[5,128,128]{2,1,0:T(8,128)} %copy-done.10, f32[5,128,128]{2,1,0:T(8,128)} %copy-done.11), custom_call_target="tpu_custom_call" | custom-call | flops 4294967296 | bytes 1048576 | tf_op jit(solution)/shard_map/near_field/pallas_call | solution.py:243
  96.7 3.4 %collective-permute-done.5.behind_x = f32[128,128]{1,0:T(8,128)S(1)} collective-permute-done((f32[128,128]{1,0:T(8,128)}, f32[128,128]{1,0:T(8,128)S(1)}, u32[]{:S(2)}, u32[]{:S(2)}) %collective-permute-start.5) | collective-permute-done | bytes 65568 | tf_op jit(solution)/shard_map/ppermute | solution.py:21
  100.8 1.3 collective-permute-done.6.behind_y
  102.2 4.0 %collective-permute-done.7.behind_xy = f32[128,128]{1,0:T(8,128)S(1)} collective-permute-done((f32[128,128]{1,0:T(8,128)S(1)}, f32[128,128]{1,0:T(8,128)S(1)}, u32[]{:S(2)}, u32[]{:S(2)}) %collective-permute-start.7) | collective-permute-done | bytes 65568 | tf_op jit(solution)/shard_map/ppermute | solution.py:21
  106.8 29.3 %gather.1 = f32[64,256]{1,0:T(8,128)} custom-call(s32[4]{0:T(128)} %add_multiply_fusion.bases, f32[64,256]{1,0:T(8,128)} %copy-done.2, f32[128,128]{1,0:T(8,128)} %near_field.1.own, f32[128,128]{1,0:T(8,128)} %copy-done.5, f32[128,128]{1,0:T(8,128)} %copy-done.6, f32[128,128]{1,0:T(8,128)} %copy-done.7), custom_call_target="tpu_custom_call" | custom-call | tf_op jit(solution)/shard_map/gather/pallas_call | solution.py:305
  136.1 1.5 %fusion.7 = (f32[64,256]{1,0:T(8,128)}, f32[64,256]{1,0:T(8,128)}) fusion(f32[64,256]{1,0:T(8,128)} %gather.1, f32[64,256]{1,0:T(8,128)S(1)} %copy-done, f32[2,64,256]{2,1,0:T(8,128)S(1)} %get-tuple-element.14, f32[2,64,256]{2,1,0:T(8,128)S(1)} %get-tuple-element.15), kind=kLoop, calls=%fused_computation.20 | loop fusion | flops 311296 | bytes 524288 | tf_op jit(solution)/shard_map/add | solution.py:398
  (55 shorter events, 6.9 us)
Async XLA Ops:
  0.6 1.0 copy-start
  0.6 1.0 copy-start.1
  0.7 1.0 copy-start.8
  2.2 10.2 %copy-start.3 = (f32[4,64,256]{2,1,0:T(8,128)}, f32[4,64,256]{2,1,0:T(8,128)S(1)}, u32[]{:S(2)}) copy-start(f32[4,64,256]{2,1,0:T(8,128)S(1)} %pad_maximum_fusion.refs_1_) | copy-start | bytes 786436
  2.2 16.8 %collective-permute-start.2 = (f32[4,64,256]{2,1,0:T(8,128)S(1)}, f32[4,64,256]{2,1,0:T(8,128)S(1)}, u32[]{:S(2)}, u32[]{:S(2)}) collective-permute-start(f32[4,64,256]{2,1,0:T(8,128)S(1)} %pad_maximum_fusion.refs_1_), channel_id=1, source_target_pairs={{0,28},{4,0},{8,4},{12,8},{16,12},{20,16},{24,20},{28,24},{1,29},{... | collective-permute-start | bytes 786440 | tf_op jit(solution)/shard_map/ppermute | solution.py:21
  5.6 13.4 %collective-permute-start = (f32[4,64,256]{2,1,0:T(8,128)S(1)}, f32[4,64,256]{2,1,0:T(8,128)S(1)}, u32[]{:S(2)}, u32[]{:S(2)}) collective-permute-start(f32[4,64,256]{2,1,0:T(8,128)S(1)} %pad_maximum_fusion.refs_1_), channel_id=1, source_target_pairs={{0,3},{1,0},{2,1},{3,2},{4,7},{5,4},{6,5},{7,6},{8,11},{9,8},{10,9... | collective-permute-start | bytes 786440 | tf_op jit(solution)/shard_map/ppermute | solution.py:21
  9.2 9.8 %collective-permute-start.8 = (f32[2,2,256]{2,1,0:T(2,128)S(1)}, f32[2,2,256]{2,1,0:T(2,128)S(1)}, u32[]{:S(2)}, u32[]{:S(2)}) collective-permute-start(f32[2,2,256]{2,1,0:T(2,128)S(1)} %get-tuple-element.12), channel_id=1, source_target_pairs={{0,4},{4,8},{8,12},{12,16},{16,20},{20,24},{24,28},{28,0},{1,5},{5... | collective-permute-start | bytes 12296 | tf_op jit(solution)/shard_map/ppermute | solution.py:21
  9.2 9.8 %collective-permute-start.9 = (f32[2,2,256]{2,1,0:T(2,128)S(1)}, f32[2,2,256]{2,1,0:T(2,128)S(1)}, u32[]{:S(2)}, u32[]{:S(2)}) collective-permute-start(f32[2,2,256]{2,1,0:T(2,128)S(1)} %get-tuple-element.13), channel_id=1, source_target_pairs={{0,28},{4,0},{8,4},{12,8},{16,12},{20,16},{24,20},{28,24},{1,29},{... | collective-permute-start | bytes 12296 | tf_op jit(solution)/shard_map/ppermute | solution.py:21
  12.4 3.1 %copy-start.9 = (s32[128,8]{0,1:T(8,128)S(1)}, s32[128,8]{0,1:T(8,128)}, u32[]{:S(2)}) copy-start(s32[128,8]{0,1:T(8,128)} %param.11) | copy-start | bytes 12292
  19.0 4.9 %copy-start.12 = (f32[4,64,256]{2,1,0:T(8,128)}, f32[4,64,256]{2,1,0:T(8,128)S(1)}, u32[]{:S(2)}) copy-start(f32[4,64,256]{2,1,0:T(8,128)S(1)} %collective-permute-done.refs_1_) | copy-start | bytes 786436
  19.0 10.4 %collective-permute-start.1 = (f32[4,64,256]{2,1,0:T(8,128)S(1)}, f32[4,64,256]{2,1,0:T(8,128)S(1)}, u32[]{:S(2)}, u32[]{:S(2)}) collective-permute-start(f32[4,64,256]{2,1,0:T(8,128)S(1)} %collective-permute-done.refs_1_), channel_id=1, source_target_pairs={{0,28},{4,0},{8,4},{12,8},{16,12},{20,16},{24,20},{28,24},{1,29},{... | collective-permute-start | bytes 786440 | tf_op jit(solution)/shard_map/ppermute | solution.py:21
  19.1 0.7 copy-start.13
  36.3 9.3 %collective-permute-start.3 = (f32[5,128,128]{2,1,0:T(8,128)}, f32[5,128,128]{2,1,0:T(8,128)S(1)}, u32[]{:S(2)}, u32[]{:S(2)}) collective-permute-start(f32[5,128,128]{2,1,0:T(8,128)} %get-tuple-element.3.own), channel_id=1, source_target_pairs={{0,1},{1,2},{2,3},{3,4},{4,5},{5,6},{6,7},{7,8},{8,9},{9,10},{10,1... | collective-permute-start | bytes 983048 | tf_op jit(solution)/shard_map/ppermute | solution.py:372
  37.6 19.4 %collective-permute-start.4 = (f32[5,128,128]{2,1,0:T(8,128)}, f32[5,128,128]{2,1,0:T(8,128)S(1)}, u32[]{:S(2)}, u32[]{:S(2)}) collective-permute-start(f32[5,128,128]{2,1,0:T(8,128)} %get-tuple-element.3.own), channel_id=1, source_target_pairs={{1,0},{2,1},{3,2},{4,3},{5,4},{6,5},{7,6},{8,7},{9,8},{10,9},{11,1... | collective-permute-start | bytes 983048 | tf_op jit(solution)/shard_map/ppermute | solution.py:373
  39.0 56.4 %collective-permute-start.10 = (f32[2,68,2]{2,1,0:T(8,128)S(1)}, f32[2,68,2]{2,1,0:T(8,128)S(1)}, u32[]{:S(2)}, u32[]{:S(2)}) collective-permute-start(f32[2,68,2]{2,1,0:T(8,128)S(1)} %get-tuple-element.6), channel_id=1, source_target_pairs={{0,1},{1,2},{2,3},{3,0},{4,5},{5,6},{6,7},{7,4},{8,9},{9,10},{10,1... | collective-permute-start | bytes 3272 | tf_op jit(solution)/shard_map/ppermute | solution.py:21
  41.7 53.7 %collective-permute-start.11 = (f32[2,68,2]{2,1,0:T(8,128)S(1)}, f32[2,68,2]{2,1,0:T(8,128)S(1)}, u32[]{:S(2)}, u32[]{:S(2)}) collective-permute-start(f32[2,68,2]{2,1,0:T(8,128)S(1)} %get-tuple-element.7), channel_id=1, source_target_pairs={{0,3},{1,0},{2,1},{3,2},{4,7},{5,4},{6,5},{7,6},{8,11},{9,8},{10,9... | collective-permute-start | bytes 3272 | tf_op jit(solution)/shard_map/ppermute | solution.py:21
  45.6 11.4 %copy-start.10 = (f32[5,128,128]{2,1,0:T(8,128)}, f32[5,128,128]{2,1,0:T(8,128)S(1)}, u32[]{:S(2)}) copy-start(f32[5,128,128]{2,1,0:T(8,128)S(1)} %collective-permute-done.3.lower) | copy-start | bytes 983044
  56.9 0.7 copy-start.11
  95.3 0.8 copy-start.4
  95.3 4.8 %collective-permute-start.5 = (f32[128,128]{1,0:T(8,128)}, f32[128,128]{1,0:T(8,128)S(1)}, u32[]{:S(2)}, u32[]{:S(2)}) collective-permute-start(f32[128,128]{1,0:T(8,128)} %near_field.1.own), channel_id=1, source_target_pairs={{0,4},{4,8},{8,12},{12,16},{16,20},{20,24},{24,28},{28,0},{1,5},{5... | collective-permute-start | bytes 196616 | tf_op jit(solution)/shard_map/ppermute | solution.py:21
  96.1 6.1 %collective-permute-start.6 = (f32[128,128]{1,0:T(8,128)S(1)}, f32[128,128]{1,0:T(8,128)S(1)}, u32[]{:S(2)}, u32[]{:S(2)}) collective-permute-start(f32[128,128]{1,0:T(8,128)S(1)} %copy-done.4), channel_id=1, source_target_pairs={{0,1},{1,2},{2,3},{3,0},{4,5},{5,6},{6,7},{7,4},{8,9},{9,10},{10,1... | collective-permute-start | bytes 196616 | tf_op jit(solution)/shard_map/ppermute | solution.py:21
  100.1 0.8 copy-start.5
  100.1 6.1 %collective-permute-start.7 = (f32[128,128]{1,0:T(8,128)S(1)}, f32[128,128]{1,0:T(8,128)S(1)}, u32[]{:S(2)}, u32[]{:S(2)}) collective-permute-start(f32[128,128]{1,0:T(8,128)S(1)} %collective-permute-done.5.behind_x), channel_id=1, source_target_pairs={{0,1},{1,2},{2,3},{3,0},{4,5},{5,6},{6,7},{7,4},{8,9},{9,10},{10,1... | collective-permute-start | bytes 196616 | tf_op jit(solution)/shard_map/ppermute | solution.py:21
  102.2 4.0 %copy-start.6 = (f32[128,128]{1,0:T(8,128)}, f32[128,128]{1,0:T(8,128)S(1)}, u32[]{:S(2)}) copy-start(f32[128,128]{1,0:T(8,128)S(1)} %collective-permute-done.6.behind_y) | copy-start | bytes 196612
  (3 other events, 2.0 us)

commit v2 on v1

v2 whole, which is shorter than its diff:
```python
import math

import jax
import jax.numpy as jnp
from jax import lax
from jax.experimental import pallas as pl
from jax.experimental.pallas import tpu as pltpu
from jax.sharding import PartitionSpec as P

LANES = 128
WIDE = 256
PIECES = 6
FEATURES = 32
USED = 24
EXTRA = 16
BF16 = jnp.bfloat16
F32 = jnp.float32


def shifted(value, axis, steps):
    count = lax.axis_size(axis)
    pairs = [(source, (source + steps) % count) for source in range(count)]
    return lax.ppermute(value, axis, pairs)


def ahead(axis, steps):
    index = lax.axis_index(axis) + steps
    count = lax.axis_size(axis)
    return jnp.where(index < 0, index + count, jnp.where(index >= count, index - count, index))


def pinned(value):
    return pltpu.with_memory_space_constraint(value, pltpu.VMEM)


def rounded(value):
    return value.astype(BF16).astype(F32)


def scatter_kernel(first, last, sizes, steps, tile, *refs):
    if first:
        acc = refs[0]
    else:
        acc_in, acc = refs[:2]
    rows, cols, high_count, node_rows, node_cols = sizes
    p = lax.axis_index("tx")
    q = lax.axis_index("ty")
    base = ((p * lax.axis_size("ty") + q) * (rows * cols)).astype(F32)
    off_i = float(steps[0] * rows)
    off_j = float((steps[1] - 1) * cols)
    acc[...] = jnp.zeros(acc.shape, F32) if first else acc_in[...]
    units = [(r, c) for r in range(rows // 8) for c in range(cols // LANES)]

    def split(r, c):
        rel = tile[0, 8 * r : 8 * r + 8, LANES * c : LANES * c + LANES] - base
        high = jnp.floor(rel * (1.0 / WIDE))
        return high, rel - high * WIDE

    flags = []
    for r, c in units:
        high, _ = split(r, c)
        mine = (high >= 0.0) & (high < high_count)
        flags.append(jnp.max(jnp.where(mine, 1.0, 0.0)) > 0.0)

    for (r, c), flag in zip(units, flags):

        @pl.when(flag)
        def _():
            high, low = split(r, c)
            window = (slice(8 * r, 8 * r + 8), slice(LANES * c, LANES * c + LANES))
            z = 0.25 * tile[(1,) + window]
            z_high = rounded(z)
            z_low = z - z_high
            pot = tile[(2,) + window]
            flux = tile[(3,) + window]
            col_index = (lax.broadcasted_iota(jnp.int32, (high_count, LANES), 1) + LANES * c).astype(F32) + off_j
            high_iota = lax.broadcasted_iota(jnp.int32, (high_count, LANES), 0).astype(F32)
            low_iota = lax.broadcasted_iota(jnp.int32, (WIDE, LANES), 0).astype(F32)
            lefts = []
            rights = []
            for s in range(8):

                def row(v):
                    return v[s : s + 1, :]

                hit = high_iota == row(high)
                row_index = jnp.full((1, LANES), 8 * r + s, F32) + off_i
                values = [row_index, col_index, row(z_high), row(z_low), row(pot), row(flux)]
                lefts.append(
                    jnp.concatenate([jnp.where(hit, v, 0.0).astype(BF16) for v in values], axis=0)
                )
                rights.append(jnp.where(low_iota == row(low), 1.0, 0.0).astype(BF16))
            acc[...] += lax.dot_general(
                jnp.concatenate(lefts, axis=1),
                jnp.concatenate(rights, axis=1),
                (((1,), (1,)), ((), ())),
                preferred_element_type=F32,
            )

    if last:
        boxed = refs[-1]
        h = high_count
        row0 = (p * rows).astype(F32)
        col0 = ((q + 1) * cols).astype(F32)
        i = acc[0:h] + row0
        i = jnp.where(i >= node_rows, i - node_rows, i)
        j = acc[h : 2 * h] + col0
        j = jnp.where(j >= node_cols, j - node_cols, j)
        fields = [
            (i + 0.5) / node_rows,
            (j + 0.5) / node_cols,
            acc[2 * h : 3 * h] + acc[3 * h : 4 * h],
            acc[4 * h : 5 * h],
            acc[5 * h : 6 * h],
        ]
        for k, f in enumerate(fields):
            boxed[k, 0:h, :] = f[:, :LANES]
            boxed[k, h : 2 * h, :] = f[:, LANES:]


def scatter(steps, tile, acc, last, node_rows, node_cols):
    _, rows, cols = tile.shape
    high_count = rows * cols // WIDE
    first = acc is None
    vmem = pl.BlockSpec(memory_space=pltpu.VMEM)
    out_shape = [pltpu.VMEM((PIECES * high_count, WIDE), F32)]
    if last:
        out_shape.append(pltpu.VMEM((5, 2 * high_count, LANES), F32))
    args = (tile,) if first else (tile, pinned(acc))
    out = pl.pallas_call(
        lambda *refs: scatter_kernel(
            first, last, (rows, cols, high_count, node_rows, node_cols), steps, *refs
        ),
        out_shape=out_shape,
        in_specs=[vmem] * len(args),
        out_specs=[vmem] * len(out_shape),
        name="scatter_last" if last else "scatter_first" if first else "scatter",
        cost_estimate=pl.CostEstimate(
            flops=2 * PIECES * high_count * WIDE * rows * cols // 2,
            transcendentals=0,
            bytes_accessed=4 * (2 * PIECES * high_count * WIDE + 4 * rows * cols),
        ),
    )(*args)
    return out[1] if last else out[0]


def thirds(value):
    high = rounded(value)
    middle = rounded(value - high)
    return high, middle, value - high - middle


def near_kernel(near, listed, own, lower, upper, tile, out, tfeat, sfeat, smeta, even, odd):
    boxes = own.shape[1]
    scale = 1.0 / math.sqrt(near * LANES)
    tpitch = tfeat.shape[0] // USED
    spitch = sfeat.shape[0] // USED

    zeros = jnp.zeros((8, LANES), F32)
    ones = jnp.ones((8, LANES), F32)

    for which, ref in enumerate((lower, own, upper)):
        for group in range(boxes // 8):
            window = (slice(8 * group, 8 * group + 8), slice(None))
            x, y, z, pot, flux = (ref[(f,) + window] for f in range(5))
            pieces = []
            total = None
            for v in (x, y, z):
                high = rounded(v)
                low = rounded(v - high)
                kept = high + low
                pieces.append((high, low))
                total = kept * kept if total is None else total + kept * kept
            start = which * boxes + 8 * group
            source = []
            for high, low in pieces:
                source += [-2.0 * high, -2.0 * low, -2.0 * high, -2.0 * low]
            source += list(thirds(total)) + [ones, ones, ones]
            source += [zeros] * (USED - len(source))
            for k, v in enumerate(source):
                sfeat[k * spitch + start : k * spitch + start + 8, :] = v
            z = pieces[2][0] + pieces[2][1]
            smeta[0, start : start + 8, :] = pot
            smeta[1, start : start + 8, :] = pot * z
            smeta[2, start : start + 8, :] = flux
            if which == 1:
                target = []
                for high, low in pieces:
                    target += [high, high, low, low]
                target += [ones, ones, ones] + list(thirds(total + 0.04)) + [z]
                target += [zeros] * (USED - len(target))
                for k, v in enumerate(target):
                    tfeat[k * tpitch + 8 * group : k * tpitch + 8 * group + 8, :] = v

    def load(ref, pitch, n):
        rows = [ref[pl.ds(8 * g * pitch + n, 8, stride=pitch), :] for g in range(USED // 8)]
        return jnp.concatenate(rows + [zeros] * ((FEATURES - USED) // 8), axis=0)

    def distances(box, squared, z_ref):
        left = load(tfeat, tpitch, box).T
        z_ref[...] = jnp.broadcast_to(left[:, 18:19], (LANES, LANES))
        rights = []
        for k in range(near):
            n = listed[box * near + k]
            rights.append(load(sfeat, spitch, n).astype(BF16))
        squared[...] = jnp.dot(
            left.astype(BF16), jnp.concatenate(rights, axis=1), preferred_element_type=F32
        )

    def apply(box, squared, z_ref):
        metas = []
        for k in range(near):
            n = listed[box * near + k]
            metas.append(
                [jnp.broadcast_to(smeta[m, pl.ds(n, 1), :], (8, LANES)) for m in range(3)]
            )
        parts = []
        for t in range(LANES // 8):
            rows = slice(8 * t, 8 * t + 8)
            z = z_ref[rows, :]
            total = None
            for k in range(near):
                pot, pot_z, flux = metas[k]
                inverse = lax.rsqrt(squared[rows, LANES * k : LANES * k + LANES])
                value = inverse * (flux - (inverse * inverse) * (z * pot - pot_z))
                total = value if total is None else total + value
            parts.append(total)
        summed = jnp.concatenate(parts, axis=0).T
        out[pl.ds(box, 1), :] = jnp.sum(summed, axis=0, keepdims=True) * scale

    (even_sq, even_z), (odd_sq, odd_z) = even, odd
    distances(0, even_sq, even_z)

    def step(i, carry):
        distances(2 * i + 1, odd_sq, odd_z)
        apply(2 * i, even_sq, even_z)
        distances(jnp.minimum(2 * i + 2, boxes - 1), even_sq, even_z)
        apply(2 * i + 1, odd_sq, odd_z)
        return carry

    lax.fori_loop(0, boxes // 2, step, 0)

    _, rows, cols = tile.shape
    out[boxes : boxes + EXTRA, :] = jnp.zeros((EXTRA, LANES), F32)
    place = boxes
    for f in (1, 2):
        for r in (rows - 2, rows - 1):
            for c in range(cols // LANES):
                out[place : place + 1, :] = tile[f, r : r + 1, LANES * c : LANES * c + LANES]
                place += 1
    place = boxes + EXTRA - 8
    for f in (1, 2):
        turned = tile[f, :, cols - LANES : cols].T
        out[place : place + 2, 0:rows] = turned[LANES - 2 : LANES, :]
        place += 2


def near_apply(listed, own, lower, upper, tile, near):
    boxes = own.shape[1]
    vmem = pl.BlockSpec(memory_space=pltpu.VMEM)
    smem = pl.BlockSpec(memory_space=pltpu.SMEM)
    buffers = [pltpu.VMEM((LANES, near * LANES), F32), pltpu.VMEM((LANES, LANES), F32)]

    def kernel(listed, own, lower, upper, tile, out, tfeat, sfeat, smeta, e0, e1, o0, o1):
        near_kernel(
            near, listed, own, lower, upper, tile, out, tfeat, sfeat, smeta, (e0, e1), (o0, o1)
        )

    pairs = boxes * near * LANES * LANES
    return pl.pallas_call(
        kernel,
        out_shape=pltpu.VMEM((boxes + EXTRA, LANES), F32),
        in_specs=[smem] + [vmem] * 4,
        out_specs=vmem,
        scratch_shapes=[
            pltpu.VMEM((USED * (boxes + 8), LANES), F32),
            pltpu.VMEM((USED * (3 * boxes + 8), LANES), F32),
            pltpu.VMEM((3, 3 * boxes, LANES), F32),
        ]
        + buffers
        + buffers,
        name="near_field",
        cost_estimate=pl.CostEstimate(
            flops=pairs * 2 * FEATURES * 4, transcendentals=pairs, bytes_accessed=4 * 16 * boxes * LANES
        ),
    )(listed, pinned(own), pinned(lower), pinned(upper), tile)


def lookup(slot, bases, tables, pieces, out):
    rows, cols = slot.shape
    high_count = rows * cols // WIDE
    units = [(r, c) for r in range(rows // 8) for c in range(cols // LANES)]
    for which, table in enumerate(tables):
        whole = jnp.concatenate([table[0:high_count, :], table[high_count : 2 * high_count, :]], axis=1)
        top = rounded(whole)
        pieces[which, 0:high_count, :] = top.astype(BF16)
        pieces[which, high_count : 2 * high_count, :] = (whole - top).astype(BF16)

    def split(r, c, which):
        rel = slot[8 * r : 8 * r + 8, LANES * c : LANES * c + LANES] - bases[which]
        high = jnp.floor(rel * (1.0 / WIDE))
        return high, rel - high * WIDE

    flags = {}
    for r, c in units:
        for which in range(len(tables)):
            high, _ = split(r, c, which)
            there = (high >= 0.0) & (high < high_count)
            flags[r, c, which] = jnp.max(jnp.where(there, 1.0, 0.0)) > 0.0

    for r, c in units:
        for which in range(len(tables)):

            @pl.when(flags[r, c, which])
            def _():
                high, low = split(r, c, which)
                low_iota = lax.broadcasted_iota(jnp.int32, (WIDE, LANES), 0).astype(F32)
                high_iota = lax.broadcasted_iota(jnp.int32, (high_count, LANES), 0).astype(F32)
                hits = jnp.concatenate(
                    [jnp.where(low_iota == low[s : s + 1, :], 1.0, 0.0).astype(BF16) for s in range(8)],
                    axis=1,
                )
                picked = jnp.dot(pieces[which], hits, preferred_element_type=F32)
                lines = []
                for s in range(8):
                    window = slice(LANES * s, LANES * s + LANES)
                    both = picked[0:high_count, window] + picked[high_count : 2 * high_count, window]
                    mine = high_iota == high[s : s + 1, :]
                    lines.append(jnp.sum(jnp.where(mine, both, 0.0), axis=0, keepdims=True))
                out[8 * r : 8 * r + 8, LANES * c : LANES * c + LANES] += jnp.concatenate(lines, axis=0)


def base_of(node_count, steps):
    rank = ahead("tx", -steps[0]) * lax.axis_size("ty") + ahead("ty", -steps[1])
    return (rank * node_count).astype(F32)


def gather_own_kernel(tile, own, out, pieces):
    out[...] = jnp.zeros(out.shape, F32)
    lookup(tile.at[0], [base_of(out.shape[0] * out.shape[1], (0, 0))], [own], pieces, out)


def gather_own(tile, own):
    _, rows, cols = tile.shape
    vmem = pl.BlockSpec(memory_space=pltpu.VMEM)
    return pl.pallas_call(
        gather_own_kernel,
        out_shape=pltpu.VMEM((rows, cols), F32),
        in_specs=[vmem] * 2,
        out_specs=vmem,
        scratch_shapes=[pltpu.VMEM((1, 2 * rows * cols // WIDE, WIDE), BF16)],
        name="gather_own",
        cost_estimate=pl.CostEstimate(
            flops=rows * cols * rows * cols, transcendentals=0, bytes_accessed=4 * 4 * rows * cols
        ),
    )(tile, pinned(own))


def finish_kernel(
    tile, ahead_x, ahead_y, partial, behind_x, behind_y, behind_xy, elev_rate, pot_rate, pieces, total, padded
):
    _, rows, cols = tile.shape
    boxes = rows * cols // LANES
    total[...] = partial[...]
    bases = [base_of(rows * cols, steps) for steps in ((1, 0), (0, 1), (1, 1))]
    lookup(tile.at[0], bases, [behind_x, behind_y, behind_xy], pieces, total)

    left_cols = behind_y[boxes + EXTRA - 8 : boxes + EXTRA, 0:rows].T
    col = lax.broadcasted_iota(jnp.int32, (rows, cols), 1)
    slopes = []
    for f in (1, 2):
        here = tile[f]
        padded[8 : 8 + rows, :] = here
        for r in range(2):
            for c in range(cols // LANES):
                source = boxes + ((f - 1) * 2 + r) * (cols // LANES) + c
                padded[6 + r : 7 + r, LANES * c : LANES * c + LANES] = behind_x[source : source + 1, :]
        padded[8 + rows : 10 + rows, :] = ahead_x[f, 0:2, :]
        along_rows = (
            padded[6 : 6 + rows, :]
            - 8.0 * padded[7 : 7 + rows, :]
            + 8.0 * padded[9 : 9 + rows, :]
            - padded[10 : 10 + rows, :]
        ) / 12.0
        left = left_cols[:, 2 * (f - 1) : 2 * f]
        right = ahead_y[f, :, 0:2]
        less_1 = jnp.where(col == 0, left[:, 1:2], pltpu.roll(here, 1, 1))
        less_2 = jnp.where(
            col == 0, left[:, 0:1], jnp.where(col == 1, left[:, 1:2], pltpu.roll(here, 2, 1))
        )
        more_1 = jnp.where(col == cols - 1, right[:, 0:1], pltpu.roll(here, cols - 1, 1))
        more_2 = jnp.where(
            col == cols - 2,
            right[:, 0:1],
            jnp.where(col == cols - 1, right[:, 1:2], pltpu.roll(here, cols - 2, 1)),
        )
        along_cols = (less_2 - 8.0 * less_1 + 8.0 * more_1 - more_2) / 12.0
        slopes.append((along_rows, along_cols))
    (elev_x, elev_y), (pot_x, pot_y) = slopes
    vertical = total[...]
    lift = 1.0 + elev_x * elev_x + elev_y * elev_y
    elev_rate[...] = vertical * lift - (pot_x * elev_x + pot_y * elev_y)
    pot_rate[...] = (
        -tile[1] - 0.5 * (pot_x * pot_x + pot_y * pot_y) + 0.5 * vertical * vertical * lift
    )


def finish(tile, ahead_x, ahead_y, partial, behind):
    _, rows, cols = tile.shape
    vmem = pl.BlockSpec(memory_space=pltpu.VMEM)
    shape = jax.ShapeDtypeStruct((rows, cols), F32)
    return pl.pallas_call(
        finish_kernel,
        out_shape=(shape, shape),
        in_specs=[vmem] * 7,
        out_specs=(vmem, vmem),
        scratch_shapes=[
            pltpu.VMEM((3, 2 * rows * cols // WIDE, WIDE), BF16),
            pltpu.VMEM((rows, cols), F32),
            pltpu.VMEM((rows + 16, cols), F32),
        ],
        name="finish",
        cost_estimate=pl.CostEstimate(
            flops=3 * rows * cols * rows * cols, transcendentals=0, bytes_accessed=4 * 8 * rows * cols
        ),
    )(tile, ahead_x, ahead_y, pinned(partial), *[pinned(b) for b in behind])


def shards(potential, elevation, normal_flux, box_owner, box_place, near_boxes):
    rows, cols = potential.shape
    count_tx = lax.axis_size("tx")
    count_ty = lax.axis_size("ty")
    node_count = rows * cols
    boxes = node_count // LANES
    near = near_boxes.shape[1]
    half = boxes // 2
    assert node_count % WIDE == 0 and cols <= 256 and rows <= 128
    assert 4 * (cols // LANES) <= EXTRA - 8
    assert node_count * count_tx * count_ty < 2**24
    rank = lax.axis_index("tx") * count_ty + lax.axis_index("ty")

    slot = (box_owner * node_count + box_place).astype(F32)
    tile = jnp.stack([slot, elevation, potential, normal_flux])
    ahead_x = shifted(tile, "tx", -1)
    ahead_y = shifted(tile, "ty", -1)
    ahead_xy = shifted(ahead_y, "tx", -1)
    tile, ahead_x, ahead_y, ahead_xy = map(pinned, (tile, ahead_x, ahead_y, ahead_xy))

    sizes = (rows * count_tx, cols * count_ty)
    acc = scatter((0, 0), tile, None, False, *sizes)
    acc = scatter((1, 0), ahead_x, acc, False, *sizes)
    acc = scatter((0, 1), ahead_y, acc, False, *sizes)
    boxed = scatter((1, 1), ahead_xy, acc, True, *sizes)

    total = count_tx * count_ty
    both = ("tx", "ty")
    lower = lax.ppermute(boxed, both, [(i, i + 1) for i in range(total - 1)])
    upper = lax.ppermute(boxed, both, [(i + 1, i) for i in range(total - 1)])

    local = near_boxes - (rank - 1) * boxes
    inner = local % boxes
    listed = (local // boxes) * boxes + (inner % 2) * half + inner // 2
    listed = listed.reshape(half, 2, near).transpose(1, 0, 2).reshape(boxes * near)
    value = near_apply(listed, boxed, lower, upper, tile, near)

    behind_x = shifted(value, "tx", 1)
    behind_y = shifted(value, "ty", 1)
    diagonal = [
        (i * count_ty + j, (i + 1) % count_tx * count_ty + (j + 1) % count_ty)
        for i in range(count_tx)
        for j in range(count_ty)
    ]
    behind_xy = lax.ppermute(value, both, diagonal)
    partial = gather_own(tile, value)
    return finish(tile, ahead_x, ahead_y, partial, (behind_x, behind_y, behind_xy))


def solution(mesh):
    in_specs = (
        P("tx", "ty"),
        P("tx", "ty"),
        P("tx", "ty"),
        P("tx", "ty"),
        P("tx", "ty"),
        P(("tx", "ty"), None),
    )
    out_specs = (P("tx", "ty"), P("tx", "ty"))
    return jax.shard_map(shards, mesh=mesh, in_specs=in_specs, out_specs=out_specs, check_vma=False)
```

time: 138 us -> 94.2 us (0.68)
  Pallas kernels: 85.8 us -> 53.8 us
  local copies, waits for them, and re-layouts: 6.59 us -> 1.49 us
  starting transfers between devices: 19 us -> 14 us
  other arithmetic: 4.18 us -> 0.97 us
  waiting for transfers between devices: 21.2 us -> 22.9 us
    pallas_call x2 -> x3, Pallas kernels: 66.9 us -> 41.4 us  [the longest x1 33.6 us: near_apply(): pl.pallas_call(kernel, out_shape=pltpu.VMEM((boxes + EXTRA, LANES), F32),...]
    ppermute x10 -> x5, starting transfers between devices: 16.4 us -> 9.03 us  [shifted(): return lax.ppermute(value, axis, pairs)]
    pallas_call x4, Pallas kernels: 18.9 us -> 12.4 us  [scatter(): pl.pallas_call(lambda *refs: scatter_kernel(first, last, (rows, cols, hig...]
    ppermute x1, waiting for transfers between devices: 1.13 us -> 4.92 us  [shards(): lower = lax.ppermute(boxed, both, [(i, i + 1) for i in range(total - 1)])]
    unnamed x30 -> x8, local copies, waits for them, and re-layouts: 3.9 us -> 0.69 us
    ppermute x10 -> x5, waiting for transfers between devices: 8.72 us -> 5.54 us  [shifted(): return lax.ppermute(value, axis, pairs)]
    ppermute x0 -> x1, waiting for transfers between devices: none -> 2.47 us  [shards(): behind_xy = lax.ppermute(value, both, diagonal)]
    another operation x4 -> x0, local copies, waits for them, and re-layouts: 1.82 us -> none  [the longest x3 1.82 us: info(): jnp.stack([base, jnp.int32(di * rows), jnp.int32((dj - 1) * cols), p * ro...]
  transfers between devices with their start and end apart: 12 -> 8, of which waited for: 5 -> 6; matrix products, arithmetic and copies ran while one was open for 3% -> 1% of each run, Pallas kernels for 37% -> 9%
where the time goes in v2:
time: 94.2 us; the launch traced here: 93.9 us
  Pallas kernels  53.8 us (57%)
  waiting for transfers between devices  22.9 us (24%)
  starting transfers between devices  14 us (15%)
  local copies, waits for them, and re-layouts  1.49 us (2%)
  other arithmetic  0.97 us (1%)
    pallas_call x1, Pallas kernels, near_apply(): pl.pallas_call(kernel, out_shape=pltpu.VMEM((boxes + EXTRA, LANES), F32),...  33.6 us
    pallas_call x4, Pallas kernels, scatter(): pl.pallas_call(lambda *refs: scatter_kernel(first, last, (rows, cols, hig...  12.4 us
    ppermute x1, waiting for transfers between devices, shards(): upper = lax.ppermute(boxed, both, [(i + 1, i) for i in range(total - 1)])  9.95 us
    ppermute x5, starting transfers between devices, shifted(): return lax.ppermute(value, axis, pairs)  9.03 us
    pallas_call x1, Pallas kernels, finish(): pl.pallas_call(finish_kernel, out_shape=(shape, shape), in_specs=[vmem] *...  6.87 us
    ppermute x5, waiting for transfers between devices, shifted(): return lax.ppermute(value, axis, pairs)  5.54 us
    ppermute x1, waiting for transfers between devices, shards(): lower = lax.ppermute(boxed, both, [(i, i + 1) for i in range(total - 1)])  4.92 us
    ppermute x1, waiting for transfers between devices, shards(): behind_xy = lax.ppermute(value, both, diagonal)  2.47 us
  transfers between devices with their start and end apart: 8, of which 6 were waited for; matrix products, arithmetic and copies ran while one was open for 1% of the time, Pallas kernels for 9%

profile of v2, /device:TPU:0, one launch (start us, length us, event | category | flops | bytes accessed | tf_op | source)
XLA Modules:
  0.0 93.9 jit_solution(16752815172206637919)
XLA Ops:
  0.7 0.9 convert_bitcast_fusion
  1.6 5.1 %collective-permute-start.1 = (f32[4,64,256]{2,1,0:T(8,128)S(1)}, f32[4,64,256]{2,1,0:T(8,128)S(1)}, u32[]{:S(2)}, u32[]{:S(2)}) collective-permute-start(f32[4,64,256]{2,1,0:T(8,128)S(1)} %pad_maximum_fusion.refs_0_.tile), channel_id=1, source_target_pairs={{0,3},{1,0},{2,1},{3,2},{4,7},{5,4},{6,5},{7,6},{8,11},{9,8},{10,9... | collective-permute-start | bytes 786440 | tf_op jit(solution)/shard_map/ppermute | solution.py:23
  6.8 1.6 %collective-permute-start = (f32[4,64,256]{2,1,0:T(8,128)S(1)}, f32[4,64,256]{2,1,0:T(8,128)S(1)}, u32[]{:S(2)}, u32[]{:S(2)}) collective-permute-start(f32[4,64,256]{2,1,0:T(8,128)S(1)} %pad_maximum_fusion.refs_0_.tile), channel_id=1, source_target_pairs={{0,28},{4,0},{8,4},{12,8},{16,12},{20,16},{24,20},{28,24},{1,29},{... | collective-permute-start | bytes 786440 | tf_op jit(solution)/shard_map/ppermute | solution.py:23
  8.4 1.4 %scatter_first.1.refs_1_ = f32[384,256]{1,0:T(8,128)S(1)} custom-call(f32[4,64,256]{2,1,0:T(8,128)S(1)} %pad_maximum_fusion.refs_0_.tile), custom_call_target="tpu_custom_call" | custom-call | flops 1610612736 | bytes 1048576 | tf_op jit(solution)/shard_map/scatter_first/pallas_call | solution.py:130
  9.8 2.5 %collective-permute-done.1.refs_0_.ahead_y = f32[4,64,256]{2,1,0:T(8,128)S(1)} collective-permute-done((f32[4,64,256]{2,1,0:T(8,128)S(1)}, f32[4,64,256]{2,1,0:T(8,128)S(1)}, u32[]{:S(2)}, u32[]{:S(2)}) %collective-permute-start.1) | collective-permute-done | bytes 262176 | tf_op jit(solution)/shard_map/ppermute | solution.py:23
  12.3 1.0 %collective-permute-start.2 = (f32[4,64,256]{2,1,0:T(8,128)S(1)}, f32[4,64,256]{2,1,0:T(8,128)S(1)}, u32[]{:S(2)}, u32[]{:S(2)}) collective-permute-start(f32[4,64,256]{2,1,0:T(8,128)S(1)} %collective-permute-done.1.refs_0_.ahead_y), channel_id=1, source_target_pairs={{0,28},{4,0},{8,4},{12,8},{16,12},{20,16},{24,20},{28,24},{1,29},{... | collective-permute-start | bytes 786440 | tf_op jit(solution)/shard_map/ppermute | solution.py:23
  13.4 2.2 %scatter.2.refs_1_ = f32[384,256]{1,0:T(8,128)S(1)} custom-call(f32[4,64,256]{2,1,0:T(8,128)S(1)} %collective-permute-done.refs_0_.ahead_x, f32[384,256]{1,0:T(8,128)S(1)} %scatter_first.1.refs_1_), custom_call_target="tpu_custom_call" | custom-call | flops 1610612736 | bytes 1048576 | tf_op jit(solution)/shard_map/scatter/pallas_call | solution.py:130
  15.6 3.7 %scatter.3.refs_1_ = f32[384,256]{1,0:T(8,128)S(1)} custom-call(f32[4,64,256]{2,1,0:T(8,128)S(1)} %collective-permute-done.1.refs_0_.ahead_y, f32[384,256]{1,0:T(8,128)S(1)} %scatter.2.refs_1_), custom_call_target="tpu_custom_call" | custom-call | flops 1610612736 | bytes 1048576 | tf_op jit(solution)/shard_map/scatter/pallas_call | solution.py:130
  19.3 5.1 %scatter_last.1 = (f32[384,256]{1,0:T(8,128)}, f32[5,128,128]{2,1,0:T(8,128)S(1)}) custom-call(f32[4,64,256]{2,1,0:T(8,128)S(1)} %collective-permute-done.2.refs_0_, f32[384,256]{1,0:T(8,128)S(1)} %scatter.3.refs_1_), custom_call_target="tpu_custom_call" | custom-call | flops 1610612736 | bytes 1048576 | tf_op jit(solution)/shard_map/scatter_last/pallas_call | solution.py:130
  24.4 2.4 %collective-permute-start.3 = (f32[5,128,128]{2,1,0:T(8,128)S(1)}, f32[5,128,128]{2,1,0:T(8,128)S(1)}, u32[]{:S(2)}, u32[]{:S(2)}) collective-permute-start(f32[5,128,128]{2,1,0:T(8,128)S(1)} %get-tuple-element.3.own), channel_id=1, source_target_pairs={{0,1},{1,2},{2,3},{3,4},{4,5},{5,6},{6,7},{7,8},{8,9},{9,10},{10,1... | collective-permute-start | bytes 983048 | tf_op jit(solution)/shard_map/ppermute | solution.py:457
  26.8 1.3 %collective-permute-start.4 = (f32[5,128,128]{2,1,0:T(8,128)S(1)}, f32[5,128,128]{2,1,0:T(8,128)S(1)}, u32[]{:S(2)}, u32[]{:S(2)}) collective-permute-start(f32[5,128,128]{2,1,0:T(8,128)S(1)} %get-tuple-element.3.own), channel_id=1, source_target_pairs={{1,0},{2,1},{3,2},{4,3},{5,4},{6,5},{7,6},{8,7},{9,8},{10,9},{11,1... | collective-permute-start | bytes 983048 | tf_op jit(solution)/shard_map/ppermute | solution.py:458
  28.1 0.7 copy-done.3
  28.8 0.1 copy.8
  28.9 0.7 reshape.11.listed
  29.6 4.9 %collective-permute-done.3.lower = f32[5,128,128]{2,1,0:T(8,128)S(1)} collective-permute-done((f32[5,128,128]{2,1,0:T(8,128)S(1)}, f32[5,128,128]{2,1,0:T(8,128)S(1)}, u32[]{:S(2)}, u32[]{:S(2)}) %collective-permute-start.3) | collective-permute-done | bytes 327712 | tf_op jit(solution)/shard_map/ppermute | solution.py:457
  34.5 10.0 %collective-permute-done.4.upper = f32[5,128,128]{2,1,0:T(8,128)S(1)} collective-permute-done((f32[5,128,128]{2,1,0:T(8,128)S(1)}, f32[5,128,128]{2,1,0:T(8,128)S(1)}, u32[]{:S(2)}, u32[]{:S(2)}) %collective-permute-start.4) | collective-permute-done | bytes 327712 | tf_op jit(solution)/shard_map/ppermute | solution.py:458
  44.5 33.6 %near_field.1.own = f32[144,128]{1,0:T(8,128)S(1)} custom-call(s32[1024]{0:T(1024)} %reshape.11.listed, f32[5,128,128]{2,1,0:T(8,128)S(1)} %get-tuple-element.3.own, f32[5,128,128]{2,1,0:T(8,128)S(1)} %collective-permute-done.3.lower, f32[5,128,128]{2,1,0:T(8,128)S(1)} %collective-permute-done.4.upper, f32[4,64,256]{2,1,0:T(8,128)S(1)} %pad_maximum_fusion.refs_0_.tile), custom_call_target="tpu_custom_call" | custom-call | flops 4294967296 | bytes 1048576 | tf_op jit(solution)/shard_map/near_field/pallas_call | solution.py:270
  78.2 1.2 %collective-permute-start.6 = (f32[144,128]{1,0:T(8,128)S(1)}, f32[144,128]{1,0:T(8,128)S(1)}, u32[]{:S(2)}, u32[]{:S(2)}) collective-permute-start(f32[144,128]{1,0:T(8,128)S(1)} %near_field.1.own), channel_id=1, source_target_pairs={{0,1},{1,2},{2,3},{3,0},{4,5},{5,6},{6,7},{7,4},{8,9},{9,10},{10,1... | collective-permute-start | bytes 221192 | tf_op jit(solution)/shard_map/ppermute | solution.py:23
  79.4 1.2 %collective-permute-start.7 = (f32[144,128]{1,0:T(8,128)S(1)}, f32[144,128]{1,0:T(8,128)S(1)}, u32[]{:S(2)}, u32[]{:S(2)}) collective-permute-start(f32[144,128]{1,0:T(8,128)S(1)} %near_field.1.own), channel_id=1, source_target_pairs={{0,5},{1,6},{2,7},{3,4},{4,9},{5,10},{6,11},{7,8},{8,13},{9,14},{1... | collective-permute-start | bytes 221192 | tf_op jit(solution)/shard_map/ppermute | solution.py:473
  80.6 0.9 gather_own.1.partial
  81.6 1.3 %collective-permute-done.5.behind_x = f32[144,128]{1,0:T(8,128)S(1)} collective-permute-done((f32[144,128]{1,0:T(8,128)S(1)}, f32[144,128]{1,0:T(8,128)S(1)}, u32[]{:S(2)}, u32[]{:S(2)}) %collective-permute-start.5) | collective-permute-done | bytes 73760 | tf_op jit(solution)/shard_map/ppermute | solution.py:23
  82.9 1.7 %collective-permute-done.6.behind_y = f32[144,128]{1,0:T(8,128)S(1)} collective-permute-done((f32[144,128]{1,0:T(8,128)S(1)}, f32[144,128]{1,0:T(8,128)S(1)}, u32[]{:S(2)}, u32[]{:S(2)}) %collective-permute-start.6) | collective-permute-done | bytes 73760 | tf_op jit(solution)/shard_map/ppermute | solution.py:23
  84.6 2.5 %collective-permute-done.7.behind_xy = f32[144,128]{1,0:T(8,128)S(1)} collective-permute-done((f32[144,128]{1,0:T(8,128)S(1)}, f32[144,128]{1,0:T(8,128)S(1)}, u32[]{:S(2)}, u32[]{:S(2)}) %collective-permute-start.7) | collective-permute-done | bytes 73760 | tf_op jit(solution)/shard_map/ppermute | solution.py:473
  87.1 6.9 %finish.1 = (f32[64,256]{1,0:T(8,128)}, f32[64,256]{1,0:T(8,128)}) custom-call(f32[4,64,256]{2,1,0:T(8,128)S(1)} %pad_maximum_fusion.refs_0_.tile, f32[4,64,256]{2,1,0:T(8,128)S(1)} %collective-permute-done.refs_0_.ahead_x, f32[4,64,256]{2,1,0:T(8,128)S(1)} %collective-permute-done.1.refs_0_.ahead_y, f32[64,256]{1,0:T(8,128)S(1)} %gather_own.1.partial, ...), custom_call_target="tpu_custom_call" | custom-call | flops 805306368 | bytes 524288 | tf_op jit(solution)/shard_map/finish/pallas_call | solution.py:412
  (13 shorter events, 0.1 us)
Async XLA Ops:
  0.6 1.0 %copy-start.2 = (f32[64,256]{1,0:T(8,128)S(1)}, f32[64,256]{1,0:T(8,128)}, u32[]{:S(2)}) copy-start(f32[64,256]{1,0:T(8,128)} %param.7) | copy-start | bytes 196612
  0.6 1.0 %copy-start.1 = (f32[64,256]{1,0:T(8,128)S(1)}, f32[64,256]{1,0:T(8,128)}, u32[]{:S(2)}) copy-start(f32[64,256]{1,0:T(8,128)} %param.6) | copy-start | bytes 196612
  0.7 1.0 %copy-start = (f32[64,256]{1,0:T(8,128)S(1)}, f32[64,256]{1,0:T(8,128)}, u32[]{:S(2)}) copy-start(f32[64,256]{1,0:T(8,128)} %param.8) | copy-start | bytes 196612
  1.6 10.7 %collective-permute-start.1 = (f32[4,64,256]{2,1,0:T(8,128)S(1)}, f32[4,64,256]{2,1,0:T(8,128)S(1)}, u32[]{:S(2)}, u32[]{:S(2)}) collective-permute-start(f32[4,64,256]{2,1,0:T(8,128)S(1)} %pad_maximum_fusion.refs_0_.tile), channel_id=1, source_target_pairs={{0,3},{1,0},{2,1},{3,2},{4,7},{5,4},{6,5},{7,6},{8,11},{9,8},{10,9... | collective-permute-start | bytes 786440 | tf_op jit(solution)/shard_map/ppermute | solution.py:23
  6.8 6.6 %collective-permute-start = (f32[4,64,256]{2,1,0:T(8,128)S(1)}, f32[4,64,256]{2,1,0:T(8,128)S(1)}, u32[]{:S(2)}, u32[]{:S(2)}) collective-permute-start(f32[4,64,256]{2,1,0:T(8,128)S(1)} %pad_maximum_fusion.refs_0_.tile), channel_id=1, source_target_pairs={{0,28},{4,0},{8,4},{12,8},{16,12},{20,16},{24,20},{28,24},{1,29},{... | collective-permute-start | bytes 786440 | tf_op jit(solution)/shard_map/ppermute | solution.py:23
  12.3 7.0 %collective-permute-start.2 = (f32[4,64,256]{2,1,0:T(8,128)S(1)}, f32[4,64,256]{2,1,0:T(8,128)S(1)}, u32[]{:S(2)}, u32[]{:S(2)}) collective-permute-start(f32[4,64,256]{2,1,0:T(8,128)S(1)} %collective-permute-done.1.refs_0_.ahead_y), channel_id=1, source_target_pairs={{0,28},{4,0},{8,4},{12,8},{16,12},{20,16},{24,20},{28,24},{1,29},{... | collective-permute-start | bytes 786440 | tf_op jit(solution)/shard_map/ppermute | solution.py:23
  24.4 10.2 %collective-permute-start.3 = (f32[5,128,128]{2,1,0:T(8,128)S(1)}, f32[5,128,128]{2,1,0:T(8,128)S(1)}, u32[]{:S(2)}, u32[]{:S(2)}) collective-permute-start(f32[5,128,128]{2,1,0:T(8,128)S(1)} %get-tuple-element.3.own), channel_id=1, source_target_pairs={{0,1},{1,2},{2,3},{3,4},{4,5},{5,6},{6,7},{7,8},{8,9},{9,10},{10,1... | collective-permute-start | bytes 983048 | tf_op jit(solution)/shard_map/ppermute | solution.py:457
  26.8 17.7 %collective-permute-start.4 = (f32[5,128,128]{2,1,0:T(8,128)S(1)}, f32[5,128,128]{2,1,0:T(8,128)S(1)}, u32[]{:S(2)}, u32[]{:S(2)}) collective-permute-start(f32[5,128,128]{2,1,0:T(8,128)S(1)} %get-tuple-element.3.own), channel_id=1, source_target_pairs={{1,0},{2,1},{3,2},{4,3},{5,4},{6,5},{7,6},{8,7},{9,8},{10,9},{11,1... | collective-permute-start | bytes 983048 | tf_op jit(solution)/shard_map/ppermute | solution.py:458
  28.1 0.7 copy-start.3
  78.1 4.7 %collective-permute-start.5 = (f32[144,128]{1,0:T(8,128)S(1)}, f32[144,128]{1,0:T(8,128)S(1)}, u32[]{:S(2)}, u32[]{:S(2)}) collective-permute-start(f32[144,128]{1,0:T(8,128)S(1)} %near_field.1.own), channel_id=1, source_target_pairs={{0,4},{4,8},{8,12},{12,16},{16,20},{20,24},{24,28},{28,0},{1,5},{5... | collective-permute-start | bytes 221192 | tf_op jit(solution)/shard_map/ppermute | solution.py:23
  78.2 6.4 %collective-permute-start.6 = (f32[144,128]{1,0:T(8,128)S(1)}, f32[144,128]{1,0:T(8,128)S(1)}, u32[]{:S(2)}, u32[]{:S(2)}) collective-permute-start(f32[144,128]{1,0:T(8,128)S(1)} %near_field.1.own), channel_id=1, source_target_pairs={{0,1},{1,2},{2,3},{3,0},{4,5},{5,6},{6,7},{7,4},{8,9},{9,10},{10,1... | collective-permute-start | bytes 221192 | tf_op jit(solution)/shard_map/ppermute | solution.py:23
  79.4 7.6 %collective-permute-start.7 = (f32[144,128]{1,0:T(8,128)S(1)}, f32[144,128]{1,0:T(8,128)S(1)}, u32[]{:S(2)}, u32[]{:S(2)}) collective-permute-start(f32[144,128]{1,0:T(8,128)S(1)} %near_field.1.own), channel_id=1, source_target_pairs={{0,5},{1,6},{2,7},{3,4},{4,9},{5,10},{6,11},{7,8},{8,13},{9,14},{1... | collective-permute-start | bytes 221192 | tf_op jit(solution)/shard_map/ppermute | solution.py:473

commit v3 on v2

--- a/solution.py
+++ b/solution.py
@@ -13,6 +13,8 @@
 FEATURES = 32
 USED = 24
 EXTRA = 16
+GROUP = 4
+VMEM_LIMIT = 24 << 20
 BF16 = jnp.bfloat16
 F32 = jnp.float32
 
@@ -35,6 +37,14 @@
 
 def rounded(value):
     return value.astype(BF16).astype(F32)
+
+
+def box_split(rel, high_count):
+    box = jnp.floor(rel * (1.0 / LANES))
+    second = box >= high_count
+    high = jnp.where(second, box - high_count, box)
+    low = rel - box * LANES
+    return high, jnp.where(second, low + LANES, low)
 
 
 def scatter_kernel(first, last, sizes, steps, tile, *refs):
@@ -52,9 +62,7 @@
     units = [(r, c) for r in range(rows // 8) for c in range(cols // LANES)]
 
     def split(r, c):
-        rel = tile[0, 8 * r : 8 * r + 8, LANES * c : LANES * c + LANES] - base
-        high = jnp.floor(rel * (1.0 / WIDE))
-        return high, rel - high * WIDE
+        return box_split(tile[0, 8 * r : 8 * r + 8, LANES * c : LANES * c + LANES] - base, high_count)
 
     flags = []
     for r, c in units:
@@ -134,6 +142,7 @@
         out_shape=out_shape,
         in_specs=[vmem] * len(args),
         out_specs=[vmem] * len(out_shape),
+        compiler_params=pltpu.CompilerParams(vmem_limit_bytes=VMEM_LIMIT),
         name="scatter_last" if last else "scatter_first" if first else "scatter",
         cost_estimate=pl.CostEstimate(
             flops=2 * PIECES * high_count * WIDE * rows * cols // 2,
@@ -150,95 +159,204 @@
     return high, middle, value - high - middle
 
 
-def near_kernel(near, listed, own, lower, upper, tile, out, tfeat, sfeat, smeta, even, odd):
-    boxes = own.shape[1]
-    scale = 1.0 / math.sqrt(near * LANES)
-    tpitch = tfeat.shape[0] // USED
-    spitch = sfeat.shape[0] // USED
-
+def layout(boxes, near):
+    items = boxes * ((near + 1) // 2) + 4 * GROUP
+    return items, (8, 8 + items), (8 + 3 * items, 8 + 4 * items), 8 + 6 * items
+
+
+def plan_kernel(boxes, near, listed, plan):
+    _, own_at, other_at, _ = layout(boxes, near)
+    rank = lax.axis_index("tx") * lax.axis_size("ty") + lax.axis_index("ty")
+    offset = (rank - 1) * boxes
+    deepest = (near + 1) // 2
+
+    def one(b, carry):
+        own_items, other_items = carry
+        own = 2 * own_items
+        other = 2 * other_items
+        for k in range(near):
+            n = listed[k * boxes + b] - offset
+            mine = jnp.where((n >= boxes) & (n < 2 * boxes), 1, 0)
+            plan[own_at[1] + own] = n - boxes
+            plan[other_at[1] + other] = jnp.where(n < boxes, n, n - boxes)
+            own = own + mine
+            other = other + 1 - mine
+        plan[own_at[1] + own] = boxes
+        plan[other_at[1] + other] = 2 * boxes
+        for i in range(deepest):
+            plan[own_at[0] + own_items + i] = b
+            plan[other_at[0] + other_items + i] = b
+        return (own + 1) // 2, (other + 1) // 2
+
+    own_items, other_items = lax.fori_loop(0, boxes, one, (jnp.int32(0), jnp.int32(0)))
+    for at, count, empty in ((own_at, own_items, boxes), (other_at, other_items, 2 * boxes)):
+        for i in range(3 * GROUP):
+            plan[at[0] + count + i] = boxes
+            plan[at[1] + 2 * (count + i)] = empty
+            plan[at[1] + 2 * (count + i) + 1] = empty
+    plan[0] = (own_items + 2 * GROUP - 1) // (2 * GROUP)
+    plan[1] = (other_items + 2 * GROUP - 1) // (2 * GROUP)
+
+
+def make_plan(near_boxes):
+    boxes, near = near_boxes.shape
+    smem = pl.BlockSpec(memory_space=pltpu.SMEM)
+    return pl.pallas_call(
+        lambda *refs: plan_kernel(boxes, near, *refs),
+        out_shape=jax.ShapeDtypeStruct((layout(boxes, near)[-1],), jnp.int32),
+        in_specs=[smem],
+        out_specs=smem,
+        compiler_params=pltpu.CompilerParams(vmem_limit_bytes=VMEM_LIMIT),
+        name="plan",
+        cost_estimate=pl.CostEstimate(flops=10**7, transcendentals=0, bytes_accessed=16 * boxes * near),
+    )(near_boxes.T.reshape(boxes * near))
+
+
+def pieces_of(ref, group):
+    window = (slice(8 * group, 8 * group + 8), slice(None))
+    x, y, z, pot, flux = (ref[(f,) + window] for f in range(5))
+    pieces = []
+    total = None
+    for v in (x, y, z):
+        high = rounded(v)
+        low = rounded(v - high)
+        kept = high + low
+        pieces.append((high, low))
+        total = kept * kept if total is None else total + kept * kept
+    return pieces, total, pot, flux
+
+
+def padded_rows(values):
+    return values + [jnp.zeros_like(values[0])] * (USED - len(values))
+
+
+def strided(ref, n):
+    pitch = ref.shape[0] // USED
+    rows = [ref[pl.ds(8 * g * pitch + n, 8, stride=pitch), :] for g in range(USED // 8)]
+    return jnp.concatenate(rows + [jnp.zeros((8, LANES), F32)] * ((FEATURES - USED) // 8), axis=0)
+
+
+def store_sources(refs, sfeat, smeta):
+    pitch = sfeat.shape[0] // USED
+    ones = jnp.ones((8, LANES), F32)
     zeros = jnp.zeros((8, LANES), F32)
-    ones = jnp.ones((8, LANES), F32)
-
-    for which, ref in enumerate((lower, own, upper)):
-        for group in range(boxes // 8):
-            window = (slice(8 * group, 8 * group + 8), slice(None))
-            x, y, z, pot, flux = (ref[(f,) + window] for f in range(5))
-            pieces = []
-            total = None
-            for v in (x, y, z):
-                high = rounded(v)
-                low = rounded(v - high)
-                kept = high + low
-                pieces.append((high, low))
-                total = kept * kept if total is None else total + kept * kept
-            start = which * boxes + 8 * group
+    start = 0
+    for ref in refs:
+        for group in range(ref.shape[1] // 8):
+            pieces, total, pot, flux = pieces_of(ref, group)
             source = []
             for high, low in pieces:
                 source += [-2.0 * high, -2.0 * low, -2.0 * high, -2.0 * low]
-            source += list(thirds(total)) + [ones, ones, ones]
-            source += [zeros] * (USED - len(source))
-            for k, v in enumerate(source):
-                sfeat[k * spitch + start : k * spitch + start + 8, :] = v
+            for k, v in enumerate(padded_rows(source + list(thirds(total)) + [ones, ones, ones])):
+                sfeat[k * pitch + start : k * pitch + start + 8, :] = v
             z = pieces[2][0] + pieces[2][1]
             smeta[0, start : start + 8, :] = pot
             smeta[1, start : start + 8, :] = pot * z
             smeta[2, start : start + 8, :] = flux
-            if which == 1:
-                target = []
-                for high, low in pieces:
-                    target += [high, high, low, low]
-                target += [ones, ones, ones] + list(thirds(total + 0.04)) + [z]
-                target += [zeros] * (USED - len(target))
-                for k, v in enumerate(target):
-                    tfeat[k * tpitch + 8 * group : k * tpitch + 8 * group + 8, :] = v
-
-    def load(ref, pitch, n):
-        rows = [ref[pl.ds(8 * g * pitch + n, 8, stride=pitch), :] for g in range(USED // 8)]
-        return jnp.concatenate(rows + [zeros] * ((FEATURES - USED) // 8), axis=0)
-
-    def distances(box, squared, z_ref):
-        left = load(tfeat, tpitch, box).T
-        z_ref[...] = jnp.broadcast_to(left[:, 18:19], (LANES, LANES))
-        rights = []
-        for k in range(near):
-            n = listed[box * near + k]
-            rights.append(load(sfeat, spitch, n).astype(BF16))
-        squared[...] = jnp.dot(
-            left.astype(BF16), jnp.concatenate(rights, axis=1), preferred_element_type=F32
-        )
-
-    def apply(box, squared, z_ref):
-        metas = []
-        for k in range(near):
-            n = listed[box * near + k]
-            metas.append(
-                [jnp.broadcast_to(smeta[m, pl.ds(n, 1), :], (8, LANES)) for m in range(3)]
+            start += 8
+    for k in range(USED):
+        sfeat[k * pitch + start : k * pitch + start + 8, :] = ones if k == 12 else zeros
+    for m in range(3):
+        smeta[m, start : start + 8, :] = zeros
+
+
+def store_targets(own, tfeat, turned):
+    boxes = own.shape[1]
+    pitch = tfeat.shape[0] // USED
+    ones = jnp.ones((8, LANES), F32)
+    for group in range(boxes // 8):
+        pieces, total, _, _ = pieces_of(own, group)
+        target = []
+        for high, low in pieces:
+            target += [high, high, low, low]
+        for k, v in enumerate(padded_rows(target + [ones, ones, ones] + list(thirds(total + 0.04)))):
+            tfeat[k * pitch + 8 * group : k * pitch + 8 * group + 8, :] = v
+    turned[boxes] = jnp.zeros((LANES, FEATURES), BF16)
+
+    def turn(i, carry):
+        for u in range(8):
+            turned[8 * i + u] = strided(tfeat, 8 * i + u).T.astype(BF16)
+        return carry
+
+    lax.fori_loop(0, boxes // 8, turn, 0)
+
+
+def run_items(plan, iterations, at, turned, ztop, sfeat, smeta, sums, squares, totals):
+    empty_row = sums.shape[0] - 8
+
+    def distances(group, squared):
+        for i in range(GROUP):
+            item = group * GROUP + i
+            target = plan[at[0] + item]
+            sides = [strided(sfeat, plan[at[1] + 2 * item + k]).astype(BF16) for k in range(2)]
+            squared[i] = jnp.dot(
+                turned[target], jnp.concatenate(sides, axis=1), preferred_element_type=F32
             )
-        parts = []
-        for t in range(LANES // 8):
-            rows = slice(8 * t, 8 * t + 8)
-            z = z_ref[rows, :]
-            total = None
-            for k in range(near):
-                pot, pot_z, flux = metas[k]
-                inverse = lax.rsqrt(squared[rows, LANES * k : LANES * k + LANES])
-                value = inverse * (flux - (inverse * inverse) * (z * pot - pot_z))
-                total = value if total is None else total + value
-            parts.append(total)
-        summed = jnp.concatenate(parts, axis=0).T
-        out[pl.ds(box, 1), :] = jnp.sum(summed, axis=0, keepdims=True) * scale
-
-    (even_sq, even_z), (odd_sq, odd_z) = even, odd
-    distances(0, even_sq, even_z)
+
+    def apply(group, squared, total):
+        for i in range(GROUP):
+            item = group * GROUP + i
+            target = plan[at[0] + item]
+            lane = jnp.full((8, LANES), jnp.minimum(target, LANES - 1), jnp.int32)
+            metas = []
+            for k in range(2):
+                n = plan[at[1] + 2 * item + k]
+                metas.append([jnp.broadcast_to(smeta[m, pl.ds(n, 1), :], (8, LANES)) for m in range(3)])
+            for t in range(LANES // 8):
+                rows = slice(8 * t, 8 * t + 8)
+                z = jnp.take_along_axis(ztop[rows, :], lane, axis=1)
+                value = None
+                for k in range(2):
+                    pot, pot_z, flux = metas[k]
+                    inverse = lax.rsqrt(squared[i, rows, LANES * k : LANES * k + LANES])
+                    part = inverse * (flux - (inverse * inverse) * (z * pot - pot_z))
+                    value = part if value is None else value + part
+                total[i, rows, :] = value
+
+    def reduce(group, total, live):
+        for i in range(GROUP):
+            target = plan[at[0] + jnp.maximum(group * GROUP + i, 0)]
+            target = jnp.where(live, target, empty_row)
+            row = jnp.sum(total[i].T, axis=0, keepdims=True)
+            sums[pl.ds(target, 1), :] += row
+
+    (even_sq, odd_sq), (even_tot, odd_tot) = squares, totals
+    odd_tot[...] = jnp.zeros(odd_tot.shape, F32)
+    distances(0, even_sq)
 
     def step(i, carry):
-        distances(2 * i + 1, odd_sq, odd_z)
-        apply(2 * i, even_sq, even_z)
-        distances(jnp.minimum(2 * i + 2, boxes - 1), even_sq, even_z)
-        apply(2 * i + 1, odd_sq, odd_z)
+        distances(2 * i + 1, odd_sq)
+        apply(2 * i, even_sq, even_tot)
+        reduce(2 * i - 1, odd_tot, i > 0)
+        distances(2 * i + 2, even_sq)
+        apply(2 * i + 1, odd_sq, odd_tot)
+        reduce(2 * i, even_tot, True)
         return carry
 
-    lax.fori_loop(0, boxes // 2, step, 0)
+    lax.fori_loop(0, iterations, step, 0)
+    reduce(2 * iterations - 1, odd_tot, iterations > 0)
+
+
+def near_own_kernel(near, plan, own, sums, turned, ztop, tfeat, sfeat, smeta, s0, s1, t0, t1):
+    boxes = own.shape[1]
+    sums[...] = jnp.zeros(sums.shape, F32)
+    store_targets(own, tfeat, turned)
+    high = rounded(own[2])
+    ztop[...] = (high + rounded(own[2] - high)).T
+    store_sources([own], sfeat, smeta)
+    _, own_at, _, _ = layout(boxes, near)
+    run_items(plan, plan[0], own_at, turned, ztop, sfeat, smeta, sums, (s0, s1), (t0, t1))
+
+
+def near_other_kernel(
+    near, plan, lower, upper, tile, sums_in, turned, ztop, out, sums, sfeat, smeta, s0, s1, t0, t1
+):
+    boxes = lower.shape[1]
+    sums[...] = sums_in[...]
+    store_sources([lower, upper], sfeat, smeta)
+    _, _, other_at, _ = layout(boxes, near)
+    run_items(plan, plan[1], other_at, turned, ztop, sfeat, smeta, sums, (s0, s1), (t0, t1))
+    out[0:boxes, :] = sums[0:boxes, :] * (1.0 / math.sqrt(near * LANES))
 
     _, rows, cols = tile.shape
     out[boxes : boxes + EXTRA, :] = jnp.zeros((EXTRA, LANES), F32)
@@ -250,40 +368,64 @@
                 place += 1
     place = boxes + EXTRA - 8
     for f in (1, 2):
-        turned = tile[f, :, cols - LANES : cols].T
-        out[place : place + 2, 0:rows] = turned[LANES - 2 : LANES, :]
+        turned_cols = tile[f, :, cols - LANES : cols].T
+        out[place : place + 2, 0:rows] = turned_cols[LANES - 2 : LANES, :]
         place += 2
 
 
-def near_apply(listed, own, lower, upper, tile, near):
+def item_scratch(sources):
+    return [
+        pltpu.VMEM((USED * (sources + 8), LANES), F32),
+        pltpu.VMEM((3, sources + 8, LANES), F32),
+        pltpu.VMEM((GROUP, LANES, 2 * LANES), F32),
+        pltpu.VMEM((GROUP, LANES, 2 * LANES), F32),
+        pltpu.VMEM((GROUP, LANES, LANES), F32),
+        pltpu.VMEM((GROUP, LANES, LANES), F32),
+    ]
+
+
+def near_cost(boxes, near):
+    pairs = boxes * near * LANES * LANES // 2
+    return pl.CostEstimate(
+        flops=pairs * 2 * FEATURES * 4, transcendentals=pairs, bytes_accessed=4 * 16 * boxes * LANES
+    )
+
+
+def near_own(plan, own, near):
     boxes = own.shape[1]
+    assert boxes == LANES
     vmem = pl.BlockSpec(memory_space=pltpu.VMEM)
     smem = pl.BlockSpec(memory_space=pltpu.SMEM)
-    buffers = [pltpu.VMEM((LANES, near * LANES), F32), pltpu.VMEM((LANES, LANES), F32)]
-
-    def kernel(listed, own, lower, upper, tile, out, tfeat, sfeat, smeta, e0, e1, o0, o1):
-        near_kernel(
-            near, listed, own, lower, upper, tile, out, tfeat, sfeat, smeta, (e0, e1), (o0, o1)
-        )
-
-    pairs = boxes * near * LANES * LANES
     return pl.pallas_call(
-        kernel,
+        lambda *refs: near_own_kernel(near, *refs),
+        out_shape=(
+            pltpu.VMEM((boxes + 8, LANES), F32),
+            pltpu.VMEM((boxes + 1, LANES, FEATURES), BF16),
+            pltpu.VMEM((LANES, boxes), F32),
+        ),
+        in_specs=[smem, vmem],
+        out_specs=(vmem,) * 3,
+        scratch_shapes=[pltpu.VMEM((USED * (boxes + 8), LANES), F32)] + item_scratch(boxes),
+        compiler_params=pltpu.CompilerParams(vmem_limit_bytes=VMEM_LIMIT),
+        name="near_own",
+        cost_estimate=near_cost(boxes, near),
+    )(plan, pinned(own))
+
+
+def near_other(plan, lower, upper, tile, sums, turned, ztop, near):
+    boxes = lower.shape[1]
+    vmem = pl.BlockSpec(memory_space=pltpu.VMEM)
+    smem = pl.BlockSpec(memory_space=pltpu.SMEM)
+    return pl.pallas_call(
+        lambda *refs: near_other_kernel(near, *refs),
         out_shape=pltpu.VMEM((boxes + EXTRA, LANES), F32),
-        in_specs=[smem] + [vmem] * 4,
+        in_specs=[smem] + [vmem] * 6,
         out_specs=vmem,
-        scratch_shapes=[
-            pltpu.VMEM((USED * (boxes + 8), LANES), F32),
-            pltpu.VMEM((USED * (3 * boxes + 8), LANES), F32),
-            pltpu.VMEM((3, 3 * boxes, LANES), F32),
-        ]
-        + buffers
-        + buffers,
-        name="near_field",
-        cost_estimate=pl.CostEstimate(
-            flops=pairs * 2 * FEATURES * 4, transcendentals=pairs, bytes_accessed=4 * 16 * boxes * LANES
-        ),
-    )(listed, pinned(own), pinned(lower), pinned(upper), tile)
+        scratch_shapes=[pltpu.VMEM((boxes + 8, LANES), F32)] + item_scratch(2 * boxes),
+        compiler_params=pltpu.CompilerParams(vmem_limit_bytes=VMEM_LIMIT),
+        name="near_other",
+        cost_estimate=near_cost(boxes, near),
+    )(plan, *map(pinned, (lower, upper, tile, sums, turned, ztop)))
 
 
 def lookup(slot, bases, tables, pieces, out):
@@ -297,9 +439,8 @@
         pieces[which, high_count : 2 * high_count, :] = (whole - top).astype(BF16)
 
     def split(r, c, which):
-        rel = slot[8 * r : 8 * r + 8, LANES * c : LANES * c + LANES] - bases[which]
-        high = jnp.floor(rel * (1.0 / WIDE))
-        return high, rel - high * WIDE
+        window = (slice(8 * r, 8 * r + 8), slice(LANES * c, LANES * c + LANES))
+        return box_split(slot[window] - bases[which], high_count)
 
     flags = {}
     for r, c in units:
@@ -349,6 +490,7 @@
         in_specs=[vmem] * 2,
         out_specs=vmem,
         scratch_shapes=[pltpu.VMEM((1, 2 * rows * cols // WIDE, WIDE), BF16)],
+        compiler_params=pltpu.CompilerParams(vmem_limit_bytes=VMEM_LIMIT),
         name="gather_own",
         cost_estimate=pl.CostEstimate(
             flops=rows * cols * rows * cols, transcendentals=0, bytes_accessed=4 * 4 * rows * cols
@@ -419,6 +561,7 @@
             pltpu.VMEM((rows, cols), F32),
             pltpu.VMEM((rows + 16, cols), F32),
         ],
+        compiler_params=pltpu.CompilerParams(vmem_limit_bytes=VMEM_LIMIT),
         name="finish",
         cost_estimate=pl.CostEstimate(
             flops=3 * rows * cols * rows * cols, transcendentals=0, bytes_accessed=4 * 8 * rows * cols
@@ -433,12 +576,11 @@
     node_count = rows * cols
     boxes = node_count // LANES
     near = near_boxes.shape[1]
-    half = boxes // 2
     assert node_count % WIDE == 0 and cols <= 256 and rows <= 128
     assert 4 * (cols // LANES) <= EXTRA - 8
     assert node_count * count_tx * count_ty < 2**24
-    rank = lax.axis_index("tx") * count_ty + lax.axis_index("ty")
-
+
+    plan = make_plan(near_boxes)
     slot = (box_owner * node_count + box_place).astype(F32)
     tile = jnp.stack([slot, elevation, potential, normal_flux])
     ahead_x = shifted(tile, "tx", -1)
@@ -457,11 +599,8 @@
     lower = lax.ppermute(boxed, both, [(i, i + 1) for i in range(total - 1)])
     upper = lax.ppermute(boxed, both, [(i + 1, i) for i in range(total - 1)])
 
-    local = near_boxes - (rank - 1) * boxes
-    inner = local % boxes
-    listed = (local // boxes) * boxes + (inner % 2) * half + inner // 2
-    listed = listed.reshape(half, 2, near).transpose(1, 0, 2).reshape(boxes * near)
-    value = near_apply(listed, boxed, lower, upper, tile, near)
+    sums, turned, ztop = near_own(plan, boxed, near)
+    value = near_other(plan, lower, upper, tile, sums, turned, ztop, near)
 
     behind_x = shifted(value, "tx", 1)
     behind_y = shifted(value, "ty", 1)

time: 94.2 us -> 101 us (1.072)
  Pallas kernels: 53.8 us -> 73.8 us
  waiting for transfers between devices: 22.9 us -> 9.1 us
  starting transfers between devices: 14 us -> 15.7 us
  local copies, waits for them, and re-layouts: 1.49 us -> 0.01 us
    pallas_call x1 -> x3, Pallas kernels: 33.6 us -> 53.5 us  [the longest x1 30.9 us: near_own(): pl.pallas_call(lambda *refs: near_own_kernel(near, *refs), out_shape=(plt...]
    ppermute x1, waiting for transfers between devices: 9.95 us -> 0.01 us  [shards(): upper = lax.ppermute(boxed, both, [(i + 1, i) for i in range(total - 1)])]
    ppermute x1, waiting for transfers between devices: 4.92 us -> 0.01 us  [shards(): lower = lax.ppermute(boxed, both, [(i, i + 1) for i in range(total - 1)])]
    ppermute x1, starting transfers between devices: 2.41 us -> 4.57 us  [shards(): lower = lax.ppermute(boxed, both, [(i, i + 1) for i in range(total - 1)])]
    ppermute x1, waiting for transfers between devices: 2.47 us -> 4.17 us  [shards(): behind_xy = lax.ppermute(value, both, diagonal)]
    ppermute x1, starting transfers between devices: 1.22 us -> 0.06 us  [shards(): behind_xy = lax.ppermute(value, both, diagonal)]
  transfers between devices with their start and end apart: 8 -> 8, of which waited for: 6 -> 3; matrix products, arithmetic and copies ran while one was open for 1% -> 0% of each run, Pallas kernels for 9% -> 48%
where the time goes in v3:
time: 101 us
  Pallas kernels  73.8 us (73%)
  starting transfers between devices  15.7 us (16%)
  waiting for transfers between devices  9.1 us (9%)
  other arithmetic  1.81 us (2%)
    pallas_call x1, Pallas kernels, near_own(): pl.pallas_call(lambda *refs: near_own_kernel(near, *refs), out_shape=(plt...  30.9 us
    pallas_call x1, Pallas kernels, near_other(): pl.pallas_call(lambda *refs: near_other_kernel(near, *refs), out_shape=pl...  13.1 us
    pallas_call x4, Pallas kernels, scatter(): pl.pallas_call(lambda *refs: scatter_kernel(first, last, (rows, cols, hig...  12.4 us
    ppermute x5, starting transfers between devices, shifted(): return lax.ppermute(value, axis, pairs)  9.79 us
    pallas_call x1, Pallas kernels, make_plan(): pl.pallas_call(lambda *refs: plan_kernel(boxes, near, *refs), out_shape=j...  9.54 us
    pallas_call x1, Pallas kernels, finish(): pl.pallas_call(finish_kernel, out_shape=(shape, shape), in_specs=[vmem] *...  6.7 us
    ppermute x5, waiting for transfers between devices, shifted(): return lax.ppermute(value, axis, pairs)  4.93 us
    ppermute x1, starting transfers between devices, shards(): lower = lax.ppermute(boxed, both, [(i, i + 1) for i in range(total - 1)])  4.57 us
  transfers between devices with their start and end apart: 8, of which 3 were waited for; matrix products, arithmetic and copies ran while one was open for 0% of the time, Pallas kernels for 48%

profile of v3, /device:TPU:0, one launch (start us, length us, event | category | flops | bytes accessed | tf_op | source)
XLA Modules:
  0.0 101.2 jit_solution(16015820441586406481)
XLA Ops:
  0.6 0.9 convert_bitcast_fusion
  1.5 0.9 pad_maximum_fusion.refs_0_.refs_3_.tile
  2.4 5.1 %collective-permute-start.1 = (f32[4,64,256]{2,1,0:T(8,128)S(1)}, f32[4,64,256]{2,1,0:T(8,128)S(1)}, u32[]{:S(2)}, u32[]{:S(2)}) collective-permute-start(f32[4,64,256]{2,1,0:T(8,128)S(1)} %pad_maximum_fusion.refs_0_.refs_3_.tile), channel_id=1, source_target_pairs={{0,3},{1,0},{2,1},{3,2},{4,7},{5,4},{6,5},{7,6},{8,11},{9,8},{10,9... | collective-permute-start | bytes 786440 | tf_op jit(solution)/shard_map/ppermute | solution.py:25
  7.6 1.6 %collective-permute-start = (f32[4,64,256]{2,1,0:T(8,128)S(1)}, f32[4,64,256]{2,1,0:T(8,128)S(1)}, u32[]{:S(2)}, u32[]{:S(2)}) collective-permute-start(f32[4,64,256]{2,1,0:T(8,128)S(1)} %pad_maximum_fusion.refs_0_.refs_3_.tile), channel_id=1, source_target_pairs={{0,28},{4,0},{8,4},{12,8},{16,12},{20,16},{24,20},{28,24},{1,29},{... | collective-permute-start | bytes 786440 | tf_op jit(solution)/shard_map/ppermute | solution.py:25
  9.2 1.4 %scatter_first.1.refs_1_ = f32[384,256]{1,0:T(8,128)S(1)} custom-call(f32[4,64,256]{2,1,0:T(8,128)S(1)} %pad_maximum_fusion.refs_0_.refs_3_.tile), custom_call_target="tpu_custom_call" | custom-call | flops 1610612736 | bytes 1048576 | tf_op jit(solution)/shard_map/scatter_first/pallas_call | solution.py:138
  10.6 2.5 %collective-permute-done.1.refs_0_.ahead_y = f32[4,64,256]{2,1,0:T(8,128)S(1)} collective-permute-done((f32[4,64,256]{2,1,0:T(8,128)S(1)}, f32[4,64,256]{2,1,0:T(8,128)S(1)}, u32[]{:S(2)}, u32[]{:S(2)}) %collective-permute-start.1) | collective-permute-done | bytes 262176 | tf_op jit(solution)/shard_map/ppermute | solution.py:25
  13.1 1.0 %collective-permute-start.2 = (f32[4,64,256]{2,1,0:T(8,128)S(1)}, f32[4,64,256]{2,1,0:T(8,128)S(1)}, u32[]{:S(2)}, u32[]{:S(2)}) collective-permute-start(f32[4,64,256]{2,1,0:T(8,128)S(1)} %collective-permute-done.1.refs_0_.ahead_y), channel_id=1, source_target_pairs={{0,28},{4,0},{8,4},{12,8},{16,12},{20,16},{24,20},{28,24},{1,29},{... | collective-permute-start | bytes 786440 | tf_op jit(solution)/shard_map/ppermute | solution.py:25
  14.2 0.0 collective-permute-done.refs_0_.ahead_x
  14.2 2.2 %scatter.2.refs_1_ = f32[384,256]{1,0:T(8,128)S(1)} custom-call(f32[4,64,256]{2,1,0:T(8,128)S(1)} %collective-permute-done.refs_0_.ahead_x, f32[384,256]{1,0:T(8,128)S(1)} %scatter_first.1.refs_1_), custom_call_target="tpu_custom_call" | custom-call | flops 1610612736 | bytes 1048576 | tf_op jit(solution)/shard_map/scatter/pallas_call | solution.py:138
  16.4 3.7 %scatter.3.refs_1_ = f32[384,256]{1,0:T(8,128)S(1)} custom-call(f32[4,64,256]{2,1,0:T(8,128)S(1)} %collective-permute-done.1.refs_0_.ahead_y, f32[384,256]{1,0:T(8,128)S(1)} %scatter.2.refs_1_), custom_call_target="tpu_custom_call" | custom-call | flops 1610612736 | bytes 1048576 | tf_op jit(solution)/shard_map/scatter/pallas_call | solution.py:138
  20.1 0.0 copy-start
  20.1 5.1 %scatter_last.1 = (f32[384,256]{1,0:T(8,128)}, f32[5,128,128]{2,1,0:T(8,128)S(1)}) custom-call(f32[4,64,256]{2,1,0:T(8,128)S(1)} %collective-permute-done.2.refs_0_, f32[384,256]{1,0:T(8,128)S(1)} %scatter.3.refs_1_), custom_call_target="tpu_custom_call" | custom-call | flops 1610612736 | bytes 1048576 | tf_op jit(solution)/shard_map/scatter_last/pallas_call | solution.py:138
  25.2 1.3 %collective-permute-start.4 = (f32[5,128,128]{2,1,0:T(8,128)S(1)}, f32[5,128,128]{2,1,0:T(8,128)S(1)}, u32[]{:S(2)}, u32[]{:S(2)}) collective-permute-start(f32[5,128,128]{2,1,0:T(8,128)S(1)} %get-tuple-element.6.refs_1_), channel_id=1, source_target_pairs={{1,0},{2,1},{3,2},{4,3},{5,4},{6,5},{7,6},{8,7},{9,8},{10,9},{11,1... | collective-permute-start | bytes 983048 | tf_op jit(solution)/shard_map/ppermute | solution.py:600
  26.5 4.6 %collective-permute-start.3 = (f32[5,128,128]{2,1,0:T(8,128)S(1)}, f32[5,128,128]{2,1,0:T(8,128)S(1)}, u32[]{:S(2)}, u32[]{:S(2)}) collective-permute-start(f32[5,128,128]{2,1,0:T(8,128)S(1)} %get-tuple-element.6.refs_1_), channel_id=1, source_target_pairs={{0,1},{1,2},{2,3},{3,4},{4,5},{5,6},{6,7},{7,8},{8,9},{9,10},{10,1... | collective-permute-start | bytes 983048 | tf_op jit(solution)/shard_map/ppermute | solution.py:599
  31.0 9.5 %plan.1.refs_0_ = s32[3176]{0:T(1024)S(1)} custom-call(s32[1024]{0:T(1024)S(1)} %bitcast.8), custom_call_target="tpu_custom_call" | custom-call | flops 10000000 | bytes 16384 | tf_op jit(solution)/shard_map/plan/pallas_call | solution.py:204
  40.6 30.9 %near_own.1 = (f32[136,128]{1,0:T(8,128)S(1)}, bf16[129,128,32]{2,1,0:T(8,128)(2,1)S(1)}, f32[128,128]{1,0:T(8,128)S(1)}) custom-call(s32[3176]{0:T(1024)S(1)} %plan.1.refs_0_, f32[5,128,128]{2,1,0:T(8,128)S(1)} %get-tuple-element.6.refs_1_), custom_call_target="tpu_custom_call" | custom-call | flops 2147483648 | bytes 1048576 | tf_op jit(solution)/shard_map/near_own/pallas_call | solution.py:399
  71.5 13.1 %near_other.1.own = f32[144,128]{1,0:T(8,128)S(1)} custom-call(s32[3176]{0:T(1024)S(1)} %plan.1.refs_0_, f32[5,128,128]{2,1,0:T(8,128)S(1)} %collective-permute-done.3.refs_1_, f32[5,128,128]{2,1,0:T(8,128)S(1)} %collective-permute-done.4.refs_2_, f32[4,64,256]{2,1,0:T(8,128)S(1)} %pad_maximum_fusion.refs_0_.refs_3_.tile, ...), custom_call_target="tpu_custom_call" | custom-call | flops 2147483648 | bytes 1048576 | tf_op jit(solution)/shard_map/near_other/pallas_call | solution.py:419
  84.6 0.1 collective-permute-start.7
  84.7 1.2 %collective-permute-start.6 = (f32[144,128]{1,0:T(8,128)S(1)}, f32[144,128]{1,0:T(8,128)S(1)}, u32[]{:S(2)}, u32[]{:S(2)}) collective-permute-start(f32[144,128]{1,0:T(8,128)S(1)} %near_other.1.own), channel_id=1, source_target_pairs={{0,1},{1,2},{2,3},{3,0},{4,5},{5,6},{6,7},{7,4},{8,9},{9,10},{10,1... | collective-permute-start | bytes 221192 | tf_op jit(solution)/shard_map/ppermute | solution.py:25
  85.9 0.8 collective-permute-start.5
  86.7 1.2 %gather_own.1.partial = f32[64,256]{1,0:T(8,128)S(1)} custom-call(f32[4,64,256]{2,1,0:T(8,128)S(1)} %pad_maximum_fusion.refs_0_.refs_3_.tile, f32[144,128]{1,0:T(8,128)S(1)} %near_other.1.own), custom_call_target="tpu_custom_call" | custom-call | flops 268435456 | bytes 262144 | tf_op jit(solution)/shard_map/gather_own/pallas_call | solution.py:487
  87.9 4.2 %collective-permute-done.7.behind_xy = f32[144,128]{1,0:T(8,128)S(1)} collective-permute-done((f32[144,128]{1,0:T(8,128)S(1)}, f32[144,128]{1,0:T(8,128)S(1)}, u32[]{:S(2)}, u32[]{:S(2)}) %collective-permute-start.7) | collective-permute-done | bytes 73760 | tf_op jit(solution)/shard_map/ppermute | solution.py:612
  92.0 2.4 %collective-permute-done.6.behind_y = f32[144,128]{1,0:T(8,128)S(1)} collective-permute-done((f32[144,128]{1,0:T(8,128)S(1)}, f32[144,128]{1,0:T(8,128)S(1)}, u32[]{:S(2)}, u32[]{:S(2)}) %collective-permute-start.6) | collective-permute-done | bytes 73760 | tf_op jit(solution)/shard_map/ppermute | solution.py:25
  94.5 6.7 %finish.1 = (f32[64,256]{1,0:T(8,128)}, f32[64,256]{1,0:T(8,128)}) custom-call(f32[4,64,256]{2,1,0:T(8,128)S(1)} %pad_maximum_fusion.refs_0_.refs_3_.tile, f32[4,64,256]{2,1,0:T(8,128)S(1)} %collective-permute-done.refs_0_.ahead_x, f32[4,64,256]{2,1,0:T(8,128)S(1)} %collective-permute-done.1.refs_0_.ahead_y, f32[64,256]{1,0:T(8,128)S(1)} %gather_own.1.partial, ...), custom_call_target="tpu_custom_call" | custom-call | flops 805306368 | bytes 524288 | tf_op jit(solution)/shard_map/finish/pallas_call | solution.py:554
  (5 shorter events, 0.0 us)
Async XLA Ops:
  2.4 10.7 %collective-permute-start.1 = (f32[4,64,256]{2,1,0:T(8,128)S(1)}, f32[4,64,256]{2,1,0:T(8,128)S(1)}, u32[]{:S(2)}, u32[]{:S(2)}) collective-permute-start(f32[4,64,256]{2,1,0:T(8,128)S(1)} %pad_maximum_fusion.refs_0_.refs_3_.tile), channel_id=1, source_target_pairs={{0,3},{1,0},{2,1},{3,2},{4,7},{5,4},{6,5},{7,6},{8,11},{9,8},{10,9... | collective-permute-start | bytes 786440 | tf_op jit(solution)/shard_map/ppermute | solution.py:25
  7.6 6.6 %collective-permute-start = (f32[4,64,256]{2,1,0:T(8,128)S(1)}, f32[4,64,256]{2,1,0:T(8,128)S(1)}, u32[]{:S(2)}, u32[]{:S(2)}) collective-permute-start(f32[4,64,256]{2,1,0:T(8,128)S(1)} %pad_maximum_fusion.refs_0_.refs_3_.tile), channel_id=1, source_target_pairs={{0,28},{4,0},{8,4},{12,8},{16,12},{20,16},{24,20},{28,24},{1,29},{... | collective-permute-start | bytes 786440 | tf_op jit(solution)/shard_map/ppermute | solution.py:25
  13.1 7.0 %collective-permute-start.2 = (f32[4,64,256]{2,1,0:T(8,128)S(1)}, f32[4,64,256]{2,1,0:T(8,128)S(1)}, u32[]{:S(2)}, u32[]{:S(2)}) collective-permute-start(f32[4,64,256]{2,1,0:T(8,128)S(1)} %collective-permute-done.1.refs_0_.ahead_y), channel_id=1, source_target_pairs={{0,28},{4,0},{8,4},{12,8},{16,12},{20,16},{24,20},{28,24},{1,29},{... | collective-permute-start | bytes 786440 | tf_op jit(solution)/shard_map/ppermute | solution.py:25
  20.1 10.9 %copy-start = (s32[128,8]{0,1:T(8,128)S(1)}, s32[128,8]{0,1:T(8,128)}, u32[]{:S(2)}) copy-start(s32[128,8]{0,1:T(8,128)} %param.11) | copy-start | bytes 12292
  25.2 46.3 %collective-permute-start.4 = (f32[5,128,128]{2,1,0:T(8,128)S(1)}, f32[5,128,128]{2,1,0:T(8,128)S(1)}, u32[]{:S(2)}, u32[]{:S(2)}) collective-permute-start(f32[5,128,128]{2,1,0:T(8,128)S(1)} %get-tuple-element.6.refs_1_), channel_id=1, source_target_pairs={{1,0},{2,1},{3,2},{4,3},{5,4},{6,5},{7,6},{8,7},{9,8},{10,9},{11,1... | collective-permute-start | bytes 983048 | tf_op jit(solution)/shard_map/ppermute | solution.py:600
  26.5 45.1 %collective-permute-start.3 = (f32[5,128,128]{2,1,0:T(8,128)S(1)}, f32[5,128,128]{2,1,0:T(8,128)S(1)}, u32[]{:S(2)}, u32[]{:S(2)}) collective-permute-start(f32[5,128,128]{2,1,0:T(8,128)S(1)} %get-tuple-element.6.refs_1_), channel_id=1, source_target_pairs={{0,1},{1,2},{2,3},{3,4},{4,5},{5,6},{6,7},{7,8},{8,9},{9,10},{10,1... | collective-permute-start | bytes 983048 | tf_op jit(solution)/shard_map/ppermute | solution.py:599
  84.6 7.4 %collective-permute-start.7 = (f32[144,128]{1,0:T(8,128)S(1)}, f32[144,128]{1,0:T(8,128)S(1)}, u32[]{:S(2)}, u32[]{:S(2)}) collective-permute-start(f32[144,128]{1,0:T(8,128)S(1)} %near_other.1.own), channel_id=1, source_target_pairs={{0,5},{1,6},{2,7},{3,4},{4,9},{5,10},{6,11},{7,8},{8,13},{9,14},{1... | collective-permute-start | bytes 221192 | tf_op jit(solution)/shard_map/ppermute | solution.py:612
  84.7 9.8 %collective-permute-start.6 = (f32[144,128]{1,0:T(8,128)S(1)}, f32[144,128]{1,0:T(8,128)S(1)}, u32[]{:S(2)}, u32[]{:S(2)}) collective-permute-start(f32[144,128]{1,0:T(8,128)S(1)} %near_other.1.own), channel_id=1, source_target_pairs={{0,1},{1,2},{2,3},{3,0},{4,5},{5,6},{6,7},{7,4},{8,9},{9,10},{10,1... | collective-permute-start | bytes 221192 | tf_op jit(solution)/shard_map/ppermute | solution.py:25
  85.9 8.6 %collective-permute-start.5 = (f32[144,128]{1,0:T(8,128)S(1)}, f32[144,128]{1,0:T(8,128)S(1)}, u32[]{:S(2)}, u32[]{:S(2)}) collective-permute-start(f32[144,128]{1,0:T(8,128)S(1)} %near_other.1.own), channel_id=1, source_target_pairs={{0,4},{4,8},{8,12},{12,16},{16,20},{20,24},{24,28},{28,0},{1,5},{5... | collective-permute-start | bytes 221192 | tf_op jit(solution)/shard_map/ppermute | solution.py:25

commit v4 on v3

--- a/solution.py
+++ b/solution.py
@@ -13,7 +13,7 @@
 FEATURES = 32
 USED = 24
 EXTRA = 16
-GROUP = 4
+GROUP = 2
 VMEM_LIMIT = 24 << 20
 BF16 = jnp.bfloat16
 F32 = jnp.float32
@@ -49,7 +49,8 @@
 
 def scatter_kernel(first, last, sizes, steps, tile, *refs):
     if first:
-        acc = refs[0]
+        listed, acc, plan = refs
+        plan_rows(listed, plan)
     else:
         acc_in, acc = refs[:2]
     rows, cols, high_count, node_rows, node_cols = sizes
@@ -126,7 +127,7 @@
             boxed[k, h : 2 * h, :] = f[:, LANES:]
 
 
-def scatter(steps, tile, acc, last, node_rows, node_cols):
+def scatter(steps, tile, acc, last, node_rows, node_cols, listed=None):
     _, rows, cols = tile.shape
     high_count = rows * cols // WIDE
     first = acc is None
@@ -134,7 +135,10 @@
     out_shape = [pltpu.VMEM((PIECES * high_count, WIDE), F32)]
     if last:
         out_shape.append(pltpu.VMEM((5, 2 * high_count, LANES), F32))
-    args = (tile,) if first else (tile, pinned(acc))
+    if first:
+        near, boxes = listed.shape
+        out_shape.append(jax.ShapeDtypeStruct(((near // 2 + near + 2 + 7) // 8 * 8, boxes), jnp.int32))
+    args = (tile, listed) if first else (tile, pinned(acc))
     out = pl.pallas_call(
         lambda *refs: scatter_kernel(
             first, last, (rows, cols, high_count, node_rows, node_cols), steps, *refs
@@ -150,7 +154,7 @@
             bytes_accessed=4 * (2 * PIECES * high_count * WIDE + 4 * rows * cols),
         ),
     )(*args)
-    return out[1] if last else out[0]
+    return out[1] if last else out if first else out[0]
 
 
 def thirds(value):
@@ -159,57 +163,38 @@
     return high, middle, value - high - middle
 
 
-def layout(boxes, near):
-    items = boxes * ((near + 1) // 2) + 4 * GROUP
-    return items, (8, 8 + items), (8 + 3 * items, 8 + 4 * items), 8 + 6 * items
-
-
-def plan_kernel(boxes, near, listed, plan):
-    _, own_at, other_at, _ = layout(boxes, near)
+def plan_rows(listed, plan):
+    near, boxes = listed.shape
+    half = near // 2
     rank = lax.axis_index("tx") * lax.axis_size("ty") + lax.axis_index("ty")
-    offset = (rank - 1) * boxes
-    deepest = (near + 1) // 2
-
-    def one(b, carry):
-        own_items, other_items = carry
-        own = 2 * own_items
-        other = 2 * other_items
-        for k in range(near):
-            n = listed[k * boxes + b] - offset
-            mine = jnp.where((n >= boxes) & (n < 2 * boxes), 1, 0)
-            plan[own_at[1] + own] = n - boxes
-            plan[other_at[1] + other] = jnp.where(n < boxes, n, n - boxes)
-            own = own + mine
-            other = other + 1 - mine
-        plan[own_at[1] + own] = boxes
-        plan[other_at[1] + other] = 2 * boxes
-        for i in range(deepest):
-            plan[own_at[0] + own_items + i] = b
-            plan[other_at[0] + other_items + i] = b
-        return (own + 1) // 2, (other + 1) // 2
-
-    own_items, other_items = lax.fori_loop(0, boxes, one, (jnp.int32(0), jnp.int32(0)))
-    for at, count, empty in ((own_at, own_items, boxes), (other_at, other_items, 2 * boxes)):
-        for i in range(3 * GROUP):
-            plan[at[0] + count + i] = boxes
-            plan[at[1] + 2 * (count + i)] = empty
-            plan[at[1] + 2 * (count + i) + 1] = empty
-    plan[0] = (own_items + 2 * GROUP - 1) // (2 * GROUP)
-    plan[1] = (other_items + 2 * GROUP - 1) // (2 * GROUP)
-
-
-def make_plan(near_boxes):
-    boxes, near = near_boxes.shape
-    smem = pl.BlockSpec(memory_space=pltpu.SMEM)
-    return pl.pallas_call(
-        lambda *refs: plan_kernel(boxes, near, *refs),
-        out_shape=jax.ShapeDtypeStruct((layout(boxes, near)[-1],), jnp.int32),
-        in_specs=[smem],
-        out_specs=smem,
-        compiler_params=pltpu.CompilerParams(vmem_limit_bytes=VMEM_LIMIT),
-        name="plan",
-        cost_estimate=pl.CostEstimate(flops=10**7, transcendentals=0, bytes_accessed=16 * boxes * near),
-    )(near_boxes.T.reshape(boxes * near))
+    n = listed[...] - (rank - 1) * boxes
+    taken = jnp.zeros((1, boxes), jnp.int32)
+    left = jnp.zeros((1, boxes), jnp.int32)
+    first = [jnp.full((1, boxes), boxes, jnp.int32) for _ in range(half)]
+    rest = [jnp.full((1, boxes), 3 * boxes, jnp.int32) for _ in range(near)]
+    for k in range(near):
+        row = n[k : k + 1, :]
+        take = (row >= boxes) & (row < 2 * boxes) & (taken < half)
+        first = [jnp.where(take & (taken == j), row - boxes, v) for j, v in enumerate(first)]
+        rest = [jnp.where(take | (left != j), v, row) for j, v in enumerate(rest)]
+        step = jnp.where(take, 1, 0)
+        taken = taken + step
+        left = left + 1 - step
+    for j, v in enumerate(first + rest):
+        plan[j : j + 1, :] = v
+    over = left > half
+    flags = jnp.broadcast_to(jnp.where(over, 1.0, 0.0), (8, boxes)).astype(BF16)
+    down = lax.broadcasted_iota(jnp.int32, (boxes, boxes), 0)
+    across = lax.broadcasted_iota(jnp.int32, (boxes, boxes), 1)
+    before = jnp.where(down < across, 1.0, 0.0).astype(BF16)
+    offset = jnp.dot(flags, before, preferred_element_type=F32)[0:1, :]
+    count = jnp.dot(flags, jnp.ones((boxes, boxes), BF16), preferred_element_type=F32)[0:1, :]
+    hit = jnp.where((down.astype(F32) == offset) & over, 1.0, 0.0).astype(BF16)
+    names = lax.broadcasted_iota(jnp.int32, (8, boxes), 1).astype(F32).astype(BF16)
+    found = lax.dot_general(names, hit, (((1,), (1,)), ((), ())), preferred_element_type=F32)[0:1, :]
+    count = count.astype(jnp.int32)
+    plan[half + near : half + near + 1, :] = jnp.where(across[0:1, :] < count, found.astype(jnp.int32), boxes)
+    plan[half + near + 1 : half + near + 2, :] = count
 
 
 def pieces_of(ref, group):
@@ -281,32 +266,30 @@
     lax.fori_loop(0, boxes // 8, turn, 0)
 
 
-def run_items(plan, iterations, at, turned, ztop, sfeat, smeta, sums, squares, totals):
+def run_items(target_of, source_of, half, iterations, turned, ztop, sfeat, smeta, sums, squares, totals):
     empty_row = sums.shape[0] - 8
 
     def distances(group, squared):
         for i in range(GROUP):
             item = group * GROUP + i
-            target = plan[at[0] + item]
-            sides = [strided(sfeat, plan[at[1] + 2 * item + k]).astype(BF16) for k in range(2)]
+            sides = [strided(sfeat, source_of(item, k)).astype(BF16) for k in range(half)]
             squared[i] = jnp.dot(
-                turned[target], jnp.concatenate(sides, axis=1), preferred_element_type=F32
+                turned[target_of(item)], jnp.concatenate(sides, axis=1), preferred_element_type=F32
             )
 
     def apply(group, squared, total):
         for i in range(GROUP):
             item = group * GROUP + i
-            target = plan[at[0] + item]
-            lane = jnp.full((8, LANES), jnp.minimum(target, LANES - 1), jnp.int32)
+            lane = jnp.full((8, LANES), jnp.minimum(target_of(item), LANES - 1), jnp.int32)
             metas = []
-            for k in range(2):
-                n = plan[at[1] + 2 * item + k]
+            for k in range(half):
+                n = source_of(item, k)
                 metas.append([jnp.broadcast_to(smeta[m, pl.ds(n, 1), :], (8, LANES)) for m in range(3)])
             for t in range(LANES // 8):
                 rows = slice(8 * t, 8 * t + 8)
                 z = jnp.take_along_axis(ztop[rows, :], lane, axis=1)
                 value = None
-                for k in range(2):
+                for k in range(half):
                     pot, pot_z, flux = metas[k]
                     inverse = lax.rsqrt(squared[i, rows, LANES * k : LANES * k + LANES])
                     part = inverse * (flux - (inverse * inverse) * (z * pot - pot_z))
@@ -315,8 +298,7 @@
 
     def reduce(group, total, live):
         for i in range(GROUP):
-            target = plan[at[0] + jnp.maximum(group * GROUP + i, 0)]
-            target = jnp.where(live, target, empty_row)
+            target = jnp.where(live, target_of(jnp.maximum(group * GROUP + i, 0)), empty_row)
             row = jnp.sum(total[i].T, axis=0, keepdims=True)
             sums[pl.ds(target, 1), :] += row
 
@@ -337,25 +319,50 @@
     reduce(2 * iterations - 1, odd_tot, iterations > 0)
 
 
-def near_own_kernel(near, plan, own, sums, turned, ztop, tfeat, sfeat, smeta, s0, s1, t0, t1):
+def near_own_kernel(plan, own, sums, turned, ztop, tfeat, sfeat, smeta, s0, s1, t0, t1):
     boxes = own.shape[1]
+    half = s0.shape[2] // LANES
     sums[...] = jnp.zeros(sums.shape, F32)
     store_targets(own, tfeat, turned)
     high = rounded(own[2])
     ztop[...] = (high + rounded(own[2] - high)).T
     store_sources([own], sfeat, smeta)
-    _, own_at, _, _ = layout(boxes, near)
-    run_items(plan, plan[0], own_at, turned, ztop, sfeat, smeta, sums, (s0, s1), (t0, t1))
+
+    def target_of(item):
+        return jnp.minimum(item, boxes - 1)
+
+    def source_of(item, k):
+        return plan[k, jnp.minimum(item, boxes - 1)]
+
+    run_items(
+        target_of, source_of, half, boxes // (2 * GROUP), turned, ztop, sfeat, smeta, sums, (s0, s1), (t0, t1)
+    )
 
 
 def near_other_kernel(
-    near, plan, lower, upper, tile, sums_in, turned, ztop, out, sums, sfeat, smeta, s0, s1, t0, t1
+    near, plan, own, lower, upper, tile, sums_in, turned, ztop, out, sums, sfeat, smeta, s0, s1, t0, t1
 ):
     boxes = lower.shape[1]
+    half = s0.shape[2] // LANES
     sums[...] = sums_in[...]
-    store_sources([lower, upper], sfeat, smeta)
-    _, _, other_at, _ = layout(boxes, near)
-    run_items(plan, plan[1], other_at, turned, ztop, sfeat, smeta, sums, (s0, s1), (t0, t1))
+    store_sources([lower, own, upper], sfeat, smeta)
+    items = boxes + plan[half + near + 1, 0]
+
+    def box_of(item):
+        extra = plan[half + near, jnp.clip(item - boxes, 0, boxes - 1)]
+        return jnp.where(item < boxes, item, extra)
+
+    def target_of(item):
+        return jnp.where(item < items, box_of(item), boxes)
+
+    def source_of(item, k):
+        row = jnp.where(item < boxes, half, 2 * half) + k
+        return plan[row, jnp.minimum(box_of(item), boxes - 1)]
+
+    iterations = (items + 2 * GROUP - 1) // (2 * GROUP)
+    run_items(
+        target_of, source_of, half, iterations, turned, ztop, sfeat, smeta, sums, (s0, s1), (t0, t1)
+    )
     out[0:boxes, :] = sums[0:boxes, :] * (1.0 / math.sqrt(near * LANES))
 
     _, rows, cols = tile.shape
@@ -373,12 +380,12 @@
         place += 2
 
 
-def item_scratch(sources):
+def item_scratch(sources, half):
     return [
         pltpu.VMEM((USED * (sources + 8), LANES), F32),
         pltpu.VMEM((3, sources + 8, LANES), F32),
-        pltpu.VMEM((GROUP, LANES, 2 * LANES), F32),
-        pltpu.VMEM((GROUP, LANES, 2 * LANES), F32),
+        pltpu.VMEM((GROUP, LANES, half * LANES), F32),
+        pltpu.VMEM((GROUP, LANES, half * LANES), F32),
         pltpu.VMEM((GROUP, LANES, LANES), F32),
         pltpu.VMEM((GROUP, LANES, LANES), F32),
     ]
@@ -393,11 +400,11 @@
 
 def near_own(plan, own, near):
     boxes = own.shape[1]
-    assert boxes == LANES
+    assert boxes == LANES and boxes % (2 * GROUP) == 0 and near % 2 == 0
     vmem = pl.BlockSpec(memory_space=pltpu.VMEM)
     smem = pl.BlockSpec(memory_space=pltpu.SMEM)
     return pl.pallas_call(
-        lambda *refs: near_own_kernel(near, *refs),
+        near_own_kernel,
         out_shape=(
             pltpu.VMEM((boxes + 8, LANES), F32),
             pltpu.VMEM((boxes + 1, LANES, FEATURES), BF16),
@@ -405,27 +412,27 @@
         ),
         in_specs=[smem, vmem],
         out_specs=(vmem,) * 3,
-        scratch_shapes=[pltpu.VMEM((USED * (boxes + 8), LANES), F32)] + item_scratch(boxes),
+        scratch_shapes=[pltpu.VMEM((USED * (boxes + 8), LANES), F32)] + item_scratch(boxes, near // 2),
         compiler_params=pltpu.CompilerParams(vmem_limit_bytes=VMEM_LIMIT),
         name="near_own",
         cost_estimate=near_cost(boxes, near),
     )(plan, pinned(own))
 
 
-def near_other(plan, lower, upper, tile, sums, turned, ztop, near):
+def near_other(plan, own, lower, upper, tile, sums, turned, ztop, near):
     boxes = lower.shape[1]
     vmem = pl.BlockSpec(memory_space=pltpu.VMEM)
     smem = pl.BlockSpec(memory_space=pltpu.SMEM)
     return pl.pallas_call(
         lambda *refs: near_other_kernel(near, *refs),
         out_shape=pltpu.VMEM((boxes + EXTRA, LANES), F32),
-        in_specs=[smem] + [vmem] * 6,
+        in_specs=[smem] + [vmem] * 7,
         out_specs=vmem,
-        scratch_shapes=[pltpu.VMEM((boxes + 8, LANES), F32)] + item_scratch(2 * boxes),
+        scratch_shapes=[pltpu.VMEM((boxes + 8, LANES), F32)] + item_scratch(3 * boxes, near // 2),
         compiler_params=pltpu.CompilerParams(vmem_limit_bytes=VMEM_LIMIT),
         name="near_other",
         cost_estimate=near_cost(boxes, near),
-    )(plan, *map(pinned, (lower, upper, tile, sums, turned, ztop)))
+    )(plan, *map(pinned, (own, lower, upper, tile, sums, turned, ztop)))
 
 
 def lookup(slot, bases, tables, pieces, out):
@@ -580,7 +587,6 @@
     assert 4 * (cols // LANES) <= EXTRA - 8
     assert node_count * count_tx * count_ty < 2**24
 
-    plan = make_plan(near_boxes)
     slot = (box_owner * node_count + box_place).astype(F32)
     tile = jnp.stack([slot, elevation, potential, normal_flux])
     ahead_x = shifted(tile, "tx", -1)
@@ -589,7 +595,7 @@
     tile, ahead_x, ahead_y, ahead_xy = map(pinned, (tile, ahead_x, ahead_y, ahead_xy))
 
     sizes = (rows * count_tx, cols * count_ty)
-    acc = scatter((0, 0), tile, None, False, *sizes)
+    acc, plan = scatter((0, 0), tile, None, False, *sizes, near_boxes.T)
     acc = scatter((1, 0), ahead_x, acc, False, *sizes)
     acc = scatter((0, 1), ahead_y, acc, False, *sizes)
     boxed = scatter((1, 1), ahead_xy, acc, True, *sizes)
@@ -600,7 +606,7 @@
     upper = lax.ppermute(boxed, both, [(i + 1, i) for i in range(total - 1)])
 
     sums, turned, ztop = near_own(plan, boxed, near)
-    value = near_other(plan, lower, upper, tile, sums, turned, ztop, near)
+    value = near_other(plan, boxed, lower, upper, tile, sums, turned, ztop, near)
 
     behind_x = shifted(value, "tx", 1)
     behind_y = shifted(value, "ty", 1)

time: 101 us -> 83.7 us (0.83)
  Pallas kernels: 73.8 us -> 54.2 us
  starting transfers between devices: 15.7 us -> 19.1 us
  waiting for transfers between devices: 9.1 us -> 7.22 us
    pallas_call x2 -> x1, Pallas kernels: 40.4 us -> 17.1 us  [near_own(): pl.pallas_call(near_own_kernel, out_shape=(pltpu.VMEM((boxes + 8, LANES),...]
    pallas_call x1, Pallas kernels: 13.1 us -> 16.7 us  [near_other(): pl.pallas_call(lambda *refs: near_other_kernel(near, *refs), out_shape=pl...]
    ppermute x1, waiting for transfers between devices: 4.17 us -> 0.8 us  [shards(): behind_xy = lax.ppermute(value, both, diagonal)]
    ppermute x5, starting transfers between devices: 9.79 us -> 12 us  [shifted(): return lax.ppermute(value, axis, pairs)]
    ppermute x5, waiting for transfers between devices: 4.93 us -> 6.42 us  [shifted(): return lax.ppermute(value, axis, pairs)]
    ppermute x1, starting transfers between devices: 0.06 us -> 1.23 us  [shards(): behind_xy = lax.ppermute(value, both, diagonal)]
  transfers between devices with their start and end apart: 8 -> 8, of which waited for: 3 -> 3; matrix products, arithmetic and copies ran while one was open for 0% -> 0% of each run, Pallas kernels for 48% -> 31%
where the time goes in v4:
time: 83.7 us
  Pallas kernels  54.2 us (65%)
  starting transfers between devices  19.1 us (23%)
  waiting for transfers between devices  7.22 us (9%)
  other arithmetic  1.81 us (2%)
    pallas_call x1, Pallas kernels, near_own(): pl.pallas_call(near_own_kernel, out_shape=(pltpu.VMEM((boxes + 8, LANES),...  17.1 us
    pallas_call x1, Pallas kernels, near_other(): pl.pallas_call(lambda *refs: near_other_kernel(near, *refs), out_shape=pl...  16.7 us
    pallas_call x4, Pallas kernels, scatter(): pl.pallas_call(lambda *refs: scatter_kernel(first, last, (rows, cols, hig...  12.6 us
    ppermute x5, starting transfers between devices, shifted(): return lax.ppermute(value, axis, pairs)  12 us
    pallas_call x1, Pallas kernels, finish(): pl.pallas_call(finish_kernel, out_shape=(shape, shape), in_specs=[vmem] *...  6.7 us
    ppermute x5, waiting for transfers between devices, shifted(): return lax.ppermute(value, axis, pairs)  6.42 us
    ppermute x1, starting transfers between devices, shards(): lower = lax.ppermute(boxed, both, [(i, i + 1) for i in range(total - 1)])  4.57 us
    another operation x2, other arithmetic, shards(): tile = jnp.stack([slot, elevation, potential, normal_flux])  1.81 us
  transfers between devices with their start and end apart: 8, of which 3 were waited for; matrix products, arithmetic and copies ran while one was open for 0% of the time, Pallas kernels for 31%

profile of v4, /device:TPU:0, one launch (start us, length us, event | category | flops | bytes accessed | tf_op | source)
XLA Modules:
  0.0 83.7 jit_solution(1468050142109391197)
XLA Ops:
  0.6 0.9 %convert_bitcast_fusion = f32[1,64,256]{2,1,0:T(8,128)S(1)} fusion(s32[64,256]{1,0:T(8,128)} %param.10, s32[64,256]{1,0:T(8,128)} %param.9), kind=kLoop, calls=%fused_computation.1 | loop fusion | flops 49152 | bytes 196608 | tf_op jit(solution)/shard_map/stack | solution.py:591
  1.5 0.9 %pad_maximum_fusion.refs_0_.refs_4_.tile = f32[4,64,256]{2,1,0:T(8,128)S(1)} fusion(f32[1,64,256]{2,1,0:T(8,128)} %bitcast.7, f32[1,64,256]{2,1,0:T(8,128)} %bitcast.8, f32[1,64,256]{2,1,0:T(8,128)} %bitcast.9, f32[1,64,256]{2,1,0:T(8,128)S(1)} %convert_bitcast_fusion), kind=kLoop, calls=%fused_computation | loop fusion | flops 196608 | bytes 524288 | tf_op jit(solution)/shard_map/stack | solution.py:591
  2.4 5.1 %collective-permute-start.1 = (f32[4,64,256]{2,1,0:T(8,128)S(1)}, f32[4,64,256]{2,1,0:T(8,128)S(1)}, u32[]{:S(2)}, u32[]{:S(2)}) collective-permute-start(f32[4,64,256]{2,1,0:T(8,128)S(1)} %pad_maximum_fusion.refs_0_.refs_4_.tile), channel_id=1, source_target_pairs={{0,3},{1,0},{2,1},{3,2},{4,7},{5,4},{6,5},{7,6},{8,11},{9,8},{10,9... | collective-permute-start | bytes 786440 | tf_op jit(solution)/shard_map/ppermute | solution.py:25
  7.6 1.6 %collective-permute-start = (f32[4,64,256]{2,1,0:T(8,128)S(1)}, f32[4,64,256]{2,1,0:T(8,128)S(1)}, u32[]{:S(2)}, u32[]{:S(2)}) collective-permute-start(f32[4,64,256]{2,1,0:T(8,128)S(1)} %pad_maximum_fusion.refs_0_.refs_4_.tile), channel_id=1, source_target_pairs={{0,28},{4,0},{8,4},{12,8},{16,12},{20,16},{24,20},{28,24},{1,29},{... | collective-permute-start | bytes 786440 | tf_op jit(solution)/shard_map/ppermute | solution.py:25
  9.2 0.7 copy-done
  9.9 1.6 %scatter_first.1 = (f32[384,256]{1,0:T(8,128)S(1)}, s32[16,128]{1,0:T(8,128)S(1)}) custom-call(f32[4,64,256]{2,1,0:T(8,128)S(1)} %pad_maximum_fusion.refs_0_.refs_4_.tile, s32[8,128]{1,0:T(8,128)S(1)} %bitcast.6), custom_call_target="tpu_custom_call" | custom-call | flops 1610612736 | bytes 1048576 | tf_op jit(solution)/shard_map/scatter_first/pallas_call | solution.py:142
  11.5 1.6 %collective-permute-done.1.refs_0_.ahead_y = f32[4,64,256]{2,1,0:T(8,128)S(1)} collective-permute-done((f32[4,64,256]{2,1,0:T(8,128)S(1)}, f32[4,64,256]{2,1,0:T(8,128)S(1)}, u32[]{:S(2)}, u32[]{:S(2)}) %collective-permute-start.1) | collective-permute-done | bytes 262176 | tf_op jit(solution)/shard_map/ppermute | solution.py:25
  13.1 1.0 %collective-permute-start.2 = (f32[4,64,256]{2,1,0:T(8,128)S(1)}, f32[4,64,256]{2,1,0:T(8,128)S(1)}, u32[]{:S(2)}, u32[]{:S(2)}) collective-permute-start(f32[4,64,256]{2,1,0:T(8,128)S(1)} %collective-permute-done.1.refs_0_.ahead_y), channel_id=1, source_target_pairs={{0,28},{4,0},{8,4},{12,8},{16,12},{20,16},{24,20},{28,24},{1,29},{... | collective-permute-start | bytes 786440 | tf_op jit(solution)/shard_map/ppermute | solution.py:25
  14.2 2.2 %scatter.2.refs_1_ = f32[384,256]{1,0:T(8,128)S(1)} custom-call(f32[4,64,256]{2,1,0:T(8,128)S(1)} %collective-permute-done.refs_0_.ahead_x, f32[384,256]{1,0:T(8,128)S(1)} %get-tuple-element.9.refs_1_), custom_call_target="tpu_custom_call" | custom-call | flops 1610612736 | bytes 1048576 | tf_op jit(solution)/shard_map/scatter/pallas_call | solution.py:142
  16.4 3.7 %scatter.3.refs_1_ = f32[384,256]{1,0:T(8,128)S(1)} custom-call(f32[4,64,256]{2,1,0:T(8,128)S(1)} %collective-permute-done.1.refs_0_.ahead_y, f32[384,256]{1,0:T(8,128)S(1)} %scatter.2.refs_1_), custom_call_target="tpu_custom_call" | custom-call | flops 1610612736 | bytes 1048576 | tf_op jit(solution)/shard_map/scatter/pallas_call | solution.py:142
  20.1 0.0 collective-permute-done.2.refs_0_
  20.1 5.0 %scatter_last.1 = (f32[384,256]{1,0:T(8,128)}, f32[5,128,128]{2,1,0:T(8,128)S(1)}) custom-call(f32[4,64,256]{2,1,0:T(8,128)S(1)} %collective-permute-done.2.refs_0_, f32[384,256]{1,0:T(8,128)S(1)} %scatter.3.refs_1_), custom_call_target="tpu_custom_call" | custom-call | flops 1610612736 | bytes 1048576 | tf_op jit(solution)/shard_map/scatter_last/pallas_call | solution.py:142
  25.1 1.3 %collective-permute-start.4 = (f32[5,128,128]{2,1,0:T(8,128)S(1)}, f32[5,128,128]{2,1,0:T(8,128)S(1)}, u32[]{:S(2)}, u32[]{:S(2)}) collective-permute-start(f32[5,128,128]{2,1,0:T(8,128)S(1)} %get-tuple-element.10.own.refs_1_), channel_id=1, source_target_pairs={{1,0},{2,1},{3,2},{4,3},{5,4},{6,5},{7,6},{8,7},{9,8},{10,9},{11,1... | collective-permute-start | bytes 983048 | tf_op jit(solution)/shard_map/ppermute | solution.py:606
  26.4 4.6 %collective-permute-start.3 = (f32[5,128,128]{2,1,0:T(8,128)S(1)}, f32[5,128,128]{2,1,0:T(8,128)S(1)}, u32[]{:S(2)}, u32[]{:S(2)}) collective-permute-start(f32[5,128,128]{2,1,0:T(8,128)S(1)} %get-tuple-element.10.own.refs_1_), channel_id=1, source_target_pairs={{0,1},{1,2},{2,3},{3,4},{4,5},{5,6},{6,7},{7,8},{8,9},{9,10},{10,1... | collective-permute-start | bytes 983048 | tf_op jit(solution)/shard_map/ppermute | solution.py:605
  31.0 17.1 %near_own.1 = (f32[136,128]{1,0:T(8,128)S(1)}, bf16[129,128,32]{2,1,0:T(8,128)(2,1)S(1)}, f32[128,128]{1,0:T(8,128)S(1)}) custom-call(s32[16,128]{1,0:T(8,128)S(1)} %get-tuple-element.8.plan.refs_0_, f32[5,128,128]{2,1,0:T(8,128)S(1)} %get-tuple-element.10.own.refs_1_), custom_call_target="tpu_custom_call" | custom-call | flops 2147483648 | bytes 1048576 | tf_op jit(solution)/shard_map/near_own/pallas_call | solution.py:406
  48.1 0.0 collective-permute-done.4.refs_3_
  48.1 16.7 %near_other.1.own = f32[144,128]{1,0:T(8,128)S(1)} custom-call(s32[16,128]{1,0:T(8,128)S(1)} %get-tuple-element.8.plan.refs_0_, f32[5,128,128]{2,1,0:T(8,128)S(1)} %get-tuple-element.10.own.refs_1_, f32[5,128,128]{2,1,0:T(8,128)S(1)} %collective-permute-done.3.refs_2_, f32[5,128,128]{2,1,0:T(8,128)S(1)} %collective-permute-done.4.refs_3_, ...), custom_call_target="tpu_custom_call" | custom-call | flops 2147483648 | bytes 1048576 | tf_op jit(solution)/shard_map/near_other/pallas_call | solution.py:426
  64.8 1.2 %collective-permute-start.7 = (f32[144,128]{1,0:T(8,128)S(1)}, f32[144,128]{1,0:T(8,128)S(1)}, u32[]{:S(2)}, u32[]{:S(2)}) collective-permute-start(f32[144,128]{1,0:T(8,128)S(1)} %near_other.1.own), channel_id=1, source_target_pairs={{0,5},{1,6},{2,7},{3,4},{4,9},{5,10},{6,11},{7,8},{8,13},{9,14},{1... | collective-permute-start | bytes 221192 | tf_op jit(solution)/shard_map/ppermute | solution.py:618
  66.0 3.4 %collective-permute-start.6 = (f32[144,128]{1,0:T(8,128)S(1)}, f32[144,128]{1,0:T(8,128)S(1)}, u32[]{:S(2)}, u32[]{:S(2)}) collective-permute-start(f32[144,128]{1,0:T(8,128)S(1)} %near_other.1.own), channel_id=1, source_target_pairs={{0,1},{1,2},{2,3},{3,0},{4,5},{5,6},{6,7},{7,4},{8,9},{9,10},{10,1... | collective-permute-start | bytes 221192 | tf_op jit(solution)/shard_map/ppermute | solution.py:25
  69.4 0.9 %collective-permute-start.5 = (f32[144,128]{1,0:T(8,128)S(1)}, f32[144,128]{1,0:T(8,128)S(1)}, u32[]{:S(2)}, u32[]{:S(2)}) collective-permute-start(f32[144,128]{1,0:T(8,128)S(1)} %near_other.1.own), channel_id=1, source_target_pairs={{0,4},{4,8},{8,12},{12,16},{16,20},{20,24},{24,28},{28,0},{1,5},{5... | collective-permute-start | bytes 221192 | tf_op jit(solution)/shard_map/ppermute | solution.py:25
  70.3 1.2 %gather_own.1.partial = f32[64,256]{1,0:T(8,128)S(1)} custom-call(f32[4,64,256]{2,1,0:T(8,128)S(1)} %pad_maximum_fusion.refs_0_.refs_4_.tile, f32[144,128]{1,0:T(8,128)S(1)} %near_other.1.own), custom_call_target="tpu_custom_call" | custom-call | flops 268435456 | bytes 262144 | tf_op jit(solution)/shard_map/gather_own/pallas_call | solution.py:494
  71.4 0.8 collective-permute-done.7.behind_xy
  72.2 4.8 %collective-permute-done.6.behind_y = f32[144,128]{1,0:T(8,128)S(1)} collective-permute-done((f32[144,128]{1,0:T(8,128)S(1)}, f32[144,128]{1,0:T(8,128)S(1)}, u32[]{:S(2)}, u32[]{:S(2)}) %collective-permute-start.6) | collective-permute-done | bytes 73760 | tf_op jit(solution)/shard_map/ppermute | solution.py:25
  77.0 6.7 %finish.1 = (f32[64,256]{1,0:T(8,128)}, f32[64,256]{1,0:T(8,128)}) custom-call(f32[4,64,256]{2,1,0:T(8,128)S(1)} %pad_maximum_fusion.refs_0_.refs_4_.tile, f32[4,64,256]{2,1,0:T(8,128)S(1)} %collective-permute-done.refs_0_.ahead_x, f32[4,64,256]{2,1,0:T(8,128)S(1)} %collective-permute-done.1.refs_0_.ahead_y, f32[64,256]{1,0:T(8,128)S(1)} %gather_own.1.partial, ...), custom_call_target="tpu_custom_call" | custom-call | flops 805306368 | bytes 524288 | tf_op jit(solution)/shard_map/finish/pallas_call | solution.py:561
  (4 shorter events, 0.0 us)
Async XLA Ops:
  2.4 10.7 %collective-permute-start.1 = (f32[4,64,256]{2,1,0:T(8,128)S(1)}, f32[4,64,256]{2,1,0:T(8,128)S(1)}, u32[]{:S(2)}, u32[]{:S(2)}) collective-permute-start(f32[4,64,256]{2,1,0:T(8,128)S(1)} %pad_maximum_fusion.refs_0_.refs_4_.tile), channel_id=1, source_target_pairs={{0,3},{1,0},{2,1},{3,2},{4,7},{5,4},{6,5},{7,6},{8,11},{9,8},{10,9... | collective-permute-start | bytes 786440 | tf_op jit(solution)/shard_map/ppermute | solution.py:25
  7.6 6.6 %collective-permute-start = (f32[4,64,256]{2,1,0:T(8,128)S(1)}, f32[4,64,256]{2,1,0:T(8,128)S(1)}, u32[]{:S(2)}, u32[]{:S(2)}) collective-permute-start(f32[4,64,256]{2,1,0:T(8,128)S(1)} %pad_maximum_fusion.refs_0_.refs_4_.tile), channel_id=1, source_target_pairs={{0,28},{4,0},{8,4},{12,8},{16,12},{20,16},{24,20},{28,24},{1,29},{... | collective-permute-start | bytes 786440 | tf_op jit(solution)/shard_map/ppermute | solution.py:25
  9.2 0.7 copy-start
  13.1 6.9 %collective-permute-start.2 = (f32[4,64,256]{2,1,0:T(8,128)S(1)}, f32[4,64,256]{2,1,0:T(8,128)S(1)}, u32[]{:S(2)}, u32[]{:S(2)}) collective-permute-start(f32[4,64,256]{2,1,0:T(8,128)S(1)} %collective-permute-done.1.refs_0_.ahead_y), channel_id=1, source_target_pairs={{0,28},{4,0},{8,4},{12,8},{16,12},{20,16},{24,20},{28,24},{1,29},{... | collective-permute-start | bytes 786440 | tf_op jit(solution)/shard_map/ppermute | solution.py:25
  25.1 22.9 %collective-permute-start.4 = (f32[5,128,128]{2,1,0:T(8,128)S(1)}, f32[5,128,128]{2,1,0:T(8,128)S(1)}, u32[]{:S(2)}, u32[]{:S(2)}) collective-permute-start(f32[5,128,128]{2,1,0:T(8,128)S(1)} %get-tuple-element.10.own.refs_1_), channel_id=1, source_target_pairs={{1,0},{2,1},{3,2},{4,3},{5,4},{6,5},{7,6},{8,7},{9,8},{10,9},{11,1... | collective-permute-start | bytes 983048 | tf_op jit(solution)/shard_map/ppermute | solution.py:606
  26.4 21.7 %collective-permute-start.3 = (f32[5,128,128]{2,1,0:T(8,128)S(1)}, f32[5,128,128]{2,1,0:T(8,128)S(1)}, u32[]{:S(2)}, u32[]{:S(2)}) collective-permute-start(f32[5,128,128]{2,1,0:T(8,128)S(1)} %get-tuple-element.10.own.refs_1_), channel_id=1, source_target_pairs={{0,1},{1,2},{2,3},{3,4},{4,5},{5,6},{6,7},{7,8},{8,9},{9,10},{10,1... | collective-permute-start | bytes 983048 | tf_op jit(solution)/shard_map/ppermute | solution.py:605
  64.8 7.4 %collective-permute-start.7 = (f32[144,128]{1,0:T(8,128)S(1)}, f32[144,128]{1,0:T(8,128)S(1)}, u32[]{:S(2)}, u32[]{:S(2)}) collective-permute-start(f32[144,128]{1,0:T(8,128)S(1)} %near_other.1.own), channel_id=1, source_target_pairs={{0,5},{1,6},{2,7},{3,4},{4,9},{5,10},{6,11},{7,8},{8,13},{9,14},{1... | collective-permute-start | bytes 221192 | tf_op jit(solution)/shard_map/ppermute | solution.py:618
  66.0 11.0 %collective-permute-start.6 = (f32[144,128]{1,0:T(8,128)S(1)}, f32[144,128]{1,0:T(8,128)S(1)}, u32[]{:S(2)}, u32[]{:S(2)}) collective-permute-start(f32[144,128]{1,0:T(8,128)S(1)} %near_other.1.own), channel_id=1, source_target_pairs={{0,1},{1,2},{2,3},{3,0},{4,5},{5,6},{6,7},{7,4},{8,9},{9,10},{10,1... | collective-permute-start | bytes 221192 | tf_op jit(solution)/shard_map/ppermute | solution.py:25
  69.4 7.6 %collective-permute-start.5 = (f32[144,128]{1,0:T(8,128)S(1)}, f32[144,128]{1,0:T(8,128)S(1)}, u32[]{:S(2)}, u32[]{:S(2)}) collective-permute-start(f32[144,128]{1,0:T(8,128)S(1)} %near_other.1.own), channel_id=1, source_target_pairs={{0,4},{4,8},{8,12},{12,16},{16,20},{20,24},{24,28},{28,0},{1,5},{5... | collective-permute-start | bytes 221192 | tf_op jit(solution)/shard_map/ppermute | solution.py:25

commit v5 on v4

--- a/solution.py
+++ b/solution.py
@@ -12,8 +12,9 @@
 PIECES = 6
 FEATURES = 32
 USED = 24
+STORED = USED + 8
 EXTRA = 16
-GROUP = 2
+GROUP = 8
 VMEM_LIMIT = 24 << 20
 BF16 = jnp.bfloat16
 F32 = jnp.float32
@@ -215,14 +216,21 @@
     return values + [jnp.zeros_like(values[0])] * (USED - len(values))
 
 
-def strided(ref, n):
-    pitch = ref.shape[0] // USED
+def moment_side(ref, n):
+    pitch = ref.shape[0] // STORED
+    rows = ref[pl.ds(USED * pitch + n, 8, stride=pitch), :]
+    zeros = jnp.zeros((8, LANES), F32)
+    return jnp.concatenate([zeros, rows] + [zeros] * (FEATURES // 8 - 2), axis=0).astype(BF16)
+
+
+def strided(ref, n, stored):
+    pitch = ref.shape[0] // stored
     rows = [ref[pl.ds(8 * g * pitch + n, 8, stride=pitch), :] for g in range(USED // 8)]
     return jnp.concatenate(rows + [jnp.zeros((8, LANES), F32)] * ((FEATURES - USED) // 8), axis=0)
 
 
-def store_sources(refs, sfeat, smeta):
-    pitch = sfeat.shape[0] // USED
+def store_sources(refs, sfeat, sflux):
+    pitch = sfeat.shape[0] // STORED
     ones = jnp.ones((8, LANES), F32)
     zeros = jnp.zeros((8, LANES), F32)
     start = 0
@@ -232,17 +240,16 @@
             source = []
             for high, low in pieces:
                 source += [-2.0 * high, -2.0 * low, -2.0 * high, -2.0 * low]
-            for k, v in enumerate(padded_rows(source + list(thirds(total)) + [ones, ones, ones])):
+            z = pieces[2][0] + pieces[2][1]
+            rows = padded_rows(source + list(thirds(total)) + [ones, ones, ones])
+            rows += [pot, zeros, pot, zeros] + list(thirds(-pot * z)) + [zeros]
+            for k, v in enumerate(rows):
                 sfeat[k * pitch + start : k * pitch + start + 8, :] = v
-            z = pieces[2][0] + pieces[2][1]
-            smeta[0, start : start + 8, :] = pot
-            smeta[1, start : start + 8, :] = pot * z
-            smeta[2, start : start + 8, :] = flux
+            sflux[start : start + 8, :] = flux
             start += 8
-    for k in range(USED):
+    for k in range(STORED):
         sfeat[k * pitch + start : k * pitch + start + 8, :] = ones if k == 12 else zeros
-    for m in range(3):
-        smeta[m, start : start + 8, :] = zeros
+    sflux[start : start + 8, :] = zeros
 
 
 def store_targets(own, tfeat, turned):
@@ -260,73 +267,56 @@
 
     def turn(i, carry):
         for u in range(8):
-            turned[8 * i + u] = strided(tfeat, 8 * i + u).T.astype(BF16)
+            turned[8 * i + u] = strided(tfeat, 8 * i + u, USED).T.astype(BF16)
         return carry
 
     lax.fori_loop(0, boxes // 8, turn, 0)
 
 
-def run_items(target_of, source_of, half, iterations, turned, ztop, sfeat, smeta, sums, squares, totals):
+def run_items(target_of, source_of, half, iterations, turned, sfeat, sflux, sums, totals):
     empty_row = sums.shape[0] - 8
 
-    def distances(group, squared):
-        for i in range(GROUP):
-            item = group * GROUP + i
-            sides = [strided(sfeat, source_of(item, k)).astype(BF16) for k in range(half)]
-            squared[i] = jnp.dot(
-                turned[target_of(item)], jnp.concatenate(sides, axis=1), preferred_element_type=F32
-            )
-
-    def apply(group, squared, total):
-        for i in range(GROUP):
-            item = group * GROUP + i
-            lane = jnp.full((8, LANES), jnp.minimum(target_of(item), LANES - 1), jnp.int32)
-            metas = []
-            for k in range(half):
-                n = source_of(item, k)
-                metas.append([jnp.broadcast_to(smeta[m, pl.ds(n, 1), :], (8, LANES)) for m in range(3)])
-            for t in range(LANES // 8):
-                rows = slice(8 * t, 8 * t + 8)
-                z = jnp.take_along_axis(ztop[rows, :], lane, axis=1)
-                value = None
-                for k in range(half):
-                    pot, pot_z, flux = metas[k]
-                    inverse = lax.rsqrt(squared[i, rows, LANES * k : LANES * k + LANES])
-                    part = inverse * (flux - (inverse * inverse) * (z * pot - pot_z))
-                    value = part if value is None else value + part
-                total[i, rows, :] = value
-
-    def reduce(group, total, live):
-        for i in range(GROUP):
-            target = jnp.where(live, target_of(jnp.maximum(group * GROUP + i, 0)), empty_row)
-            row = jnp.sum(total[i].T, axis=0, keepdims=True)
-            sums[pl.ds(target, 1), :] += row
-
-    (even_sq, odd_sq), (even_tot, odd_tot) = squares, totals
-    odd_tot[...] = jnp.zeros(odd_tot.shape, F32)
-    distances(0, even_sq)
+    def apply(item, total):
+        target = target_of(item)
+        sides = [strided(sfeat, source_of(item, k), STORED).astype(BF16) for k in range(half)]
+        sides += [moment_side(sfeat, source_of(item, k)) for k in range(half)]
+        squared = jnp.dot(turned[target], jnp.concatenate(sides, axis=1), preferred_element_type=F32)
+        fluxes = [
+            jnp.broadcast_to(sflux[pl.ds(source_of(item, k), 1), :], (8, LANES)) for k in range(half)
+        ]
+        for t in range(LANES // 8):
+            rows = slice(8 * t, 8 * t + 8)
+            value = None
+            for k, flux in enumerate(fluxes):
+                inverse = lax.rsqrt(squared[rows, LANES * k : LANES * (k + 1)])
+                moment = squared[rows, LANES * (half + k) : LANES * (half + k + 1)]
+                part = inverse * (flux - (inverse * inverse) * moment)
+                value = part if value is None else value + part
+            total[rows, :] = value
+
+    def reduce(item, total, live):
+        target = jnp.where(live, target_of(jnp.maximum(item, 0)), empty_row)
+        sums[pl.ds(target, 1), :] += jnp.sum(total[...].T, axis=0, keepdims=True)
 
     def step(i, carry):
-        distances(2 * i + 1, odd_sq)
-        apply(2 * i, even_sq, even_tot)
-        reduce(2 * i - 1, odd_tot, i > 0)
-        distances(2 * i + 2, even_sq)
-        apply(2 * i + 1, odd_sq, odd_tot)
-        reduce(2 * i, even_tot, True)
+        for u in range(GROUP):
+            reduce(GROUP * (i - 1) + u, totals.at[u], i > 0)
+        for u in range(GROUP):
+            apply(GROUP * i + u, totals.at[u])
         return carry
 
+    totals[...] = jnp.zeros(totals.shape, F32)
     lax.fori_loop(0, iterations, step, 0)
-    reduce(2 * iterations - 1, odd_tot, iterations > 0)
-
-
-def near_own_kernel(plan, own, sums, turned, ztop, tfeat, sfeat, smeta, s0, s1, t0, t1):
+    for u in range(GROUP):
+        reduce(GROUP * (iterations - 1) + u, totals.at[u], iterations > 0)
+
+
+def near_own_kernel(near, plan, own, sums, turned, tfeat, sfeat, sflux, totals):
     boxes = own.shape[1]
-    half = s0.shape[2] // LANES
+    half = near // 2
     sums[...] = jnp.zeros(sums.shape, F32)
     store_targets(own, tfeat, turned)
-    high = rounded(own[2])
-    ztop[...] = (high + rounded(own[2] - high)).T
-    store_sources([own], sfeat, smeta)
+    store_sources([own], sfeat, sflux)
 
     def target_of(item):
         return jnp.minimum(item, boxes - 1)
@@ -335,17 +325,17 @@
         return plan[k, jnp.minimum(item, boxes - 1)]
 
     run_items(
-        target_of, source_of, half, boxes // (2 * GROUP), turned, ztop, sfeat, smeta, sums, (s0, s1), (t0, t1)
+        target_of, source_of, half, boxes // GROUP, turned, sfeat, sflux, sums, totals
     )
 
 
 def near_other_kernel(
-    near, plan, own, lower, upper, tile, sums_in, turned, ztop, out, sums, sfeat, smeta, s0, s1, t0, t1
+    near, plan, own, lower, upper, tile, sums_in, turned, out, sums, sfeat, sflux, totals
 ):
     boxes = lower.shape[1]
-    half = s0.shape[2] // LANES
+    half = near // 2
     sums[...] = sums_in[...]
-    store_sources([lower, own, upper], sfeat, smeta)
+    store_sources([lower, own, upper], sfeat, sflux)
     items = boxes + plan[half + near + 1, 0]
 
     def box_of(item):
@@ -359,9 +349,9 @@
         row = jnp.where(item < boxes, half, 2 * half) + k
         return plan[row, jnp.minimum(box_of(item), boxes - 1)]
 
-    iterations = (items + 2 * GROUP - 1) // (2 * GROUP)
+    iterations = (items + GROUP - 1) // GROUP
     run_items(
-        target_of, source_of, half, iterations, turned, ztop, sfeat, smeta, sums, (s0, s1), (t0, t1)
+        target_of, source_of, half, iterations, turned, sfeat, sflux, sums, totals
     )
     out[0:boxes, :] = sums[0:boxes, :] * (1.0 / math.sqrt(near * LANES))
 
@@ -380,13 +370,10 @@
         place += 2
 
 
-def item_scratch(sources, half):
+def item_scratch(sources):
     return [
-        pltpu.VMEM((USED * (sources + 8), LANES), F32),
-        pltpu.VMEM((3, sources + 8, LANES), F32),
-        pltpu.VMEM((GROUP, LANES, half * LANES), F32),
-        pltpu.VMEM((GROUP, LANES, half * LANES), F32),
-        pltpu.VMEM((GROUP, LANES, LANES), F32),
+        pltpu.VMEM((STORED * (sources + 8), LANES), F32),
+        pltpu.VMEM((sources + 8, LANES), F32),
         pltpu.VMEM((GROUP, LANES, LANES), F32),
     ]
 
@@ -400,39 +387,38 @@
 
 def near_own(plan, own, near):
     boxes = own.shape[1]
-    assert boxes == LANES and boxes % (2 * GROUP) == 0 and near % 2 == 0
+    assert boxes == LANES and boxes % GROUP == 0 and near % 2 == 0
     vmem = pl.BlockSpec(memory_space=pltpu.VMEM)
     smem = pl.BlockSpec(memory_space=pltpu.SMEM)
     return pl.pallas_call(
-        near_own_kernel,
+        lambda *refs: near_own_kernel(near, *refs),
         out_shape=(
             pltpu.VMEM((boxes + 8, LANES), F32),
             pltpu.VMEM((boxes + 1, LANES, FEATURES), BF16),
-            pltpu.VMEM((LANES, boxes), F32),
         ),
         in_specs=[smem, vmem],
-        out_specs=(vmem,) * 3,
-        scratch_shapes=[pltpu.VMEM((USED * (boxes + 8), LANES), F32)] + item_scratch(boxes, near // 2),
+        out_specs=(vmem,) * 2,
+        scratch_shapes=[pltpu.VMEM((USED * (boxes + 8), LANES), F32)] + item_scratch(boxes),
         compiler_params=pltpu.CompilerParams(vmem_limit_bytes=VMEM_LIMIT),
         name="near_own",
         cost_estimate=near_cost(boxes, near),
     )(plan, pinned(own))
 
 
-def near_other(plan, own, lower, upper, tile, sums, turned, ztop, near):
+def near_other(plan, own, lower, upper, tile, sums, turned, near):
     boxes = lower.shape[1]
     vmem = pl.BlockSpec(memory_space=pltpu.VMEM)
     smem = pl.BlockSpec(memory_space=pltpu.SMEM)
     return pl.pallas_call(
         lambda *refs: near_other_kernel(near, *refs),
         out_shape=pltpu.VMEM((boxes + EXTRA, LANES), F32),
-        in_specs=[smem] + [vmem] * 7,
+        in_specs=[smem] + [vmem] * 6,
         out_specs=vmem,
-        scratch_shapes=[pltpu.VMEM((boxes + 8, LANES), F32)] + item_scratch(3 * boxes, near // 2),
+        scratch_shapes=[pltpu.VMEM((boxes + 8, LANES), F32)] + item_scratch(3 * boxes),
         compiler_params=pltpu.CompilerParams(vmem_limit_bytes=VMEM_LIMIT),
         name="near_other",
         cost_estimate=near_cost(boxes, near),
-    )(plan, *map(pinned, (own, lower, upper, tile, sums, turned, ztop)))
+    )(plan, *map(pinned, (own, lower, upper, tile, sums, turned)))
 
 
 def lookup(slot, bases, tables, pieces, out):
@@ -483,54 +469,40 @@
     return (rank * node_count).astype(F32)
 
 
-def gather_own_kernel(tile, own, out, pieces):
+def own_kernel(tile, table, out, pieces):
     out[...] = jnp.zeros(out.shape, F32)
-    lookup(tile.at[0], [base_of(out.shape[0] * out.shape[1], (0, 0))], [own], pieces, out)
-
-
-def gather_own(tile, own):
-    _, rows, cols = tile.shape
-    vmem = pl.BlockSpec(memory_space=pltpu.VMEM)
-    return pl.pallas_call(
-        gather_own_kernel,
-        out_shape=pltpu.VMEM((rows, cols), F32),
-        in_specs=[vmem] * 2,
-        out_specs=vmem,
-        scratch_shapes=[pltpu.VMEM((1, 2 * rows * cols // WIDE, WIDE), BF16)],
-        compiler_params=pltpu.CompilerParams(vmem_limit_bytes=VMEM_LIMIT),
-        name="gather_own",
-        cost_estimate=pl.CostEstimate(
-            flops=rows * cols * rows * cols, transcendentals=0, bytes_accessed=4 * 4 * rows * cols
-        ),
-    )(tile, pinned(own))
-
-
-def finish_kernel(
-    tile, ahead_x, ahead_y, partial, behind_x, behind_y, behind_xy, elev_rate, pot_rate, pieces, total, padded
-):
+    lookup(tile.at[0], [base_of(out.shape[0] * out.shape[1], (0, 0))], [table], pieces, out)
+
+
+def row_kernel(tile, ahead_x, partial, behind_x, out, slopes, pieces, padded):
     _, rows, cols = tile.shape
     boxes = rows * cols // LANES
-    total[...] = partial[...]
-    bases = [base_of(rows * cols, steps) for steps in ((1, 0), (0, 1), (1, 1))]
-    lookup(tile.at[0], bases, [behind_x, behind_y, behind_xy], pieces, total)
-
-    left_cols = behind_y[boxes + EXTRA - 8 : boxes + EXTRA, 0:rows].T
-    col = lax.broadcasted_iota(jnp.int32, (rows, cols), 1)
-    slopes = []
+    out[...] = partial[...]
+    lookup(tile.at[0], [base_of(rows * cols, (1, 0))], [behind_x], pieces, out)
     for f in (1, 2):
-        here = tile[f]
-        padded[8 : 8 + rows, :] = here
+        padded[8 : 8 + rows, :] = tile[f]
         for r in range(2):
             for c in range(cols // LANES):
                 source = boxes + ((f - 1) * 2 + r) * (cols // LANES) + c
                 padded[6 + r : 7 + r, LANES * c : LANES * c + LANES] = behind_x[source : source + 1, :]
         padded[8 + rows : 10 + rows, :] = ahead_x[f, 0:2, :]
-        along_rows = (
+        slopes[f - 1] = (
             padded[6 : 6 + rows, :]
             - 8.0 * padded[7 : 7 + rows, :]
             + 8.0 * padded[9 : 9 + rows, :]
             - padded[10 : 10 + rows, :]
         ) / 12.0
+
+
+def col_kernel(tile, ahead_y, partial, behind_y, out, slopes, pieces):
+    _, rows, cols = tile.shape
+    boxes = rows * cols // LANES
+    out[...] = partial[...]
+    lookup(tile.at[0], [base_of(rows * cols, (0, 1))], [behind_y], pieces, out)
+    left_cols = behind_y[boxes + EXTRA - 8 : boxes + EXTRA, 0:rows].T
+    col = lax.broadcasted_iota(jnp.int32, (rows, cols), 1)
+    for f in (1, 2):
+        here = tile[f]
         left = left_cols[:, 2 * (f - 1) : 2 * f]
         right = ahead_y[f, :, 0:2]
         less_1 = jnp.where(col == 0, left[:, 1:2], pltpu.roll(here, 1, 1))
@@ -543,9 +515,15 @@
             right[:, 0:1],
             jnp.where(col == cols - 1, right[:, 1:2], pltpu.roll(here, cols - 2, 1)),
         )
-        along_cols = (less_2 - 8.0 * less_1 + 8.0 * more_1 - more_2) / 12.0
-        slopes.append((along_rows, along_cols))
-    (elev_x, elev_y), (pot_x, pot_y) = slopes
+        slopes[f - 1] = (less_2 - 8.0 * less_1 + 8.0 * more_1 - more_2) / 12.0
+
+
+def last_kernel(tile, row_slopes, col_slopes, partial, behind_xy, elev_rate, pot_rate, pieces, total):
+    _, rows, cols = tile.shape
+    total[...] = partial[...]
+    lookup(tile.at[0], [base_of(rows * cols, (1, 1))], [behind_xy], pieces, total)
+    elev_x, pot_x = row_slopes[0], row_slopes[1]
+    elev_y, pot_y = col_slopes[0], col_slopes[1]
     vertical = total[...]
     lift = 1.0 + elev_x * elev_x + elev_y * elev_y
     elev_rate[...] = vertical * lift - (pot_x * elev_x + pot_y * elev_y)
@@ -554,26 +532,66 @@
     )
 
 
-def finish(tile, ahead_x, ahead_y, partial, behind):
+def lookup_call(kernel, name, out_shape, args, scratch):
+    _, rows, cols = args[0].shape
+    vmem = pl.BlockSpec(memory_space=pltpu.VMEM)
+    return pl.pallas_call(
+        kernel,
+        out_shape=out_shape,
+        in_specs=[vmem] * len(args),
+        out_specs=(vmem,) * len(out_shape),
+        scratch_shapes=[pltpu.VMEM((1, 2 * rows * cols // WIDE, WIDE), BF16)] + scratch,
+        compiler_params=pltpu.CompilerParams(vmem_limit_bytes=VMEM_LIMIT),
+        name=name,
+        cost_estimate=pl.CostEstimate(
+            flops=rows * cols * rows * cols, transcendentals=0, bytes_accessed=4 * 8 * rows * cols
+        ),
+    )(*map(pinned, args))
+
+
+def look_up_all(tile, ahead_x, ahead_y, value, behind_x, behind_y, behind_xy):
     _, rows, cols = tile.shape
+    values = pltpu.VMEM((rows, cols), F32)
+    slopes = pltpu.VMEM((2, rows, cols), F32)
+    (partial,) = lookup_call(own_kernel, "lookup_own", (values,), (tile, value), [])
+    partial, row_slopes = lookup_call(
+        row_kernel,
+        "lookup_x",
+        (values, slopes),
+        (tile, ahead_x, partial, behind_x),
+        [pltpu.VMEM((rows + 16, cols), F32)],
+    )
+    partial, col_slopes = lookup_call(
+        col_kernel, "lookup_y", (values, slopes), (tile, ahead_y, partial, behind_y), []
+    )
+    shape = jax.ShapeDtypeStruct((rows, cols), F32)
+    return lookup_call(
+        last_kernel,
+        "lookup_xy",
+        (shape, shape),
+        (tile, row_slopes, col_slopes, partial, behind_xy),
+        [pltpu.VMEM((rows, cols), F32)],
+    )
+
+
+def pack_kernel(owner, place, elevation, potential, flux, tile):
+    node_count = owner.shape[0] * owner.shape[1]
+    tile[0] = (owner[...] * node_count + place[...]).astype(F32)
+    tile[1] = elevation[...]
+    tile[2] = potential[...]
+    tile[3] = flux[...]
+
+
+def pack(owner, place, elevation, potential, flux):
     vmem = pl.BlockSpec(memory_space=pltpu.VMEM)
-    shape = jax.ShapeDtypeStruct((rows, cols), F32)
     return pl.pallas_call(
-        finish_kernel,
-        out_shape=(shape, shape),
-        in_specs=[vmem] * 7,
-        out_specs=(vmem, vmem),
-        scratch_shapes=[
-            pltpu.VMEM((3, 2 * rows * cols // WIDE, WIDE), BF16),
-            pltpu.VMEM((rows, cols), F32),
-            pltpu.VMEM((rows + 16, cols), F32),
-        ],
+        pack_kernel,
+        out_shape=pltpu.VMEM((4,) + owner.shape, F32),
+        in_specs=[vmem] * 5,
+        out_specs=vmem,
         compiler_params=pltpu.CompilerParams(vmem_limit_bytes=VMEM_LIMIT),
-        name="finish",
-        cost_estimate=pl.CostEstimate(
-            flops=3 * rows * cols * rows * cols, transcendentals=0, bytes_accessed=4 * 8 * rows * cols
-        ),
-    )(tile, ahead_x, ahead_y, pinned(partial), *[pinned(b) for b in behind])
+        name="pack",
+    )(owner, place, elevation, potential, flux)
 
 
 def shards(potential, elevation, normal_flux, box_owner, box_place, near_boxes):
@@ -587,8 +605,7 @@
     assert 4 * (cols // LANES) <= EXTRA - 8
     assert node_count * count_tx * count_ty < 2**24
 
-    slot = (box_owner * node_count + box_place).astype(F32)
-    tile = jnp.stack([slot, elevation, potential, normal_flux])
+    tile = pack(box_owner, box_place, elevation, potential, normal_flux)
     ahead_x = shifted(tile, "tx", -1)
     ahead_y = shifted(tile, "ty", -1)
     ahead_xy = shifted(ahead_y, "tx", -1)
@@ -605,8 +622,8 @@
     lower = lax.ppermute(boxed, both, [(i, i + 1) for i in range(total - 1)])
     upper = lax.ppermute(boxed, both, [(i + 1, i) for i in range(total - 1)])
 
-    sums, turned, ztop = near_own(plan, boxed, near)
-    value = near_other(plan, boxed, lower, upper, tile, sums, turned, ztop, near)
+    sums, turned = near_own(plan, boxed, near)
+    value = near_other(plan, boxed, lower, upper, tile, sums, turned, near)
 
     behind_x = shifted(value, "tx", 1)
     behind_y = shifted(value, "ty", 1)
@@ -616,8 +633,7 @@
         for j in range(count_ty)
     ]
     behind_xy = lax.ppermute(value, both, diagonal)
-    partial = gather_own(tile, value)
-    return finish(tile, ahead_x, ahead_y, partial, (behind_x, behind_y, behind_xy))
+    return look_up_all(tile, ahead_x, ahead_y, value, behind_x, behind_y, behind_xy)
 
 
 def solution(mesh):

time: 83.7 us -> 79.8 us (0.953)
  Pallas kernels: 54.2 us -> 49.7 us
  local copies, waits for them, and re-layouts: 0.69 us -> 4.87 us
  other arithmetic: 1.81 us -> 0 us
  waiting for transfers between devices: 7.22 us -> 5.63 us
    unnamed x2 -> x12, local copies, waits for them, and re-layouts: 0.69 us -> 4.87 us
    pallas_call x1, Pallas kernels: 16.7 us -> 14 us  [near_other(): pl.pallas_call(lambda *refs: near_other_kernel(near, *refs), out_shape=pl...]
    another operation x2 -> x0, other arithmetic: 1.81 us -> none  [shards(): tile = jnp.stack([slot, elevation, potential, normal_flux])]
    pallas_call x3 -> x6, Pallas kernels: 24.9 us -> 23.1 us  [the longest x1 15 us: near_own(): pl.pallas_call(lambda *refs: near_own_kernel(near, *refs), out_shape=(plt...]
    ppermute x5, waiting for transfers between devices: 6.42 us -> 4.99 us  [shifted(): return lax.ppermute(value, axis, pairs)]
  transfers between devices with their start and end apart: 8 -> 8, of which waited for: 3 -> 4; matrix products, arithmetic and copies ran while one was open for 0% -> 0% of each run, Pallas kernels for 31% -> 34%
where the time goes in v5:
time: 79.8 us; the launch traced here: 79.3 us
  Pallas kernels  49.7 us (62%)
  starting transfers between devices  18.4 us (23%)
  waiting for transfers between devices  5.63 us (7%)
  local copies, waits for them, and re-layouts  4.87 us (6%)
    pallas_call x1, Pallas kernels, near_own(): pl.pallas_call(lambda *refs: near_own_kernel(near, *refs), out_shape=(plt...  15 us
    pallas_call x1, Pallas kernels, near_other(): pl.pallas_call(lambda *refs: near_other_kernel(near, *refs), out_shape=pl...  14 us
    pallas_call x4, Pallas kernels, scatter(): pl.pallas_call(lambda *refs: scatter_kernel(first, last, (rows, cols, hig...  12.6 us
    ppermute x5, starting transfers between devices, shifted(): return lax.ppermute(value, axis, pairs)  11.6 us
    pallas_call x4, Pallas kernels, lookup_call(): pl.pallas_call(kernel, out_shape=out_shape, in_specs=[vmem] * len(args),...  8.1 us
    ppermute x5, waiting for transfers between devices, shifted(): return lax.ppermute(value, axis, pairs)  4.99 us
    unnamed x12, local copies, waits for them, and re-layouts  4.87 us
    ppermute x1, starting transfers between devices, shards(): lower = lax.ppermute(boxed, both, [(i, i + 1) for i in range(total - 1)])  4.57 us
  transfers between devices with their start and end apart: 8, of which 4 were waited for; matrix products, arithmetic and copies ran while one was open for 0% of the time, Pallas kernels for 34%

profile of v5, /device:TPU:0, one launch (start us, length us, event | category | flops | bytes accessed | tf_op | source)
XLA Modules:
  0.0 79.3 jit_solution(17156129579955183176)
XLA Ops:
  1.5 0.8 %copy-done.1 = s32[64,256]{1,0:T(8,128)S(1)} copy-done((s32[64,256]{1,0:T(8,128)S(1)}, s32[64,256]{1,0:T(8,128)}, u32[]{:S(2)}) %copy-start.1) | copy-done | bytes 65560
  2.3 0.8 %copy-done.2 = f32[64,256]{1,0:T(8,128)S(1)} copy-done((f32[64,256]{1,0:T(8,128)S(1)}, f32[64,256]{1,0:T(8,128)}, u32[]{:S(2)}) %copy-start.2) | copy-done | bytes 65560
  3.2 0.8 %copy-done.3 = f32[64,256]{1,0:T(8,128)S(1)} copy-done((f32[64,256]{1,0:T(8,128)S(1)}, f32[64,256]{1,0:T(8,128)}, u32[]{:S(2)}) %copy-start.3) | copy-done | bytes 65560
  4.0 0.8 %copy-done.4 = f32[64,256]{1,0:T(8,128)S(1)} copy-done((f32[64,256]{1,0:T(8,128)S(1)}, f32[64,256]{1,0:T(8,128)}, u32[]{:S(2)}) %copy-start.4) | copy-done | bytes 65560
  4.9 5.1 %collective-permute-start.1 = (f32[4,64,256]{2,1,0:T(8,128)S(1)}, f32[4,64,256]{2,1,0:T(8,128)S(1)}, u32[]{:S(2)}, u32[]{:S(2)}) collective-permute-start(f32[4,64,256]{2,1,0:T(8,128)S(1)} %pack.1.refs_0_.refs_4_.tile), channel_id=1, source_target_pairs={{0,3},{1,0},{2,1},{3,2},{4,7},{5,4},{6,5},{7,6},{8,11},{9,8},{10,9... | collective-permute-start | bytes 786440 | tf_op jit(solution)/shard_map/ppermute | solution.py:26
  10.0 1.6 %collective-permute-start = (f32[4,64,256]{2,1,0:T(8,128)S(1)}, f32[4,64,256]{2,1,0:T(8,128)S(1)}, u32[]{:S(2)}, u32[]{:S(2)}) collective-permute-start(f32[4,64,256]{2,1,0:T(8,128)S(1)} %pack.1.refs_0_.refs_4_.tile), channel_id=1, source_target_pairs={{0,28},{4,0},{8,4},{12,8},{16,12},{20,16},{24,20},{28,24},{1,29},{... | collective-permute-start | bytes 786440 | tf_op jit(solution)/shard_map/ppermute | solution.py:26
  12.3 1.6 %scatter_first.1 = (f32[384,256]{1,0:T(8,128)S(1)}, s32[16,128]{1,0:T(8,128)S(1)}) custom-call(f32[4,64,256]{2,1,0:T(8,128)S(1)} %pack.1.refs_0_.refs_4_.tile, s32[8,128]{1,0:T(8,128)S(1)} %bitcast.1), custom_call_target="tpu_custom_call" | custom-call | flops 1610612736 | bytes 1048576 | tf_op jit(solution)/shard_map/scatter_first/pallas_call | solution.py:143
  13.9 1.6 %collective-permute-done.1.refs_0_.ahead_y = f32[4,64,256]{2,1,0:T(8,128)S(1)} collective-permute-done((f32[4,64,256]{2,1,0:T(8,128)S(1)}, f32[4,64,256]{2,1,0:T(8,128)S(1)}, u32[]{:S(2)}, u32[]{:S(2)}) %collective-permute-start.1) | collective-permute-done | bytes 262176 | tf_op jit(solution)/shard_map/ppermute | solution.py:26
  15.6 1.0 %collective-permute-start.2 = (f32[4,64,256]{2,1,0:T(8,128)S(1)}, f32[4,64,256]{2,1,0:T(8,128)S(1)}, u32[]{:S(2)}, u32[]{:S(2)}) collective-permute-start(f32[4,64,256]{2,1,0:T(8,128)S(1)} %collective-permute-done.1.refs_0_.ahead_y), channel_id=1, source_target_pairs={{0,28},{4,0},{8,4},{12,8},{16,12},{20,16},{24,20},{28,24},{1,29},{... | collective-permute-start | bytes 786440 | tf_op jit(solution)/shard_map/ppermute | solution.py:26
  16.6 2.2 %scatter.2.refs_1_ = f32[384,256]{1,0:T(8,128)S(1)} custom-call(f32[4,64,256]{2,1,0:T(8,128)S(1)} %collective-permute-done.refs_0_.ahead_x, f32[384,256]{1,0:T(8,128)S(1)} %get-tuple-element.12.refs_1_), custom_call_target="tpu_custom_call" | custom-call | flops 1610612736 | bytes 1048576 | tf_op jit(solution)/shard_map/scatter/pallas_call | solution.py:143
  18.8 3.7 %scatter.3.refs_1_ = f32[384,256]{1,0:T(8,128)S(1)} custom-call(f32[4,64,256]{2,1,0:T(8,128)S(1)} %collective-permute-done.1.refs_0_.ahead_y, f32[384,256]{1,0:T(8,128)S(1)} %scatter.2.refs_1_), custom_call_target="tpu_custom_call" | custom-call | flops 1610612736 | bytes 1048576 | tf_op jit(solution)/shard_map/scatter/pallas_call | solution.py:143
  22.5 5.1 %scatter_last.1 = (f32[384,256]{1,0:T(8,128)}, f32[5,128,128]{2,1,0:T(8,128)S(1)}) custom-call(f32[4,64,256]{2,1,0:T(8,128)S(1)} %collective-permute-done.2.refs_0_, f32[384,256]{1,0:T(8,128)S(1)} %scatter.3.refs_1_), custom_call_target="tpu_custom_call" | custom-call | flops 1610612736 | bytes 1048576 | tf_op jit(solution)/shard_map/scatter_last/pallas_call | solution.py:143
  27.6 1.3 %collective-permute-start.4 = (f32[5,128,128]{2,1,0:T(8,128)S(1)}, f32[5,128,128]{2,1,0:T(8,128)S(1)}, u32[]{:S(2)}, u32[]{:S(2)}) collective-permute-start(f32[5,128,128]{2,1,0:T(8,128)S(1)} %get-tuple-element.13.refs_1_), channel_id=1, source_target_pairs={{1,0},{2,1},{3,2},{4,3},{5,4},{6,5},{7,6},{8,7},{9,8},{10,9},{11,1... | collective-permute-start | bytes 983048 | tf_op jit(solution)/shard_map/ppermute | solution.py:623
  28.8 4.6 %collective-permute-start.3 = (f32[5,128,128]{2,1,0:T(8,128)S(1)}, f32[5,128,128]{2,1,0:T(8,128)S(1)}, u32[]{:S(2)}, u32[]{:S(2)}) collective-permute-start(f32[5,128,128]{2,1,0:T(8,128)S(1)} %get-tuple-element.13.refs_1_), channel_id=1, source_target_pairs={{0,1},{1,2},{2,3},{3,4},{4,5},{5,6},{6,7},{7,8},{8,9},{9,10},{10,1... | collective-permute-start | bytes 983048 | tf_op jit(solution)/shard_map/ppermute | solution.py:622
  33.4 15.0 %near_own.1 = (f32[136,128]{1,0:T(8,128)S(1)}, bf16[129,128,32]{2,1,0:T(8,128)(2,1)S(1)}) custom-call(s32[16,128]{1,0:T(8,128)S(1)} %get-tuple-element.11.refs_0_, f32[5,128,128]{2,1,0:T(8,128)S(1)} %get-tuple-element.13.refs_1_), custom_call_target="tpu_custom_call" | custom-call | flops 2147483648 | bytes 1048576 | tf_op jit(solution)/shard_map/near_own/pallas_call | solution.py:393
  48.5 14.0 %near_other.1.table = f32[144,128]{1,0:T(8,128)S(1)} custom-call(s32[16,128]{1,0:T(8,128)S(1)} %get-tuple-element.11.refs_0_, f32[5,128,128]{2,1,0:T(8,128)S(1)} %get-tuple-element.13.refs_1_, f32[5,128,128]{2,1,0:T(8,128)S(1)} %collective-permute-done.3.refs_2_, f32[5,128,128]{2,1,0:T(8,128)S(1)} %collective-permute-done.4.refs_3_, ...), custom_call_target="tpu_custom_call" | custom-call | flops 2147483648 | bytes 1048576 | tf_op jit(solution)/shard_map/near_other/pallas_call | solution.py:412
  62.5 3.8 %collective-permute-start.5 = (f32[144,128]{1,0:T(8,128)S(1)}, f32[144,128]{1,0:T(8,128)S(1)}, u32[]{:S(2)}, u32[]{:S(2)}) collective-permute-start(f32[144,128]{1,0:T(8,128)S(1)} %near_other.1.table), channel_id=1, source_target_pairs={{0,4},{4,8},{8,12},{12,16},{16,20},{20,24},{24,28},{28,0},{1,5},{5... | collective-permute-start | bytes 221192 | tf_op jit(solution)/shard_map/ppermute | solution.py:26
  66.3 0.9 %collective-permute-start.7 = (f32[144,128]{1,0:T(8,128)S(1)}, f32[144,128]{1,0:T(8,128)S(1)}, u32[]{:S(2)}, u32[]{:S(2)}) collective-permute-start(f32[144,128]{1,0:T(8,128)S(1)} %near_other.1.table), channel_id=1, source_target_pairs={{0,5},{1,6},{2,7},{3,4},{4,9},{5,10},{6,11},{7,8},{8,13},{9,14},{1... | collective-permute-start | bytes 221192 | tf_op jit(solution)/shard_map/ppermute | solution.py:635
  67.2 1.2 %lookup_own.1.partial = f32[64,256]{1,0:T(8,128)S(1)} custom-call(f32[4,64,256]{2,1,0:T(8,128)S(1)} %pack.1.refs_0_.refs_4_.tile, f32[144,128]{1,0:T(8,128)S(1)} %near_other.1.table), custom_call_target="tpu_custom_call" | custom-call | flops 268435456 | bytes 524288 | tf_op jit(solution)/shard_map/lookup_own/pallas_call | solution.py:538
  68.4 1.7 %collective-permute-done.5.behind_x = f32[144,128]{1,0:T(8,128)S(1)} collective-permute-done((f32[144,128]{1,0:T(8,128)S(1)}, f32[144,128]{1,0:T(8,128)S(1)}, u32[]{:S(2)}, u32[]{:S(2)}) %collective-permute-start.5) | collective-permute-done | bytes 73760 | tf_op jit(solution)/shard_map/ppermute | solution.py:26
  70.1 1.5 %lookup_x.1 = (f32[64,256]{1,0:T(8,128)S(1)}, f32[2,64,256]{2,1,0:T(8,128)S(1)}) custom-call(f32[4,64,256]{2,1,0:T(8,128)S(1)} %pack.1.refs_0_.refs_4_.tile, f32[4,64,256]{2,1,0:T(8,128)S(1)} %collective-permute-done.refs_0_.ahead_x, f32[64,256]{1,0:T(8,128)S(1)} %lookup_own.1.partial, f32[144,128]{1,0:T(8,128)S(1)} %collective-permute-done.5.behind_x), custom_call_target="tpu_custom_call" | custom-call | flops 268435456 | bytes 524288 | tf_op jit(solution)/shard_map/lookup_x/pallas_call | solution.py:538
  71.7 1.6 %collective-permute-done.6.behind_y = f32[144,128]{1,0:T(8,128)S(1)} collective-permute-done((f32[144,128]{1,0:T(8,128)S(1)}, f32[144,128]{1,0:T(8,128)S(1)}, u32[]{:S(2)}, u32[]{:S(2)}) %collective-permute-start.6) | collective-permute-done | bytes 73760 | tf_op jit(solution)/shard_map/ppermute | solution.py:26
  73.3 2.1 %lookup_y.1 = (f32[64,256]{1,0:T(8,128)S(1)}, f32[2,64,256]{2,1,0:T(8,128)S(1)}) custom-call(f32[4,64,256]{2,1,0:T(8,128)S(1)} %pack.1.refs_0_.refs_4_.tile, f32[4,64,256]{2,1,0:T(8,128)S(1)} %collective-permute-done.1.refs_0_.ahead_y, f32[64,256]{1,0:T(8,128)S(1)} %get-tuple-element.17.partial, f32[144,128]{1,0:T(8,128)S(1)} %collective-permute-done.6.behind_y), custom_call_target="tpu_custom_call" | custom-call | flops 268435456 | bytes 524288 | tf_op jit(solution)/shard_map/lookup_y/pallas_call | solution.py:538
  76.0 3.4 %lookup_xy.1 = (f32[64,256]{1,0:T(8,128)}, f32[64,256]{1,0:T(8,128)}) custom-call(f32[4,64,256]{2,1,0:T(8,128)S(1)} %pack.1.refs_0_.refs_4_.tile, f32[2,64,256]{2,1,0:T(8,128)S(1)} %get-tuple-element.16.row_slopes, f32[2,64,256]{2,1,0:T(8,128)S(1)} %get-tuple-element.18.col_slopes, f32[64,256]{1,0:T(8,128)S(1)} %get-tuple-element.19.partial, ...), custom_call_target="tpu_custom_call" | custom-call | flops 268435456 | bytes 524288 | tf_op jit(solution)/shard_map/lookup_xy/pallas_call | solution.py:538
  (15 shorter events, 2.2 us)
Async XLA Ops:
  0.6 0.8 %copy-start = (s32[64,256]{1,0:T(8,128)S(1)}, s32[64,256]{1,0:T(8,128)}, u32[]{:S(2)}) copy-start(s32[64,256]{1,0:T(8,128)} %owner.1) | copy-start | bytes 196612
  1.5 0.8 %copy-start.1 = (s32[64,256]{1,0:T(8,128)S(1)}, s32[64,256]{1,0:T(8,128)}, u32[]{:S(2)}) copy-start(s32[64,256]{1,0:T(8,128)} %place.1) | copy-start | bytes 196612
  2.3 0.8 %copy-start.2 = (f32[64,256]{1,0:T(8,128)S(1)}, f32[64,256]{1,0:T(8,128)}, u32[]{:S(2)}) copy-start(f32[64,256]{1,0:T(8,128)} %elevation.1) | copy-start | bytes 196612
  3.2 0.8 %copy-start.3 = (f32[64,256]{1,0:T(8,128)S(1)}, f32[64,256]{1,0:T(8,128)}, u32[]{:S(2)}) copy-start(f32[64,256]{1,0:T(8,128)} %potential.1) | copy-start | bytes 196612
  4.0 0.8 %copy-start.4 = (f32[64,256]{1,0:T(8,128)S(1)}, f32[64,256]{1,0:T(8,128)}, u32[]{:S(2)}) copy-start(f32[64,256]{1,0:T(8,128)} %flux.1) | copy-start | bytes 196612
  4.9 10.7 %collective-permute-start.1 = (f32[4,64,256]{2,1,0:T(8,128)S(1)}, f32[4,64,256]{2,1,0:T(8,128)S(1)}, u32[]{:S(2)}, u32[]{:S(2)}) collective-permute-start(f32[4,64,256]{2,1,0:T(8,128)S(1)} %pack.1.refs_0_.refs_4_.tile), channel_id=1, source_target_pairs={{0,3},{1,0},{2,1},{3,2},{4,7},{5,4},{6,5},{7,6},{8,11},{9,8},{10,9... | collective-permute-start | bytes 786440 | tf_op jit(solution)/shard_map/ppermute | solution.py:26
  10.0 6.6 %collective-permute-start = (f32[4,64,256]{2,1,0:T(8,128)S(1)}, f32[4,64,256]{2,1,0:T(8,128)S(1)}, u32[]{:S(2)}, u32[]{:S(2)}) collective-permute-start(f32[4,64,256]{2,1,0:T(8,128)S(1)} %pack.1.refs_0_.refs_4_.tile), channel_id=1, source_target_pairs={{0,28},{4,0},{8,4},{12,8},{16,12},{20,16},{24,20},{28,24},{1,29},{... | collective-permute-start | bytes 786440 | tf_op jit(solution)/shard_map/ppermute | solution.py:26
  11.6 0.7 copy-start.5
  15.6 6.9 %collective-permute-start.2 = (f32[4,64,256]{2,1,0:T(8,128)S(1)}, f32[4,64,256]{2,1,0:T(8,128)S(1)}, u32[]{:S(2)}, u32[]{:S(2)}) collective-permute-start(f32[4,64,256]{2,1,0:T(8,128)S(1)} %collective-permute-done.1.refs_0_.ahead_y), channel_id=1, source_target_pairs={{0,28},{4,0},{8,4},{12,8},{16,12},{20,16},{24,20},{28,24},{1,29},{... | collective-permute-start | bytes 786440 | tf_op jit(solution)/shard_map/ppermute | solution.py:26
  27.6 20.9 %collective-permute-start.4 = (f32[5,128,128]{2,1,0:T(8,128)S(1)}, f32[5,128,128]{2,1,0:T(8,128)S(1)}, u32[]{:S(2)}, u32[]{:S(2)}) collective-permute-start(f32[5,128,128]{2,1,0:T(8,128)S(1)} %get-tuple-element.13.refs_1_), channel_id=1, source_target_pairs={{1,0},{2,1},{3,2},{4,3},{5,4},{6,5},{7,6},{8,7},{9,8},{10,9},{11,1... | collective-permute-start | bytes 983048 | tf_op jit(solution)/shard_map/ppermute | solution.py:623
  28.8 19.6 %collective-permute-start.3 = (f32[5,128,128]{2,1,0:T(8,128)S(1)}, f32[5,128,128]{2,1,0:T(8,128)S(1)}, u32[]{:S(2)}, u32[]{:S(2)}) collective-permute-start(f32[5,128,128]{2,1,0:T(8,128)S(1)} %get-tuple-element.13.refs_1_), channel_id=1, source_target_pairs={{0,1},{1,2},{2,3},{3,4},{4,5},{5,6},{6,7},{7,8},{8,9},{9,10},{10,1... | collective-permute-start | bytes 983048 | tf_op jit(solution)/shard_map/ppermute | solution.py:622
  62.5 7.6 %collective-permute-start.5 = (f32[144,128]{1,0:T(8,128)S(1)}, f32[144,128]{1,0:T(8,128)S(1)}, u32[]{:S(2)}, u32[]{:S(2)}) collective-permute-start(f32[144,128]{1,0:T(8,128)S(1)} %near_other.1.table), channel_id=1, source_target_pairs={{0,4},{4,8},{8,12},{12,16},{16,20},{20,24},{24,28},{28,0},{1,5},{5... | collective-permute-start | bytes 221192 | tf_op jit(solution)/shard_map/ppermute | solution.py:26
  66.3 7.0 %collective-permute-start.6 = (f32[144,128]{1,0:T(8,128)S(1)}, f32[144,128]{1,0:T(8,128)S(1)}, u32[]{:S(2)}, u32[]{:S(2)}) collective-permute-start(f32[144,128]{1,0:T(8,128)S(1)} %near_other.1.table), channel_id=1, source_target_pairs={{0,1},{1,2},{2,3},{3,0},{4,5},{5,6},{6,7},{7,4},{8,9},{9,10},{10,1... | collective-permute-start | bytes 221192 | tf_op jit(solution)/shard_map/ppermute | solution.py:26
  66.3 9.6 %collective-permute-start.7 = (f32[144,128]{1,0:T(8,128)S(1)}, f32[144,128]{1,0:T(8,128)S(1)}, u32[]{:S(2)}, u32[]{:S(2)}) collective-permute-start(f32[144,128]{1,0:T(8,128)S(1)} %near_other.1.table), channel_id=1, source_target_pairs={{0,5},{1,6},{2,7},{3,4},{4,9},{5,10},{6,11},{7,8},{8,13},{9,14},{1... | collective-permute-start | bytes 221192 | tf_op jit(solution)/shard_map/ppermute | solution.py:635

commit v6 on v5

--- a/solution.py
+++ b/solution.py
@@ -48,9 +48,19 @@
     return high, jnp.where(second, low + LANES, low)
 
 
+def list_active(test, count, active):
+    flags = [jnp.max(jnp.where(test(unit), 1.0, 0.0)) > 0.0 for unit in range(count)]
+    found = jnp.int32(0)
+    for unit, flag in enumerate(flags):
+        active[found] = unit
+        found = found + jnp.where(flag, 1, 0)
+    return found
+
+
 def scatter_kernel(first, last, sizes, steps, tile, *refs):
+    active = refs[-1]
     if first:
-        listed, acc, plan = refs
+        listed, acc, plan = refs[:3]
         plan_rows(listed, plan)
     else:
         acc_in, acc = refs[:2]
@@ -61,54 +71,56 @@
     off_i = float(steps[0] * rows)
     off_j = float((steps[1] - 1) * cols)
     acc[...] = jnp.zeros(acc.shape, F32) if first else acc_in[...]
-    units = [(r, c) for r in range(rows // 8) for c in range(cols // LANES)]
-
-    def split(r, c):
-        return box_split(tile[0, 8 * r : 8 * r + 8, LANES * c : LANES * c + LANES] - base, high_count)
-
-    flags = []
-    for r, c in units:
-        high, _ = split(r, c)
-        mine = (high >= 0.0) & (high < high_count)
-        flags.append(jnp.max(jnp.where(mine, 1.0, 0.0)) > 0.0)
-
-    for (r, c), flag in zip(units, flags):
-
-        @pl.when(flag)
-        def _():
-            high, low = split(r, c)
-            window = (slice(8 * r, 8 * r + 8), slice(LANES * c, LANES * c + LANES))
-            z = 0.25 * tile[(1,) + window]
-            z_high = rounded(z)
-            z_low = z - z_high
-            pot = tile[(2,) + window]
-            flux = tile[(3,) + window]
-            col_index = (lax.broadcasted_iota(jnp.int32, (high_count, LANES), 1) + LANES * c).astype(F32) + off_j
-            high_iota = lax.broadcasted_iota(jnp.int32, (high_count, LANES), 0).astype(F32)
-            low_iota = lax.broadcasted_iota(jnp.int32, (WIDE, LANES), 0).astype(F32)
-            lefts = []
-            rights = []
-            for s in range(8):
-
-                def row(v):
-                    return v[s : s + 1, :]
-
-                hit = high_iota == row(high)
-                row_index = jnp.full((1, LANES), 8 * r + s, F32) + off_i
-                values = [row_index, col_index, row(z_high), row(z_low), row(pot), row(flux)]
-                lefts.append(
-                    jnp.concatenate([jnp.where(hit, v, 0.0).astype(BF16) for v in values], axis=0)
-                )
-                rights.append(jnp.where(low_iota == row(low), 1.0, 0.0).astype(BF16))
-            acc[...] += lax.dot_general(
-                jnp.concatenate(lefts, axis=1),
-                jnp.concatenate(rights, axis=1),
-                (((1,), (1,)), ((), ())),
-                preferred_element_type=F32,
+    across = cols // LANES
+
+    def window_of(unit):
+        row, col = unit // across * 8, unit % across * LANES
+        if not isinstance(unit, int):
+            row, col = pl.multiple_of(row, 8), pl.multiple_of(col, LANES)
+        return row, col, (pl.ds(row, 8), pl.ds(col, LANES))
+
+    def mine(unit):
+        high, _ = box_split(tile[(0,) + window_of(unit)[2]] - base, high_count)
+        return (high >= 0.0) & (high < high_count)
+
+    def add(i, carry):
+        row0, col0, window = window_of(active[i])
+        high, low = box_split(tile[(0,) + window] - base, high_count)
+        z = 0.25 * tile[(1,) + window]
+        z_high = rounded(z)
+        z_low = z - z_high
+        pot = tile[(2,) + window]
+        flux = tile[(3,) + window]
+        shift = col0.astype(F32) + off_j
+        col_index = lax.broadcasted_iota(jnp.int32, (high_count, LANES), 1).astype(F32) + shift
+        high_iota = lax.broadcasted_iota(jnp.int32, (high_count, LANES), 0).astype(F32)
+        low_iota = lax.broadcasted_iota(jnp.int32, (WIDE, LANES), 0).astype(F32)
+        lefts = []
+        rights = []
+        for s in range(8):
+
+            def row(v):
+                return v[s : s + 1, :]
+
+            hit = high_iota == row(high)
+            row_index = jnp.full((1, LANES), (row0 + s).astype(F32) + off_i, F32)
+            values = [row_index, col_index, row(z_high), row(z_low), row(pot), row(flux)]
+            lefts.append(
+                jnp.concatenate([jnp.where(hit, v, 0.0).astype(BF16) for v in values], axis=0)
             )
+            rights.append(jnp.where(low_iota == row(low), 1.0, 0.0).astype(BF16))
+        acc[...] += lax.dot_general(
+            jnp.concatenate(lefts, axis=1),
+            jnp.concatenate(rights, axis=1),
+            (((1,), (1,)), ((), ())),
+            preferred_element_type=F32,
+        )
+        return carry
+
+    lax.fori_loop(0, list_active(mine, rows // 8 * across, active), add, 0)
 
     if last:
-        boxed = refs[-1]
+        boxed = refs[-2]
         h = high_count
         row0 = (p * rows).astype(F32)
         col0 = ((q + 1) * cols).astype(F32)
@@ -147,6 +159,7 @@
         out_shape=out_shape,
         in_specs=[vmem] * len(args),
         out_specs=[vmem] * len(out_shape),
+        scratch_shapes=[pltpu.SMEM((rows * cols // (8 * LANES),), jnp.int32)],
         compiler_params=pltpu.CompilerParams(vmem_limit_bytes=VMEM_LIMIT),
         name="scatter_last" if last else "scatter_first" if first else "scatter",
         cost_estimate=pl.CostEstimate(
@@ -199,7 +212,7 @@
 
 
 def pieces_of(ref, group):
-    window = (slice(8 * group, 8 * group + 8), slice(None))
+    window = (pl.ds(pl.multiple_of(8 * group, 8), 8), slice(None))
     x, y, z, pot, flux = (ref[(f,) + window] for f in range(5))
     pieces = []
     total = None
@@ -233,9 +246,10 @@
     pitch = sfeat.shape[0] // STORED
     ones = jnp.ones((8, LANES), F32)
     zeros = jnp.zeros((8, LANES), F32)
-    start = 0
-    for ref in refs:
-        for group in range(ref.shape[1] // 8):
+    boxes = refs[0].shape[1]
+    for which, ref in enumerate(refs):
+
+        def store(group, carry):
             pieces, total, pot, flux = pieces_of(ref, group)
             source = []
             for high, low in pieces:
@@ -243,10 +257,14 @@
             z = pieces[2][0] + pieces[2][1]
             rows = padded_rows(source + list(thirds(total)) + [ones, ones, ones])
             rows += [pot, zeros, pot, zeros] + list(thirds(-pot * z)) + [zeros]
+            start = pl.multiple_of(which * boxes + 8 * group, 8)
             for k, v in enumerate(rows):
-                sfeat[k * pitch + start : k * pitch + start + 8, :] = v
-            sflux[start : start + 8, :] = flux
-            start += 8
+                sfeat[pl.ds(pl.multiple_of(k * pitch + start, 8), 8), :] = v
+            sflux[pl.ds(start, 8), :] = flux
+            return carry
+
+        lax.fori_loop(0, boxes // 8, store, 0, unroll=2)
+    start = len(refs) * boxes
     for k in range(STORED):
         sfeat[k * pitch + start : k * pitch + start + 8, :] = ones if k == 12 else zeros
     sflux[start : start + 8, :] = zeros
@@ -256,13 +274,17 @@
     boxes = own.shape[1]
     pitch = tfeat.shape[0] // USED
     ones = jnp.ones((8, LANES), F32)
-    for group in range(boxes // 8):
+
+    def store(group, carry):
         pieces, total, _, _ = pieces_of(own, group)
         target = []
         for high, low in pieces:
             target += [high, high, low, low]
         for k, v in enumerate(padded_rows(target + [ones, ones, ones] + list(thirds(total + 0.04)))):
-            tfeat[k * pitch + 8 * group : k * pitch + 8 * group + 8, :] = v
+            tfeat[pl.ds(pl.multiple_of(k * pitch + 8 * group, 8), 8), :] = v
+        return carry
+
+    lax.fori_loop(0, boxes // 8, store, 0, unroll=2)
     turned[boxes] = jnp.zeros((LANES, FEATURES), BF16)
 
     def turn(i, carry):
@@ -421,47 +443,45 @@
     )(plan, *map(pinned, (own, lower, upper, tile, sums, turned)))
 
 
-def lookup(slot, bases, tables, pieces, out):
+def lookup(slot, base, table, pieces, active, out):
     rows, cols = slot.shape
     high_count = rows * cols // WIDE
-    units = [(r, c) for r in range(rows // 8) for c in range(cols // LANES)]
-    for which, table in enumerate(tables):
-        whole = jnp.concatenate([table[0:high_count, :], table[high_count : 2 * high_count, :]], axis=1)
-        top = rounded(whole)
-        pieces[which, 0:high_count, :] = top.astype(BF16)
-        pieces[which, high_count : 2 * high_count, :] = (whole - top).astype(BF16)
-
-    def split(r, c, which):
-        window = (slice(8 * r, 8 * r + 8), slice(LANES * c, LANES * c + LANES))
-        return box_split(slot[window] - bases[which], high_count)
-
-    flags = {}
-    for r, c in units:
-        for which in range(len(tables)):
-            high, _ = split(r, c, which)
-            there = (high >= 0.0) & (high < high_count)
-            flags[r, c, which] = jnp.max(jnp.where(there, 1.0, 0.0)) > 0.0
-
-    for r, c in units:
-        for which in range(len(tables)):
-
-            @pl.when(flags[r, c, which])
-            def _():
-                high, low = split(r, c, which)
-                low_iota = lax.broadcasted_iota(jnp.int32, (WIDE, LANES), 0).astype(F32)
-                high_iota = lax.broadcasted_iota(jnp.int32, (high_count, LANES), 0).astype(F32)
-                hits = jnp.concatenate(
-                    [jnp.where(low_iota == low[s : s + 1, :], 1.0, 0.0).astype(BF16) for s in range(8)],
-                    axis=1,
-                )
-                picked = jnp.dot(pieces[which], hits, preferred_element_type=F32)
-                lines = []
-                for s in range(8):
-                    window = slice(LANES * s, LANES * s + LANES)
-                    both = picked[0:high_count, window] + picked[high_count : 2 * high_count, window]
-                    mine = high_iota == high[s : s + 1, :]
-                    lines.append(jnp.sum(jnp.where(mine, both, 0.0), axis=0, keepdims=True))
-                out[8 * r : 8 * r + 8, LANES * c : LANES * c + LANES] += jnp.concatenate(lines, axis=0)
+    across = cols // LANES
+    whole = jnp.concatenate([table[0:high_count, :], table[high_count : 2 * high_count, :]], axis=1)
+    top = rounded(whole)
+    pieces[0:high_count, :] = top.astype(BF16)
+    pieces[high_count : 2 * high_count, :] = (whole - top).astype(BF16)
+
+    def window_of(unit):
+        row, col = unit // across * 8, unit % across * LANES
+        if not isinstance(unit, int):
+            row, col = pl.multiple_of(row, 8), pl.multiple_of(col, LANES)
+        return pl.ds(row, 8), pl.ds(col, LANES)
+
+    def there(unit):
+        high, _ = box_split(slot[window_of(unit)] - base, high_count)
+        return (high >= 0.0) & (high < high_count)
+
+    def add(i, carry):
+        window = window_of(active[i])
+        high, low = box_split(slot[window] - base, high_count)
+        low_iota = lax.broadcasted_iota(jnp.int32, (WIDE, LANES), 0).astype(F32)
+        high_iota = lax.broadcasted_iota(jnp.int32, (high_count, LANES), 0).astype(F32)
+        hits = jnp.concatenate(
+            [jnp.where(low_iota == low[s : s + 1, :], 1.0, 0.0).astype(BF16) for s in range(8)],
+            axis=1,
+        )
+        picked = jnp.dot(pieces[...], hits, preferred_element_type=F32)
+        lines = []
+        for s in range(8):
+            part = slice(LANES * s, LANES * s + LANES)
+            both = picked[0:high_count, part] + picked[high_count : 2 * high_count, part]
+            mine = high_iota == high[s : s + 1, :]
+            lines.append(jnp.sum(jnp.where(mine, both, 0.0), axis=0, keepdims=True))
+        out[window] += jnp.concatenate(lines, axis=0)
+        return carry
+
+    lax.fori_loop(0, list_active(there, rows // 8 * across, active), add, 0)
 
 
 def base_of(node_count, steps):
@@ -469,16 +489,16 @@
     return (rank * node_count).astype(F32)
 
 
-def own_kernel(tile, table, out, pieces):
+def own_kernel(tile, table, out, pieces, active):
     out[...] = jnp.zeros(out.shape, F32)
-    lookup(tile.at[0], [base_of(out.shape[0] * out.shape[1], (0, 0))], [table], pieces, out)
-
-
-def row_kernel(tile, ahead_x, partial, behind_x, out, slopes, pieces, padded):
+    lookup(tile.at[0], base_of(out.shape[0] * out.shape[1], (0, 0)), table, pieces, active, out)
+
+
+def row_kernel(tile, ahead_x, partial, behind_x, out, slopes, pieces, active, padded):
     _, rows, cols = tile.shape
     boxes = rows * cols // LANES
     out[...] = partial[...]
-    lookup(tile.at[0], [base_of(rows * cols, (1, 0))], [behind_x], pieces, out)
+    lookup(tile.at[0], base_of(rows * cols, (1, 0)), behind_x, pieces, active, out)
     for f in (1, 2):
         padded[8 : 8 + rows, :] = tile[f]
         for r in range(2):
@@ -494,11 +514,11 @@
         ) / 12.0
 
 
-def col_kernel(tile, ahead_y, partial, behind_y, out, slopes, pieces):
+def col_kernel(tile, ahead_y, partial, behind_y, out, slopes, pieces, active):
     _, rows, cols = tile.shape
     boxes = rows * cols // LANES
     out[...] = partial[...]
-    lookup(tile.at[0], [base_of(rows * cols, (0, 1))], [behind_y], pieces, out)
+    lookup(tile.at[0], base_of(rows * cols, (0, 1)), behind_y, pieces, active, out)
     left_cols = behind_y[boxes + EXTRA - 8 : boxes + EXTRA, 0:rows].T
     col = lax.broadcasted_iota(jnp.int32, (rows, cols), 1)
     for f in (1, 2):
@@ -518,10 +538,10 @@
         slopes[f - 1] = (less_2 - 8.0 * less_1 + 8.0 * more_1 - more_2) / 12.0
 
 
-def last_kernel(tile, row_slopes, col_slopes, partial, behind_xy, elev_rate, pot_rate, pieces, total):
+def last_kernel(tile, row_slopes, col_slopes, partial, behind_xy, elev_rate, pot_rate, pieces, active, total):
     _, rows, cols = tile.shape
     total[...] = partial[...]
-    lookup(tile.at[0], [base_of(rows * cols, (1, 1))], [behind_xy], pieces, total)
+    lookup(tile.at[0], base_of(rows * cols, (1, 1)), behind_xy, pieces, active, total)
     elev_x, pot_x = row_slopes[0], row_slopes[1]
     elev_y, pot_y = col_slopes[0], col_slopes[1]
     vertical = total[...]
@@ -540,7 +560,11 @@
         out_shape=out_shape,
         in_specs=[vmem] * len(args),
         out_specs=(vmem,) * len(out_shape),
-        scratch_shapes=[pltpu.VMEM((1, 2 * rows * cols // WIDE, WIDE), BF16)] + scratch,
+        scratch_shapes=[
+            pltpu.VMEM((2 * rows * cols // WIDE, WIDE), BF16),
+            pltpu.SMEM((rows * cols // (8 * LANES),), jnp.int32),
+        ]
+        + scratch,
         compiler_params=pltpu.CompilerParams(vmem_limit_bytes=VMEM_LIMIT),
         name=name,
         cost_estimate=pl.CostEstimate(
@@ -574,21 +598,36 @@
     )
 
 
-def pack_kernel(owner, place, elevation, potential, flux, tile):
+def pack_kernel(owner, place, elevation, potential, flux, tile, owner_here, place_here, arrived):
+    copies = [
+        pltpu.make_async_copy(source, target, arrived.at[i])
+        for i, (source, target) in enumerate(
+            (
+                (owner, owner_here),
+                (place, place_here),
+                (elevation, tile.at[1]),
+                (potential, tile.at[2]),
+                (flux, tile.at[3]),
+            )
+        )
+    ]
+    for copy in copies:
+        copy.start()
+    copies[0].wait()
+    copies[1].wait()
     node_count = owner.shape[0] * owner.shape[1]
-    tile[0] = (owner[...] * node_count + place[...]).astype(F32)
-    tile[1] = elevation[...]
-    tile[2] = potential[...]
-    tile[3] = flux[...]
+    tile[0] = (owner_here[...] * node_count + place_here[...]).astype(F32)
+    for copy in copies[2:]:
+        copy.wait()
 
 
 def pack(owner, place, elevation, potential, flux):
-    vmem = pl.BlockSpec(memory_space=pltpu.VMEM)
     return pl.pallas_call(
         pack_kernel,
         out_shape=pltpu.VMEM((4,) + owner.shape, F32),
-        in_specs=[vmem] * 5,
-        out_specs=vmem,
+        in_specs=[pl.BlockSpec(memory_space=pltpu.HBM)] * 5,
+        out_specs=pl.BlockSpec(memory_space=pltpu.VMEM),
+        scratch_shapes=[pltpu.VMEM(owner.shape, jnp.int32)] * 2 + [pltpu.SemaphoreType.DMA((5,))],
         compiler_params=pltpu.CompilerParams(vmem_limit_bytes=VMEM_LIMIT),
         name="pack",
     )(owner, place, elevation, potential, flux)

time: 79.8 us -> 80.9 us (1.014)
  Pallas kernels: 49.7 us -> 51.1 us
    ppermute x5, waiting for transfers between devices: 4.99 us -> 5.84 us  [shifted(): return lax.ppermute(value, axis, pairs)]
  transfers between devices with their start and end apart: 8 -> 8, of which waited for: 4 -> 3; matrix products, arithmetic and copies ran while one was open for 0% -> 0% of each run, Pallas kernels for 34% -> 34%
where the time goes in v6:
time: 80.9 us; the launch traced here: 80.2 us
  Pallas kernels  51.1 us (63%)
  starting transfers between devices  17.6 us (22%)
  waiting for transfers between devices  5.85 us (7%)
  local copies, waits for them, and re-layouts  4.87 us (6%)
    pallas_call x1, Pallas kernels, near_own(): pl.pallas_call(lambda *refs: near_own_kernel(near, *refs), out_shape=(plt...  15.1 us
    pallas_call x1, Pallas kernels, near_other(): pl.pallas_call(lambda *refs: near_other_kernel(near, *refs), out_shape=pl...  14.8 us
    pallas_call x4, Pallas kernels, scatter(): pl.pallas_call(lambda *refs: scatter_kernel(first, last, (rows, cols, hig...  12.6 us
    ppermute x5, starting transfers between devices, shifted(): return lax.ppermute(value, axis, pairs)  11.6 us
    pallas_call x4, Pallas kernels, lookup_call(): pl.pallas_call(kernel, out_shape=out_shape, in_specs=[vmem] * len(args),...  8.11 us
    ppermute x5, waiting for transfers between devices, shifted(): return lax.ppermute(value, axis, pairs)  5.84 us
    unnamed x12, local copies, waits for them, and re-layouts  4.87 us
    ppermute x1, starting transfers between devices, shards(): lower = lax.ppermute(boxed, both, [(i, i + 1) for i in range(total - 1)])  4.57 us
  transfers between devices with their start and end apart: 8, of which 3 were waited for; matrix products, arithmetic and copies ran while one was open for 0% of the time, Pallas kernels for 34%

profile of v6, /device:TPU:0, one launch (start us, length us, event | category | flops | bytes accessed | tf_op | source)
XLA Modules:
  0.0 80.2 jit_solution(2790308531083718220)
XLA Ops:
  0.6 0.8 %copy-done = s32[64,256]{1,0:T(8,128)S(1)} copy-done((s32[64,256]{1,0:T(8,128)S(1)}, s32[64,256]{1,0:T(8,128)}, u32[]{:S(2)}) %copy-start) | copy-done | bytes 65560
  1.5 0.8 %copy-done.1 = s32[64,256]{1,0:T(8,128)S(1)} copy-done((s32[64,256]{1,0:T(8,128)S(1)}, s32[64,256]{1,0:T(8,128)}, u32[]{:S(2)}) %copy-start.1) | copy-done | bytes 65560
  2.3 0.8 %copy-done.2 = f32[64,256]{1,0:T(8,128)S(1)} copy-done((f32[64,256]{1,0:T(8,128)S(1)}, f32[64,256]{1,0:T(8,128)}, u32[]{:S(2)}) %copy-start.2) | copy-done | bytes 65560
  3.2 0.8 %copy-done.3 = f32[64,256]{1,0:T(8,128)S(1)} copy-done((f32[64,256]{1,0:T(8,128)S(1)}, f32[64,256]{1,0:T(8,128)}, u32[]{:S(2)}) %copy-start.3) | copy-done | bytes 65560
  4.0 0.8 %copy-done.4 = f32[64,256]{1,0:T(8,128)S(1)} copy-done((f32[64,256]{1,0:T(8,128)S(1)}, f32[64,256]{1,0:T(8,128)}, u32[]{:S(2)}) %copy-start.4) | copy-done | bytes 65560
  5.3 5.1 %collective-permute-start.1 = (f32[4,64,256]{2,1,0:T(8,128)S(1)}, f32[4,64,256]{2,1,0:T(8,128)S(1)}, u32[]{:S(2)}, u32[]{:S(2)}) collective-permute-start(f32[4,64,256]{2,1,0:T(8,128)S(1)} %pack.1.refs_0_.refs_4_.tile), channel_id=1, source_target_pairs={{0,3},{1,0},{2,1},{3,2},{4,7},{5,4},{6,5},{7,6},{8,11},{9,8},{10,9... | collective-permute-start | bytes 786440 | tf_op jit(solution)/shard_map/ppermute | solution.py:26
  10.4 1.6 %collective-permute-start = (f32[4,64,256]{2,1,0:T(8,128)S(1)}, f32[4,64,256]{2,1,0:T(8,128)S(1)}, u32[]{:S(2)}, u32[]{:S(2)}) collective-permute-start(f32[4,64,256]{2,1,0:T(8,128)S(1)} %pack.1.refs_0_.refs_4_.tile), channel_id=1, source_target_pairs={{0,28},{4,0},{8,4},{12,8},{16,12},{20,16},{24,20},{28,24},{1,29},{... | collective-permute-start | bytes 786440 | tf_op jit(solution)/shard_map/ppermute | solution.py:26
  12.7 1.6 %scatter_first.1 = (f32[384,256]{1,0:T(8,128)S(1)}, s32[16,128]{1,0:T(8,128)S(1)}) custom-call(f32[4,64,256]{2,1,0:T(8,128)S(1)} %pack.1.refs_0_.refs_4_.tile, s32[8,128]{1,0:T(8,128)S(1)} %bitcast.1), custom_call_target="tpu_custom_call" | custom-call | flops 1610612736 | bytes 1048576 | tf_op jit(solution)/shard_map/scatter_first/pallas_call | solution.py:155
  14.4 1.6 %collective-permute-done.1.refs_0_.ahead_y = f32[4,64,256]{2,1,0:T(8,128)S(1)} collective-permute-done((f32[4,64,256]{2,1,0:T(8,128)S(1)}, f32[4,64,256]{2,1,0:T(8,128)S(1)}, u32[]{:S(2)}, u32[]{:S(2)}) %collective-permute-start.1) | collective-permute-done | bytes 262176 | tf_op jit(solution)/shard_map/ppermute | solution.py:26
  16.0 1.0 %collective-permute-start.2 = (f32[4,64,256]{2,1,0:T(8,128)S(1)}, f32[4,64,256]{2,1,0:T(8,128)S(1)}, u32[]{:S(2)}, u32[]{:S(2)}) collective-permute-start(f32[4,64,256]{2,1,0:T(8,128)S(1)} %collective-permute-done.1.refs_0_.ahead_y), channel_id=1, source_target_pairs={{0,28},{4,0},{8,4},{12,8},{16,12},{20,16},{24,20},{28,24},{1,29},{... | collective-permute-start | bytes 786440 | tf_op jit(solution)/shard_map/ppermute | solution.py:26
  17.0 2.3 %scatter.2.refs_1_ = f32[384,256]{1,0:T(8,128)S(1)} custom-call(f32[4,64,256]{2,1,0:T(8,128)S(1)} %collective-permute-done.refs_0_.ahead_x, f32[384,256]{1,0:T(8,128)S(1)} %get-tuple-element.12.refs_1_), custom_call_target="tpu_custom_call" | custom-call | flops 1610612736 | bytes 1048576 | tf_op jit(solution)/shard_map/scatter/pallas_call | solution.py:155
  19.3 3.6 %scatter.3.refs_1_ = f32[384,256]{1,0:T(8,128)S(1)} custom-call(f32[4,64,256]{2,1,0:T(8,128)S(1)} %collective-permute-done.1.refs_0_.ahead_y, f32[384,256]{1,0:T(8,128)S(1)} %scatter.2.refs_1_), custom_call_target="tpu_custom_call" | custom-call | flops 1610612736 | bytes 1048576 | tf_op jit(solution)/shard_map/scatter/pallas_call | solution.py:155
  22.9 5.2 %scatter_last.1 = (f32[384,256]{1,0:T(8,128)}, f32[5,128,128]{2,1,0:T(8,128)S(1)}) custom-call(f32[4,64,256]{2,1,0:T(8,128)S(1)} %collective-permute-done.2.refs_0_, f32[384,256]{1,0:T(8,128)S(1)} %scatter.3.refs_1_), custom_call_target="tpu_custom_call" | custom-call | flops 1610612736 | bytes 1048576 | tf_op jit(solution)/shard_map/scatter_last/pallas_call | solution.py:155
  28.0 1.3 %collective-permute-start.4 = (f32[5,128,128]{2,1,0:T(8,128)S(1)}, f32[5,128,128]{2,1,0:T(8,128)S(1)}, u32[]{:S(2)}, u32[]{:S(2)}) collective-permute-start(f32[5,128,128]{2,1,0:T(8,128)S(1)} %get-tuple-element.13.refs_1_), channel_id=1, source_target_pairs={{1,0},{2,1},{3,2},{4,3},{5,4},{6,5},{7,6},{8,7},{9,8},{10,9},{11,1... | collective-permute-start | bytes 983048 | tf_op jit(solution)/shard_map/ppermute | solution.py:662
  29.3 4.6 %collective-permute-start.3 = (f32[5,128,128]{2,1,0:T(8,128)S(1)}, f32[5,128,128]{2,1,0:T(8,128)S(1)}, u32[]{:S(2)}, u32[]{:S(2)}) collective-permute-start(f32[5,128,128]{2,1,0:T(8,128)S(1)} %get-tuple-element.13.refs_1_), channel_id=1, source_target_pairs={{0,1},{1,2},{2,3},{3,4},{4,5},{5,6},{6,7},{7,8},{8,9},{9,10},{10,1... | collective-permute-start | bytes 983048 | tf_op jit(solution)/shard_map/ppermute | solution.py:661
  33.9 15.1 %near_own.1 = (f32[136,128]{1,0:T(8,128)S(1)}, bf16[129,128,32]{2,1,0:T(8,128)(2,1)S(1)}) custom-call(s32[16,128]{1,0:T(8,128)S(1)} %get-tuple-element.11.refs_0_, f32[5,128,128]{2,1,0:T(8,128)S(1)} %get-tuple-element.13.refs_1_), custom_call_target="tpu_custom_call" | custom-call | flops 2147483648 | bytes 1048576 | tf_op jit(solution)/shard_map/near_own/pallas_call | solution.py:415
  49.0 14.8 %near_other.1.table = f32[144,128]{1,0:T(8,128)S(1)} custom-call(s32[16,128]{1,0:T(8,128)S(1)} %get-tuple-element.11.refs_0_, f32[5,128,128]{2,1,0:T(8,128)S(1)} %get-tuple-element.13.refs_1_, f32[5,128,128]{2,1,0:T(8,128)S(1)} %collective-permute-done.3.refs_2_, f32[5,128,128]{2,1,0:T(8,128)S(1)} %collective-permute-done.4.refs_3_, ...), custom_call_target="tpu_custom_call" | custom-call | flops 2147483648 | bytes 1048576 | tf_op jit(solution)/shard_map/near_other/pallas_call | solution.py:434
  63.9 3.8 %collective-permute-start.5 = (f32[144,128]{1,0:T(8,128)S(1)}, f32[144,128]{1,0:T(8,128)S(1)}, u32[]{:S(2)}, u32[]{:S(2)}) collective-permute-start(f32[144,128]{1,0:T(8,128)S(1)} %near_other.1.table), channel_id=1, source_target_pairs={{0,4},{4,8},{8,12},{12,16},{16,20},{20,24},{24,28},{28,0},{1,5},{5... | collective-permute-start | bytes 221192 | tf_op jit(solution)/shard_map/ppermute | solution.py:26
  67.9 1.0 %lookup_own.1.partial = f32[64,256]{1,0:T(8,128)S(1)} custom-call(f32[4,64,256]{2,1,0:T(8,128)S(1)} %pack.1.refs_0_.refs_4_.tile, f32[144,128]{1,0:T(8,128)S(1)} %near_other.1.table), custom_call_target="tpu_custom_call" | custom-call | flops 268435456 | bytes 524288 | tf_op jit(solution)/shard_map/lookup_own/pallas_call | solution.py:558
  68.8 1.2 %collective-permute-done.5.behind_x = f32[144,128]{1,0:T(8,128)S(1)} collective-permute-done((f32[144,128]{1,0:T(8,128)S(1)}, f32[144,128]{1,0:T(8,128)S(1)}, u32[]{:S(2)}, u32[]{:S(2)}) %collective-permute-start.5) | collective-permute-done | bytes 73760 | tf_op jit(solution)/shard_map/ppermute | solution.py:26
  70.0 1.6 %lookup_x.1 = (f32[64,256]{1,0:T(8,128)S(1)}, f32[2,64,256]{2,1,0:T(8,128)S(1)}) custom-call(f32[4,64,256]{2,1,0:T(8,128)S(1)} %pack.1.refs_0_.refs_4_.tile, f32[4,64,256]{2,1,0:T(8,128)S(1)} %collective-permute-done.refs_0_.ahead_x, f32[64,256]{1,0:T(8,128)S(1)} %lookup_own.1.partial, f32[144,128]{1,0:T(8,128)S(1)} %collective-permute-done.5.behind_x), custom_call_target="tpu_custom_call" | custom-call | flops 268435456 | bytes 524288 | tf_op jit(solution)/shard_map/lookup_x/pallas_call | solution.py:558
  71.5 3.1 %collective-permute-done.6.behind_y = f32[144,128]{1,0:T(8,128)S(1)} collective-permute-done((f32[144,128]{1,0:T(8,128)S(1)}, f32[144,128]{1,0:T(8,128)S(1)}, u32[]{:S(2)}, u32[]{:S(2)}) %collective-permute-start.6) | collective-permute-done | bytes 73760 | tf_op jit(solution)/shard_map/ppermute | solution.py:26
  74.6 2.1 %lookup_y.1 = (f32[64,256]{1,0:T(8,128)S(1)}, f32[2,64,256]{2,1,0:T(8,128)S(1)}) custom-call(f32[4,64,256]{2,1,0:T(8,128)S(1)} %pack.1.refs_0_.refs_4_.tile, f32[4,64,256]{2,1,0:T(8,128)S(1)} %collective-permute-done.1.refs_0_.ahead_y, f32[64,256]{1,0:T(8,128)S(1)} %get-tuple-element.17.partial, f32[144,128]{1,0:T(8,128)S(1)} %collective-permute-done.6.behind_y), custom_call_target="tpu_custom_call" | custom-call | flops 268435456 | bytes 524288 | tf_op jit(solution)/shard_map/lookup_y/pallas_call | solution.py:558
  76.7 3.5 %lookup_xy.1 = (f32[64,256]{1,0:T(8,128)}, f32[64,256]{1,0:T(8,128)}) custom-call(f32[4,64,256]{2,1,0:T(8,128)S(1)} %pack.1.refs_0_.refs_4_.tile, f32[2,64,256]{2,1,0:T(8,128)S(1)} %get-tuple-element.16.row_slopes, f32[2,64,256]{2,1,0:T(8,128)S(1)} %get-tuple-element.18.col_slopes, f32[64,256]{1,0:T(8,128)S(1)} %get-tuple-element.19.partial, ...), custom_call_target="tpu_custom_call" | custom-call | flops 268435456 | bytes 524288 | tf_op jit(solution)/shard_map/lookup_xy/pallas_call | solution.py:558
  (15 shorter events, 1.3 us)
Async XLA Ops:
  0.6 0.8 %copy-start = (s32[64,256]{1,0:T(8,128)S(1)}, s32[64,256]{1,0:T(8,128)}, u32[]{:S(2)}) copy-start(s32[64,256]{1,0:T(8,128)} %owner.1) | copy-start | bytes 196612
  1.5 0.8 %copy-start.1 = (s32[64,256]{1,0:T(8,128)S(1)}, s32[64,256]{1,0:T(8,128)}, u32[]{:S(2)}) copy-start(s32[64,256]{1,0:T(8,128)} %place.1) | copy-start | bytes 196612
  2.3 0.8 %copy-start.2 = (f32[64,256]{1,0:T(8,128)S(1)}, f32[64,256]{1,0:T(8,128)}, u32[]{:S(2)}) copy-start(f32[64,256]{1,0:T(8,128)} %elevation.1) | copy-start | bytes 196612
  3.2 0.8 %copy-start.3 = (f32[64,256]{1,0:T(8,128)S(1)}, f32[64,256]{1,0:T(8,128)}, u32[]{:S(2)}) copy-start(f32[64,256]{1,0:T(8,128)} %potential.1) | copy-start | bytes 196612
  4.0 0.8 %copy-start.4 = (f32[64,256]{1,0:T(8,128)S(1)}, f32[64,256]{1,0:T(8,128)}, u32[]{:S(2)}) copy-start(f32[64,256]{1,0:T(8,128)} %flux.1) | copy-start | bytes 196612
  5.3 10.7 %collective-permute-start.1 = (f32[4,64,256]{2,1,0:T(8,128)S(1)}, f32[4,64,256]{2,1,0:T(8,128)S(1)}, u32[]{:S(2)}, u32[]{:S(2)}) collective-permute-start(f32[4,64,256]{2,1,0:T(8,128)S(1)} %pack.1.refs_0_.refs_4_.tile), channel_id=1, source_target_pairs={{0,3},{1,0},{2,1},{3,2},{4,7},{5,4},{6,5},{7,6},{8,11},{9,8},{10,9... | collective-permute-start | bytes 786440 | tf_op jit(solution)/shard_map/ppermute | solution.py:26
  10.4 6.6 %collective-permute-start = (f32[4,64,256]{2,1,0:T(8,128)S(1)}, f32[4,64,256]{2,1,0:T(8,128)S(1)}, u32[]{:S(2)}, u32[]{:S(2)}) collective-permute-start(f32[4,64,256]{2,1,0:T(8,128)S(1)} %pack.1.refs_0_.refs_4_.tile), channel_id=1, source_target_pairs={{0,28},{4,0},{8,4},{12,8},{16,12},{20,16},{24,20},{28,24},{1,29},{... | collective-permute-start | bytes 786440 | tf_op jit(solution)/shard_map/ppermute | solution.py:26
  12.0 0.7 copy-start.5
  16.0 6.9 %collective-permute-start.2 = (f32[4,64,256]{2,1,0:T(8,128)S(1)}, f32[4,64,256]{2,1,0:T(8,128)S(1)}, u32[]{:S(2)}, u32[]{:S(2)}) collective-permute-start(f32[4,64,256]{2,1,0:T(8,128)S(1)} %collective-permute-done.1.refs_0_.ahead_y), channel_id=1, source_target_pairs={{0,28},{4,0},{8,4},{12,8},{16,12},{20,16},{24,20},{28,24},{1,29},{... | collective-permute-start | bytes 786440 | tf_op jit(solution)/shard_map/ppermute | solution.py:26
  28.0 21.0 %collective-permute-start.4 = (f32[5,128,128]{2,1,0:T(8,128)S(1)}, f32[5,128,128]{2,1,0:T(8,128)S(1)}, u32[]{:S(2)}, u32[]{:S(2)}) collective-permute-start(f32[5,128,128]{2,1,0:T(8,128)S(1)} %get-tuple-element.13.refs_1_), channel_id=1, source_target_pairs={{1,0},{2,1},{3,2},{4,3},{5,4},{6,5},{7,6},{8,7},{9,8},{10,9},{11,1... | collective-permute-start | bytes 983048 | tf_op jit(solution)/shard_map/ppermute | solution.py:662
  29.3 19.7 %collective-permute-start.3 = (f32[5,128,128]{2,1,0:T(8,128)S(1)}, f32[5,128,128]{2,1,0:T(8,128)S(1)}, u32[]{:S(2)}, u32[]{:S(2)}) collective-permute-start(f32[5,128,128]{2,1,0:T(8,128)S(1)} %get-tuple-element.13.refs_1_), channel_id=1, source_target_pairs={{0,1},{1,2},{2,3},{3,4},{4,5},{5,6},{6,7},{7,8},{8,9},{9,10},{10,1... | collective-permute-start | bytes 983048 | tf_op jit(solution)/shard_map/ppermute | solution.py:661
  63.9 6.1 %collective-permute-start.5 = (f32[144,128]{1,0:T(8,128)S(1)}, f32[144,128]{1,0:T(8,128)S(1)}, u32[]{:S(2)}, u32[]{:S(2)}) collective-permute-start(f32[144,128]{1,0:T(8,128)S(1)} %near_other.1.table), channel_id=1, source_target_pairs={{0,4},{4,8},{8,12},{12,16},{16,20},{20,24},{24,28},{28,0},{1,5},{5... | collective-permute-start | bytes 221192 | tf_op jit(solution)/shard_map/ppermute | solution.py:26
  67.7 6.9 %collective-permute-start.6 = (f32[144,128]{1,0:T(8,128)S(1)}, f32[144,128]{1,0:T(8,128)S(1)}, u32[]{:S(2)}, u32[]{:S(2)}) collective-permute-start(f32[144,128]{1,0:T(8,128)S(1)} %near_other.1.table), channel_id=1, source_target_pairs={{0,1},{1,2},{2,3},{3,0},{4,5},{5,6},{6,7},{7,4},{8,9},{9,10},{10,1... | collective-permute-start | bytes 221192 | tf_op jit(solution)/shard_map/ppermute | solution.py:26
  67.7 9.0 %collective-permute-start.7 = (f32[144,128]{1,0:T(8,128)S(1)}, f32[144,128]{1,0:T(8,128)S(1)}, u32[]{:S(2)}, u32[]{:S(2)}) collective-permute-start(f32[144,128]{1,0:T(8,128)S(1)} %near_other.1.table), channel_id=1, source_target_pairs={{0,5},{1,6},{2,7},{3,4},{4,9},{5,10},{6,11},{7,8},{8,13},{9,14},{1... | collective-permute-start | bytes 221192 | tf_op jit(solution)/shard_map/ppermute | solution.py:674

commit v7 on v6

--- a/solution.py
+++ b/solution.py
@@ -83,9 +83,10 @@
         high, _ = box_split(tile[(0,) + window_of(unit)[2]] - base, high_count)
         return (high >= 0.0) & (high < high_count)
 
-    def add(i, carry):
-        row0, col0, window = window_of(active[i])
+    def sides(i, live):
+        row0, col0, window = window_of(active[jnp.where(live, i, 0)])
         high, low = box_split(tile[(0,) + window] - base, high_count)
+        high = jnp.where(live, high, -1.0)
         z = 0.25 * tile[(1,) + window]
         z_high = rounded(z)
         z_low = z - z_high
@@ -109,15 +110,22 @@
                 jnp.concatenate([jnp.where(hit, v, 0.0).astype(BF16) for v in values], axis=0)
             )
             rights.append(jnp.where(low_iota == row(low), 1.0, 0.0).astype(BF16))
+        return lefts, rights
+
+    def add(i, carry):
+        lefts, rights = sides(2 * i, True)
+        more = sides(2 * i + 1, 2 * i + 1 < count)
         acc[...] += lax.dot_general(
-            jnp.concatenate(lefts, axis=1),
-            jnp.concatenate(rights, axis=1),
+            jnp.concatenate(lefts + more[0], axis=1),
+            jnp.concatenate(rights + more[1], axis=1),
             (((1,), (1,)), ((), ())),
             preferred_element_type=F32,
         )
         return carry
 
-    lax.fori_loop(0, list_active(mine, rows // 8 * across, active), add, 0)
+    count = list_active(mine, rows // 8 * across, active)
+
+    lax.fori_loop(0, (count + 1) // 2, add, 0)
 
     if last:
         boxed = refs[-2]
@@ -462,26 +470,34 @@
         high, _ = box_split(slot[window_of(unit)] - base, high_count)
         return (high >= 0.0) & (high < high_count)
 
+    def nodes_of(i, live):
+        window = window_of(active[jnp.where(live, i, 0)])
+        high, low = box_split(slot[window] - base, high_count)
+        return window, jnp.where(live, high, -1.0), low
+
     def add(i, carry):
-        window = window_of(active[i])
-        high, low = box_split(slot[window] - base, high_count)
         low_iota = lax.broadcasted_iota(jnp.int32, (WIDE, LANES), 0).astype(F32)
         high_iota = lax.broadcasted_iota(jnp.int32, (high_count, LANES), 0).astype(F32)
-        hits = jnp.concatenate(
-            [jnp.where(low_iota == low[s : s + 1, :], 1.0, 0.0).astype(BF16) for s in range(8)],
-            axis=1,
-        )
-        picked = jnp.dot(pieces[...], hits, preferred_element_type=F32)
-        lines = []
-        for s in range(8):
-            part = slice(LANES * s, LANES * s + LANES)
-            both = picked[0:high_count, part] + picked[high_count : 2 * high_count, part]
-            mine = high_iota == high[s : s + 1, :]
-            lines.append(jnp.sum(jnp.where(mine, both, 0.0), axis=0, keepdims=True))
-        out[window] += jnp.concatenate(lines, axis=0)
+        both = (nodes_of(2 * i, True), nodes_of(2 * i + 1, 2 * i + 1 < count))
+        hits = [
+            jnp.where(low_iota == low[s : s + 1, :], 1.0, 0.0).astype(BF16)
+            for _, _, low in both
+            for s in range(8)
+        ]
+        picked = jnp.dot(pieces[...], jnp.concatenate(hits, axis=1), preferred_element_type=F32)
+        for half, (window, high, _) in enumerate(both):
+            lines = []
+            for s in range(8):
+                start = LANES * (8 * half + s)
+                part = slice(start, start + LANES)
+                value = picked[0:high_count, part] + picked[high_count : 2 * high_count, part]
+                mine = high_iota == high[s : s + 1, :]
+                lines.append(jnp.sum(jnp.where(mine, value, 0.0), axis=0, keepdims=True))
+            out[window] += jnp.concatenate(lines, axis=0)
         return carry
 
-    lax.fori_loop(0, list_active(there, rows // 8 * across, active), add, 0)
+    count = list_active(there, rows // 8 * across, active)
+    lax.fori_loop(0, (count + 1) // 2, add, 0)
 
 
 def base_of(node_count, steps):
@@ -598,41 +614,6 @@
     )
 
 
-def pack_kernel(owner, place, elevation, potential, flux, tile, owner_here, place_here, arrived):
-    copies = [
-        pltpu.make_async_copy(source, target, arrived.at[i])
-        for i, (source, target) in enumerate(
-            (
-                (owner, owner_here),
-                (place, place_here),
-                (elevation, tile.at[1]),
-                (potential, tile.at[2]),
-                (flux, tile.at[3]),
-            )
-        )
-    ]
-    for copy in copies:
-        copy.start()
-    copies[0].wait()
-    copies[1].wait()
-    node_count = owner.shape[0] * owner.shape[1]
-    tile[0] = (owner_here[...] * node_count + place_here[...]).astype(F32)
-    for copy in copies[2:]:
-        copy.wait()
-
-
-def pack(owner, place, elevation, potential, flux):
-    return pl.pallas_call(
-        pack_kernel,
-        out_shape=pltpu.VMEM((4,) + owner.shape, F32),
-        in_specs=[pl.BlockSpec(memory_space=pltpu.HBM)] * 5,
-        out_specs=pl.BlockSpec(memory_space=pltpu.VMEM),
-        scratch_shapes=[pltpu.VMEM(owner.shape, jnp.int32)] * 2 + [pltpu.SemaphoreType.DMA((5,))],
-        compiler_params=pltpu.CompilerParams(vmem_limit_bytes=VMEM_LIMIT),
-        name="pack",
-    )(owner, place, elevation, potential, flux)
-
-
 def shards(potential, elevation, normal_flux, box_owner, box_place, near_boxes):
     rows, cols = potential.shape
     count_tx = lax.axis_size("tx")
@@ -644,7 +625,8 @@
     assert 4 * (cols // LANES) <= EXTRA - 8
     assert node_count * count_tx * count_ty < 2**24
 
-    tile = pack(box_owner, box_place, elevation, potential, normal_flux)
+    slot = (box_owner * node_count + box_place).astype(F32)
+    tile = jnp.stack([slot, elevation, potential, normal_flux])
     ahead_x = shifted(tile, "tx", -1)
     ahead_y = shifted(tile, "ty", -1)
     ahead_xy = shifted(ahead_y, "tx", -1)

time: 80.9 us -> 74.8 us (0.925)
  Pallas kernels: 51.1 us -> 46.6 us
  local copies, waits for them, and re-layouts: 4.87 us -> 0.69 us
  other arithmetic: 0 us -> 1.81 us
  starting transfers between devices: 17.6 us -> 18.5 us
    unnamed x12 -> x2, local copies, waits for them, and re-layouts: 4.87 us -> 0.69 us
    pallas_call x4, Pallas kernels: 12.6 us -> 10.5 us  [scatter(): pl.pallas_call(lambda *refs: scatter_kernel(first, last, (rows, cols, hig...]
    pallas_call x4, Pallas kernels: 8.11 us -> 6.17 us  [lookup_call(): pl.pallas_call(kernel, out_shape=out_shape, in_specs=[vmem] * len(args),...]
    another operation x0 -> x2, other arithmetic: none -> 1.81 us  [shards(): tile = jnp.stack([slot, elevation, potential, normal_flux])]
    ppermute x1, starting transfers between devices: 0.19 us -> 1.67 us  [shards(): behind_xy = lax.ppermute(value, both, diagonal)]
where the time goes in v7:
time: 74.8 us; the launch traced here: 74.1 us
  Pallas kernels  46.6 us (62%)
  starting transfers between devices  18.5 us (25%)
  waiting for transfers between devices  5.74 us (8%)
  other arithmetic  1.81 us (2%)
  between operations  0.75 us (1%)
    pallas_call x1, Pallas kernels, near_own(): pl.pallas_call(lambda *refs: near_own_kernel(near, *refs), out_shape=(plt...  15.1 us
    pallas_call x1, Pallas kernels, near_other(): pl.pallas_call(lambda *refs: near_other_kernel(near, *refs), out_shape=pl...  14.8 us
    ppermute x5, starting transfers between devices, shifted(): return lax.ppermute(value, axis, pairs)  11 us
    pallas_call x4, Pallas kernels, scatter(): pl.pallas_call(lambda *refs: scatter_kernel(first, last, (rows, cols, hig...  10.5 us
    pallas_call x4, Pallas kernels, lookup_call(): pl.pallas_call(kernel, out_shape=out_shape, in_specs=[vmem] * len(args),...  6.17 us
    ppermute x5, waiting for transfers between devices, shifted(): return lax.ppermute(value, axis, pairs)  5.73 us
    ppermute x1, starting transfers between devices, shards(): lower = lax.ppermute(boxed, both, [(i, i + 1) for i in range(total - 1)])  4.57 us
    another operation x2, other arithmetic, shards(): tile = jnp.stack([slot, elevation, potential, normal_flux])  1.81 us
  transfers between devices with their start and end apart: 8, of which 3 were waited for; matrix products, arithmetic and copies ran while one was open for 0% of the time, Pallas kernels for 34%

profile of v7, /device:TPU:0, one launch (start us, length us, event | category | flops | bytes accessed | tf_op | source)
XLA Modules:
  0.0 74.1 jit_solution(6004368849511383376)
XLA Ops:
  0.6 0.9 %convert_bitcast_fusion = f32[1,64,256]{2,1,0:T(8,128)S(1)} fusion(s32[64,256]{1,0:T(8,128)} %param.10, s32[64,256]{1,0:T(8,128)} %param.9), kind=kLoop, calls=%fused_computation.1 | loop fusion | flops 49152 | bytes 196608 | tf_op jit(solution)/shard_map/stack | solution.py:629
  1.5 0.9 %pad_maximum_fusion.refs_0_.refs_4_.tile = f32[4,64,256]{2,1,0:T(8,128)S(1)} fusion(f32[1,64,256]{2,1,0:T(8,128)} %bitcast.7, f32[1,64,256]{2,1,0:T(8,128)} %bitcast.8, f32[1,64,256]{2,1,0:T(8,128)} %bitcast.9, f32[1,64,256]{2,1,0:T(8,128)S(1)} %convert_bitcast_fusion), kind=kLoop, calls=%fused_computation | loop fusion | flops 196608 | bytes 524288 | tf_op jit(solution)/shard_map/stack | solution.py:629
  2.4 5.1 %collective-permute-start.1 = (f32[4,64,256]{2,1,0:T(8,128)S(1)}, f32[4,64,256]{2,1,0:T(8,128)S(1)}, u32[]{:S(2)}, u32[]{:S(2)}) collective-permute-start(f32[4,64,256]{2,1,0:T(8,128)S(1)} %pad_maximum_fusion.refs_0_.refs_4_.tile), channel_id=1, source_target_pairs={{0,3},{1,0},{2,1},{3,2},{4,7},{5,4},{6,5},{7,6},{8,11},{9,8},{10,9... | collective-permute-start | bytes 786440 | tf_op jit(solution)/shard_map/ppermute | solution.py:26
  7.6 1.6 %collective-permute-start = (f32[4,64,256]{2,1,0:T(8,128)S(1)}, f32[4,64,256]{2,1,0:T(8,128)S(1)}, u32[]{:S(2)}, u32[]{:S(2)}) collective-permute-start(f32[4,64,256]{2,1,0:T(8,128)S(1)} %pad_maximum_fusion.refs_0_.refs_4_.tile), channel_id=1, source_target_pairs={{0,28},{4,0},{8,4},{12,8},{16,12},{20,16},{24,20},{28,24},{1,29},{... | collective-permute-start | bytes 786440 | tf_op jit(solution)/shard_map/ppermute | solution.py:26
  9.2 0.7 copy-done
  9.9 1.6 %scatter_first.1 = (f32[384,256]{1,0:T(8,128)S(1)}, s32[16,128]{1,0:T(8,128)S(1)}) custom-call(f32[4,64,256]{2,1,0:T(8,128)S(1)} %pad_maximum_fusion.refs_0_.refs_4_.tile, s32[8,128]{1,0:T(8,128)S(1)} %bitcast.6), custom_call_target="tpu_custom_call" | custom-call | flops 1610612736 | bytes 1048576 | tf_op jit(solution)/shard_map/scatter_first/pallas_call | solution.py:163
  11.5 1.6 %collective-permute-done.1.refs_0_.ahead_y = f32[4,64,256]{2,1,0:T(8,128)S(1)} collective-permute-done((f32[4,64,256]{2,1,0:T(8,128)S(1)}, f32[4,64,256]{2,1,0:T(8,128)S(1)}, u32[]{:S(2)}, u32[]{:S(2)}) %collective-permute-start.1) | collective-permute-done | bytes 262176 | tf_op jit(solution)/shard_map/ppermute | solution.py:26
  13.1 1.0 %collective-permute-start.2 = (f32[4,64,256]{2,1,0:T(8,128)S(1)}, f32[4,64,256]{2,1,0:T(8,128)S(1)}, u32[]{:S(2)}, u32[]{:S(2)}) collective-permute-start(f32[4,64,256]{2,1,0:T(8,128)S(1)} %collective-permute-done.1.refs_0_.ahead_y), channel_id=1, source_target_pairs={{0,28},{4,0},{8,4},{12,8},{16,12},{20,16},{24,20},{28,24},{1,29},{... | collective-permute-start | bytes 786440 | tf_op jit(solution)/shard_map/ppermute | solution.py:26
  14.2 0.0 collective-permute-done.refs_0_.ahead_x
  14.2 2.1 %scatter.2.refs_1_ = f32[384,256]{1,0:T(8,128)S(1)} custom-call(f32[4,64,256]{2,1,0:T(8,128)S(1)} %collective-permute-done.refs_0_.ahead_x, f32[384,256]{1,0:T(8,128)S(1)} %get-tuple-element.12.refs_1_), custom_call_target="tpu_custom_call" | custom-call | flops 1610612736 | bytes 1048576 | tf_op jit(solution)/shard_map/scatter/pallas_call | solution.py:163
  16.2 2.7 %scatter.3.refs_1_ = f32[384,256]{1,0:T(8,128)S(1)} custom-call(f32[4,64,256]{2,1,0:T(8,128)S(1)} %collective-permute-done.1.refs_0_.ahead_y, f32[384,256]{1,0:T(8,128)S(1)} %scatter.2.refs_1_), custom_call_target="tpu_custom_call" | custom-call | flops 1610612736 | bytes 1048576 | tf_op jit(solution)/shard_map/scatter/pallas_call | solution.py:163
  19.0 4.1 %scatter_last.1 = (f32[384,256]{1,0:T(8,128)}, f32[5,128,128]{2,1,0:T(8,128)S(1)}) custom-call(f32[4,64,256]{2,1,0:T(8,128)S(1)} %collective-permute-done.2.refs_0_, f32[384,256]{1,0:T(8,128)S(1)} %scatter.3.refs_1_), custom_call_target="tpu_custom_call" | custom-call | flops 1610612736 | bytes 1048576 | tf_op jit(solution)/shard_map/scatter_last/pallas_call | solution.py:163
  23.0 1.3 %collective-permute-start.4 = (f32[5,128,128]{2,1,0:T(8,128)S(1)}, f32[5,128,128]{2,1,0:T(8,128)S(1)}, u32[]{:S(2)}, u32[]{:S(2)}) collective-permute-start(f32[5,128,128]{2,1,0:T(8,128)S(1)} %get-tuple-element.13.refs_1_), channel_id=1, source_target_pairs={{1,0},{2,1},{3,2},{4,3},{5,4},{6,5},{7,6},{8,7},{9,8},{10,9},{11,1... | collective-permute-start | bytes 983048 | tf_op jit(solution)/shard_map/ppermute | solution.py:644
  24.3 4.6 %collective-permute-start.3 = (f32[5,128,128]{2,1,0:T(8,128)S(1)}, f32[5,128,128]{2,1,0:T(8,128)S(1)}, u32[]{:S(2)}, u32[]{:S(2)}) collective-permute-start(f32[5,128,128]{2,1,0:T(8,128)S(1)} %get-tuple-element.13.refs_1_), channel_id=1, source_target_pairs={{0,1},{1,2},{2,3},{3,4},{4,5},{5,6},{6,7},{7,8},{8,9},{9,10},{10,1... | collective-permute-start | bytes 983048 | tf_op jit(solution)/shard_map/ppermute | solution.py:643
  28.9 15.1 %near_own.1 = (f32[136,128]{1,0:T(8,128)S(1)}, bf16[129,128,32]{2,1,0:T(8,128)(2,1)S(1)}) custom-call(s32[16,128]{1,0:T(8,128)S(1)} %get-tuple-element.11.refs_0_, f32[5,128,128]{2,1,0:T(8,128)S(1)} %get-tuple-element.13.refs_1_), custom_call_target="tpu_custom_call" | custom-call | flops 2147483648 | bytes 1048576 | tf_op jit(solution)/shard_map/near_own/pallas_call | solution.py:423
  44.1 14.8 %near_other.1.table = f32[144,128]{1,0:T(8,128)S(1)} custom-call(s32[16,128]{1,0:T(8,128)S(1)} %get-tuple-element.11.refs_0_, f32[5,128,128]{2,1,0:T(8,128)S(1)} %get-tuple-element.13.refs_1_, f32[5,128,128]{2,1,0:T(8,128)S(1)} %collective-permute-done.3.refs_2_, f32[5,128,128]{2,1,0:T(8,128)S(1)} %collective-permute-done.4.refs_3_, ...), custom_call_target="tpu_custom_call" | custom-call | flops 2147483648 | bytes 1048576 | tf_op jit(solution)/shard_map/near_other/pallas_call | solution.py:442
  58.9 3.2 %collective-permute-start.5 = (f32[144,128]{1,0:T(8,128)S(1)}, f32[144,128]{1,0:T(8,128)S(1)}, u32[]{:S(2)}, u32[]{:S(2)}) collective-permute-start(f32[144,128]{1,0:T(8,128)S(1)} %near_other.1.table), channel_id=1, source_target_pairs={{0,4},{4,8},{8,12},{12,16},{16,20},{20,24},{24,28},{28,0},{1,5},{5... | collective-permute-start | bytes 221192 | tf_op jit(solution)/shard_map/ppermute | solution.py:26
  62.1 1.7 %collective-permute-start.7 = (f32[144,128]{1,0:T(8,128)S(1)}, f32[144,128]{1,0:T(8,128)S(1)}, u32[]{:S(2)}, u32[]{:S(2)}) collective-permute-start(f32[144,128]{1,0:T(8,128)S(1)} %near_other.1.table), channel_id=1, source_target_pairs={{0,5},{1,6},{2,7},{3,4},{4,9},{5,10},{6,11},{7,8},{8,13},{9,14},{1... | collective-permute-start | bytes 221192 | tf_op jit(solution)/shard_map/ppermute | solution.py:656
  63.8 0.8 %lookup_own.1.partial = f32[64,256]{1,0:T(8,128)S(1)} custom-call(f32[4,64,256]{2,1,0:T(8,128)S(1)} %pad_maximum_fusion.refs_0_.refs_4_.tile, f32[144,128]{1,0:T(8,128)S(1)} %near_other.1.table), custom_call_target="tpu_custom_call" | custom-call | flops 268435456 | bytes 524288 | tf_op jit(solution)/shard_map/lookup_own/pallas_call | solution.py:574
  64.7 0.5 collective-permute-done.5.behind_x
  65.2 1.3 %lookup_x.1 = (f32[64,256]{1,0:T(8,128)S(1)}, f32[2,64,256]{2,1,0:T(8,128)S(1)}) custom-call(f32[4,64,256]{2,1,0:T(8,128)S(1)} %pad_maximum_fusion.refs_0_.refs_4_.tile, f32[4,64,256]{2,1,0:T(8,128)S(1)} %collective-permute-done.refs_0_.ahead_x, f32[64,256]{1,0:T(8,128)S(1)} %lookup_own.1.partial, f32[144,128]{1,0:T(8,128)S(1)} %collective-permute-done.5.behind_x), custom_call_target="tpu_custom_call" | custom-call | flops 268435456 | bytes 524288 | tf_op jit(solution)/shard_map/lookup_x/pallas_call | solution.py:574
  66.5 3.6 %collective-permute-done.6.behind_y = f32[144,128]{1,0:T(8,128)S(1)} collective-permute-done((f32[144,128]{1,0:T(8,128)S(1)}, f32[144,128]{1,0:T(8,128)S(1)}, u32[]{:S(2)}, u32[]{:S(2)}) %collective-permute-start.6) | collective-permute-done | bytes 73760 | tf_op jit(solution)/shard_map/ppermute | solution.py:26
  70.0 1.5 %lookup_y.1 = (f32[64,256]{1,0:T(8,128)S(1)}, f32[2,64,256]{2,1,0:T(8,128)S(1)}) custom-call(f32[4,64,256]{2,1,0:T(8,128)S(1)} %pad_maximum_fusion.refs_0_.refs_4_.tile, f32[4,64,256]{2,1,0:T(8,128)S(1)} %collective-permute-done.1.refs_0_.ahead_y, f32[64,256]{1,0:T(8,128)S(1)} %get-tuple-element.17.partial, f32[144,128]{1,0:T(8,128)S(1)} %collective-permute-done.6.behind_y), custom_call_target="tpu_custom_call" | custom-call | flops 268435456 | bytes 524288 | tf_op jit(solution)/shard_map/lookup_y/pallas_call | solution.py:574
  71.6 2.5 %lookup_xy.1 = (f32[64,256]{1,0:T(8,128)}, f32[64,256]{1,0:T(8,128)}) custom-call(f32[4,64,256]{2,1,0:T(8,128)S(1)} %pad_maximum_fusion.refs_0_.refs_4_.tile, f32[2,64,256]{2,1,0:T(8,128)S(1)} %get-tuple-element.16.row_slopes, f32[2,64,256]{2,1,0:T(8,128)S(1)} %get-tuple-element.18.col_slopes, f32[64,256]{1,0:T(8,128)S(1)} %get-tuple-element.19.partial, ...), custom_call_target="tpu_custom_call" | custom-call | flops 268435456 | bytes 524288 | tf_op jit(solution)/shard_map/lookup_xy/pallas_call | solution.py:574
  (6 shorter events, 0.0 us)
Async XLA Ops:
  2.4 10.7 %collective-permute-start.1 = (f32[4,64,256]{2,1,0:T(8,128)S(1)}, f32[4,64,256]{2,1,0:T(8,128)S(1)}, u32[]{:S(2)}, u32[]{:S(2)}) collective-permute-start(f32[4,64,256]{2,1,0:T(8,128)S(1)} %pad_maximum_fusion.refs_0_.refs_4_.tile), channel_id=1, source_target_pairs={{0,3},{1,0},{2,1},{3,2},{4,7},{5,4},{6,5},{7,6},{8,11},{9,8},{10,9... | collective-permute-start | bytes 786440 | tf_op jit(solution)/shard_map/ppermute | solution.py:26
  7.6 6.6 %collective-permute-start = (f32[4,64,256]{2,1,0:T(8,128)S(1)}, f32[4,64,256]{2,1,0:T(8,128)S(1)}, u32[]{:S(2)}, u32[]{:S(2)}) collective-permute-start(f32[4,64,256]{2,1,0:T(8,128)S(1)} %pad_maximum_fusion.refs_0_.refs_4_.tile), channel_id=1, source_target_pairs={{0,28},{4,0},{8,4},{12,8},{16,12},{20,16},{24,20},{28,24},{1,29},{... | collective-permute-start | bytes 786440 | tf_op jit(solution)/shard_map/ppermute | solution.py:26
  9.2 0.7 copy-start
  13.1 5.8 %collective-permute-start.2 = (f32[4,64,256]{2,1,0:T(8,128)S(1)}, f32[4,64,256]{2,1,0:T(8,128)S(1)}, u32[]{:S(2)}, u32[]{:S(2)}) collective-permute-start(f32[4,64,256]{2,1,0:T(8,128)S(1)} %collective-permute-done.1.refs_0_.ahead_y), channel_id=1, source_target_pairs={{0,28},{4,0},{8,4},{12,8},{16,12},{20,16},{24,20},{28,24},{1,29},{... | collective-permute-start | bytes 786440 | tf_op jit(solution)/shard_map/ppermute | solution.py:26
  23.0 21.0 %collective-permute-start.4 = (f32[5,128,128]{2,1,0:T(8,128)S(1)}, f32[5,128,128]{2,1,0:T(8,128)S(1)}, u32[]{:S(2)}, u32[]{:S(2)}) collective-permute-start(f32[5,128,128]{2,1,0:T(8,128)S(1)} %get-tuple-element.13.refs_1_), channel_id=1, source_target_pairs={{1,0},{2,1},{3,2},{4,3},{5,4},{6,5},{7,6},{8,7},{9,8},{10,9},{11,1... | collective-permute-start | bytes 983048 | tf_op jit(solution)/shard_map/ppermute | solution.py:644
  24.3 19.7 %collective-permute-start.3 = (f32[5,128,128]{2,1,0:T(8,128)S(1)}, f32[5,128,128]{2,1,0:T(8,128)S(1)}, u32[]{:S(2)}, u32[]{:S(2)}) collective-permute-start(f32[5,128,128]{2,1,0:T(8,128)S(1)} %get-tuple-element.13.refs_1_), channel_id=1, source_target_pairs={{0,1},{1,2},{2,3},{3,4},{4,5},{5,6},{6,7},{7,8},{8,9},{9,10},{10,1... | collective-permute-start | bytes 983048 | tf_op jit(solution)/shard_map/ppermute | solution.py:643
  58.9 6.3 %collective-permute-start.5 = (f32[144,128]{1,0:T(8,128)S(1)}, f32[144,128]{1,0:T(8,128)S(1)}, u32[]{:S(2)}, u32[]{:S(2)}) collective-permute-start(f32[144,128]{1,0:T(8,128)S(1)} %near_other.1.table), channel_id=1, source_target_pairs={{0,4},{4,8},{8,12},{12,16},{16,20},{20,24},{24,28},{28,0},{1,5},{5... | collective-permute-start | bytes 221192 | tf_op jit(solution)/shard_map/ppermute | solution.py:26
  62.1 7.9 %collective-permute-start.6 = (f32[144,128]{1,0:T(8,128)S(1)}, f32[144,128]{1,0:T(8,128)S(1)}, u32[]{:S(2)}, u32[]{:S(2)}) collective-permute-start(f32[144,128]{1,0:T(8,128)S(1)} %near_other.1.table), channel_id=1, source_target_pairs={{0,1},{1,2},{2,3},{3,0},{4,5},{5,6},{6,7},{7,4},{8,9},{9,10},{10,1... | collective-permute-start | bytes 221192 | tf_op jit(solution)/shard_map/ppermute | solution.py:26
  62.1 9.4 %collective-permute-start.7 = (f32[144,128]{1,0:T(8,128)S(1)}, f32[144,128]{1,0:T(8,128)S(1)}, u32[]{:S(2)}, u32[]{:S(2)}) collective-permute-start(f32[144,128]{1,0:T(8,128)S(1)} %near_other.1.table), channel_id=1, source_target_pairs={{0,5},{1,6},{2,7},{3,4},{4,9},{5,10},{6,11},{7,8},{8,13},{9,14},{1... | collective-permute-start | bytes 221192 | tf_op jit(solution)/shard_map/ppermute | solution.py:656

commit v8 on v7

--- a/solution.py
+++ b/solution.py
@@ -14,7 +14,9 @@
 USED = 24
 STORED = USED + 8
 EXTRA = 16
-GROUP = 8
+UNITS = 5
+OWN_GROUP = 16
+OTHER_GROUP = 16
 VMEM_LIMIT = 24 << 20
 BF16 = jnp.bfloat16
 F32 = jnp.float32
@@ -113,19 +115,21 @@
         return lefts, rights
 
     def add(i, carry):
-        lefts, rights = sides(2 * i, True)
-        more = sides(2 * i + 1, 2 * i + 1 < count)
+        lefts, rights = [], []
+        for u in range(UNITS):
+            left, right = sides(UNITS * i + u, UNITS * i + u < count)
+            lefts += left
+            rights += right
         acc[...] += lax.dot_general(
-            jnp.concatenate(lefts + more[0], axis=1),
-            jnp.concatenate(rights + more[1], axis=1),
+            jnp.concatenate(lefts, axis=1),
+            jnp.concatenate(rights, axis=1),
             (((1,), (1,)), ((), ())),
             preferred_element_type=F32,
         )
         return carry
 
     count = list_active(mine, rows // 8 * across, active)
-
-    lax.fori_loop(0, (count + 1) // 2, add, 0)
+    lax.fori_loop(0, (count + UNITS - 1) // UNITS, add, 0)
 
     if last:
         boxed = refs[-2]
@@ -305,6 +309,7 @@
 
 def run_items(target_of, source_of, half, iterations, turned, sfeat, sflux, sums, totals):
     empty_row = sums.shape[0] - 8
+    group = totals.shape[0]
 
     def apply(item, total):
         target = target_of(item)
@@ -329,16 +334,16 @@
         sums[pl.ds(target, 1), :] += jnp.sum(total[...].T, axis=0, keepdims=True)
 
     def step(i, carry):
-        for u in range(GROUP):
-            reduce(GROUP * (i - 1) + u, totals.at[u], i > 0)
-        for u in range(GROUP):
-            apply(GROUP * i + u, totals.at[u])
+        for u in range(group):
+            reduce(group * (i - 1) + u, totals.at[u], i > 0)
+        for u in range(group):
+            apply(group * i + u, totals.at[u])
         return carry
 
     totals[...] = jnp.zeros(totals.shape, F32)
     lax.fori_loop(0, iterations, step, 0)
-    for u in range(GROUP):
-        reduce(GROUP * (iterations - 1) + u, totals.at[u], iterations > 0)
+    for u in range(group):
+        reduce(group * (iterations - 1) + u, totals.at[u], iterations > 0)
 
 
 def near_own_kernel(near, plan, own, sums, turned, tfeat, sfeat, sflux, totals):
@@ -355,7 +360,7 @@
         return plan[k, jnp.minimum(item, boxes - 1)]
 
     run_items(
-        target_of, source_of, half, boxes // GROUP, turned, sfeat, sflux, sums, totals
+        target_of, source_of, half, boxes // OWN_GROUP, turned, sfeat, sflux, sums, totals
     )
 
 
@@ -379,7 +384,7 @@
         row = jnp.where(item < boxes, half, 2 * half) + k
         return plan[row, jnp.minimum(box_of(item), boxes - 1)]
 
-    iterations = (items + GROUP - 1) // GROUP
+    iterations = (items + OTHER_GROUP - 1) // OTHER_GROUP
     run_items(
         target_of, source_of, half, iterations, turned, sfeat, sflux, sums, totals
     )
@@ -400,11 +405,11 @@
         place += 2
 
 
-def item_scratch(sources):
+def item_scratch(sources, group):
     return [
         pltpu.VMEM((STORED * (sources + 8), LANES), F32),
         pltpu.VMEM((sources + 8, LANES), F32),
-        pltpu.VMEM((GROUP, LANES, LANES), F32),
+        pltpu.VMEM((group, LANES, LANES), F32),
     ]
 
 
@@ -417,7 +422,7 @@
 
 def near_own(plan, own, near):
     boxes = own.shape[1]
-    assert boxes == LANES and boxes % GROUP == 0 and near % 2 == 0
+    assert boxes == LANES and boxes % OWN_GROUP == 0 and near % 2 == 0
     vmem = pl.BlockSpec(memory_space=pltpu.VMEM)
     smem = pl.BlockSpec(memory_space=pltpu.SMEM)
     return pl.pallas_call(
@@ -428,7 +433,7 @@
         ),
         in_specs=[smem, vmem],
         out_specs=(vmem,) * 2,
-        scratch_shapes=[pltpu.VMEM((USED * (boxes + 8), LANES), F32)] + item_scratch(boxes),
+        scratch_shapes=[pltpu.VMEM((USED * (boxes + 8), LANES), F32)] + item_scratch(boxes, OWN_GROUP),
         compiler_params=pltpu.CompilerParams(vmem_limit_bytes=VMEM_LIMIT),
         name="near_own",
         cost_estimate=near_cost(boxes, near),
@@ -444,7 +449,7 @@
         out_shape=pltpu.VMEM((boxes + EXTRA, LANES), F32),
         in_specs=[smem] + [vmem] * 6,
         out_specs=vmem,
-        scratch_shapes=[pltpu.VMEM((boxes + 8, LANES), F32)] + item_scratch(3 * boxes),
+        scratch_shapes=[pltpu.VMEM((boxes + 8, LANES), F32)] + item_scratch(3 * boxes, OTHER_GROUP),
         compiler_params=pltpu.CompilerParams(vmem_limit_bytes=VMEM_LIMIT),
         name="near_other",
         cost_estimate=near_cost(boxes, near),
@@ -478,17 +483,17 @@
     def add(i, carry):
         low_iota = lax.broadcasted_iota(jnp.int32, (WIDE, LANES), 0).astype(F32)
         high_iota = lax.broadcasted_iota(jnp.int32, (high_count, LANES), 0).astype(F32)
-        both = (nodes_of(2 * i, True), nodes_of(2 * i + 1, 2 * i + 1 < count))
+        units = [nodes_of(UNITS * i + u, UNITS * i + u < count) for u in range(UNITS)]
         hits = [
             jnp.where(low_iota == low[s : s + 1, :], 1.0, 0.0).astype(BF16)
-            for _, _, low in both
+            for _, _, low in units
             for s in range(8)
         ]
         picked = jnp.dot(pieces[...], jnp.concatenate(hits, axis=1), preferred_element_type=F32)
-        for half, (window, high, _) in enumerate(both):
+        for u, (window, high, _) in enumerate(units):
             lines = []
             for s in range(8):
-                start = LANES * (8 * half + s)
+                start = LANES * (8 * u + s)
                 part = slice(start, start + LANES)
                 value = picked[0:high_count, part] + picked[high_count : 2 * high_count, part]
                 mine = high_iota == high[s : s + 1, :]
@@ -497,7 +502,7 @@
         return carry
 
     count = list_active(there, rows // 8 * across, active)
-    lax.fori_loop(0, (count + 1) // 2, add, 0)
+    lax.fori_loop(0, (count + UNITS - 1) // UNITS, add, 0)
 
 
 def base_of(node_count, steps):

time: 74.8 us -> 72.2 us (0.965)
  Pallas kernels: 46.6 us -> 42 us
  waiting for transfers between devices: 5.74 us -> 7.92 us
    pallas_call x4, Pallas kernels: 10.5 us -> 9.09 us  [scatter(): pl.pallas_call(lambda *refs: scatter_kernel(first, last, (rows, cols, hig...]
    pallas_call x1, Pallas kernels: 14.8 us -> 13.6 us  [near_other(): pl.pallas_call(lambda *refs: near_other_kernel(near, *refs), out_shape=pl...]
    ppermute x5, waiting for transfers between devices: 5.73 us -> 6.85 us  [shifted(): return lax.ppermute(value, axis, pairs)]
    ppermute x1, waiting for transfers between devices: 0.01 us -> 1.06 us  [shards(): behind_xy = lax.ppermute(value, both, diagonal)]
    pallas_call x1, Pallas kernels: 15.1 us -> 14.2 us  [near_own(): pl.pallas_call(lambda *refs: near_own_kernel(near, *refs), out_shape=(plt...]
    pallas_call x4, Pallas kernels: 6.17 us -> 5.2 us  [lookup_call(): pl.pallas_call(kernel, out_shape=out_shape, in_specs=[vmem] * len(args),...]
  transfers between devices with their start and end apart: 8 -> 8, of which waited for: 3 -> 4; matrix products, arithmetic and copies ran while one was open for 0% -> 0% of each run, Pallas kernels for 34% -> 32%
where the time goes in v8:
time: 72.2 us; the launch traced here: 71.7 us
  Pallas kernels  42 us (58%)
  starting transfers between devices  18.5 us (26%)
  waiting for transfers between devices  7.92 us (11%)
  other arithmetic  1.81 us (3%)
  between operations  0.74 us (1%)
    pallas_call x1, Pallas kernels, near_own(): pl.pallas_call(lambda *refs: near_own_kernel(near, *refs), out_shape=(plt...  14.2 us
    pallas_call x1, Pallas kernels, near_other(): pl.pallas_call(lambda *refs: near_other_kernel(near, *refs), out_shape=pl...  13.6 us
    ppermute x5, starting transfers between devices, shifted(): return lax.ppermute(value, axis, pairs)  11.5 us
    pallas_call x4, Pallas kernels, scatter(): pl.pallas_call(lambda *refs: scatter_kernel(first, last, (rows, cols, hig...  9.09 us
    ppermute x5, waiting for transfers between devices, shifted(): return lax.ppermute(value, axis, pairs)  6.85 us
    pallas_call x4, Pallas kernels, lookup_call(): pl.pallas_call(kernel, out_shape=out_shape, in_specs=[vmem] * len(args),...  5.2 us
    ppermute x1, starting transfers between devices, shards(): lower = lax.ppermute(boxed, both, [(i, i + 1) for i in range(total - 1)])  4.57 us
    another operation x2, other arithmetic, shards(): tile = jnp.stack([slot, elevation, potential, normal_flux])  1.81 us
  transfers between devices with their start and end apart: 8, of which 4 were waited for; matrix products, arithmetic and copies ran while one was open for 0% of the time, Pallas kernels for 32%

profile of v8, /device:TPU:0, one launch (start us, length us, event | category | flops | bytes accessed | tf_op | source)
XLA Modules:
  0.0 71.7 jit_solution(5844556122118854539)
XLA Ops:
  0.6 0.9 %convert_bitcast_fusion = f32[1,64,256]{2,1,0:T(8,128)S(1)} fusion(s32[64,256]{1,0:T(8,128)} %param.10, s32[64,256]{1,0:T(8,128)} %param.9), kind=kLoop, calls=%fused_computation.1 | loop fusion | flops 49152 | bytes 196608 | tf_op jit(solution)/shard_map/stack | solution.py:634
  1.5 0.9 %pad_maximum_fusion.refs_0_.refs_4_.tile = f32[4,64,256]{2,1,0:T(8,128)S(1)} fusion(f32[1,64,256]{2,1,0:T(8,128)} %bitcast.7, f32[1,64,256]{2,1,0:T(8,128)} %bitcast.8, f32[1,64,256]{2,1,0:T(8,128)} %bitcast.9, f32[1,64,256]{2,1,0:T(8,128)S(1)} %convert_bitcast_fusion), kind=kLoop, calls=%fused_computation | loop fusion | flops 196608 | bytes 524288 | tf_op jit(solution)/shard_map/stack | solution.py:634
  2.4 5.1 %collective-permute-start.1 = (f32[4,64,256]{2,1,0:T(8,128)S(1)}, f32[4,64,256]{2,1,0:T(8,128)S(1)}, u32[]{:S(2)}, u32[]{:S(2)}) collective-permute-start(f32[4,64,256]{2,1,0:T(8,128)S(1)} %pad_maximum_fusion.refs_0_.refs_4_.tile), channel_id=1, source_target_pairs={{0,3},{1,0},{2,1},{3,2},{4,7},{5,4},{6,5},{7,6},{8,11},{9,8},{10,9... | collective-permute-start | bytes 786440 | tf_op jit(solution)/shard_map/ppermute | solution.py:28
  7.6 1.6 %collective-permute-start = (f32[4,64,256]{2,1,0:T(8,128)S(1)}, f32[4,64,256]{2,1,0:T(8,128)S(1)}, u32[]{:S(2)}, u32[]{:S(2)}) collective-permute-start(f32[4,64,256]{2,1,0:T(8,128)S(1)} %pad_maximum_fusion.refs_0_.refs_4_.tile), channel_id=1, source_target_pairs={{0,28},{4,0},{8,4},{12,8},{16,12},{20,16},{24,20},{28,24},{1,29},{... | collective-permute-start | bytes 786440 | tf_op jit(solution)/shard_map/ppermute | solution.py:28
  9.2 0.7 copy-done
  9.9 1.6 %scatter_first.1 = (f32[384,256]{1,0:T(8,128)S(1)}, s32[16,128]{1,0:T(8,128)S(1)}) custom-call(f32[4,64,256]{2,1,0:T(8,128)S(1)} %pad_maximum_fusion.refs_0_.refs_4_.tile, s32[8,128]{1,0:T(8,128)S(1)} %bitcast.6), custom_call_target="tpu_custom_call" | custom-call | flops 1610612736 | bytes 1048576 | tf_op jit(solution)/shard_map/scatter_first/pallas_call | solution.py:167
  11.5 1.6 %collective-permute-done.1.refs_0_.ahead_y = f32[4,64,256]{2,1,0:T(8,128)S(1)} collective-permute-done((f32[4,64,256]{2,1,0:T(8,128)S(1)}, f32[4,64,256]{2,1,0:T(8,128)S(1)}, u32[]{:S(2)}, u32[]{:S(2)}) %collective-permute-start.1) | collective-permute-done | bytes 262176 | tf_op jit(solution)/shard_map/ppermute | solution.py:28
  13.1 1.0 %collective-permute-start.2 = (f32[4,64,256]{2,1,0:T(8,128)S(1)}, f32[4,64,256]{2,1,0:T(8,128)S(1)}, u32[]{:S(2)}, u32[]{:S(2)}) collective-permute-start(f32[4,64,256]{2,1,0:T(8,128)S(1)} %collective-permute-done.1.refs_0_.ahead_y), channel_id=1, source_target_pairs={{0,28},{4,0},{8,4},{12,8},{16,12},{20,16},{24,20},{28,24},{1,29},{... | collective-permute-start | bytes 786440 | tf_op jit(solution)/shard_map/ppermute | solution.py:28
  14.2 1.4 %scatter.2.refs_1_ = f32[384,256]{1,0:T(8,128)S(1)} custom-call(f32[4,64,256]{2,1,0:T(8,128)S(1)} %collective-permute-done.refs_0_.ahead_x, f32[384,256]{1,0:T(8,128)S(1)} %get-tuple-element.12.refs_1_), custom_call_target="tpu_custom_call" | custom-call | flops 1610612736 | bytes 1048576 | tf_op jit(solution)/shard_map/scatter/pallas_call | solution.py:167
  15.6 2.7 %scatter.3.refs_1_ = f32[384,256]{1,0:T(8,128)S(1)} custom-call(f32[4,64,256]{2,1,0:T(8,128)S(1)} %collective-permute-done.1.refs_0_.ahead_y, f32[384,256]{1,0:T(8,128)S(1)} %scatter.2.refs_1_), custom_call_target="tpu_custom_call" | custom-call | flops 1610612736 | bytes 1048576 | tf_op jit(solution)/shard_map/scatter/pallas_call | solution.py:167
  18.3 3.4 %scatter_last.1 = (f32[384,256]{1,0:T(8,128)}, f32[5,128,128]{2,1,0:T(8,128)S(1)}) custom-call(f32[4,64,256]{2,1,0:T(8,128)S(1)} %collective-permute-done.2.refs_0_, f32[384,256]{1,0:T(8,128)S(1)} %scatter.3.refs_1_), custom_call_target="tpu_custom_call" | custom-call | flops 1610612736 | bytes 1048576 | tf_op jit(solution)/shard_map/scatter_last/pallas_call | solution.py:167
  21.7 1.3 %collective-permute-start.4 = (f32[5,128,128]{2,1,0:T(8,128)S(1)}, f32[5,128,128]{2,1,0:T(8,128)S(1)}, u32[]{:S(2)}, u32[]{:S(2)}) collective-permute-start(f32[5,128,128]{2,1,0:T(8,128)S(1)} %get-tuple-element.13.refs_1_), channel_id=1, source_target_pairs={{1,0},{2,1},{3,2},{4,3},{5,4},{6,5},{7,6},{8,7},{9,8},{10,9},{11,1... | collective-permute-start | bytes 983048 | tf_op jit(solution)/shard_map/ppermute | solution.py:649
  23.0 4.6 %collective-permute-start.3 = (f32[5,128,128]{2,1,0:T(8,128)S(1)}, f32[5,128,128]{2,1,0:T(8,128)S(1)}, u32[]{:S(2)}, u32[]{:S(2)}) collective-permute-start(f32[5,128,128]{2,1,0:T(8,128)S(1)} %get-tuple-element.13.refs_1_), channel_id=1, source_target_pairs={{0,1},{1,2},{2,3},{3,4},{4,5},{5,6},{6,7},{7,8},{8,9},{9,10},{10,1... | collective-permute-start | bytes 983048 | tf_op jit(solution)/shard_map/ppermute | solution.py:648
  27.5 14.2 %near_own.1 = (f32[136,128]{1,0:T(8,128)S(1)}, bf16[129,128,32]{2,1,0:T(8,128)(2,1)S(1)}) custom-call(s32[16,128]{1,0:T(8,128)S(1)} %get-tuple-element.11.refs_0_, f32[5,128,128]{2,1,0:T(8,128)S(1)} %get-tuple-element.13.refs_1_), custom_call_target="tpu_custom_call" | custom-call | flops 2147483648 | bytes 1048576 | tf_op jit(solution)/shard_map/near_own/pallas_call | solution.py:428
  41.7 13.6 %near_other.1.table = f32[144,128]{1,0:T(8,128)S(1)} custom-call(s32[16,128]{1,0:T(8,128)S(1)} %get-tuple-element.11.refs_0_, f32[5,128,128]{2,1,0:T(8,128)S(1)} %get-tuple-element.13.refs_1_, f32[5,128,128]{2,1,0:T(8,128)S(1)} %collective-permute-done.3.refs_2_, f32[5,128,128]{2,1,0:T(8,128)S(1)} %collective-permute-done.4.refs_3_, ...), custom_call_target="tpu_custom_call" | custom-call | flops 2147483648 | bytes 1048576 | tf_op jit(solution)/shard_map/near_other/pallas_call | solution.py:447
  55.3 3.7 %collective-permute-start.5 = (f32[144,128]{1,0:T(8,128)S(1)}, f32[144,128]{1,0:T(8,128)S(1)}, u32[]{:S(2)}, u32[]{:S(2)}) collective-permute-start(f32[144,128]{1,0:T(8,128)S(1)} %near_other.1.table), channel_id=1, source_target_pairs={{0,4},{4,8},{8,12},{12,16},{16,20},{20,24},{24,28},{28,0},{1,5},{5... | collective-permute-start | bytes 221192 | tf_op jit(solution)/shard_map/ppermute | solution.py:28
  59.0 1.2 %collective-permute-start.7 = (f32[144,128]{1,0:T(8,128)S(1)}, f32[144,128]{1,0:T(8,128)S(1)}, u32[]{:S(2)}, u32[]{:S(2)}) collective-permute-start(f32[144,128]{1,0:T(8,128)S(1)} %near_other.1.table), channel_id=1, source_target_pairs={{0,5},{1,6},{2,7},{3,4},{4,9},{5,10},{6,11},{7,8},{8,13},{9,14},{1... | collective-permute-start | bytes 221192 | tf_op jit(solution)/shard_map/ppermute | solution.py:661
  60.2 0.7 %lookup_own.1.partial = f32[64,256]{1,0:T(8,128)S(1)} custom-call(f32[4,64,256]{2,1,0:T(8,128)S(1)} %pad_maximum_fusion.refs_0_.refs_4_.tile, f32[144,128]{1,0:T(8,128)S(1)} %near_other.1.table), custom_call_target="tpu_custom_call" | custom-call | flops 268435456 | bytes 524288 | tf_op jit(solution)/shard_map/lookup_own/pallas_call | solution.py:579
  61.0 1.1 %collective-permute-done.5.behind_x = f32[144,128]{1,0:T(8,128)S(1)} collective-permute-done((f32[144,128]{1,0:T(8,128)S(1)}, f32[144,128]{1,0:T(8,128)S(1)}, u32[]{:S(2)}, u32[]{:S(2)}) %collective-permute-start.5) | collective-permute-done | bytes 73760 | tf_op jit(solution)/shard_map/ppermute | solution.py:28
  62.1 0.8 %lookup_x.1 = (f32[64,256]{1,0:T(8,128)S(1)}, f32[2,64,256]{2,1,0:T(8,128)S(1)}) custom-call(f32[4,64,256]{2,1,0:T(8,128)S(1)} %pad_maximum_fusion.refs_0_.refs_4_.tile, f32[4,64,256]{2,1,0:T(8,128)S(1)} %collective-permute-done.refs_0_.ahead_x, f32[64,256]{1,0:T(8,128)S(1)} %lookup_own.1.partial, f32[144,128]{1,0:T(8,128)S(1)} %collective-permute-done.5.behind_x), custom_call_target="tpu_custom_call" | custom-call | flops 268435456 | bytes 524288 | tf_op jit(solution)/shard_map/lookup_x/pallas_call | solution.py:579
  62.9 4.1 %collective-permute-done.6.behind_y = f32[144,128]{1,0:T(8,128)S(1)} collective-permute-done((f32[144,128]{1,0:T(8,128)S(1)}, f32[144,128]{1,0:T(8,128)S(1)}, u32[]{:S(2)}, u32[]{:S(2)}) %collective-permute-start.6) | collective-permute-done | bytes 73760 | tf_op jit(solution)/shard_map/ppermute | solution.py:28
  67.0 1.7 %lookup_y.1 = (f32[64,256]{1,0:T(8,128)S(1)}, f32[2,64,256]{2,1,0:T(8,128)S(1)}) custom-call(f32[4,64,256]{2,1,0:T(8,128)S(1)} %pad_maximum_fusion.refs_0_.refs_4_.tile, f32[4,64,256]{2,1,0:T(8,128)S(1)} %collective-permute-done.1.refs_0_.ahead_y, f32[64,256]{1,0:T(8,128)S(1)} %get-tuple-element.17.partial, f32[144,128]{1,0:T(8,128)S(1)} %collective-permute-done.6.behind_y), custom_call_target="tpu_custom_call" | custom-call | flops 268435456 | bytes 524288 | tf_op jit(solution)/shard_map/lookup_y/pallas_call | solution.py:579
  68.7 1.1 %collective-permute-done.7.behind_xy = f32[144,128]{1,0:T(8,128)S(1)} collective-permute-done((f32[144,128]{1,0:T(8,128)S(1)}, f32[144,128]{1,0:T(8,128)S(1)}, u32[]{:S(2)}, u32[]{:S(2)}) %collective-permute-start.7) | collective-permute-done | bytes 73760 | tf_op jit(solution)/shard_map/ppermute | solution.py:661
  69.7 2.0 %lookup_xy.1 = (f32[64,256]{1,0:T(8,128)}, f32[64,256]{1,0:T(8,128)}) custom-call(f32[4,64,256]{2,1,0:T(8,128)S(1)} %pad_maximum_fusion.refs_0_.refs_4_.tile, f32[2,64,256]{2,1,0:T(8,128)S(1)} %get-tuple-element.16.row_slopes, f32[2,64,256]{2,1,0:T(8,128)S(1)} %get-tuple-element.18.col_slopes, f32[64,256]{1,0:T(8,128)S(1)} %get-tuple-element.19.partial, ...), custom_call_target="tpu_custom_call" | custom-call | flops 268435456 | bytes 524288 | tf_op jit(solution)/shard_map/lookup_xy/pallas_call | solution.py:579
  (6 shorter events, 0.0 us)
Async XLA Ops:
  2.4 10.7 %collective-permute-start.1 = (f32[4,64,256]{2,1,0:T(8,128)S(1)}, f32[4,64,256]{2,1,0:T(8,128)S(1)}, u32[]{:S(2)}, u32[]{:S(2)}) collective-permute-start(f32[4,64,256]{2,1,0:T(8,128)S(1)} %pad_maximum_fusion.refs_0_.refs_4_.tile), channel_id=1, source_target_pairs={{0,3},{1,0},{2,1},{3,2},{4,7},{5,4},{6,5},{7,6},{8,11},{9,8},{10,9... | collective-permute-start | bytes 786440 | tf_op jit(solution)/shard_map/ppermute | solution.py:28
  7.6 6.6 %collective-permute-start = (f32[4,64,256]{2,1,0:T(8,128)S(1)}, f32[4,64,256]{2,1,0:T(8,128)S(1)}, u32[]{:S(2)}, u32[]{:S(2)}) collective-permute-start(f32[4,64,256]{2,1,0:T(8,128)S(1)} %pad_maximum_fusion.refs_0_.refs_4_.tile), channel_id=1, source_target_pairs={{0,28},{4,0},{8,4},{12,8},{16,12},{20,16},{24,20},{28,24},{1,29},{... | collective-permute-start | bytes 786440 | tf_op jit(solution)/shard_map/ppermute | solution.py:28
  9.2 0.7 copy-start
  13.1 5.1 %collective-permute-start.2 = (f32[4,64,256]{2,1,0:T(8,128)S(1)}, f32[4,64,256]{2,1,0:T(8,128)S(1)}, u32[]{:S(2)}, u32[]{:S(2)}) collective-permute-start(f32[4,64,256]{2,1,0:T(8,128)S(1)} %collective-permute-done.1.refs_0_.ahead_y), channel_id=1, source_target_pairs={{0,28},{4,0},{8,4},{12,8},{16,12},{20,16},{24,20},{28,24},{1,29},{... | collective-permute-start | bytes 786440 | tf_op jit(solution)/shard_map/ppermute | solution.py:28
  21.7 20.0 %collective-permute-start.4 = (f32[5,128,128]{2,1,0:T(8,128)S(1)}, f32[5,128,128]{2,1,0:T(8,128)S(1)}, u32[]{:S(2)}, u32[]{:S(2)}) collective-permute-start(f32[5,128,128]{2,1,0:T(8,128)S(1)} %get-tuple-element.13.refs_1_), channel_id=1, source_target_pairs={{1,0},{2,1},{3,2},{4,3},{5,4},{6,5},{7,6},{8,7},{9,8},{10,9},{11,1... | collective-permute-start | bytes 983048 | tf_op jit(solution)/shard_map/ppermute | solution.py:649
  23.0 18.8 %collective-permute-start.3 = (f32[5,128,128]{2,1,0:T(8,128)S(1)}, f32[5,128,128]{2,1,0:T(8,128)S(1)}, u32[]{:S(2)}, u32[]{:S(2)}) collective-permute-start(f32[5,128,128]{2,1,0:T(8,128)S(1)} %get-tuple-element.13.refs_1_), channel_id=1, source_target_pairs={{0,1},{1,2},{2,3},{3,4},{4,5},{5,6},{6,7},{7,8},{8,9},{9,10},{10,1... | collective-permute-start | bytes 983048 | tf_op jit(solution)/shard_map/ppermute | solution.py:648
  55.3 6.8 %collective-permute-start.5 = (f32[144,128]{1,0:T(8,128)S(1)}, f32[144,128]{1,0:T(8,128)S(1)}, u32[]{:S(2)}, u32[]{:S(2)}) collective-permute-start(f32[144,128]{1,0:T(8,128)S(1)} %near_other.1.table), channel_id=1, source_target_pairs={{0,4},{4,8},{8,12},{12,16},{16,20},{20,24},{24,28},{28,0},{1,5},{5... | collective-permute-start | bytes 221192 | tf_op jit(solution)/shard_map/ppermute | solution.py:28
  59.0 8.0 %collective-permute-start.6 = (f32[144,128]{1,0:T(8,128)S(1)}, f32[144,128]{1,0:T(8,128)S(1)}, u32[]{:S(2)}, u32[]{:S(2)}) collective-permute-start(f32[144,128]{1,0:T(8,128)S(1)} %near_other.1.table), channel_id=1, source_target_pairs={{0,1},{1,2},{2,3},{3,0},{4,5},{5,6},{6,7},{7,4},{8,9},{9,10},{10,1... | collective-permute-start | bytes 221192 | tf_op jit(solution)/shard_map/ppermute | solution.py:28
  59.0 10.7 %collective-permute-start.7 = (f32[144,128]{1,0:T(8,128)S(1)}, f32[144,128]{1,0:T(8,128)S(1)}, u32[]{:S(2)}, u32[]{:S(2)}) collective-permute-start(f32[144,128]{1,0:T(8,128)S(1)} %near_other.1.table), channel_id=1, source_target_pairs={{0,5},{1,6},{2,7},{3,4},{4,9},{5,10},{6,11},{7,8},{8,13},{9,14},{1... | collective-permute-start | bytes 221192 | tf_op jit(solution)/shard_map/ppermute | solution.py:661

commit v9 on v8

--- a/solution.py
+++ b/solution.py
@@ -162,7 +162,7 @@
         out_shape.append(pltpu.VMEM((5, 2 * high_count, LANES), F32))
     if first:
         near, boxes = listed.shape
-        out_shape.append(jax.ShapeDtypeStruct(((near // 2 + near + 2 + 7) // 8 * 8, boxes), jnp.int32))
+        out_shape.append(jax.ShapeDtypeStruct(((2 * near + 7) // 8 * 8, boxes), jnp.int32))
     args = (tile, listed) if first else (tile, pinned(acc))
     out = pl.pallas_call(
         lambda *refs: scatter_kernel(
@@ -208,19 +208,23 @@
         left = left + 1 - step
     for j, v in enumerate(first + rest):
         plan[j : j + 1, :] = v
-    over = left > half
-    flags = jnp.broadcast_to(jnp.where(over, 1.0, 0.0), (8, boxes)).astype(BF16)
     down = lax.broadcasted_iota(jnp.int32, (boxes, boxes), 0)
     across = lax.broadcasted_iota(jnp.int32, (boxes, boxes), 1)
     before = jnp.where(down < across, 1.0, 0.0).astype(BF16)
-    offset = jnp.dot(flags, before, preferred_element_type=F32)[0:1, :]
-    count = jnp.dot(flags, jnp.ones((boxes, boxes), BF16), preferred_element_type=F32)[0:1, :]
-    hit = jnp.where((down.astype(F32) == offset) & over, 1.0, 0.0).astype(BF16)
     names = lax.broadcasted_iota(jnp.int32, (8, boxes), 1).astype(F32).astype(BF16)
-    found = lax.dot_general(names, hit, (((1,), (1,)), ((), ())), preferred_element_type=F32)[0:1, :]
-    count = count.astype(jnp.int32)
-    plan[half + near : half + near + 1, :] = jnp.where(across[0:1, :] < count, found.astype(jnp.int32), boxes)
-    plan[half + near + 1 : half + near + 2, :] = count
+    for pair in range(half // 2):
+        over = left > half + 2 * pair
+        flags = jnp.broadcast_to(jnp.where(over, 1.0, 0.0), (8, boxes)).astype(BF16)
+        offset = jnp.dot(flags, before, preferred_element_type=F32)[0:1, :]
+        count = jnp.dot(flags, jnp.ones((boxes, boxes), BF16), preferred_element_type=F32)[0:1, :]
+        hit = jnp.where((down.astype(F32) == offset) & over, 1.0, 0.0).astype(BF16)
+        found = lax.dot_general(
+            names, hit, (((1,), (1,)), ((), ())), preferred_element_type=F32
+        )[0:1, :].astype(jnp.int32)
+        count = count.astype(jnp.int32)
+        place = half + near + 2 * pair
+        plan[place : place + 1, :] = jnp.where(across[0:1, :] < count, found, boxes)
+        plan[place + 1 : place + 2, :] = count
 
 
 def pieces_of(ref, group):
@@ -300,11 +304,11 @@
     turned[boxes] = jnp.zeros((LANES, FEATURES), BF16)
 
     def turn(i, carry):
-        for u in range(8):
-            turned[8 * i + u] = strided(tfeat, 8 * i + u, USED).T.astype(BF16)
+        for u in range(16):
+            turned[16 * i + u] = strided(tfeat, 16 * i + u, USED).T.astype(BF16)
         return carry
 
-    lax.fori_loop(0, boxes // 8, turn, 0)
+    lax.fori_loop(0, boxes // 16, turn, 0)
 
 
 def run_items(target_of, source_of, half, iterations, turned, sfeat, sflux, sums, totals):
@@ -371,22 +375,36 @@
     half = near // 2
     sums[...] = sums_in[...]
     store_sources([lower, own, upper], sfeat, sflux)
-    items = boxes + plan[half + near + 1, 0]
-
-    def box_of(item):
-        extra = plan[half + near, jnp.clip(item - boxes, 0, boxes - 1)]
-        return jnp.where(item < boxes, item, extra)
-
-    def target_of(item):
-        return jnp.where(item < items, box_of(item), boxes)
-
-    def source_of(item, k):
-        row = jnp.where(item < boxes, half, 2 * half) + k
-        return plan[row, jnp.minimum(box_of(item), boxes - 1)]
-
-    iterations = (items + OTHER_GROUP - 1) // OTHER_GROUP
+
+    def main_target(item):
+        return jnp.clip(item, 0, boxes - 1)
+
+    def main_source(item, k):
+        return plan[half + k, main_target(item)]
+
     run_items(
-        target_of, source_of, half, iterations, turned, sfeat, sflux, sums, totals
+        main_target, main_source, half, boxes // OTHER_GROUP, turned, sfeat, sflux, sums, totals
+    )
+
+    counts = [plan[half + near + 2 * pair + 1, 0] for pair in range(half // 2)]
+
+    def extra(item):
+        box, row, start = jnp.int32(boxes), jnp.int32(2 * half), jnp.int32(0)
+        for pair, count in enumerate(counts):
+            inside = (item >= start) & (item < start + count)
+            name = plan[half + near + 2 * pair, jnp.clip(item - start, 0, boxes - 1)]
+            box = jnp.where(inside, name, box)
+            row = jnp.where(inside, 2 * half + 2 * pair, row)
+            start = start + count
+        return box, row
+
+    def extra_source(item, k):
+        box, row = extra(item)
+        return plan[row + k, jnp.minimum(box, boxes - 1)]
+
+    iterations = (sum(counts) + OTHER_GROUP - 1) // OTHER_GROUP
+    run_items(
+        lambda item: extra(item)[0], extra_source, 2, iterations, turned, sfeat, sflux, sums, totals
     )
     out[0:boxes, :] = sums[0:boxes, :] * (1.0 / math.sqrt(near * LANES))
 
@@ -422,7 +440,8 @@
 
 def near_own(plan, own, near):
     boxes = own.shape[1]
-    assert boxes == LANES and boxes % OWN_GROUP == 0 and near % 2 == 0
+    assert boxes == LANES and boxes % OWN_GROUP == 0 and near % 4 == 0
+    assert boxes % OTHER_GROUP == 0
     vmem = pl.BlockSpec(memory_space=pltpu.VMEM)
     smem = pl.BlockSpec(memory_space=pltpu.SMEM)
     return pl.pallas_call(

time: 72.2 us -> 69.7 us (0.965)
  waiting for transfers between devices: 7.92 us -> 6.28 us
  Pallas kernels: 42 us -> 41.2 us
    ppermute x1, waiting for transfers between devices: 1.06 us -> 0.01 us  [shards(): behind_xy = lax.ppermute(value, both, diagonal)]
  transfers between devices with their start and end apart: 8 -> 8, of which waited for: 4 -> 3; matrix products, arithmetic and copies ran while one was open for 0% -> 0% of each run, Pallas kernels for 32% -> 33%
where the time goes in v9:
time: 69.7 us; the launch traced here: 69.2 us
  Pallas kernels  41.2 us (59%)
  starting transfers between devices  18.5 us (27%)
  waiting for transfers between devices  6.28 us (9%)
  other arithmetic  1.81 us (3%)
  between operations  0.75 us (1%)
    pallas_call x1, Pallas kernels, near_own(): pl.pallas_call(lambda *refs: near_own_kernel(near, *refs), out_shape=(plt...  13.6 us
    pallas_call x1, Pallas kernels, near_other(): pl.pallas_call(lambda *refs: near_other_kernel(near, *refs), out_shape=pl...  13.3 us
    ppermute x5, starting transfers between devices, shifted(): return lax.ppermute(value, axis, pairs)  10.9 us
    pallas_call x4, Pallas kernels, scatter(): pl.pallas_call(lambda *refs: scatter_kernel(first, last, (rows, cols, hig...  9.12 us
    ppermute x5, waiting for transfers between devices, shifted(): return lax.ppermute(value, axis, pairs)  6.28 us
    pallas_call x4, Pallas kernels, lookup_call(): pl.pallas_call(kernel, out_shape=out_shape, in_specs=[vmem] * len(args),...  5.22 us
    ppermute x1, starting transfers between devices, shards(): lower = lax.ppermute(boxed, both, [(i, i + 1) for i in range(total - 1)])  4.57 us
    another operation x2, other arithmetic, shards(): tile = jnp.stack([slot, elevation, potential, normal_flux])  1.81 us
  transfers between devices with their start and end apart: 8, of which 3 were waited for; matrix products, arithmetic and copies ran while one was open for 0% of the time, Pallas kernels for 33%

profile of v9, /device:TPU:0, one launch (start us, length us, event | category | flops | bytes accessed | tf_op | source)
XLA Modules:
  0.0 69.2 jit_solution(11005773848550865095)
XLA Ops:
  0.6 0.9 %convert_bitcast_fusion = f32[1,64,256]{2,1,0:T(8,128)S(1)} fusion(s32[64,256]{1,0:T(8,128)} %param.10, s32[64,256]{1,0:T(8,128)} %param.9), kind=kLoop, calls=%fused_computation.1 | loop fusion | flops 49152 | bytes 196608 | tf_op jit(solution)/shard_map/stack | solution.py:653
  1.5 0.9 %pad_maximum_fusion.refs_0_.refs_4_.tile = f32[4,64,256]{2,1,0:T(8,128)S(1)} fusion(f32[1,64,256]{2,1,0:T(8,128)} %bitcast.7, f32[1,64,256]{2,1,0:T(8,128)} %bitcast.8, f32[1,64,256]{2,1,0:T(8,128)} %bitcast.9, f32[1,64,256]{2,1,0:T(8,128)S(1)} %convert_bitcast_fusion), kind=kLoop, calls=%fused_computation | loop fusion | flops 196608 | bytes 524288 | tf_op jit(solution)/shard_map/stack | solution.py:653
  2.4 5.1 %collective-permute-start.1 = (f32[4,64,256]{2,1,0:T(8,128)S(1)}, f32[4,64,256]{2,1,0:T(8,128)S(1)}, u32[]{:S(2)}, u32[]{:S(2)}) collective-permute-start(f32[4,64,256]{2,1,0:T(8,128)S(1)} %pad_maximum_fusion.refs_0_.refs_4_.tile), channel_id=1, source_target_pairs={{0,3},{1,0},{2,1},{3,2},{4,7},{5,4},{6,5},{7,6},{8,11},{9,8},{10,9... | collective-permute-start | bytes 786440 | tf_op jit(solution)/shard_map/ppermute | solution.py:28
  7.6 1.6 %collective-permute-start = (f32[4,64,256]{2,1,0:T(8,128)S(1)}, f32[4,64,256]{2,1,0:T(8,128)S(1)}, u32[]{:S(2)}, u32[]{:S(2)}) collective-permute-start(f32[4,64,256]{2,1,0:T(8,128)S(1)} %pad_maximum_fusion.refs_0_.refs_4_.tile), channel_id=1, source_target_pairs={{0,28},{4,0},{8,4},{12,8},{16,12},{20,16},{24,20},{28,24},{1,29},{... | collective-permute-start | bytes 786440 | tf_op jit(solution)/shard_map/ppermute | solution.py:28
  9.2 0.7 copy-done
  9.9 1.7 %scatter_first.1 = (f32[384,256]{1,0:T(8,128)S(1)}, s32[16,128]{1,0:T(8,128)S(1)}) custom-call(f32[4,64,256]{2,1,0:T(8,128)S(1)} %pad_maximum_fusion.refs_0_.refs_4_.tile, s32[8,128]{1,0:T(8,128)S(1)} %bitcast.6), custom_call_target="tpu_custom_call" | custom-call | flops 1610612736 | bytes 1048576 | tf_op jit(solution)/shard_map/scatter_first/pallas_call | solution.py:167
  11.5 1.6 %collective-permute-done.1.refs_0_.ahead_y = f32[4,64,256]{2,1,0:T(8,128)S(1)} collective-permute-done((f32[4,64,256]{2,1,0:T(8,128)S(1)}, f32[4,64,256]{2,1,0:T(8,128)S(1)}, u32[]{:S(2)}, u32[]{:S(2)}) %collective-permute-start.1) | collective-permute-done | bytes 262176 | tf_op jit(solution)/shard_map/ppermute | solution.py:28
  13.1 1.0 %collective-permute-start.2 = (f32[4,64,256]{2,1,0:T(8,128)S(1)}, f32[4,64,256]{2,1,0:T(8,128)S(1)}, u32[]{:S(2)}, u32[]{:S(2)}) collective-permute-start(f32[4,64,256]{2,1,0:T(8,128)S(1)} %collective-permute-done.1.refs_0_.ahead_y), channel_id=1, source_target_pairs={{0,28},{4,0},{8,4},{12,8},{16,12},{20,16},{24,20},{28,24},{1,29},{... | collective-permute-start | bytes 786440 | tf_op jit(solution)/shard_map/ppermute | solution.py:28
  14.2 0.0 collective-permute-done.refs_0_.ahead_x
  14.2 1.4 %scatter.2.refs_1_ = f32[384,256]{1,0:T(8,128)S(1)} custom-call(f32[4,64,256]{2,1,0:T(8,128)S(1)} %collective-permute-done.refs_0_.ahead_x, f32[384,256]{1,0:T(8,128)S(1)} %get-tuple-element.12.refs_1_), custom_call_target="tpu_custom_call" | custom-call | flops 1610612736 | bytes 1048576 | tf_op jit(solution)/shard_map/scatter/pallas_call | solution.py:167
  15.6 2.7 %scatter.3.refs_1_ = f32[384,256]{1,0:T(8,128)S(1)} custom-call(f32[4,64,256]{2,1,0:T(8,128)S(1)} %collective-permute-done.1.refs_0_.ahead_y, f32[384,256]{1,0:T(8,128)S(1)} %scatter.2.refs_1_), custom_call_target="tpu_custom_call" | custom-call | flops 1610612736 | bytes 1048576 | tf_op jit(solution)/shard_map/scatter/pallas_call | solution.py:167
  18.3 3.4 %scatter_last.1 = (f32[384,256]{1,0:T(8,128)}, f32[5,128,128]{2,1,0:T(8,128)S(1)}) custom-call(f32[4,64,256]{2,1,0:T(8,128)S(1)} %collective-permute-done.2.refs_0_, f32[384,256]{1,0:T(8,128)S(1)} %scatter.3.refs_1_), custom_call_target="tpu_custom_call" | custom-call | flops 1610612736 | bytes 1048576 | tf_op jit(solution)/shard_map/scatter_last/pallas_call | solution.py:167
  21.7 1.3 %collective-permute-start.4 = (f32[5,128,128]{2,1,0:T(8,128)S(1)}, f32[5,128,128]{2,1,0:T(8,128)S(1)}, u32[]{:S(2)}, u32[]{:S(2)}) collective-permute-start(f32[5,128,128]{2,1,0:T(8,128)S(1)} %get-tuple-element.13.refs_1_), channel_id=1, source_target_pairs={{1,0},{2,1},{3,2},{4,3},{5,4},{6,5},{7,6},{8,7},{9,8},{10,9},{11,1... | collective-permute-start | bytes 983048 | tf_op jit(solution)/shard_map/ppermute | solution.py:668
  23.0 4.6 %collective-permute-start.3 = (f32[5,128,128]{2,1,0:T(8,128)S(1)}, f32[5,128,128]{2,1,0:T(8,128)S(1)}, u32[]{:S(2)}, u32[]{:S(2)}) collective-permute-start(f32[5,128,128]{2,1,0:T(8,128)S(1)} %get-tuple-element.13.refs_1_), channel_id=1, source_target_pairs={{0,1},{1,2},{2,3},{3,4},{4,5},{5,6},{6,7},{7,8},{8,9},{9,10},{10,1... | collective-permute-start | bytes 983048 | tf_op jit(solution)/shard_map/ppermute | solution.py:667
  27.5 13.6 %near_own.1 = (f32[136,128]{1,0:T(8,128)S(1)}, bf16[129,128,32]{2,1,0:T(8,128)(2,1)S(1)}) custom-call(s32[16,128]{1,0:T(8,128)S(1)} %get-tuple-element.11.refs_0_, f32[5,128,128]{2,1,0:T(8,128)S(1)} %get-tuple-element.13.refs_1_), custom_call_target="tpu_custom_call" | custom-call | flops 2147483648 | bytes 1048576 | tf_op jit(solution)/shard_map/near_own/pallas_call | solution.py:447
  41.2 13.3 %near_other.1.table = f32[144,128]{1,0:T(8,128)S(1)} custom-call(s32[16,128]{1,0:T(8,128)S(1)} %get-tuple-element.11.refs_0_, f32[5,128,128]{2,1,0:T(8,128)S(1)} %get-tuple-element.13.refs_1_, f32[5,128,128]{2,1,0:T(8,128)S(1)} %collective-permute-done.3.refs_2_, f32[5,128,128]{2,1,0:T(8,128)S(1)} %collective-permute-done.4.refs_3_, ...), custom_call_target="tpu_custom_call" | custom-call | flops 2147483648 | bytes 1048576 | tf_op jit(solution)/shard_map/near_other/pallas_call | solution.py:466
  54.5 3.1 %collective-permute-start.5 = (f32[144,128]{1,0:T(8,128)S(1)}, f32[144,128]{1,0:T(8,128)S(1)}, u32[]{:S(2)}, u32[]{:S(2)}) collective-permute-start(f32[144,128]{1,0:T(8,128)S(1)} %near_other.1.table), channel_id=1, source_target_pairs={{0,4},{4,8},{8,12},{12,16},{16,20},{20,24},{24,28},{28,0},{1,5},{5... | collective-permute-start | bytes 221192 | tf_op jit(solution)/shard_map/ppermute | solution.py:28
  57.6 1.7 %collective-permute-start.7 = (f32[144,128]{1,0:T(8,128)S(1)}, f32[144,128]{1,0:T(8,128)S(1)}, u32[]{:S(2)}, u32[]{:S(2)}) collective-permute-start(f32[144,128]{1,0:T(8,128)S(1)} %near_other.1.table), channel_id=1, source_target_pairs={{0,5},{1,6},{2,7},{3,4},{4,9},{5,10},{6,11},{7,8},{8,13},{9,14},{1... | collective-permute-start | bytes 221192 | tf_op jit(solution)/shard_map/ppermute | solution.py:680
  59.3 0.7 %lookup_own.1.partial = f32[64,256]{1,0:T(8,128)S(1)} custom-call(f32[4,64,256]{2,1,0:T(8,128)S(1)} %pad_maximum_fusion.refs_0_.refs_4_.tile, f32[144,128]{1,0:T(8,128)S(1)} %near_other.1.table), custom_call_target="tpu_custom_call" | custom-call | flops 268435456 | bytes 524288 | tf_op jit(solution)/shard_map/lookup_own/pallas_call | solution.py:598
  60.1 0.6 collective-permute-done.5.behind_x
  60.6 0.8 %lookup_x.1 = (f32[64,256]{1,0:T(8,128)S(1)}, f32[2,64,256]{2,1,0:T(8,128)S(1)}) custom-call(f32[4,64,256]{2,1,0:T(8,128)S(1)} %pad_maximum_fusion.refs_0_.refs_4_.tile, f32[4,64,256]{2,1,0:T(8,128)S(1)} %collective-permute-done.refs_0_.ahead_x, f32[64,256]{1,0:T(8,128)S(1)} %lookup_own.1.partial, f32[144,128]{1,0:T(8,128)S(1)} %collective-permute-done.5.behind_x), custom_call_target="tpu_custom_call" | custom-call | flops 268435456 | bytes 524288 | tf_op jit(solution)/shard_map/lookup_x/pallas_call | solution.py:598
  61.5 4.1 %collective-permute-done.6.behind_y = f32[144,128]{1,0:T(8,128)S(1)} collective-permute-done((f32[144,128]{1,0:T(8,128)S(1)}, f32[144,128]{1,0:T(8,128)S(1)}, u32[]{:S(2)}, u32[]{:S(2)}) %collective-permute-start.6) | collective-permute-done | bytes 73760 | tf_op jit(solution)/shard_map/ppermute | solution.py:28
  65.5 1.7 %lookup_y.1 = (f32[64,256]{1,0:T(8,128)S(1)}, f32[2,64,256]{2,1,0:T(8,128)S(1)}) custom-call(f32[4,64,256]{2,1,0:T(8,128)S(1)} %pad_maximum_fusion.refs_0_.refs_4_.tile, f32[4,64,256]{2,1,0:T(8,128)S(1)} %collective-permute-done.1.refs_0_.ahead_y, f32[64,256]{1,0:T(8,128)S(1)} %get-tuple-element.17.partial, f32[144,128]{1,0:T(8,128)S(1)} %collective-permute-done.6.behind_y), custom_call_target="tpu_custom_call" | custom-call | flops 268435456 | bytes 524288 | tf_op jit(solution)/shard_map/lookup_y/pallas_call | solution.py:598
  67.2 2.0 %lookup_xy.1 = (f32[64,256]{1,0:T(8,128)}, f32[64,256]{1,0:T(8,128)}) custom-call(f32[4,64,256]{2,1,0:T(8,128)S(1)} %pad_maximum_fusion.refs_0_.refs_4_.tile, f32[2,64,256]{2,1,0:T(8,128)S(1)} %get-tuple-element.16.row_slopes, f32[2,64,256]{2,1,0:T(8,128)S(1)} %get-tuple-element.18.col_slopes, f32[64,256]{1,0:T(8,128)S(1)} %get-tuple-element.19.partial, ...), custom_call_target="tpu_custom_call" | custom-call | flops 268435456 | bytes 524288 | tf_op jit(solution)/shard_map/lookup_xy/pallas_call | solution.py:598
  (6 shorter events, 0.0 us)
Async XLA Ops:
  2.4 10.7 %collective-permute-start.1 = (f32[4,64,256]{2,1,0:T(8,128)S(1)}, f32[4,64,256]{2,1,0:T(8,128)S(1)}, u32[]{:S(2)}, u32[]{:S(2)}) collective-permute-start(f32[4,64,256]{2,1,0:T(8,128)S(1)} %pad_maximum_fusion.refs_0_.refs_4_.tile), channel_id=1, source_target_pairs={{0,3},{1,0},{2,1},{3,2},{4,7},{5,4},{6,5},{7,6},{8,11},{9,8},{10,9... | collective-permute-start | bytes 786440 | tf_op jit(solution)/shard_map/ppermute | solution.py:28
  7.6 6.6 %collective-permute-start = (f32[4,64,256]{2,1,0:T(8,128)S(1)}, f32[4,64,256]{2,1,0:T(8,128)S(1)}, u32[]{:S(2)}, u32[]{:S(2)}) collective-permute-start(f32[4,64,256]{2,1,0:T(8,128)S(1)} %pad_maximum_fusion.refs_0_.refs_4_.tile), channel_id=1, source_target_pairs={{0,28},{4,0},{8,4},{12,8},{16,12},{20,16},{24,20},{28,24},{1,29},{... | collective-permute-start | bytes 786440 | tf_op jit(solution)/shard_map/ppermute | solution.py:28
  9.2 0.7 copy-start
  13.1 5.1 %collective-permute-start.2 = (f32[4,64,256]{2,1,0:T(8,128)S(1)}, f32[4,64,256]{2,1,0:T(8,128)S(1)}, u32[]{:S(2)}, u32[]{:S(2)}) collective-permute-start(f32[4,64,256]{2,1,0:T(8,128)S(1)} %collective-permute-done.1.refs_0_.ahead_y), channel_id=1, source_target_pairs={{0,28},{4,0},{8,4},{12,8},{16,12},{20,16},{24,20},{28,24},{1,29},{... | collective-permute-start | bytes 786440 | tf_op jit(solution)/shard_map/ppermute | solution.py:28
  21.7 19.5 %collective-permute-start.4 = (f32[5,128,128]{2,1,0:T(8,128)S(1)}, f32[5,128,128]{2,1,0:T(8,128)S(1)}, u32[]{:S(2)}, u32[]{:S(2)}) collective-permute-start(f32[5,128,128]{2,1,0:T(8,128)S(1)} %get-tuple-element.13.refs_1_), channel_id=1, source_target_pairs={{1,0},{2,1},{3,2},{4,3},{5,4},{6,5},{7,6},{8,7},{9,8},{10,9},{11,1... | collective-permute-start | bytes 983048 | tf_op jit(solution)/shard_map/ppermute | solution.py:668
  23.0 18.2 %collective-permute-start.3 = (f32[5,128,128]{2,1,0:T(8,128)S(1)}, f32[5,128,128]{2,1,0:T(8,128)S(1)}, u32[]{:S(2)}, u32[]{:S(2)}) collective-permute-start(f32[5,128,128]{2,1,0:T(8,128)S(1)} %get-tuple-element.13.refs_1_), channel_id=1, source_target_pairs={{0,1},{1,2},{2,3},{3,4},{4,5},{5,6},{6,7},{7,8},{8,9},{9,10},{10,1... | collective-permute-start | bytes 983048 | tf_op jit(solution)/shard_map/ppermute | solution.py:667
  54.5 6.2 %collective-permute-start.5 = (f32[144,128]{1,0:T(8,128)S(1)}, f32[144,128]{1,0:T(8,128)S(1)}, u32[]{:S(2)}, u32[]{:S(2)}) collective-permute-start(f32[144,128]{1,0:T(8,128)S(1)} %near_other.1.table), channel_id=1, source_target_pairs={{0,4},{4,8},{8,12},{12,16},{16,20},{20,24},{24,28},{28,0},{1,5},{5... | collective-permute-start | bytes 221192 | tf_op jit(solution)/shard_map/ppermute | solution.py:28
  57.6 7.9 %collective-permute-start.6 = (f32[144,128]{1,0:T(8,128)S(1)}, f32[144,128]{1,0:T(8,128)S(1)}, u32[]{:S(2)}, u32[]{:S(2)}) collective-permute-start(f32[144,128]{1,0:T(8,128)S(1)} %near_other.1.table), channel_id=1, source_target_pairs={{0,1},{1,2},{2,3},{3,0},{4,5},{5,6},{6,7},{7,4},{8,9},{9,10},{10,1... | collective-permute-start | bytes 221192 | tf_op jit(solution)/shard_map/ppermute | solution.py:28
  57.6 9.6 %collective-permute-start.7 = (f32[144,128]{1,0:T(8,128)S(1)}, f32[144,128]{1,0:T(8,128)S(1)}, u32[]{:S(2)}, u32[]{:S(2)}) collective-permute-start(f32[144,128]{1,0:T(8,128)S(1)} %near_other.1.table), channel_id=1, source_target_pairs={{0,5},{1,6},{2,7},{3,4},{4,9},{5,10},{6,11},{7,8},{8,13},{9,14},{1... | collective-permute-start | bytes 221192 | tf_op jit(solution)/shard_map/ppermute | solution.py:680

commit v10 on v9

--- a/solution.py
+++ b/solution.py
@@ -672,12 +672,7 @@
 
     behind_x = shifted(value, "tx", 1)
     behind_y = shifted(value, "ty", 1)
-    diagonal = [
-        (i * count_ty + j, (i + 1) % count_tx * count_ty + (j + 1) % count_ty)
-        for i in range(count_tx)
-        for j in range(count_ty)
-    ]
-    behind_xy = lax.ppermute(value, both, diagonal)
+    behind_xy = shifted(behind_y, "tx", 1)
     return look_up_all(tile, ahead_x, ahead_y, value, behind_x, behind_y, behind_xy)
 
 

time: 69.7 us -> 71.3 us (1.023); the launches traced: 69.2 us -> 70.1 us
  waiting for transfers between devices: 6.28 us -> 8.24 us
  starting transfers between devices: 18.5 us -> 17.4 us
    ppermute x5 -> x6, waiting for transfers between devices: 6.28 us -> 8.23 us  [shifted(): return lax.ppermute(value, axis, pairs)]
    ppermute x1 -> x0, starting transfers between devices: 1.72 us -> none  [shards(): behind_xy = lax.ppermute(value, both, diagonal)]
    ppermute x5 -> x6, starting transfers between devices: 10.9 us -> 11.5 us  [shifted(): return lax.ppermute(value, axis, pairs)]
  transfers between devices with their start and end apart: 8 -> 8, of which waited for: 3 -> 3; matrix products, arithmetic and copies ran while one was open for 0% -> 0% of each run, Pallas kernels for 33% -> 32%
where the time goes in v10:
time: 71.3 us; the launch traced here: 70.1 us
  Pallas kernels  41.2 us (58%)
  starting transfers between devices  17.4 us (24%)
  waiting for transfers between devices  8.24 us (12%)
  other arithmetic  1.81 us (3%)
  between operations  0.75 us (1%)
    pallas_call x1, Pallas kernels, near_own(): pl.pallas_call(lambda *refs: near_own_kernel(near, *refs), out_shape=(plt...  13.6 us
    pallas_call x1, Pallas kernels, near_other(): pl.pallas_call(lambda *refs: near_other_kernel(near, *refs), out_shape=pl...  13.3 us
    ppermute x6, starting transfers between devices, shifted(): return lax.ppermute(value, axis, pairs)  11.5 us
    pallas_call x4, Pallas kernels, scatter(): pl.pallas_call(lambda *refs: scatter_kernel(first, last, (rows, cols, hig...  9.12 us
    ppermute x6, waiting for transfers between devices, shifted(): return lax.ppermute(value, axis, pairs)  8.23 us
    pallas_call x4, Pallas kernels, lookup_call(): pl.pallas_call(kernel, out_shape=out_shape, in_specs=[vmem] * len(args),...  5.23 us
    ppermute x1, starting transfers between devices, shards(): lower = lax.ppermute(boxed, both, [(i, i + 1) for i in range(total - 1)])  4.57 us
    another operation x2, other arithmetic, shards(): tile = jnp.stack([slot, elevation, potential, normal_flux])  1.81 us
  transfers between devices with their start and end apart: 8, of which 3 were waited for; matrix products, arithmetic and copies ran while one was open for 0% of the time, Pallas kernels for 32%

profile of v10, /device:TPU:0, one launch (start us, length us, event | category | flops | bytes accessed | tf_op | source)
XLA Modules:
  0.0 70.1 jit_solution(12290932570030693490)
XLA Ops:
  0.6 0.9 %convert_bitcast_fusion = f32[1,64,256]{2,1,0:T(8,128)S(1)} fusion(s32[64,256]{1,0:T(8,128)} %param.10, s32[64,256]{1,0:T(8,128)} %param.9), kind=kLoop, calls=%fused_computation.1 | loop fusion | flops 49152 | bytes 196608 | tf_op jit(solution)/shard_map/stack | solution.py:653
  1.5 0.9 %pad_maximum_fusion.refs_0_.refs_4_.tile = f32[4,64,256]{2,1,0:T(8,128)S(1)} fusion(f32[1,64,256]{2,1,0:T(8,128)} %bitcast.7, f32[1,64,256]{2,1,0:T(8,128)} %bitcast.8, f32[1,64,256]{2,1,0:T(8,128)} %bitcast.9, f32[1,64,256]{2,1,0:T(8,128)S(1)} %convert_bitcast_fusion), kind=kLoop, calls=%fused_computation | loop fusion | flops 196608 | bytes 524288 | tf_op jit(solution)/shard_map/stack | solution.py:653
  2.4 5.1 %collective-permute-start.1 = (f32[4,64,256]{2,1,0:T(8,128)S(1)}, f32[4,64,256]{2,1,0:T(8,128)S(1)}, u32[]{:S(2)}, u32[]{:S(2)}) collective-permute-start(f32[4,64,256]{2,1,0:T(8,128)S(1)} %pad_maximum_fusion.refs_0_.refs_4_.tile), channel_id=1, source_target_pairs={{0,3},{1,0},{2,1},{3,2},{4,7},{5,4},{6,5},{7,6},{8,11},{9,8},{10,9... | collective-permute-start | bytes 786440 | tf_op jit(solution)/shard_map/ppermute | solution.py:28
  7.6 1.6 %collective-permute-start = (f32[4,64,256]{2,1,0:T(8,128)S(1)}, f32[4,64,256]{2,1,0:T(8,128)S(1)}, u32[]{:S(2)}, u32[]{:S(2)}) collective-permute-start(f32[4,64,256]{2,1,0:T(8,128)S(1)} %pad_maximum_fusion.refs_0_.refs_4_.tile), channel_id=1, source_target_pairs={{0,28},{4,0},{8,4},{12,8},{16,12},{20,16},{24,20},{28,24},{1,29},{... | collective-permute-start | bytes 786440 | tf_op jit(solution)/shard_map/ppermute | solution.py:28
  9.2 0.7 copy-done
  9.9 1.7 %scatter_first.1 = (f32[384,256]{1,0:T(8,128)S(1)}, s32[16,128]{1,0:T(8,128)S(1)}) custom-call(f32[4,64,256]{2,1,0:T(8,128)S(1)} %pad_maximum_fusion.refs_0_.refs_4_.tile, s32[8,128]{1,0:T(8,128)S(1)} %bitcast.6), custom_call_target="tpu_custom_call" | custom-call | flops 1610612736 | bytes 1048576 | tf_op jit(solution)/shard_map/scatter_first/pallas_call | solution.py:167
  11.5 1.6 %collective-permute-done.1.refs_0_.ahead_y = f32[4,64,256]{2,1,0:T(8,128)S(1)} collective-permute-done((f32[4,64,256]{2,1,0:T(8,128)S(1)}, f32[4,64,256]{2,1,0:T(8,128)S(1)}, u32[]{:S(2)}, u32[]{:S(2)}) %collective-permute-start.1) | collective-permute-done | bytes 262176 | tf_op jit(solution)/shard_map/ppermute | solution.py:28
  13.1 1.0 %collective-permute-start.2 = (f32[4,64,256]{2,1,0:T(8,128)S(1)}, f32[4,64,256]{2,1,0:T(8,128)S(1)}, u32[]{:S(2)}, u32[]{:S(2)}) collective-permute-start(f32[4,64,256]{2,1,0:T(8,128)S(1)} %collective-permute-done.1.refs_0_.ahead_y), channel_id=1, source_target_pairs={{0,28},{4,0},{8,4},{12,8},{16,12},{20,16},{24,20},{28,24},{1,29},{... | collective-permute-start | bytes 786440 | tf_op jit(solution)/shard_map/ppermute | solution.py:28
  14.2 1.4 %scatter.2.refs_1_ = f32[384,256]{1,0:T(8,128)S(1)} custom-call(f32[4,64,256]{2,1,0:T(8,128)S(1)} %collective-permute-done.refs_0_.ahead_x, f32[384,256]{1,0:T(8,128)S(1)} %get-tuple-element.12.refs_1_), custom_call_target="tpu_custom_call" | custom-call | flops 1610612736 | bytes 1048576 | tf_op jit(solution)/shard_map/scatter/pallas_call | solution.py:167
  15.6 2.7 %scatter.3.refs_1_ = f32[384,256]{1,0:T(8,128)S(1)} custom-call(f32[4,64,256]{2,1,0:T(8,128)S(1)} %collective-permute-done.1.refs_0_.ahead_y, f32[384,256]{1,0:T(8,128)S(1)} %scatter.2.refs_1_), custom_call_target="tpu_custom_call" | custom-call | flops 1610612736 | bytes 1048576 | tf_op jit(solution)/shard_map/scatter/pallas_call | solution.py:167
  18.3 3.4 %scatter_last.1 = (f32[384,256]{1,0:T(8,128)}, f32[5,128,128]{2,1,0:T(8,128)S(1)}) custom-call(f32[4,64,256]{2,1,0:T(8,128)S(1)} %collective-permute-done.2.refs_0_, f32[384,256]{1,0:T(8,128)S(1)} %scatter.3.refs_1_), custom_call_target="tpu_custom_call" | custom-call | flops 1610612736 | bytes 1048576 | tf_op jit(solution)/shard_map/scatter_last/pallas_call | solution.py:167
  21.7 1.3 %collective-permute-start.4 = (f32[5,128,128]{2,1,0:T(8,128)S(1)}, f32[5,128,128]{2,1,0:T(8,128)S(1)}, u32[]{:S(2)}, u32[]{:S(2)}) collective-permute-start(f32[5,128,128]{2,1,0:T(8,128)S(1)} %get-tuple-element.13.refs_1_), channel_id=1, source_target_pairs={{1,0},{2,1},{3,2},{4,3},{5,4},{6,5},{7,6},{8,7},{9,8},{10,9},{11,1... | collective-permute-start | bytes 983048 | tf_op jit(solution)/shard_map/ppermute | solution.py:668
  23.0 4.6 %collective-permute-start.3 = (f32[5,128,128]{2,1,0:T(8,128)S(1)}, f32[5,128,128]{2,1,0:T(8,128)S(1)}, u32[]{:S(2)}, u32[]{:S(2)}) collective-permute-start(f32[5,128,128]{2,1,0:T(8,128)S(1)} %get-tuple-element.13.refs_1_), channel_id=1, source_target_pairs={{0,1},{1,2},{2,3},{3,4},{4,5},{5,6},{6,7},{7,8},{8,9},{9,10},{10,1... | collective-permute-start | bytes 983048 | tf_op jit(solution)/shard_map/ppermute | solution.py:667
  27.5 13.6 %near_own.1 = (f32[136,128]{1,0:T(8,128)S(1)}, bf16[129,128,32]{2,1,0:T(8,128)(2,1)S(1)}) custom-call(s32[16,128]{1,0:T(8,128)S(1)} %get-tuple-element.11.refs_0_, f32[5,128,128]{2,1,0:T(8,128)S(1)} %get-tuple-element.13.refs_1_), custom_call_target="tpu_custom_call" | custom-call | flops 2147483648 | bytes 1048576 | tf_op jit(solution)/shard_map/near_own/pallas_call | solution.py:447
  41.2 13.3 %near_other.1.table = f32[144,128]{1,0:T(8,128)S(1)} custom-call(s32[16,128]{1,0:T(8,128)S(1)} %get-tuple-element.11.refs_0_, f32[5,128,128]{2,1,0:T(8,128)S(1)} %get-tuple-element.13.refs_1_, f32[5,128,128]{2,1,0:T(8,128)S(1)} %collective-permute-done.3.refs_2_, f32[5,128,128]{2,1,0:T(8,128)S(1)} %collective-permute-done.4.refs_3_, ...), custom_call_target="tpu_custom_call" | custom-call | flops 2147483648 | bytes 1048576 | tf_op jit(solution)/shard_map/near_other/pallas_call | solution.py:466
  54.5 1.2 %collective-permute-start.6 = (f32[144,128]{1,0:T(8,128)S(1)}, f32[144,128]{1,0:T(8,128)S(1)}, u32[]{:S(2)}, u32[]{:S(2)}) collective-permute-start(f32[144,128]{1,0:T(8,128)S(1)} %near_other.1.table), channel_id=1, source_target_pairs={{0,1},{1,2},{2,3},{3,0},{4,5},{5,6},{6,7},{7,4},{8,9},{9,10},{10,1... | collective-permute-start | bytes 221192 | tf_op jit(solution)/shard_map/ppermute | solution.py:28
  55.7 2.0 %collective-permute-start.5 = (f32[144,128]{1,0:T(8,128)S(1)}, f32[144,128]{1,0:T(8,128)S(1)}, u32[]{:S(2)}, u32[]{:S(2)}) collective-permute-start(f32[144,128]{1,0:T(8,128)S(1)} %near_other.1.table), channel_id=1, source_target_pairs={{0,4},{4,8},{8,12},{12,16},{16,20},{20,24},{24,28},{28,0},{1,5},{5... | collective-permute-start | bytes 221192 | tf_op jit(solution)/shard_map/ppermute | solution.py:28
  57.7 5.7 %collective-permute-done.6.behind_y = f32[144,128]{1,0:T(8,128)S(1)} collective-permute-done((f32[144,128]{1,0:T(8,128)S(1)}, f32[144,128]{1,0:T(8,128)S(1)}, u32[]{:S(2)}, u32[]{:S(2)}) %collective-permute-start.6) | collective-permute-done | bytes 73760 | tf_op jit(solution)/shard_map/ppermute | solution.py:28
  63.4 0.5 collective-permute-start.7
  64.0 0.7 %lookup_own.1.partial = f32[64,256]{1,0:T(8,128)S(1)} custom-call(f32[4,64,256]{2,1,0:T(8,128)S(1)} %pad_maximum_fusion.refs_0_.refs_4_.tile, f32[144,128]{1,0:T(8,128)S(1)} %near_other.1.table), custom_call_target="tpu_custom_call" | custom-call | flops 268435456 | bytes 524288 | tf_op jit(solution)/shard_map/lookup_own/pallas_call | solution.py:598
  64.7 0.8 %lookup_x.1 = (f32[64,256]{1,0:T(8,128)S(1)}, f32[2,64,256]{2,1,0:T(8,128)S(1)}) custom-call(f32[4,64,256]{2,1,0:T(8,128)S(1)} %pad_maximum_fusion.refs_0_.refs_4_.tile, f32[4,64,256]{2,1,0:T(8,128)S(1)} %collective-permute-done.refs_0_.ahead_x, f32[64,256]{1,0:T(8,128)S(1)} %lookup_own.1.partial, f32[144,128]{1,0:T(8,128)S(1)} %collective-permute-done.5.behind_x), custom_call_target="tpu_custom_call" | custom-call | flops 268435456 | bytes 524288 | tf_op jit(solution)/shard_map/lookup_x/pallas_call | solution.py:598
  65.5 1.7 %lookup_y.1 = (f32[64,256]{1,0:T(8,128)S(1)}, f32[2,64,256]{2,1,0:T(8,128)S(1)}) custom-call(f32[4,64,256]{2,1,0:T(8,128)S(1)} %pad_maximum_fusion.refs_0_.refs_4_.tile, f32[4,64,256]{2,1,0:T(8,128)S(1)} %collective-permute-done.1.refs_0_.ahead_y, f32[64,256]{1,0:T(8,128)S(1)} %get-tuple-element.17.partial, f32[144,128]{1,0:T(8,128)S(1)} %collective-permute-done.6.behind_y), custom_call_target="tpu_custom_call" | custom-call | flops 268435456 | bytes 524288 | tf_op jit(solution)/shard_map/lookup_y/pallas_call | solution.py:598
  67.2 0.9 %collective-permute-done.7.behind_xy = f32[144,128]{1,0:T(8,128)S(1)} collective-permute-done((f32[144,128]{1,0:T(8,128)S(1)}, f32[144,128]{1,0:T(8,128)S(1)}, u32[]{:S(2)}, u32[]{:S(2)}) %collective-permute-start.7) | collective-permute-done | bytes 73760 | tf_op jit(solution)/shard_map/ppermute | solution.py:28
  68.1 2.0 %lookup_xy.1 = (f32[64,256]{1,0:T(8,128)}, f32[64,256]{1,0:T(8,128)}) custom-call(f32[4,64,256]{2,1,0:T(8,128)S(1)} %pad_maximum_fusion.refs_0_.refs_4_.tile, f32[2,64,256]{2,1,0:T(8,128)S(1)} %get-tuple-element.16.row_slopes, f32[2,64,256]{2,1,0:T(8,128)S(1)} %get-tuple-element.18.col_slopes, f32[64,256]{1,0:T(8,128)S(1)} %get-tuple-element.19.partial, ...), custom_call_target="tpu_custom_call" | custom-call | flops 268435456 | bytes 524288 | tf_op jit(solution)/shard_map/lookup_xy/pallas_call | solution.py:598
  (6 shorter events, 0.0 us)
Async XLA Ops:
  2.4 10.7 %collective-permute-start.1 = (f32[4,64,256]{2,1,0:T(8,128)S(1)}, f32[4,64,256]{2,1,0:T(8,128)S(1)}, u32[]{:S(2)}, u32[]{:S(2)}) collective-permute-start(f32[4,64,256]{2,1,0:T(8,128)S(1)} %pad_maximum_fusion.refs_0_.refs_4_.tile), channel_id=1, source_target_pairs={{0,3},{1,0},{2,1},{3,2},{4,7},{5,4},{6,5},{7,6},{8,11},{9,8},{10,9... | collective-permute-start | bytes 786440 | tf_op jit(solution)/shard_map/ppermute | solution.py:28
  7.6 6.6 %collective-permute-start = (f32[4,64,256]{2,1,0:T(8,128)S(1)}, f32[4,64,256]{2,1,0:T(8,128)S(1)}, u32[]{:S(2)}, u32[]{:S(2)}) collective-permute-start(f32[4,64,256]{2,1,0:T(8,128)S(1)} %pad_maximum_fusion.refs_0_.refs_4_.tile), channel_id=1, source_target_pairs={{0,28},{4,0},{8,4},{12,8},{16,12},{20,16},{24,20},{28,24},{1,29},{... | collective-permute-start | bytes 786440 | tf_op jit(solution)/shard_map/ppermute | solution.py:28
  9.2 0.7 copy-start
  13.1 5.1 %collective-permute-start.2 = (f32[4,64,256]{2,1,0:T(8,128)S(1)}, f32[4,64,256]{2,1,0:T(8,128)S(1)}, u32[]{:S(2)}, u32[]{:S(2)}) collective-permute-start(f32[4,64,256]{2,1,0:T(8,128)S(1)} %collective-permute-done.1.refs_0_.ahead_y), channel_id=1, source_target_pairs={{0,28},{4,0},{8,4},{12,8},{16,12},{20,16},{24,20},{28,24},{1,29},{... | collective-permute-start | bytes 786440 | tf_op jit(solution)/shard_map/ppermute | solution.py:28
  21.7 19.5 %collective-permute-start.4 = (f32[5,128,128]{2,1,0:T(8,128)S(1)}, f32[5,128,128]{2,1,0:T(8,128)S(1)}, u32[]{:S(2)}, u32[]{:S(2)}) collective-permute-start(f32[5,128,128]{2,1,0:T(8,128)S(1)} %get-tuple-element.13.refs_1_), channel_id=1, source_target_pairs={{1,0},{2,1},{3,2},{4,3},{5,4},{6,5},{7,6},{8,7},{9,8},{10,9},{11,1... | collective-permute-start | bytes 983048 | tf_op jit(solution)/shard_map/ppermute | solution.py:668
  23.0 18.2 %collective-permute-start.3 = (f32[5,128,128]{2,1,0:T(8,128)S(1)}, f32[5,128,128]{2,1,0:T(8,128)S(1)}, u32[]{:S(2)}, u32[]{:S(2)}) collective-permute-start(f32[5,128,128]{2,1,0:T(8,128)S(1)} %get-tuple-element.13.refs_1_), channel_id=1, source_target_pairs={{0,1},{1,2},{2,3},{3,4},{4,5},{5,6},{6,7},{7,8},{8,9},{9,10},{10,1... | collective-permute-start | bytes 983048 | tf_op jit(solution)/shard_map/ppermute | solution.py:667
  54.5 9.0 %collective-permute-start.6 = (f32[144,128]{1,0:T(8,128)S(1)}, f32[144,128]{1,0:T(8,128)S(1)}, u32[]{:S(2)}, u32[]{:S(2)}) collective-permute-start(f32[144,128]{1,0:T(8,128)S(1)} %near_other.1.table), channel_id=1, source_target_pairs={{0,1},{1,2},{2,3},{3,0},{4,5},{5,6},{6,7},{7,4},{8,9},{9,10},{10,1... | collective-permute-start | bytes 221192 | tf_op jit(solution)/shard_map/ppermute | solution.py:28
  55.7 9.0 %collective-permute-start.5 = (f32[144,128]{1,0:T(8,128)S(1)}, f32[144,128]{1,0:T(8,128)S(1)}, u32[]{:S(2)}, u32[]{:S(2)}) collective-permute-start(f32[144,128]{1,0:T(8,128)S(1)} %near_other.1.table), channel_id=1, source_target_pairs={{0,4},{4,8},{8,12},{12,16},{16,20},{20,24},{24,28},{28,0},{1,5},{5... | collective-permute-start | bytes 221192 | tf_op jit(solution)/shard_map/ppermute | solution.py:28
  63.4 4.7 %collective-permute-start.7 = (f32[144,128]{1,0:T(8,128)S(1)}, f32[144,128]{1,0:T(8,128)S(1)}, u32[]{:S(2)}, u32[]{:S(2)}) collective-permute-start(f32[144,128]{1,0:T(8,128)S(1)} %collective-permute-done.6.behind_y), channel_id=1, source_target_pairs={{0,4},{4,8},{8,12},{12,16},{16,20},{20,24},{24,28},{28,0},{1,5},{5... | collective-permute-start | bytes 221192 | tf_op jit(solution)/shard_map/ppermute | solution.py:28

commit v11 on v9

--- a/solution.py
+++ b/solution.py
@@ -16,7 +16,8 @@
 EXTRA = 16
 UNITS = 5
 OWN_GROUP = 16
-OTHER_GROUP = 16
+OTHER_GROUP = 32
+EXTRA_GROUP = 16
 VMEM_LIMIT = 24 << 20
 BF16 = jnp.bfloat16
 F32 = jnp.float32
@@ -402,9 +403,10 @@
         box, row = extra(item)
         return plan[row + k, jnp.minimum(box, boxes - 1)]
 
-    iterations = (sum(counts) + OTHER_GROUP - 1) // OTHER_GROUP
+    iterations = (sum(counts) + EXTRA_GROUP - 1) // EXTRA_GROUP
+    some = totals.at[0:EXTRA_GROUP]
     run_items(
-        lambda item: extra(item)[0], extra_source, 2, iterations, turned, sfeat, sflux, sums, totals
+        lambda item: extra(item)[0], extra_source, 2, iterations, turned, sfeat, sflux, sums, some
     )
     out[0:boxes, :] = sums[0:boxes, :] * (1.0 / math.sqrt(near * LANES))
 

time: 69.7 us -> 69.3 us (level)
  no operation moved by 1% of the time
where the time goes in v11:
time: 69.3 us; the launch traced here: 69 us
  Pallas kernels  40.9 us (59%)
  starting transfers between devices  18.5 us (27%)
  waiting for transfers between devices  6.31 us (9%)
  other arithmetic  1.81 us (3%)
  between operations  0.75 us (1%)
    pallas_call x1, Pallas kernels, near_own(): pl.pallas_call(lambda *refs: near_own_kernel(near, *refs), out_shape=(plt...  13.6 us
    pallas_call x1, Pallas kernels, near_other(): pl.pallas_call(lambda *refs: near_other_kernel(near, *refs), out_shape=pl...  13 us
    ppermute x5, starting transfers between devices, shifted(): return lax.ppermute(value, axis, pairs)  10.9 us
    pallas_call x4, Pallas kernels, scatter(): pl.pallas_call(lambda *refs: scatter_kernel(first, last, (rows, cols, hig...  9.13 us
    ppermute x5, waiting for transfers between devices, shifted(): return lax.ppermute(value, axis, pairs)  6.3 us
    pallas_call x4, Pallas kernels, lookup_call(): pl.pallas_call(kernel, out_shape=out_shape, in_specs=[vmem] * len(args),...  5.22 us
    ppermute x1, starting transfers between devices, shards(): lower = lax.ppermute(boxed, both, [(i, i + 1) for i in range(total - 1)])  4.57 us
    another operation x2, other arithmetic, shards(): tile = jnp.stack([slot, elevation, potential, normal_flux])  1.81 us
  transfers between devices with their start and end apart: 8, of which 3 were waited for; matrix products, arithmetic and copies ran while one was open for 0% of the time, Pallas kernels for 33%

profile of v11, /device:TPU:0, one launch (start us, length us, event | category | flops | bytes accessed | tf_op | source)
XLA Modules:
  0.0 69.0 jit_solution(17419936872534718139)
XLA Ops:
  0.6 0.9 %convert_bitcast_fusion = f32[1,64,256]{2,1,0:T(8,128)S(1)} fusion(s32[64,256]{1,0:T(8,128)} %param.10, s32[64,256]{1,0:T(8,128)} %param.9), kind=kLoop, calls=%fused_computation.1 | loop fusion | flops 49152 | bytes 196608 | tf_op jit(solution)/shard_map/stack | solution.py:655
  1.5 0.9 %pad_maximum_fusion.refs_0_.refs_4_.tile = f32[4,64,256]{2,1,0:T(8,128)S(1)} fusion(f32[1,64,256]{2,1,0:T(8,128)} %bitcast.7, f32[1,64,256]{2,1,0:T(8,128)} %bitcast.8, f32[1,64,256]{2,1,0:T(8,128)} %bitcast.9, f32[1,64,256]{2,1,0:T(8,128)S(1)} %convert_bitcast_fusion), kind=kLoop, calls=%fused_computation | loop fusion | flops 196608 | bytes 524288 | tf_op jit(solution)/shard_map/stack | solution.py:655
  2.4 5.1 %collective-permute-start.1 = (f32[4,64,256]{2,1,0:T(8,128)S(1)}, f32[4,64,256]{2,1,0:T(8,128)S(1)}, u32[]{:S(2)}, u32[]{:S(2)}) collective-permute-start(f32[4,64,256]{2,1,0:T(8,128)S(1)} %pad_maximum_fusion.refs_0_.refs_4_.tile), channel_id=1, source_target_pairs={{0,3},{1,0},{2,1},{3,2},{4,7},{5,4},{6,5},{7,6},{8,11},{9,8},{10,9... | collective-permute-start | bytes 786440 | tf_op jit(solution)/shard_map/ppermute | solution.py:29
  7.6 1.6 %collective-permute-start = (f32[4,64,256]{2,1,0:T(8,128)S(1)}, f32[4,64,256]{2,1,0:T(8,128)S(1)}, u32[]{:S(2)}, u32[]{:S(2)}) collective-permute-start(f32[4,64,256]{2,1,0:T(8,128)S(1)} %pad_maximum_fusion.refs_0_.refs_4_.tile), channel_id=1, source_target_pairs={{0,28},{4,0},{8,4},{12,8},{16,12},{20,16},{24,20},{28,24},{1,29},{... | collective-permute-start | bytes 786440 | tf_op jit(solution)/shard_map/ppermute | solution.py:29
  9.2 0.7 copy-done
  9.9 1.7 %scatter_first.1 = (f32[384,256]{1,0:T(8,128)S(1)}, s32[16,128]{1,0:T(8,128)S(1)}) custom-call(f32[4,64,256]{2,1,0:T(8,128)S(1)} %pad_maximum_fusion.refs_0_.refs_4_.tile, s32[8,128]{1,0:T(8,128)S(1)} %bitcast.6), custom_call_target="tpu_custom_call" | custom-call | flops 1610612736 | bytes 1048576 | tf_op jit(solution)/shard_map/scatter_first/pallas_call | solution.py:168
  11.5 1.6 %collective-permute-done.1.refs_0_.ahead_y = f32[4,64,256]{2,1,0:T(8,128)S(1)} collective-permute-done((f32[4,64,256]{2,1,0:T(8,128)S(1)}, f32[4,64,256]{2,1,0:T(8,128)S(1)}, u32[]{:S(2)}, u32[]{:S(2)}) %collective-permute-start.1) | collective-permute-done | bytes 262176 | tf_op jit(solution)/shard_map/ppermute | solution.py:29
  13.1 1.0 %collective-permute-start.2 = (f32[4,64,256]{2,1,0:T(8,128)S(1)}, f32[4,64,256]{2,1,0:T(8,128)S(1)}, u32[]{:S(2)}, u32[]{:S(2)}) collective-permute-start(f32[4,64,256]{2,1,0:T(8,128)S(1)} %collective-permute-done.1.refs_0_.ahead_y), channel_id=1, source_target_pairs={{0,28},{4,0},{8,4},{12,8},{16,12},{20,16},{24,20},{28,24},{1,29},{... | collective-permute-start | bytes 786440 | tf_op jit(solution)/shard_map/ppermute | solution.py:29
  14.2 1.4 %scatter.2.refs_1_ = f32[384,256]{1,0:T(8,128)S(1)} custom-call(f32[4,64,256]{2,1,0:T(8,128)S(1)} %collective-permute-done.refs_0_.ahead_x, f32[384,256]{1,0:T(8,128)S(1)} %get-tuple-element.12.refs_1_), custom_call_target="tpu_custom_call" | custom-call | flops 1610612736 | bytes 1048576 | tf_op jit(solution)/shard_map/scatter/pallas_call | solution.py:168
  15.6 2.7 %scatter.3.refs_1_ = f32[384,256]{1,0:T(8,128)S(1)} custom-call(f32[4,64,256]{2,1,0:T(8,128)S(1)} %collective-permute-done.1.refs_0_.ahead_y, f32[384,256]{1,0:T(8,128)S(1)} %scatter.2.refs_1_), custom_call_target="tpu_custom_call" | custom-call | flops 1610612736 | bytes 1048576 | tf_op jit(solution)/shard_map/scatter/pallas_call | solution.py:168
  18.3 3.4 %scatter_last.1 = (f32[384,256]{1,0:T(8,128)}, f32[5,128,128]{2,1,0:T(8,128)S(1)}) custom-call(f32[4,64,256]{2,1,0:T(8,128)S(1)} %collective-permute-done.2.refs_0_, f32[384,256]{1,0:T(8,128)S(1)} %scatter.3.refs_1_), custom_call_target="tpu_custom_call" | custom-call | flops 1610612736 | bytes 1048576 | tf_op jit(solution)/shard_map/scatter_last/pallas_call | solution.py:168
  21.7 1.3 %collective-permute-start.4 = (f32[5,128,128]{2,1,0:T(8,128)S(1)}, f32[5,128,128]{2,1,0:T(8,128)S(1)}, u32[]{:S(2)}, u32[]{:S(2)}) collective-permute-start(f32[5,128,128]{2,1,0:T(8,128)S(1)} %get-tuple-element.13.refs_1_), channel_id=1, source_target_pairs={{1,0},{2,1},{3,2},{4,3},{5,4},{6,5},{7,6},{8,7},{9,8},{10,9},{11,1... | collective-permute-start | bytes 983048 | tf_op jit(solution)/shard_map/ppermute | solution.py:670
  23.0 4.6 %collective-permute-start.3 = (f32[5,128,128]{2,1,0:T(8,128)S(1)}, f32[5,128,128]{2,1,0:T(8,128)S(1)}, u32[]{:S(2)}, u32[]{:S(2)}) collective-permute-start(f32[5,128,128]{2,1,0:T(8,128)S(1)} %get-tuple-element.13.refs_1_), channel_id=1, source_target_pairs={{0,1},{1,2},{2,3},{3,4},{4,5},{5,6},{6,7},{7,8},{8,9},{9,10},{10,1... | collective-permute-start | bytes 983048 | tf_op jit(solution)/shard_map/ppermute | solution.py:669
  27.5 13.6 %near_own.1 = (f32[136,128]{1,0:T(8,128)S(1)}, bf16[129,128,32]{2,1,0:T(8,128)(2,1)S(1)}) custom-call(s32[16,128]{1,0:T(8,128)S(1)} %get-tuple-element.11.refs_0_, f32[5,128,128]{2,1,0:T(8,128)S(1)} %get-tuple-element.13.refs_1_), custom_call_target="tpu_custom_call" | custom-call | flops 2147483648 | bytes 1048576 | tf_op jit(solution)/shard_map/near_own/pallas_call | solution.py:449
  41.2 0.0 collective-permute-done.4.refs_3_
  41.2 13.0 %near_other.1.table = f32[144,128]{1,0:T(8,128)S(1)} custom-call(s32[16,128]{1,0:T(8,128)S(1)} %get-tuple-element.11.refs_0_, f32[5,128,128]{2,1,0:T(8,128)S(1)} %get-tuple-element.13.refs_1_, f32[5,128,128]{2,1,0:T(8,128)S(1)} %collective-permute-done.3.refs_2_, f32[5,128,128]{2,1,0:T(8,128)S(1)} %collective-permute-done.4.refs_3_, ...), custom_call_target="tpu_custom_call" | custom-call | flops 2147483648 | bytes 1048576 | tf_op jit(solution)/shard_map/near_other/pallas_call | solution.py:468
  54.2 3.2 %collective-permute-start.5 = (f32[144,128]{1,0:T(8,128)S(1)}, f32[144,128]{1,0:T(8,128)S(1)}, u32[]{:S(2)}, u32[]{:S(2)}) collective-permute-start(f32[144,128]{1,0:T(8,128)S(1)} %near_other.1.table), channel_id=1, source_target_pairs={{0,4},{4,8},{8,12},{12,16},{16,20},{20,24},{24,28},{28,0},{1,5},{5... | collective-permute-start | bytes 221192 | tf_op jit(solution)/shard_map/ppermute | solution.py:29
  57.3 1.7 %collective-permute-start.7 = (f32[144,128]{1,0:T(8,128)S(1)}, f32[144,128]{1,0:T(8,128)S(1)}, u32[]{:S(2)}, u32[]{:S(2)}) collective-permute-start(f32[144,128]{1,0:T(8,128)S(1)} %near_other.1.table), channel_id=1, source_target_pairs={{0,5},{1,6},{2,7},{3,4},{4,9},{5,10},{6,11},{7,8},{8,13},{9,14},{1... | collective-permute-start | bytes 221192 | tf_op jit(solution)/shard_map/ppermute | solution.py:682
  59.0 0.7 %lookup_own.1.partial = f32[64,256]{1,0:T(8,128)S(1)} custom-call(f32[4,64,256]{2,1,0:T(8,128)S(1)} %pad_maximum_fusion.refs_0_.refs_4_.tile, f32[144,128]{1,0:T(8,128)S(1)} %near_other.1.table), custom_call_target="tpu_custom_call" | custom-call | flops 268435456 | bytes 524288 | tf_op jit(solution)/shard_map/lookup_own/pallas_call | solution.py:600
  59.8 1.3 %collective-permute-done.5.behind_x = f32[144,128]{1,0:T(8,128)S(1)} collective-permute-done((f32[144,128]{1,0:T(8,128)S(1)}, f32[144,128]{1,0:T(8,128)S(1)}, u32[]{:S(2)}, u32[]{:S(2)}) %collective-permute-start.5) | collective-permute-done | bytes 73760 | tf_op jit(solution)/shard_map/ppermute | solution.py:29
  61.1 0.8 %lookup_x.1 = (f32[64,256]{1,0:T(8,128)S(1)}, f32[2,64,256]{2,1,0:T(8,128)S(1)}) custom-call(f32[4,64,256]{2,1,0:T(8,128)S(1)} %pad_maximum_fusion.refs_0_.refs_4_.tile, f32[4,64,256]{2,1,0:T(8,128)S(1)} %collective-permute-done.refs_0_.ahead_x, f32[64,256]{1,0:T(8,128)S(1)} %lookup_own.1.partial, f32[144,128]{1,0:T(8,128)S(1)} %collective-permute-done.5.behind_x), custom_call_target="tpu_custom_call" | custom-call | flops 268435456 | bytes 524288 | tf_op jit(solution)/shard_map/lookup_x/pallas_call | solution.py:600
  61.9 3.3 %collective-permute-done.6.behind_y = f32[144,128]{1,0:T(8,128)S(1)} collective-permute-done((f32[144,128]{1,0:T(8,128)S(1)}, f32[144,128]{1,0:T(8,128)S(1)}, u32[]{:S(2)}, u32[]{:S(2)}) %collective-permute-start.6) | collective-permute-done | bytes 73760 | tf_op jit(solution)/shard_map/ppermute | solution.py:29
  65.3 1.7 %lookup_y.1 = (f32[64,256]{1,0:T(8,128)S(1)}, f32[2,64,256]{2,1,0:T(8,128)S(1)}) custom-call(f32[4,64,256]{2,1,0:T(8,128)S(1)} %pad_maximum_fusion.refs_0_.refs_4_.tile, f32[4,64,256]{2,1,0:T(8,128)S(1)} %collective-permute-done.1.refs_0_.ahead_y, f32[64,256]{1,0:T(8,128)S(1)} %get-tuple-element.17.partial, f32[144,128]{1,0:T(8,128)S(1)} %collective-permute-done.6.behind_y), custom_call_target="tpu_custom_call" | custom-call | flops 268435456 | bytes 524288 | tf_op jit(solution)/shard_map/lookup_y/pallas_call | solution.py:600
  67.0 2.0 %lookup_xy.1 = (f32[64,256]{1,0:T(8,128)}, f32[64,256]{1,0:T(8,128)}) custom-call(f32[4,64,256]{2,1,0:T(8,128)S(1)} %pad_maximum_fusion.refs_0_.refs_4_.tile, f32[2,64,256]{2,1,0:T(8,128)S(1)} %get-tuple-element.16.row_slopes, f32[2,64,256]{2,1,0:T(8,128)S(1)} %get-tuple-element.18.col_slopes, f32[64,256]{1,0:T(8,128)S(1)} %get-tuple-element.19.partial, ...), custom_call_target="tpu_custom_call" | custom-call | flops 268435456 | bytes 524288 | tf_op jit(solution)/shard_map/lookup_xy/pallas_call | solution.py:600
  (6 shorter events, 0.0 us)
Async XLA Ops:
  2.4 10.7 %collective-permute-start.1 = (f32[4,64,256]{2,1,0:T(8,128)S(1)}, f32[4,64,256]{2,1,0:T(8,128)S(1)}, u32[]{:S(2)}, u32[]{:S(2)}) collective-permute-start(f32[4,64,256]{2,1,0:T(8,128)S(1)} %pad_maximum_fusion.refs_0_.refs_4_.tile), channel_id=1, source_target_pairs={{0,3},{1,0},{2,1},{3,2},{4,7},{5,4},{6,5},{7,6},{8,11},{9,8},{10,9... | collective-permute-start | bytes 786440 | tf_op jit(solution)/shard_map/ppermute | solution.py:29
  7.6 6.6 %collective-permute-start = (f32[4,64,256]{2,1,0:T(8,128)S(1)}, f32[4,64,256]{2,1,0:T(8,128)S(1)}, u32[]{:S(2)}, u32[]{:S(2)}) collective-permute-start(f32[4,64,256]{2,1,0:T(8,128)S(1)} %pad_maximum_fusion.refs_0_.refs_4_.tile), channel_id=1, source_target_pairs={{0,28},{4,0},{8,4},{12,8},{16,12},{20,16},{24,20},{28,24},{1,29},{... | collective-permute-start | bytes 786440 | tf_op jit(solution)/shard_map/ppermute | solution.py:29
  9.2 0.7 copy-start
  13.1 5.1 %collective-permute-start.2 = (f32[4,64,256]{2,1,0:T(8,128)S(1)}, f32[4,64,256]{2,1,0:T(8,128)S(1)}, u32[]{:S(2)}, u32[]{:S(2)}) collective-permute-start(f32[4,64,256]{2,1,0:T(8,128)S(1)} %collective-permute-done.1.refs_0_.ahead_y), channel_id=1, source_target_pairs={{0,28},{4,0},{8,4},{12,8},{16,12},{20,16},{24,20},{28,24},{1,29},{... | collective-permute-start | bytes 786440 | tf_op jit(solution)/shard_map/ppermute | solution.py:29
  21.7 19.5 %collective-permute-start.4 = (f32[5,128,128]{2,1,0:T(8,128)S(1)}, f32[5,128,128]{2,1,0:T(8,128)S(1)}, u32[]{:S(2)}, u32[]{:S(2)}) collective-permute-start(f32[5,128,128]{2,1,0:T(8,128)S(1)} %get-tuple-element.13.refs_1_), channel_id=1, source_target_pairs={{1,0},{2,1},{3,2},{4,3},{5,4},{6,5},{7,6},{8,7},{9,8},{10,9},{11,1... | collective-permute-start | bytes 983048 | tf_op jit(solution)/shard_map/ppermute | solution.py:670
  23.0 18.2 %collective-permute-start.3 = (f32[5,128,128]{2,1,0:T(8,128)S(1)}, f32[5,128,128]{2,1,0:T(8,128)S(1)}, u32[]{:S(2)}, u32[]{:S(2)}) collective-permute-start(f32[5,128,128]{2,1,0:T(8,128)S(1)} %get-tuple-element.13.refs_1_), channel_id=1, source_target_pairs={{0,1},{1,2},{2,3},{3,4},{4,5},{5,6},{6,7},{7,8},{8,9},{9,10},{10,1... | collective-permute-start | bytes 983048 | tf_op jit(solution)/shard_map/ppermute | solution.py:669
  54.2 7.0 %collective-permute-start.5 = (f32[144,128]{1,0:T(8,128)S(1)}, f32[144,128]{1,0:T(8,128)S(1)}, u32[]{:S(2)}, u32[]{:S(2)}) collective-permute-start(f32[144,128]{1,0:T(8,128)S(1)} %near_other.1.table), channel_id=1, source_target_pairs={{0,4},{4,8},{8,12},{12,16},{16,20},{20,24},{24,28},{28,0},{1,5},{5... | collective-permute-start | bytes 221192 | tf_op jit(solution)/shard_map/ppermute | solution.py:29
  57.3 8.0 %collective-permute-start.6 = (f32[144,128]{1,0:T(8,128)S(1)}, f32[144,128]{1,0:T(8,128)S(1)}, u32[]{:S(2)}, u32[]{:S(2)}) collective-permute-start(f32[144,128]{1,0:T(8,128)S(1)} %near_other.1.table), channel_id=1, source_target_pairs={{0,1},{1,2},{2,3},{3,0},{4,5},{5,6},{6,7},{7,4},{8,9},{9,10},{10,1... | collective-permute-start | bytes 221192 | tf_op jit(solution)/shard_map/ppermute | solution.py:29
  57.3 9.6 %collective-permute-start.7 = (f32[144,128]{1,0:T(8,128)S(1)}, f32[144,128]{1,0:T(8,128)S(1)}, u32[]{:S(2)}, u32[]{:S(2)}) collective-permute-start(f32[144,128]{1,0:T(8,128)S(1)} %near_other.1.table), channel_id=1, source_target_pairs={{0,5},{1,6},{2,7},{3,4},{4,9},{5,10},{6,11},{7,8},{8,13},{9,14},{1... | collective-permute-start | bytes 221192 | tf_op jit(solution)/shard_map/ppermute | solution.py:682
